TPU v7x, 32 devices: a whole 2x2x4 slice. The times are simulated.
32 devices in a mesh: req: 8 (over z, x), seq: 4 (over y, core).
Axes of the slice: x: 2, y: 2, z: 4, core: 2. Of those that a mesh axis runs over, the one named last changes fastest.
Arguments:
- pool_states: float32 [104, 64, 64, 128], P('req', 'seq'), may hold values from -6 to 6
- inner_window: bfloat16 [104, 3, 4096], P('req', None, 'seq'), may hold values from -6 to 6
- state_window: bfloat16 [104, 3, 256], P('req', None, 'seq'), may hold values from -6 to 6
- move_plan: int32 [104, 2], P('req'), may hold values from 0 to 12, as said below
- active_mask: int32 [104], P('req'), may hold values 0 or 1
- inputs_inner: bfloat16 [8, 2048, 4096], P('req', 'seq'), may hold values from -6 to 6
- inputs_state: bfloat16 [8, 2048, 256], P('req', 'seq'), may hold values from -6 to 6
- gate_rows: bfloat16 [8, 2048, 4096], P('req', 'seq'), may hold values from -6 to 6
- step_raw: bfloat16 [8, 2048, 64], P('req', 'seq'), may hold values from -8 to 60
- lengths: int32 [8], P('req'), may hold values from 4 to 2048
- conv_weight: float32 [4, 4352], replicated, may hold values from -3 to 3
- conv_bias: float32 [4352], replicated, may hold values from -3 to 3
- step_bias: float32 [64], replicated, may hold values from -3.3 to -2.7
- decay_log: float32 [64], replicated, may hold values from -10 to 0
- skip_weight: float32 [64], replicated, may hold values from 0.5 to 1.5
- norm_weight: float32 [4096], replicated, may hold values from 0.25 to 1.75
Outputs:
- new_states: float32 [104, 64, 64, 128], P('req', 'seq')
- new_inner_window: bfloat16 [104, 3, 4096], P('req', None, 'seq')
- new_state_window: bfloat16 [104, 3, 256], P('req', None, 'seq')
- mixer_out: bfloat16 [8, 2048, 4096], P('req', 'seq')
Inputs may be any that keep to these rules, and one draw needn't show every extreme that they name: `move_plan`: every pair of a destination index along req and a slot 0 .. 12 is named exactly once; the rows of one device name one destination at most 4 times, and some destination exactly 4 times.
All inputs are finite; a program needn't handle non-finite values. No bound on the sum of `active_mask` on one device may be relied on, other than what follows from the above.
Results may differ from a plain program's by a relative error of at most 0.0087.
Values may be sent and summed in bfloat16 or wider, within the bound.
No kernel may reach another device: no remote copies, remote signals or barrier semaphores. Data moves between devices by JAX's collectives and lax.ppermute only.
A program may use at most 192 MiB of HBM per device.

v0:
```python
import jax
import jax.numpy as jnp
from jax import lax
from jax.sharding import PartitionSpec as P

HEAD_DIM = 64
STATE_DIM = 128
KERNEL = 4
BLOCK_LEN = 256
PREFILLS = 1
INNER_DIM = 4096


EPSILON = 1e-05


def shifted(value, axis, steps):
    count = lax.axis_size(axis)
    leading, last = (max(0, -steps), min(count, count - steps))
    return lax.ppermute(value, axis, [(source, source + steps) for source in range(leading, last)])


def entering(shard, axis, combine, identity):
    peers, index = (lax.axis_size(axis), lax.axis_index(axis))
    everything = jax.tree.map(lambda part: lax.all_gather(part, axis), shard)
    start = jax.tree.map(
        lambda part, zero: jnp.broadcast_to(jnp.asarray(zero, part.dtype), part.shape),
        shard,
        identity,
    )

    def hop(k, before):
        reached = k < index
        new = combine(before, jax.tree.map(lambda part: part[k], everything))
        return jax.tree.map(lambda a, b: jnp.where(reached, a, b), new, before)

    return lax.fori_loop(0, peers, hop, start)


def conv_silu(window, new_rows, weight, bias_values):
    extended = jnp.concatenate([window, new_rows], axis=1).astype(jnp.float32)
    length = new_rows.shape[1]
    running = jnp.zeros(new_rows.shape, jnp.float32) + bias_values
    for offset in range(weight.shape[0]):
        running = running + weight[offset] * extended[:, offset : offset + length]
    return jax.nn.silu(running).astype(jnp.bfloat16)


def block_local(value_rows, write_rows, read_rows, step_rows, decay_rates):
    log_decay = step_rows * decay_rates
    running_log = jnp.cumsum(log_decay, axis=0)
    scores = lax.dot_general(
        read_rows, write_rows, (((1,), (1,)), ((), ())), preferred_element_type=jnp.float32
    )
    log_heads = running_log.T
    log_gaps = log_heads[:, :, None] - log_heads[:, None, :]
    positions = jnp.arange(running_log.shape[0])
    causal = positions[:, None] >= positions[None, :]
    decays = jnp.where(causal, jnp.exp(jnp.where(causal, log_gaps, 0.0)), 0.0)
    weights = (scores[None] * decays * step_rows.T[:, None, :]).astype(jnp.bfloat16)
    intra_part = jnp.einsum("hts,shp->thp", weights, value_rows, preferred_element_type=jnp.float32)
    to_end = jnp.exp(running_log[-1:] - running_log) * step_rows
    scaled = (to_end[:, :, None] * value_rows.astype(jnp.float32)).astype(jnp.bfloat16)
    block_state = jnp.einsum("shp,sn->hpn", scaled, write_rows, preferred_element_type=jnp.float32)
    return (intra_part, block_state, running_log)


def local_parts(value_rows, write_rows, read_rows, step_rows, decay_rates):
    batch_size = value_rows.shape[0]
    block_count = value_rows.shape[1] // BLOCK_LEN

    def to_items(source):
        return source.reshape((batch_size * block_count, BLOCK_LEN) + source.shape[2:])

    def from_items(source):
        return source.reshape((batch_size, block_count) + source.shape[1:])

    def one_item(pieces):
        return block_local(pieces[0], pieces[1], pieces[2], pieces[3], decay_rates)

    results = lax.map(
        one_item,
        (to_items(value_rows), to_items(write_rows), to_items(read_rows), to_items(step_rows)),
    )
    return tuple((from_items(result) for result in results))


def blocked(source):
    return source.reshape(
        (source.shape[0], source.shape[1] // BLOCK_LEN, BLOCK_LEN) + source.shape[2:]
    )


def fold_states(initial, block_states, running_logs):

    def fold_advance(carried, pieces):
        return (jnp.exp(pieces[1][:, -1])[:, :, None, None] * carried + pieces[0], None)

    final_state, unused = lax.scan(
        fold_advance, initial, (jnp.moveaxis(block_states, 1, 0), jnp.moveaxis(running_logs, 1, 0))
    )
    return final_state


def run_states(initial, block_states, running_logs, read_blocks):

    def run_advance(carried, pieces):
        block_state, running_log, read_block = pieces
        inter_part = (
            jnp.einsum(
                "bqn,bhpn->bqhp",
                read_block.astype(jnp.float32),
                carried,
                precision=lax.Precision.HIGHEST,
            )
            * jnp.exp(running_log)[:, :, :, None]
        )
        updated = jnp.exp(running_log[:, -1])[:, :, None, None] * carried + block_state
        return (updated, inter_part)

    final_state, inter_parts = lax.scan(
        run_advance,
        initial,
        (
            jnp.moveaxis(block_states, 1, 0),
            jnp.moveaxis(running_logs, 1, 0),
            jnp.moveaxis(read_blocks, 1, 0),
        ),
    )
    return (final_state, jnp.moveaxis(inter_parts, 0, 1))


def assemble(intra_part, inter_parts, value_rows, skip_own, valid_rows):
    combined = (intra_part + inter_parts).reshape(value_rows.shape) + skip_own[
        :, None
    ] * value_rows.astype(jnp.float32)
    combined = combined * valid_rows[:, :, None, None]
    return combined.astype(jnp.bfloat16).reshape(value_rows.shape[0], value_rows.shape[1], -1)


def gated_norm(payload_array, gate_part, norm_weight):
    gated_rows = payload_array.astype(jnp.float32) * jax.nn.silu(gate_part.astype(jnp.float32))
    norm_scale = lax.rsqrt(jnp.mean(gated_rows * gated_rows, axis=-1, keepdims=True) + EPSILON)
    return (gated_rows * norm_scale * norm_weight).astype(jnp.bfloat16)


def last_rows(raw_rows, positions):

    def pick_rows(source_rows, indices):
        return jnp.take(source_rows, indices, axis=0)

    return jax.vmap(pick_rows)(raw_rows, positions)


def migrate(pool_states, inner_window, state_window, move_plan, active_mask):
    slot_count = pool_states.shape[0]
    peer_count = lax.axis_size("req")
    capacity = (2 * slot_count + peer_count - 1) // peer_count
    keep_flag = active_mask.astype(jnp.float32)
    target_device = move_plan[:, 0]
    target_slot = move_plan[:, 1]
    slot_index = jnp.arange(slot_count, dtype=jnp.int32)
    earlier = (target_device[None, :] == target_device[:, None]) & (
        slot_index[None, :] < slot_index[:, None]
    )
    send_rank = jnp.sum(earlier.astype(jnp.int32), axis=1)
    matches = (target_device[None, None, :] == jnp.arange(peer_count)[:, None, None]) & (
        send_rank[None, None, :] == jnp.arange(capacity)[None, :, None]
    )
    source_slot = jnp.sum(jnp.where(matches, slot_index[None, None, :], 0), axis=2).reshape(-1)
    filled = jnp.any(matches, axis=2).reshape(-1)
    slot_tags = jnp.where(filled, jnp.take(target_slot, source_slot), -1).reshape(
        peer_count, capacity
    )

    def packed(source):
        taken_rows = jnp.take(source, source_slot, axis=0)
        return taken_rows.reshape((peer_count, capacity) + source.shape[1:])

    send_states = packed(pool_states * keep_flag[:, None, None, None])
    send_inner = packed(inner_window.astype(jnp.float32) * keep_flag[:, None, None])
    send_outer = packed(state_window.astype(jnp.float32) * keep_flag[:, None, None])
    got_states, got_inner, got_outer, got_tags = (
        lax.all_to_all(send_states, "req", split_axis=0, concat_axis=0, tiled=True),
        lax.all_to_all(send_inner, "req", split_axis=0, concat_axis=0, tiled=True),
        lax.all_to_all(send_outer, "req", split_axis=0, concat_axis=0, tiled=True),
        lax.all_to_all(slot_tags, "req", split_axis=0, concat_axis=0, tiled=True),
    )
    flat_tags = got_tags.reshape(-1)
    arrivals = jnp.arange(flat_tags.shape[0], dtype=jnp.int32)
    chosen = jnp.sum(
        jnp.where(flat_tags[None, :] == slot_index[:, None], arrivals[None, :], 0), axis=1
    )

    def placed(source):
        return jnp.take(source.reshape((-1,) + source.shape[2:]), chosen, axis=0)

    return (
        placed(got_states),
        placed(got_inner).astype(jnp.bfloat16),
        placed(got_outer).astype(jnp.bfloat16),
    )


def combine_carries(earlier_part, later_part):
    return (
        earlier_part[0] * later_part[0],
        later_part[1] + later_part[0][:, :, None, None] * earlier_part[1],
    )


def on_device(
    pool_states,
    inner_window,
    state_window,
    move_plan,
    active_mask,
    inputs_inner,
    inputs_state,
    gate_rows,
    step_raw,
    lengths,
    conv_weight,
    conv_bias,
    step_bias,
    decay_log,
    skip_weight,
    norm_weight,
):
    moved_states, moved_inner, moved_outer = migrate(
        pool_states, inner_window, state_window, move_plan, active_mask
    )
    chain_index = lax.axis_index("seq")
    chain_size = lax.axis_size("seq")
    local_length = inputs_inner.shape[1]
    local_heads = moved_states.shape[1]
    decay_rates = -jnp.exp(decay_log)
    offsets = jnp.arange(KERNEL - 1, dtype=jnp.int32)
    raw_rows = jnp.concatenate([inputs_inner, inputs_state], axis=2)
    earlier_rows = shifted(raw_rows[:, local_length - KERNEL + 1 :], "seq", 1)
    initial, head_inner, head_outer = (
        lax.all_gather(moved_states[:PREFILLS], "seq", axis=1, tiled=True),
        lax.all_gather(moved_inner[:PREFILLS].astype(jnp.float32), "seq", axis=2, tiled=True),
        lax.all_gather(moved_outer[:PREFILLS].astype(jnp.float32), "seq", axis=2, tiled=True),
    )
    first_window = jnp.concatenate([head_inner, head_outer], axis=2).astype(jnp.bfloat16)
    window = jnp.where(chain_index == 0, first_window, earlier_rows)
    mixed_rows = conv_silu(window, raw_rows, conv_weight, conv_bias)
    positions = chain_index * local_length + jnp.arange(local_length, dtype=jnp.int32)
    valid_rows = (positions[None, :] < lengths[:, None]).astype(jnp.float32)
    step_sizes = jax.nn.softplus(step_raw.astype(jnp.float32) + step_bias) * valid_rows[:, :, None]
    value_rows = mixed_rows[:, :, :INNER_DIM].reshape(PREFILLS, local_length, -1, HEAD_DIM)
    write_rows = mixed_rows[:, :, INNER_DIM : INNER_DIM + STATE_DIM]
    read_rows = mixed_rows[:, :, INNER_DIM + STATE_DIM :]
    intra_part, block_states, running_logs = local_parts(
        value_rows, write_rows, read_rows, step_sizes, decay_rates
    )
    local_end = fold_states(jnp.zeros_like(block_states[:, 0]), block_states, running_logs)
    device_decay = jnp.exp(jnp.sum(step_sizes * decay_rates, axis=1))
    every_decay = lax.all_gather(device_decay[None], "seq", axis=0, tiled=True)
    prior_decay, prior_state = entering(
        (device_decay, local_end),
        "seq",
        combine_carries,
        (jnp.ones_like(device_decay), jnp.zeros_like(local_end)),
    )
    incoming = prior_state + prior_decay[:, :, None, None] * initial
    unused_final, inter_parts = run_states(incoming, block_states, running_logs, blocked(read_rows))
    later_mask = jnp.arange(chain_size)[:, None, None] > chain_index
    suffix = jnp.prod(jnp.where(later_mask, every_decay, 1.0), axis=0)
    whole_decay = jnp.prod(every_decay, axis=0)
    window_pos = lengths[:, None] - (KERNEL - 1) + offsets[None, :] - chain_index * local_length
    inside = ((window_pos >= 0) & (window_pos < local_length)).astype(jnp.float32)
    window_term = (
        last_rows(raw_rows, jnp.clip(window_pos, 0, local_length - 1)).astype(jnp.float32)
        * inside[:, :, None]
    )
    state_sum, inner_sum, outer_sum = (
        lax.psum_scatter(
            local_end * suffix[:, :, None, None], "seq", scatter_dimension=1, tiled=True
        ),
        lax.psum_scatter(window_term[:, :, :INNER_DIM], "seq", scatter_dimension=2, tiled=True),
        lax.psum_scatter(window_term[:, :, INNER_DIM:], "seq", scatter_dimension=2, tiled=True),
    )
    own_decay = lax.dynamic_slice_in_dim(whole_decay, chain_index * local_heads, local_heads, 1)
    final_own = state_sum + own_decay[:, :, None, None] * moved_states[:PREFILLS]
    kept_inner = inner_sum.astype(jnp.bfloat16)
    kept_outer = outer_sum.astype(jnp.bfloat16)
    mixer_rows = assemble(intra_part, inter_parts, value_rows, skip_weight, valid_rows)
    mixer_out = gated_norm(mixer_rows, gate_rows, norm_weight)
    new_states = jnp.concatenate([final_own, moved_states[PREFILLS:]], axis=0)
    new_inner = jnp.concatenate([kept_inner, moved_inner[PREFILLS:]], axis=0)
    new_outer = jnp.concatenate([kept_outer, moved_outer[PREFILLS:]], axis=0)
    return (new_states, new_inner, new_outer, mixer_out)


def solution(mesh):
    return jax.shard_map(
        on_device,
        mesh=mesh,
        in_specs=(
            P("req", "seq", None, None),
            P("req", None, "seq"),
            P("req", None, "seq"),
            P("req", None),
            P("req"),
            P("req", "seq", None),
            P("req", "seq", None),
            P("req", "seq", None),
            P("req", "seq", None),
            P("req"),
            P(),
            P(),
            P(),
            P(),
            P(),
            P(),
        ),
        out_specs=(
            P("req", "seq", None, None),
            P("req", None, "seq"),
            P("req", None, "seq"),
            P("req", "seq", None),
        ),
        check_vma=False,
    )
```

profile of v0, /device:TPU:0, one launch (start us, length us, event | category | flops | bytes accessed | tf_op | source)
XLA Modules:
  0.0 568.2 jit_solution(16587530665239196977)
XLA Ops:
  10.2 7.3 %all-to-all-start = ((s32[8,1,4]{2,1,0:T(1,128)}), s32[8,1,4]{2,1,0:T(1,128)S(1)}, u32[]{:S(2)}, u32[]{:S(2)}) async-start(s32[8,1,4]{2,1,0:T(1,128)} %copy.129), calls=%async_computation | async-start | bytes 8192 | tf_op jit(solution)/shard_map/all_to_all | solution.py:187
  27.0 7.4 %broadcast_multiply_fusion = f32[13,16,64,128]{3,2,1,0:T(8,128)} fusion(f32[13,16,64,128]{3,2,1,0:T(8,128)} %param.24, f32[13]{0:T(128)S(1)} %convert_element_type.130), kind=kLoop, calls=%fused_computation.93 | loop fusion | flops 1703936 | bytes 13631540 | tf_op jit(solution)/shard_map/mul | solution.py:180
  34.4 11.1 %gather_fusion.5 = f32[32,16,64,128]{3,2,1,0:T(8,128)} fusion(f32[13,16,64,128]{3,2,1,0:T(8,128)} %broadcast_multiply_fusion, s32[1024]{0:T(1024)S(1)} %pad_clamp_fusion.1), kind=kCustom, calls=%fused_computation.5 | custom fusion | bytes 33554560 | tf_op jit(solution)/shard_map/jit(_take)/gather | solution.py:177
  46.4 12.4 %broadcast_select_fusion.2 = f32[8,4,16,64,128]{4,3,2,1,0:T(8,128)} fusion(f32[8,4,16,64,128]{4,3,2,1,0:T(8,128)} %bitcast.227, pred[8,4]{1,0:T(8,128)(4,1)S(1)} %copy.130), kind=kLoop, calls=%fused_computation.89 | loop fusion | flops 4194304 | bytes 33554464 | tf_op jit(solution)/shard_map/jit(_take)/select_n | solution.py:177
  61.4 5.8 %all-to-all-start.2 = ((bf16[8,2,384]{2,1,0:T(2,128)(2,1)}), bf16[8,2,384]{2,1,0:T(2,128)(2,1)S(1)}, u32[]{:S(2)}, u32[]{:S(2)}) async-start(bf16[8,2,384]{2,1,0:T(2,128)(2,1)} %reshape.672), calls=%async_computation.2 | async-start | bytes 24576 | tf_op jit(solution)/shard_map/all_to_all | solution.py:186
  67.2 6.5 %all-to-all-done.2 = bf16[8,2,384]{2,1,0:T(2,128)(2,1)S(1)} async-done(((bf16[8,2,384]{2,1,0:T(2,128)(2,1)}), bf16[8,2,384]{2,1,0:T(2,128)(2,1)S(1)}, u32[]{:S(2)}, u32[]{:S(2)}) %all-to-all-start.2) | async-done | bytes 12320 | tf_op jit(solution)/shard_map/all_to_all | solution.py:186
  78.9 6.7 %all-reduce = f32[256]{0:T(256)S(1)} all-reduce(f32[256]{0:T(256)S(1)} %exponential_dynamic-update-slice_fusion), channel_id=2, replica_groups=mesh['req'=8,'seq'=4] {'seq'}, use_global_device_ids=true, to_apply=%add | all-reduce | flops 256 | bytes 2048
  86.1 5.8 %all-to-all-start.3 = ((f32[8,4,16,64,128]{4,3,2,1,0:T(8,128)}), f32[8,4,16,64,128]{4,3,2,1,0:T(8,128)}, u32[]{:S(2)}, u32[]{:S(2)}) async-start(f32[8,4,16,64,128]{4,3,2,1,0:T(8,128)} %broadcast_select_fusion.2), calls=%async_computation.4 | async-start | bytes 33554432 | tf_op jit(solution)/shard_map/all_to_all | solution.py:184
  94.6 5.4 all_gather.21
  101.0 5.4 all_gather.20
  109.6 5.7 %multiply_convert_fusion.5 = bf16[1,512,4352]{2,1,0:T(8,128)(2,1)S(1)} fusion(f32[1,515,4352]{2,1,0:T(8,128)S(1)} %maximum_convert_fusion, f32[4352]{0:T(1024)S(1)} %get-tuple-element.394, f32[4352]{0:T(1024)S(1)} %get-tuple-element.395, f32[4352]{0:T(1024)S(1)} %get-tuple-element.393, f32[4352]{0:T(1024)S(1)} %get-tuple-element.392, f32[4352]{0:T(1024)S(1)} %copy-done.13), kind=kLoop, calls=%fused_computation.80 | loop fusion | flops 28966912 | bytes 40195072 | tf_op jit(solution)/shard_map/convert_element_type | solution.py:46
  119.9 12.6 %reshape.650 = bf16[2,256,64,64]{3,2,1,0:T(8,128)(2,1)} reshape(bf16[1,512,4096]{2,1,0:T(8,128)(2,1)} %slice.132) | data formatting | bytes 8388608 | tf_op jit(solution)/shard_map/reshape;reshape | solution.py:73
  132.5 10.5 %copy.141 = bf16[2,256,64,64]{1,3,2,0:T(8,128)(2,1)} copy(bf16[2,256,64,64]{3,2,1,0:T(8,128)(2,1)} %reshape.650) | data formatting | bytes 8388608 | tf_op jit(solution)/shard_map/while | solution.py:81
  143.9 24.7 %while.53 = (s32[]{:T(128)}, f32[2,256,64,64]{1,3,2,0:T(8,128)}, f32[2,64,64,128]{3,2,1,0:T(8,128)}, f32[2,256,64]{1,2,0:T(8,128)S(1)}, bf16[2,256,64,64]{1,3,2,...) while((s32[]{:T(128)}, f32[2,256,64,64]{1,3,2,0:T(8,128)}, ...), condition=%wide.region_7.8_spmd, body=%wide.region_4.7_spmd.sunk | while | flops 852639936 | bytes 62990296 | solution.py:81
  145.3 8.0 %bitcast_dynamic-update-slice_fusion.8 = f32[2,256,64,64]{1,3,2,0:T(8,128)} fusion(f32[2,256,64,64]{1,3,2,0:T(8,128)} %get-tuple-element.638, s32[]{:T(128)S(6)} %copy.206, f32[64,256]{1,0:T(8,128)S(1)} %bitcast.234, f32[64,256]{1,0:T(8,128)S(1)} %get-tuple-element.606, f32[256,256]{1,0:T(8,128)S(1)} %fusion.80, ...), kind=kOutput, calls=%fused_computation.27.clone.1 | convolution fusion | flops 562036736 | bytes 6816768 | tf_op jit(solution)/shard_map/while/body/eval_jaxpr/hts,shp->thp/dot_general | solution.py:61
  157.6 7.9 %bitcast_dynamic-update-slice_fusion.8 = f32[2,256,64,64]{1,3,2,0:T(8,128)} fusion(f32[2,256,64,64]{1,3,2,0:T(8,128)} %get-tuple-element.638, s32[]{:T(128)S(6)} %copy.206, f32[64,256]{1,0:T(8,128)S(1)} %bitcast.234, f32[64,256]{1,0:T(8,128)S(1)} %get-tuple-element.606, f32[256,256]{1,0:T(8,128)S(1)} %fusion.80, ...), kind=kOutput, calls=%fused_computation.27.clone.1 | convolution fusion | flops 562036736 | bytes 6816768 | tf_op jit(solution)/shard_map/while/body/eval_jaxpr/hts,shp->thp/dot_general | solution.py:61
  168.8 3.9 while.55
  174.5 3.7 copy.158
  179.9 275.0 %all-to-all-done.3 = f32[8,4,16,64,128]{4,3,2,1,0:T(8,128)} async-done(((f32[8,4,16,64,128]{4,3,2,1,0:T(8,128)}), f32[8,4,16,64,128]{4,3,2,1,0:T(8,128)}, u32[]{:S(2)}, u32[]{:S(2)}) %all-to-all-start.3) | async-done | bytes 16777248 | tf_op jit(solution)/shard_map/all_to_all | solution.py:184
  454.9 9.6 %gather_fusion.6 = f32[13,16,64,128]{3,2,1,0:T(8,128)} fusion(f32[32,16,64,128]{3,2,1,0:T(8,128)} %bitcast.38, s32[1024]{0:T(1024)S(1)} %pad_clamp_fusion), kind=kCustom, calls=%fused_computation.6 | custom fusion | bytes 13631540 | tf_op jit(solution)/shard_map/jit(_take)/gather | solution.py:196
  464.5 7.4 %broadcast_select_fusion.3 = f32[13,16,64,128]{3,2,1,0:T(8,128)} fusion(f32[13,16,64,128]{3,2,1,0:T(8,128)} %gather_fusion.6, pred[13]{0:T(512)(128)(4,1)S(1)} %compare_and_fusion.2), kind=kLoop, calls=%fused_computation.92 | loop fusion | flops 1703936 | bytes 13631501 | tf_op jit(solution)/shard_map/jit(_take)/select_n | solution.py:196
  476.8 8.7 %while.56 = (s32[]{:T(128)}, f32[1,64]{1,0:T(1,128)S(1)}, f32[1,64,64,128]{3,2,1,0:T(8,128)S(1)}, s32[]{:T(128)}, f32[4,1,64]{2,1,0:T(1,128)S(1)}, /*index=5*/f32[4,1,64,64,128]{4,3,2,1,0:T(8,128)}, s32[]{:T(128)}, s32[]{:T(128)}) while((s32[]{:T(128)}, f32[1,64]{1,0:T(1,128)S(1)}, f32[1,64,64,128]{3,2,1,0:T(8,128)S(1)}, ...), condition=%wide.region_17.18_spmd.clone, body=%wide.region_16.17_spmd.clone.sunk | while | flops 2097348 | bytes 6293119 | solution.py:37
  485.5 3.6 slice-done
  489.1 3.5 pad_maximum_fusion
  498.0 9.0 %while.54 = (s32[]{:T(128)}, f32[1,64,64,128]{3,2,1,0:T(8,128)S(1)}, f32[2,1,256,64,64]{2,4,3,1,0:T(8,128)}, f32[2,1,256,64]{2,3,1,0:T(8,128)S(1)}, f32[2,1,64,6...) while((s32[]{:T(128)}, f32[1,64,64,128]{3,2,1,0:T(8,128)S(1)}, ...), condition=%wide.region_19.20_spmd, body=%wide.region_18.19_spmd.sunk | while | flops 1612709888 | bytes 29689720 | solution.py:121
  498.1 3.9 bitcast_dynamic-update-slice_fusion.11
  502.6 3.8 bitcast_dynamic-update-slice_fusion.11
  507.0 11.7 %bitcast_add_fusion.3 = f32[2,256,64,64]{1,3,2,0:T(8,128)} fusion(f32[2,256,64,64]{1,3,2,0:T(8,128)} %get-tuple-element.220, f32[2,1,256,64,64]{2,4,3,1,0:T(8,128)} %get-tuple-element.223), kind=kLoop, calls=%fused_computation.85 | loop fusion | flops 2097152 | bytes 25165824 | tf_op jit(solution)/shard_map/add | solution.py:134
  518.7 16.3 %copy.157 = f32[2,256,64,64]{3,2,1,0:T(8,128)} copy(f32[2,256,64,64]{1,3,2,0:T(8,128)} %bitcast_add_fusion.3) | data formatting | bytes 16777216 | tf_op jit(solution)/shard_map/reshape | solution.py:134
  534.9 14.8 %reshape.651 = f32[1,512,4096]{2,1,0:T(8,128)} reshape(f32[2,256,64,64]{3,2,1,0:T(8,128)} %copy.157) | data formatting | bytes 16777216 | tf_op jit(solution)/shard_map/reshape | solution.py:134
  549.7 8.5 %multiply_reduce_fusion = (f32[512]{0:T(512)S(1)}, f32[1,512,4096]{2,1,0:T(8,128)S(1)}) fusion(bf16[1,512,4096]{2,1,0:T(8,128)(2,1)} %param.31, f32[512]{0:T(512)S(1)} %copy-done.15, f32[1,512,4096]{2,1,0:T(8,128)} %reshape.651, bf16[1,512,4352]{2,1,0:T(8,128)(2,1)} %copy-done.6, f32[4096]{0:T(1024)S(1)} %mul.312), kind=kLoop, calls=%fused_computation.87 | loop fusion | flops 29359616 | bytes 25186304 | tf_op jit(solution)/shard_map/reduce_sum | solution.py:143
  558.2 3.5 multiply_convert_fusion.6
  (224 shorter events, 68.4 us)
Async XLA Ops:
  7.2 12.9 %copy-start.8 = (bf16[1,512,256]{2,1,0:T(8,128)(2,1)S(1)}, bf16[1,512,256]{2,1,0:T(8,128)(2,1)}, u32[]{:S(2)}) copy-start(bf16[1,512,256]{2,1,0:T(8,128)(2,1)} %param.30) | copy-start | bytes 786436
  7.2 19.8 %copy-start.20 = (s32[13]{0:T(128)S(1)}, s32[13]{0:T(128)}, u32[]{:S(2)}) copy-start(s32[13]{0:T(128)} %param.28) | copy-start | bytes 160
  10.2 51.2 %all-to-all-start = ((s32[8,1,4]{2,1,0:T(1,128)}), s32[8,1,4]{2,1,0:T(1,128)S(1)}, u32[]{:S(2)}, u32[]{:S(2)}) async-start(s32[8,1,4]{2,1,0:T(1,128)} %copy.129), calls=%async_computation | async-start | bytes 8192 | tf_op jit(solution)/shard_map/all_to_all | solution.py:187
  17.5 161.6 %reduce-scatter.12.cloned.1.call-start = ((), (), s32[]{:S(2)}) async-start(), calls=%async_computation.11 | async-start | bytes 163840
  22.2 84.1 %collective-permute-start = (bf16[1,3,4352]{2,1,0:T(4,128)(2,1)S(1)}, bf16[1,3,4352]{2,1,0:T(4,128)(2,1)S(1)}, u32[]{:S(2)}, u32[]{:S(2)}) collective-permute-start(bf16[1,3,4352]{2,1,0:T(4,128)(2,1)S(1)} %slice.127), channel_id=1, source_target_pairs={{0,1},{1,2},{2,3},{4,5},{5,6},{6,7},{8,9},{9,10},{10,11},{12,13},{... | collective-permute-start | bytes 78344 | tf_op jit(solution)/shard_map/ppermute | solution.py:20
  34.4 11.2 %copy-start.17 = (bf16[13,3,64]{2,0,1:T(8,128)(2,1)S(1)}, bf16[13,3,64]{2,0,1:T(8,128)(2,1)}, u32[]{:S(2)}) copy-start(bf16[13,3,64]{2,0,1:T(8,128)(2,1)} %param.26) | copy-start | bytes 14980
  46.3 12.6 %copy-start.9 = (bf16[13,3,1024]{2,0,1:T(8,128)(2,1)S(1)}, bf16[13,3,1024]{2,0,1:T(8,128)(2,1)}, u32[]{:S(2)}) copy-start(bf16[13,3,1024]{2,0,1:T(8,128)(2,1)} %param.25) | copy-start | bytes 239620
  46.3 14.3 %copy-start.21 = (f32[64]{0:T(128)S(1)}, f32[64]{0:T(128)}, u32[]{:S(2)}) copy-start(f32[64]{0:T(128)} %param.37) | copy-start | bytes 772
  46.3 30.8 %copy-start.11 = (bf16[1,512,64]{1,2,0:T(8,128)(2,1)S(1)}, bf16[1,512,64]{1,2,0:T(8,128)(2,1)}, u32[]{:S(2)}) copy-start(bf16[1,512,64]{1,2,0:T(8,128)(2,1)} %param.32) | copy-start | bytes 196612
  46.3 30.8 %copy-start.18 = (f32[64]{0:T(128)S(1)}, f32[64]{0:T(128)}, u32[]{:S(2)}) copy-start(f32[64]{0:T(128)} %param.36) | copy-start | bytes 772
  46.3 31.2 %copy-start.22 = (u32[32]{0:T(128)S(1)}, u32[32]{0:T(128)}, u32[]{:S(2)}) copy-start(u32[32]{0:T(128)} %constant.239) | copy-start | bytes 388
  61.4 12.3 %all-to-all-start.2 = ((bf16[8,2,384]{2,1,0:T(2,128)(2,1)}), bf16[8,2,384]{2,1,0:T(2,128)(2,1)S(1)}, u32[]{:S(2)}, u32[]{:S(2)}) async-start(bf16[8,2,384]{2,1,0:T(2,128)(2,1)} %reshape.672), calls=%async_computation.2 | async-start | bytes 24576 | tf_op jit(solution)/shard_map/all_to_all | solution.py:186
  67.2 11.7 %copy-start.14 = (f32[512]{0:T(512)}, f32[512]{0:T(512)S(1)}, u32[]{:S(2)}) copy-start(f32[512]{0:T(512)S(1)} %fusion.50) | copy-start | bytes 6148
  73.7 12.4 %all-to-all-start.1 = ((bf16[8,4,3,1024]{3,1,2,0:T(4,128)(2,1)}), bf16[8,4,3,1024]{3,1,2,0:T(4,128)(2,1)S(1)}, u32[]{:S(2)}, u32[]{:S(2)}) async-start(bf16[8,4,3,1024]{3,1,2,0:T(4,128)(2,1)} %copy_select_fusion), calls=%async_computation.1 | async-start | bytes 393216 | tf_op jit(solution)/shard_map/all_to_all | solution.py:185
  85.7 6.4 %copy-start.10 = (f32[4,4352]{1,0:T(4,128)S(1)}, f32[4,4352]{1,0:T(4,128)}, u32[]{:S(2)}) copy-start(f32[4,4352]{1,0:T(4,128)} %param.34) | copy-start | bytes 208900
  86.1 368.8 %all-to-all-start.3 = ((f32[8,4,16,64,128]{4,3,2,1,0:T(8,128)}), f32[8,4,16,64,128]{4,3,2,1,0:T(8,128)}, u32[]{:S(2)}, u32[]{:S(2)}) async-start(f32[8,4,16,64,128]{4,3,2,1,0:T(8,128)} %broadcast_select_fusion.2), calls=%async_computation.4 | async-start | bytes 33554432 | tf_op jit(solution)/shard_map/all_to_all | solution.py:184
  91.9 380.1 %reduce-scatter.8.cloned.1.call-start = ((), (), s32[]{:S(2)}) async-start(), calls=%async_computation.7 | async-start | bytes 2621440 | tf_op jit(solution)/shard_map/reduce_scatter | solution.py:279
  94.4 85.5 %copy-start.12 = (bf16[13,3,64]{2,1,0:T(4,128)(2,1)}, bf16[13,3,64]{2,1,0:T(4,128)(2,1)S(1)}, u32[]{:S(2)}) copy-start(bf16[13,3,64]{2,1,0:T(4,128)(2,1)S(1)} %select_convert_fusion.1) | copy-start | bytes 14980
  145.3 8.3 %copy-start = (f32[2,64,64,128]{3,2,1,0:T(8,128)S(1)}, f32[2,64,64,128]{3,2,1,0:T(8,128)}, u32[]{:S(2)}) copy-start(f32[2,64,64,128]{3,2,1,0:T(8,128)} %get-tuple-element.639) | copy-start | bytes 12582916 | tf_op jit(solution)/shard_map/while
  145.3 8.3 %copy-start.5 = (bf16[2,256,64,64]{1,3,2,0:T(8,128)(2,1)S(1)}, bf16[2,256,64,64]{1,3,2,0:T(8,128)(2,1)}, u32[]{:S(2)}) copy-start(bf16[2,256,64,64]{1,3,2,0:T(8,128)(2,1)} %get-tuple-element.652) | copy-start | bytes 12582916 | tf_op jit(solution)/shard_map/while
  157.6 8.3 %copy-start = (f32[2,64,64,128]{3,2,1,0:T(8,128)S(1)}, f32[2,64,64,128]{3,2,1,0:T(8,128)}, u32[]{:S(2)}) copy-start(f32[2,64,64,128]{3,2,1,0:T(8,128)} %get-tuple-element.639) | copy-start | bytes 12582916 | tf_op jit(solution)/shard_map/while
  157.6 8.3 %copy-start.5 = (bf16[2,256,64,64]{1,3,2,0:T(8,128)(2,1)S(1)}, bf16[2,256,64,64]{1,3,2,0:T(8,128)(2,1)}, u32[]{:S(2)}) copy-start(bf16[2,256,64,64]{1,3,2,0:T(8,128)(2,1)} %get-tuple-element.652) | copy-start | bytes 12582916 | tf_op jit(solution)/shard_map/while
  172.7 5.5 copy-start.3
  172.7 6.1 %copy-start.19 = (f32[64]{0:T(128)S(1)}, f32[64]{0:T(128)}, u32[]{:S(2)}) copy-start(f32[64]{0:T(128)} %param.38) | copy-start | bytes 772
  174.4 300.2 %reduce-scatter.10.cloned.1.call-start = ((), (), s32[]{:S(2)}) async-start(), calls=%async_computation.10 | async-start | bytes 2621440
  178.2 298.6 %all-gather.7.cloned.1.call-start = ((), (), s32[]{:S(2)}) async-start(), calls=%async_computation.9 | async-start | bytes 10485760 | tf_op jit(solution)/shard_map/all_gather | solution.py:25
  178.8 316.7 %all-gather.5.cloned.1.call-start = ((), (), s32[]{:S(2)}) async-start(), calls=%async_computation.8 | async-start | bytes 2621440 | tf_op jit(solution)/shard_map/all_gather | solution.py:242
  464.5 9.5 %slice-start.1 = ((bf16[13,3,64]{2,1,0:T(4,128)(2,1)}), bf16[12,3,64]{2,1,0:T(4,128)(2,1)S(1)}, s32[]{:S(2)}) async-start(bf16[13,3,64]{2,1,0:T(4,128)(2,1)} %copy-done.12), calls=%async_computation.13 | async-start | bytes 24576 | tf_op jit(solution)/shard_map/slice | solution.py:293
  485.5 7.1 %copy-start.4 = (f32[1,64,64,128]{3,2,1,0:T(8,128)}, f32[1,64,64,128]{3,2,1,0:T(8,128)S(1)}, u32[]{:S(2)}) copy-start(f32[1,64,64,128]{3,2,1,0:T(8,128)S(1)} %get-tuple-element.221) | copy-start | bytes 6291460
  498.0 4.1 copy-start.2
  534.9 14.8 %copy-start.15 = (f32[512]{0:T(512)S(1)}, f32[512]{0:T(512)}, u32[]{:S(2)}) copy-start(f32[512]{0:T(512)} %copy-done.14) | copy-start | bytes 6148
  549.7 8.5 %copy-start.16 = (f32[4096]{0:T(1024)S(1)}, f32[4096]{0:T(1024)}, u32[]{:S(2)}) copy-start(f32[4096]{0:T(1024)} %param.39) | copy-start | bytes 49156
  (7 other events, 18.9 us)
Sparse Core Ops, SparseCore 0:
  27.1 21.7 reduce-scatter.11
  174.6 32.2 reduce-scatter.7
  209.4 31.1 reduce-scatter.9
  242.1 58.2 all-gather.6
  474.1 21.3 all-gather.4
where the time goes:
time: 570 us; the launch traced here: 568 us
  waiting for transfers between devices  285 us (50%)
  local copies, waits for them, and re-layouts  112 us (20%)
  other arithmetic  87.9 us (15%)
  matrix products  25.4 us (4%)
  starting transfers between devices  23.9 us (4%)
  blocking collectives  17.5 us (3%)
  between operations  15.7 us (3%)
    all_to_all x1, waiting for transfers between devices, migrate(): lax.all_to_all(send_states, 'req', split_axis=0, concat_axis=0, tiled=True)  275 us
    reshape x2, local copies, waits for them, and re-layouts, assemble(): (intra_part + inter_parts).reshape(value_rows.shape)  31 us
    unnamed x50, local copies, waits for them, and re-layouts  16 us
    dot_general x2, matrix products, block_local(): jnp.einsum('hts,shp->thp', weights, value_rows, preferred_element_type=jn...  15.9 us
    select_n x2, other arithmetic, packed(): taken_rows = jnp.take(source, source_slot, axis=0)  13.3 us
    another operation x1, local copies, waits for them, and re-layouts, to_items(): source.reshape((batch_size * block_count, BLOCK_LEN) + source.shape[2:])  12.6 us
    gather x3, local copies, waits for them, and re-layouts, packed(): taken_rows = jnp.take(source, source_slot, axis=0)  12.5 us
    add x1, other arithmetic, assemble(): intra_part + inter_parts  11.7 us
  transfers between devices with their start and end apart: 10, of which 4 were waited for; matrix products, arithmetic and copies ran while one was open for 25% of the time, Pallas kernels for 0%

commit v1 on v0

v1 whole, which is shorter than its diff:
```python
import math

import jax
import jax.numpy as jnp
from jax import lax
from jax.experimental import pallas as pl
from jax.experimental.pallas import tpu as pltpu
from jax.sharding import PartitionSpec as P


HEAD_DIM = 64
STATE_DIM = 128
KERNEL = 4
BLOCK_LEN = 256
GROUP = 8
HALF = BLOCK_LEN // 2
GROUP_DIM = GROUP * HEAD_DIM
PAIR_DIM = 2 * HEAD_DIM
LANES = 128
TILE = 128
EPSILON = 1e-05
LOG2E = math.log2(math.e)
F32 = jnp.float32
BF16 = jnp.bfloat16


def dot(a, b, dims=((1,), (0,)), precision=None):
    return lax.dot_general(a, b, (dims, ((), ())), precision=precision, preferred_element_type=F32)


def silu(v):
    return v / (1.0 + jnp.exp(-v))


def conv_silu(tail, rows, weight, bias_row):
    extended = jnp.concatenate([tail, rows.astype(F32)], axis=0)
    count = rows.shape[0]
    start = tail.shape[0] - KERNEL + 1
    running = bias_row + weight[0:1] * extended[start : start + count]
    for k in range(1, KERNEL):
        running = running + weight[k : k + 1] * extended[start + k : start + k + count]
    return silu(running)


def pair_of(columns, i, low):
    return jnp.where(low, columns[:, 2 * i : 2 * i + 1], columns[:, 2 * i + 1 : 2 * i + 2])


def block_kernel(
    chain_ref,
    tail_ref,
    prev_ref,
    rows_ref,
    state_tail_ref,
    state_prev_ref,
    state_rows_ref,
    step_ref,
    rate_ref,
    weight_ref,
    bias_ref,
    state_weight_ref,
    state_bias_ref,
    skip_ref,
    part_ref,
    end_ref,
    read_ref,
    decay_ref,
    scores_scr,
    cum_scr,
    cum_t_scr,
    to_end_scr,
    decay_scr,
    write_t_scr,
    offset_scr,
    carry_scr,
):
    block = pl.program_id(0)
    group = pl.program_id(1)
    first = block == 0

    @pl.when(group == 0)
    def _():
        state_tail = jnp.where(first, state_tail_ref[...], state_prev_ref[8:16, :].astype(F32))
        mixed = conv_silu(state_tail, state_rows_ref[...], state_weight_ref[...], state_bias_ref[...])
        write = mixed[:, :STATE_DIM]
        read = mixed[:, STATE_DIM:].astype(BF16)
        read_ref[...] = read
        write_b = write.astype(BF16)
        scores_scr[...] = dot(read, write_b, ((1,), (1,)))
        write_t_scr[...] = write_b.astype(F32).T.astype(BF16)
        row = lax.broadcasted_iota(jnp.int32, (BLOCK_LEN, BLOCK_LEN), 0)
        col = lax.broadcasted_iota(jnp.int32, (BLOCK_LEN, BLOCK_LEN), 1)
        triangle = (row >= col).astype(F32)
        step = step_ref[...]
        cum = dot(triangle, step * rate_ref[...], precision=lax.Precision.HIGHEST)
        cum_scr[...] = cum
        cum_t_scr[...] = cum.T
        last = cum[BLOCK_LEN - 1 :, :]
        to_end_scr[...] = jnp.exp2(last - cum) * step
        decay_scr[...] = jnp.exp2(cum)
        offset = jnp.where(first, 0.0, offset_scr[0:1, :])
        decay_ref[...] = jnp.exp2(offset + cum)
        offset_scr[0:1, :] = offset + last

    shift = lax.rem(LANES - group * GROUP, LANES)
    cum = pltpu.roll(cum_scr[...], shift, 1)
    step = pltpu.roll(step_ref[...], shift, 1)
    to_end = pltpu.roll(to_end_scr[...], shift, 1)
    decay = pltpu.roll(decay_scr[...], shift, 1)
    cum_t = cum_t_scr[pl.ds(pl.multiple_of(group * GROUP, GROUP), GROUP), :]
    read = read_ref[...]
    write_t = write_t_scr[...]
    carry = jnp.where(first, 0.0, carry_scr[group])
    carry_b = carry.astype(BF16)
    low = lax.broadcasted_iota(jnp.int32, (1, PAIR_DIM), 1) < HEAD_DIM
    causal = lax.broadcasted_iota(jnp.int32, (HALF, HALF), 0) >= lax.broadcasted_iota(
        jnp.int32, (HALF, HALF), 1
    )
    scores_top = scores_scr[0:HALF, 0:HALF]
    scores_left = scores_scr[HALF:, 0:HALF]
    scores_right = scores_scr[HALF:, HALF:]

    def head_weights(i):
        later = cum[:, i : i + 1]
        earlier = cum_t[i : i + 1, :]
        gap_top = jnp.where(causal, later[:HALF] - earlier[:, :HALF], -1e30)
        gap_left = later[HALF:] - earlier[:, :HALF]
        gap_right = jnp.where(causal, later[HALF:] - earlier[:, HALF:], -1e30)
        top = (scores_top * jnp.exp2(gap_top)).astype(BF16)
        left = (scores_left * jnp.exp2(gap_left)).astype(BF16)
        right = (scores_right * jnp.exp2(gap_right)).astype(BF16)
        return top, jnp.concatenate([left, right], axis=1)

    for i in range(GROUP // 2):
        span = slice(i * PAIR_DIM, (i + 1) * PAIR_DIM)
        tail = jnp.where(first, tail_ref[:, span], prev_ref[8:16, span].astype(F32))
        mixed = conv_silu(tail, rows_ref[:, span], weight_ref[:, span], bias_ref[:, span])
        value = mixed.astype(BF16).astype(F32)
        stepped = (pair_of(step, i, low) * value).astype(BF16)
        scaled = (pair_of(to_end, i, low) * value).astype(BF16)
        stepped_low = jnp.where(low, stepped, jnp.zeros_like(stepped))
        stepped_high = jnp.where(low, jnp.zeros_like(stepped), stepped)
        top_0, bottom_0 = head_weights(2 * i)
        top_1, bottom_1 = head_weights(2 * i + 1)
        intra_top = dot(top_0, stepped_low[:HALF]) + dot(top_1, stepped_high[:HALF])
        intra_bottom = dot(bottom_0, stepped_low) + dot(bottom_1, stepped_high)
        inter = dot(read, carry_b[:, span]) * pair_of(decay, i, low)
        direct = inter + skip_ref[:, span] * value
        part_ref[0:HALF, span] = intra_top + direct[:HALF]
        part_ref[HALF:, span] = intra_bottom + direct[HALF:]
        kept = pair_of(decay[BLOCK_LEN - 1 :, :], i, low) * carry[:, span]
        ending = kept + dot(write_t, scaled)
        carry_scr[group, :, span] = ending
        end_ref[0, :, span] = ending.astype(BF16)


def block_parts(chain, tail, rows, state_rows, step, rate, weight, bias_row, skip_row, ends):
    length = rows.shape[0]
    channels = rows.shape[1]
    blocks = length // BLOCK_LEN
    groups = channels // GROUP_DIM
    end_groups = groups // ends
    state_dim = state_rows.shape[1]
    state_at = channels // state_dim
    per_block = BLOCK_LEN // 16

    def before(b):
        return jnp.maximum(b * per_block - 1, 0)

    def end_at(b, g, chain):
        return lax.rem(g // end_groups - chain[0] + ends, ends), 0, lax.rem(g, end_groups)

    return pl.pallas_call(
        block_kernel,
        grid_spec=pltpu.PrefetchScalarGridSpec(
        num_scalar_prefetch=1,
        grid=(blocks, groups),
        in_specs=[
            pl.BlockSpec((8, GROUP_DIM), lambda b, g, c: (0, g)),
            pl.BlockSpec((16, GROUP_DIM), lambda b, g, c: (before(b), g)),
            pl.BlockSpec((BLOCK_LEN, GROUP_DIM), lambda b, g, c: (b, g)),
            pl.BlockSpec((8, state_dim), lambda b, g, c: (0, state_at)),
            pl.BlockSpec((16, state_dim), lambda b, g, c: (before(b), 0)),
            pl.BlockSpec((BLOCK_LEN, state_dim), lambda b, g, c: (b, 0)),
            pl.BlockSpec((BLOCK_LEN, LANES), lambda b, g, c: (b, 0)),
            pl.BlockSpec((1, LANES), lambda b, g, c: (0, 0)),
            pl.BlockSpec((KERNEL, GROUP_DIM), lambda b, g, c: (0, g)),
            pl.BlockSpec((1, GROUP_DIM), lambda b, g, c: (0, g)),
            pl.BlockSpec((KERNEL, state_dim), lambda b, g, c: (0, state_at)),
            pl.BlockSpec((1, state_dim), lambda b, g, c: (0, state_at)),
            pl.BlockSpec((1, GROUP_DIM), lambda b, g, c: (0, g)),
        ],
        out_specs=[
            pl.BlockSpec((BLOCK_LEN, GROUP_DIM), lambda b, g, c: (b, g)),
            pl.BlockSpec((1, STATE_DIM, GROUP_DIM), end_at),
            pl.BlockSpec((BLOCK_LEN, STATE_DIM), lambda b, g, c: (b, 0)),
            pl.BlockSpec((BLOCK_LEN, LANES), lambda b, g, c: (b, 0)),
        ],
        scratch_shapes=[
            pltpu.VMEM((BLOCK_LEN, BLOCK_LEN), F32),
            pltpu.VMEM((BLOCK_LEN, LANES), F32),
            pltpu.VMEM((LANES, BLOCK_LEN), F32),
            pltpu.VMEM((BLOCK_LEN, LANES), F32),
            pltpu.VMEM((BLOCK_LEN, LANES), F32),
            pltpu.VMEM((STATE_DIM, BLOCK_LEN), BF16),
            pltpu.VMEM((8, LANES), F32),
            pltpu.VMEM((groups, STATE_DIM, GROUP_DIM), F32),
        ],
        ),
        out_shape=[
            jax.ShapeDtypeStruct((length, channels), F32),
            jax.ShapeDtypeStruct((ends, STATE_DIM, channels // ends), BF16),
            jax.ShapeDtypeStruct((length, STATE_DIM), BF16),
            jax.ShapeDtypeStruct((length, LANES), F32),
        ],
        compiler_params=pltpu.CompilerParams(dimension_semantics=("arbitrary", "arbitrary")),
        cost_estimate=pl.CostEstimate(
            flops=6_000_000_000, bytes_accessed=20_000_000, transcendentals=10_000_000
        ),
        name="block_parts",
    )(
        chain,
        tail,
        rows,
        rows,
        tail,
        state_rows,
        state_rows,
        step,
        rate,
        weight,
        bias_row,
        weight,
        bias_row,
        skip_row,
    )


def finish_kernel(
    place_ref, part_ref, gate_ref, read_ref, decay_ref, state_ref, norm_ref, out_ref, gated_scr
):
    tile = pl.program_id(0)
    chunks, _, width = state_ref.shape
    positions = (
        place_ref[0] + tile * TILE + lax.broadcasted_iota(jnp.int32, (TILE, PAIR_DIM), 0)
    )
    valid = (positions < place_ref[1]).astype(F32)
    low = lax.broadcasted_iota(jnp.int32, (1, PAIR_DIM), 1) < HEAD_DIM
    read = read_ref[...]
    decay = decay_ref[...]
    total = jnp.zeros((TILE, PAIR_DIM), F32)
    for chunk in range(chunks):
        from_chunk = lax.rem(place_ref[2] - chunk + chunks, chunks)
        for i in range(width // PAIR_DIM):
            pair = chunk * (width // PAIR_DIM) + i
            span = slice(pair * PAIR_DIM, (pair + 1) * PAIR_DIM)
            inter = dot(read, state_ref[from_chunk, :, i * PAIR_DIM : (i + 1) * PAIR_DIM])
            y = part_ref[:, span] + inter * pair_of(decay, pair, low)
            y = (y * valid).astype(BF16).astype(F32)
            gated = y * silu(gate_ref[:, span].astype(F32))
            gated_scr[:, span] = gated
            total = total + gated * gated
    channels = chunks * width
    mean = jnp.sum(total, axis=1, keepdims=True) * (1.0 / channels)
    scale = lax.rsqrt(mean + EPSILON)
    for pair in range(channels // PAIR_DIM):
        span = slice(pair * PAIR_DIM, (pair + 1) * PAIR_DIM)
        out_ref[:, span] = (gated_scr[:, span] * scale * norm_ref[:, span]).astype(BF16)


def finish(place, part, gate, read, decay, states, norm_row):
    length, channels = part.shape
    return pl.pallas_call(
        finish_kernel,
        grid=(length // TILE,),
        in_specs=[
            pl.BlockSpec(memory_space=pltpu.SMEM),
            pl.BlockSpec((TILE, channels), lambda t: (t, 0)),
            pl.BlockSpec((TILE, channels), lambda t: (t, 0)),
            pl.BlockSpec((TILE, STATE_DIM), lambda t: (t, 0)),
            pl.BlockSpec((TILE, LANES), lambda t: (t, 0)),
            pl.BlockSpec(states.shape, lambda t: (0, 0, 0)),
            pl.BlockSpec((1, channels), lambda t: (0, 0)),
        ],
        out_specs=pl.BlockSpec((TILE, channels), lambda t: (t, 0)),
        out_shape=jax.ShapeDtypeStruct((length, channels), BF16),
        scratch_shapes=[pltpu.VMEM((TILE, channels), F32)],
        compiler_params=pltpu.CompilerParams(dimension_semantics=("arbitrary",)),
        cost_estimate=pl.CostEstimate(
            flops=3_000_000_000, bytes_accessed=16_000_000, transcendentals=4_000_000
        ),
        name="finish",
    )(place, part, gate, read, decay, states, norm_row)


def pack_kernel(keep_ref, state_ref, out_ref):
    keep = keep_ref[pl.program_id(0)].astype(F32)
    out_ref[:, 0] = (state_ref[0] * keep).astype(BF16)


def pack(keep, states):
    slots, peers, piece, width = states.shape
    return pl.pallas_call(
        pack_kernel,
        grid=(slots,),
        in_specs=[
            pl.BlockSpec(memory_space=pltpu.SMEM),
            pl.BlockSpec((1, peers, piece, width), lambda t: (t, 0, 0, 0)),
        ],
        out_specs=pl.BlockSpec((peers, 1, piece, width), lambda t: (0, t, 0, 0)),
        out_shape=jax.ShapeDtypeStruct((peers, slots, piece, width), BF16),
        compiler_params=pltpu.CompilerParams(dimension_semantics=("arbitrary",)),
        name="pack",
    )(keep, states)


def unpack_kernel(final_ref, pieces_ref, out_ref):
    slot = pl.program_id(0)
    peers, piece = out_ref.shape[1:3]

    @pl.when(slot == 0)
    def _():
        for p in range(peers):
            out_ref[0, p] = final_ref[:, p * piece : (p + 1) * piece].T

    @pl.when(slot > 0)
    def _():
        out_ref[0] = pieces_ref[:, 0].astype(F32)


def unpack(final, pieces):
    peers, others, piece, width = pieces.shape
    slots = others + 1
    return pl.pallas_call(
        unpack_kernel,
        grid=(slots,),
        in_specs=[
            pl.BlockSpec(final.shape, lambda t: (0, 0)),
            pl.BlockSpec((peers, 1, piece, width), lambda t: (0, jnp.maximum(t - 1, 0), 0, 0)),
        ],
        out_specs=pl.BlockSpec((1, peers, piece, width), lambda t: (t, 0, 0, 0)),
        out_shape=jax.ShapeDtypeStruct((slots, peers, piece, width), F32),
        compiler_params=pltpu.CompilerParams(dimension_semantics=("arbitrary",)),
        name="unpack",
    )(final, pieces)


def combine_kernel(chain_ref, first_ref, ends_ref, decay_ref, entering_ref, final_ref):
    chain = chain_ref[0]
    count = ends_ref.shape[0]
    state = first_ref[...].astype(F32).T
    for k in range(count):
        entering_ref[lax.rem(k - chain + count, count)] = state.astype(BF16)
        end = ends_ref[lax.rem(chain - k + count, count)].astype(F32)
        state = state * decay_ref[k : k + 1, :] + end
    final_ref[...] = state


def combine(chain, first, ends, decay):
    whole = pl.BlockSpec(memory_space=pltpu.VMEM)
    return pl.pallas_call(
        combine_kernel,
        in_specs=[pl.BlockSpec(memory_space=pltpu.SMEM), whole, whole, whole],
        out_shape=[
            jax.ShapeDtypeStruct(ends.shape, BF16),
            jax.ShapeDtypeStruct(ends.shape[1:], F32),
        ],
        name="combine",
    )(chain, first, ends, decay)


def exchange(value, axis):
    return lax.all_to_all(value, axis, split_axis=0, concat_axis=0, tiled=True)


def rotate(values, axis):
    count = lax.axis_size(axis)
    got = [values[0]]
    for hop in range(1, count):
        pairs = [(source, (source + hop) % count) for source in range(count)]
        got.append(lax.ppermute(values[hop], axis, pairs))
    return jnp.stack(got)


def rows_at(source, indices):
    return source.at[indices].get(mode="promise_in_bounds")


def device_body(
    pool_states,
    inner_window,
    state_window,
    move_plan,
    active_mask,
    inputs_inner,
    inputs_state,
    gate_rows,
    step_raw,
    lengths,
    conv_weight,
    conv_bias,
    step_bias,
    decay_log,
    skip_weight,
    norm_weight,
):
    peers = lax.axis_size("req")
    own_peer = lax.axis_index("req")
    chain_size = lax.axis_size("seq")
    chain_index = lax.axis_index("seq")
    slots, local_heads = pool_states.shape[:2]
    piece = local_heads * HEAD_DIM // peers
    taps = KERNEL - 1
    keep_flag = active_mask.astype(F32)

    pieces = pack(active_mask, pool_states.reshape(slots, peers, piece, STATE_DIM))
    spread = exchange(pieces, "req").reshape(peers * slots, piece, STATE_DIM)

    inner_local = inner_window.shape[2]
    outer_local = state_window.shape[2]
    own_windows = jnp.concatenate([inner_window, state_window], axis=2).reshape(slots, -1)
    own_windows = (own_windows.astype(F32) * keep_flag[:, None]).astype(BF16)
    width = own_windows.shape[1]
    padding = jnp.zeros((slots, -(width + 2) % LANES), BF16)
    packed = jnp.concatenate([own_windows, move_plan.astype(BF16), padding], axis=1)
    every = lax.all_gather(packed, "req", axis=0, tiled=True)
    every_plan = every[:, width : width + 2].astype(F32).astype(jnp.int32)
    targets = every_plan[:, 0] * slots + every_plan[:, 1]
    order = jnp.arange(peers * slots, dtype=jnp.int32)
    sources = jnp.sum(jnp.where(targets[None, :] == order[:, None], order[None, :], 0), axis=1)
    own_sources = lax.dynamic_slice_in_dim(sources, own_peer * slots, slots)
    moved_windows = rows_at(every, own_sources)[:, :width].reshape(slots, taps, -1)

    rows = inputs_inner[0]
    state_rows = inputs_state[0]
    local_length = rows.shape[0]
    inner_dim = rows.shape[1]
    start = chain_index * local_length
    length = lengths[0]
    window_pos = length - taps + jnp.arange(taps, dtype=jnp.int32) - start
    inside = (window_pos >= 0) & (window_pos < local_length)
    safe_pos = jnp.clip(window_pos, 0, local_length - 1)
    ends = jnp.concatenate(
        [rows[local_length - taps :], state_rows[local_length - taps :]], axis=1
    )
    kept_here = jnp.concatenate([rows_at(rows, safe_pos), rows_at(state_rows, safe_pos)], axis=1)
    kept_here = jnp.where(inside[:, None], kept_here, jnp.zeros_like(kept_here))
    channels = ends.shape[1]
    window_local = inner_local + outer_local
    heads = decay_log.shape[0]
    head_pad = LANES - heads
    rate = -LOG2E * jnp.exp(decay_log)
    positions = start + jnp.arange(local_length, dtype=jnp.int32)
    valid_rows = (positions < length).astype(F32)
    step = jax.nn.softplus(step_raw[0].astype(F32) + step_bias) * valid_rows[:, None]
    device_log = jnp.sum(step * rate, axis=0)
    log_high = lax.reduce_precision(device_log, 8, 7)
    log_middle = lax.reduce_precision(device_log - log_high, 8, 7)
    log_low = lax.reduce_precision(device_log - log_high - log_middle, 8, 7)
    log_parts = jnp.stack([log_high, log_middle, log_low]).astype(BF16)
    shared = lax.all_gather(
        jnp.concatenate([log_parts, moved_windows[0], ends, kept_here], axis=1), "seq", axis=0
    )
    every_log = jnp.sum(shared[:, :, :heads].astype(F32), axis=1)
    shared = shared[:, :, heads:]
    own_log = lax.dynamic_slice_in_dim(every_log, chain_index * local_heads, local_heads, 1)
    own_decay = jnp.repeat(jnp.exp2(own_log), HEAD_DIM, axis=1)
    first_window = jnp.concatenate(
        [
            shared[:, :, :inner_local].transpose(1, 0, 2).reshape(taps, -1),
            shared[:, :, inner_local:window_local].transpose(1, 0, 2).reshape(taps, -1),
        ],
        axis=1,
    )
    earlier_rows = lax.dynamic_index_in_dim(
        shared[:, :, window_local : window_local + channels],
        jnp.maximum(chain_index - 1, 0),
        0,
        keepdims=False,
    )
    tail = jnp.where(chain_index == 0, first_window, earlier_rows).astype(F32)
    tail = jnp.concatenate([jnp.zeros((8 - taps, channels), F32), tail], axis=0)
    kept = jnp.sum(shared[:, :, window_local + channels :].astype(F32), axis=0).astype(BF16)
    kept_inner = lax.dynamic_slice_in_dim(kept, chain_index * inner_local, inner_local, 1)
    kept_outer = lax.dynamic_slice_in_dim(
        kept, inner_dim + chain_index * outer_local, outer_local, 1
    )

    chain = chain_index.astype(jnp.int32)[None]
    part, local_end, read_rows, decay = block_parts(
        chain,
        tail,
        rows,
        state_rows,
        jnp.pad(step, ((0, 0), (0, head_pad))),
        jnp.pad(rate, (0, head_pad))[None],
        conv_weight,
        conv_bias[None],
        jnp.repeat(skip_weight, HEAD_DIM)[None],
        chain_size,
    )
    own_ends = rotate(local_end, "seq")

    order_by_peer = sources.reshape(peers, slots)
    peer_order = jnp.arange(peers, dtype=jnp.int32)
    first_sources = rows_at(order_by_peer[:, 0], lax.rem(own_peer + peer_order, peers))
    first_pieces = rotate(rows_at(spread, first_sources), "req")
    first_pieces = rows_at(first_pieces, lax.rem(own_peer + peers - peer_order, peers))
    rest = rows_at(spread, order_by_peer[:, 1:].reshape(-1)).reshape(
        peers, slots - 1, piece, STATE_DIM
    )
    rest_pieces = exchange(rest, "req")

    entering, final = combine(
        chain, first_pieces.reshape(local_heads * HEAD_DIM, STATE_DIM), own_ends, own_decay
    )
    incoming = rotate(entering, "seq")

    place = jnp.stack([start, length, chain_index]).astype(jnp.int32)
    mixer_out = finish(
        place, part, gate_rows[0], read_rows, decay, incoming, norm_weight[None]
    )
    new_states = unpack(final, rest_pieces).reshape(pool_states.shape)
    new_inner = jnp.concatenate(
        [kept_inner[None], moved_windows[1:, :, :inner_local]], axis=0
    )
    new_outer = jnp.concatenate(
        [kept_outer[None], moved_windows[1:, :, inner_local:]], axis=0
    )
    return (new_states, new_inner, new_outer, mixer_out[None])


def solution(mesh):
    return jax.shard_map(
        device_body,
        mesh=mesh,
        in_specs=(
            P("req", "seq", None, None),
            P("req", None, "seq"),
            P("req", None, "seq"),
            P("req", None),
            P("req"),
            P("req", "seq", None),
            P("req", "seq", None),
            P("req", "seq", None),
            P("req", "seq", None),
            P("req"),
            P(),
            P(),
            P(),
            P(),
            P(),
            P(),
        ),
        out_specs=(
            P("req", "seq", None, None),
            P("req", None, "seq"),
            P("req", None, "seq"),
            P("req", "seq", None),
        ),
        check_vma=False,
    )
```

time: 570 us -> 286 us (0.50)
  waiting for transfers between devices: 285 us -> 19.6 us
  blocking collectives: 17.5 us -> 96.1 us
  other arithmetic: 87.9 us -> 18.2 us
  local copies, waits for them, and re-layouts: 112 us -> 44.7 us
  Pallas kernels: 0 us -> 65.1 us
  matrix products: 25.4 us -> 0 us
  between operations: 15.7 us -> 1.49 us
  starting transfers between devices: 23.9 us -> 36.4 us
    all_to_all x4 -> x2, waiting for transfers between devices: 282 us -> 0.01 us  [exchange(): return lax.all_to_all(value, axis, split_axis=0, concat_axis=0, tiled=True)]
    all_gather x2, blocking collectives: 10.8 us -> 96.1 us  [the longest x1 90 us: device_body(): every = lax.all_gather(packed, 'req', axis=0, tiled=True)]
    pallas_call x0 -> x5, Pallas kernels: none -> 65.1 us  [the longest x1 32 us: block_parts(): pl.pallas_call(block_kernel, grid_spec=pltpu.PrefetchScalarGridSpec(num_s...]
    reshape x4 -> x5, local copies, waits for them, and re-layouts: 31.2 us -> 2.28 us  [the longest x1 0.8 us: device_body(): rows_at(every, own_sources)[:, :width].reshape(slots, taps, -1)]
    select_n x16 -> x8, other arithmetic: 29.2 us -> 2.36 us  [the longest x1 0.86 us: device_body(): kept_here = jnp.where(inside[:, None], kept_here, jnp.zeros_like(kept_here))]
    dot_general x8 -> x0, matrix products: 25.4 us -> none  [the longest x2 15.9 us: block_local(): jnp.einsum('hts,shp->thp', weights, value_rows, preferred_element_type=jn...]
    ppermute x1 -> x13, starting transfers between devices: 1.46 us -> 24.5 us  [rotate(): got.append(lax.ppermute(values[hop], axis, pairs))]
    ppermute x1 -> x13, waiting for transfers between devices: 0.01 us -> 19.6 us  [rotate(): got.append(lax.ppermute(values[hop], axis, pairs))]
  transfers between devices with their start and end apart: 10 -> 15, of which waited for: 4 -> 6; matrix products, arithmetic and copies ran while one was open for 25% -> 21% of each run, Pallas kernels for 0% -> 16%
where the time goes in v1:
time: 286 us; the launch traced here: 282 us
  blocking collectives  96.1 us (34%)
  Pallas kernels  65.1 us (23%)
  local copies, waits for them, and re-layouts  44.7 us (16%)
  starting transfers between devices  36.4 us (13%)
  waiting for transfers between devices  19.6 us (7%)
  other arithmetic  18.2 us (6%)
    all_gather x1, blocking collectives, device_body(): every = lax.all_gather(packed, 'req', axis=0, tiled=True)  90 us
    pallas_call x1, Pallas kernels, block_parts(): pl.pallas_call(block_kernel, grid_spec=pltpu.PrefetchScalarGridSpec(num_s...  32 us
    ppermute x13, starting transfers between devices, rotate(): got.append(lax.ppermute(values[hop], axis, pairs))  24.5 us
    ppermute x13, waiting for transfers between devices, rotate(): got.append(lax.ppermute(values[hop], axis, pairs))  19.6 us
    gather x7, local copies, waits for them, and re-layouts, rows_at(): return source.at[indices].get(mode='promise_in_bounds')  14.8 us
    all_to_all x2, starting transfers between devices, exchange(): return lax.all_to_all(value, axis, split_axis=0, concat_axis=0, tiled=True)  11.9 us
    pallas_call x1, Pallas kernels, finish(): pl.pallas_call(finish_kernel, grid=(length // TILE,), in_specs=[pl.BlockS...  11.6 us
    pallas_call x1, Pallas kernels, unpack(): pl.pallas_call(unpack_kernel, grid=(slots,), in_specs=[pl.BlockSpec(final...  9.38 us
  transfers between devices with their start and end apart: 15, of which 6 were waited for; matrix products, arithmetic and copies ran while one was open for 21% of the time, Pallas kernels for 16%

profile of v1, /device:TPU:0, one launch (start us, length us, event | category | flops | bytes accessed | tf_op | source)
XLA Modules:
  0.0 281.7 jit_solution(7718367293755374772)
XLA Ops:
  0.6 9.3 %pack.1 = bf16[8,13,128,128]{3,2,1,0:T(8,128)(2,1)} custom-call(s32[13]{0:T(128)} %keep_ref.1, f32[13,8,128,128]{3,2,1,0:T(8,128)} %bitcast.107), custom_call_target="tpu_custom_call" | custom-call | tf_op jit(solution)/shard_map/pack/pallas_call | solution.py:303
  10.0 7.4 %all-to-all-start = ((bf16[8,13,128,128]{3,2,1,0:T(8,128)(2,1)}), bf16[8,13,128,128]{3,2,1,0:T(8,128)(2,1)S(1)}, u32[]{:S(2)}, u32[]{:S(2)}) async-start(bf16[8,13,128,128]{3,2,1,0:T(8,128)(2,1)} %pack.1), calls=%async_computation | async-start | bytes 6815744 | tf_op jit(solution)/shard_map/all_to_all | solution.py:373
  22.7 1.8 reshape.246
  24.6 1.7 multiply_convert_fusion
  26.2 1.6 concatenate.27
  27.9 90.0 %all-gather.1 = bf16[8,13,3328]{2,1,0:T(8,128)(2,1)} all-gather(bf16[1,13,3328]{2,1,0:T(8,128)(2,1)} %bitcast.113), channel_id=1, replica_groups=mesh['req'=8,'seq'=4] {'req'}, dimensions={0}, use_global_device_ids=true | all-gather | bytes 778752 | tf_op jit(solution)/shard_map/all_gather | solution.py:426
  117.9 2.2 reshape.307
  122.7 2.5 gather_fusion.3
  127.4 2.2 gather_fusion.5
  129.7 4.1 %gather_fusion.4 = bf16[3,4096]{1,0:T(4,128)(2,1)} fusion(bf16[512,4096]{1,0:T(8,128)(2,1)} %bitcast.119, s32[1024]{0:T(1024)} %get-tuple-element.53), kind=kCustom, calls=%fused_computation.4 | custom fusion | bytes 49164 | tf_op jit(solution)/shard_map/gather | solution.py:386
  134.4 1.6 multiply_reduce_fusion
  136.7 1.5 slice_bitcast_fusion.13
  139.9 6.1 %all-gather.2 = bf16[4,3,9856]{2,1,0:T(4,128)(2,1)S(1)} all-gather(bf16[1,3,9856]{2,1,0:T(4,128)(2,1)S(1)} %bitcast.114), channel_id=2, replica_groups=mesh['req'=8,'seq'=4] {'seq'}, dimensions={0}, use_global_device_ids=true | all-gather | bytes 295680 | tf_op jit(solution)/shard_map/all_gather | solution.py:461
  146.8 1.7 pad.10.step_ref
  151.7 1.7 slice_reduce_fusion
  153.4 2.7 gather_fusion.6
  156.1 4.5 %all-to-all-start.1 = ((bf16[8,12,128,128]{3,2,1,0:T(8,128)(2,1)}), bf16[8,12,128,128]{3,2,1,0:T(8,128)(2,1)}, u32[]{:S(2)}, u32[]{:S(2)}) async-start(bf16[8,12,128,128]{3,2,1,0:T(8,128)(2,1)} %bitcast.106), calls=%async_computation.1 | async-start | bytes 6291456 | tf_op jit(solution)/shard_map/all_to_all | solution.py:373
  162.1 32.0 %block_parts.1 = (f32[512,4096]{1,0:T(8,128)}, bf16[4,128,1024]{2,1,0:T(8,128)(2,1)}, bf16[512,128]{1,0:T(8,128)(2,1)}, f32[512,128]{1,0:T(8,128)}) custom-call(s32[1]{0:T(128)} %bitcast.chain_ref, f32[8,4352]{1,0:T(8,128)} %pad_convert_fusion.tail_ref.state_tail_ref, bf16[512,4096]{1,0:T(8,128)(2,1)} %bitcast.120, bf16[512,4096]{1,0:T(8,128)(2,1)} %bitcast.121, ...), custom_call_target="tpu_custom_call" | custom-call | flops 6000000000 | bytes 20000000 | tf_op jit(solution)/shard_map/block_parts/pallas_call | solution.py:173
  194.1 2.2 fusion.20
  199.1 1.6 slice.175
  206.2 1.7 collective-permute-start
  207.9 3.1 %collective-permute-done.8 = bf16[128,1024]{1,0:T(8,128)(2,1)} collective-permute-done((bf16[128,1024]{1,0:T(8,128)(2,1)}, bf16[128,1024]{1,0:T(8,128)(2,1)}, u32[]{:S(2)}, u32[]{:S(2)}) %collective-permute-start.8) | collective-permute-done | bytes 262176 | tf_op jit(solution)/shard_map/ppermute | solution.py:381
  211.0 2.3 pad_maximum_fusion.ends_ref
  213.3 4.6 %collective-permute-start.6 = (bf16[128,128]{1,0:T(8,128)(2,1)S(1)}, bf16[128,128]{1,0:T(8,128)(2,1)S(1)}, u32[]{:S(2)}, u32[]{:S(2)}) collective-permute-start(bf16[128,128]{1,0:T(8,128)(2,1)S(1)} %get-tuple-element.40), channel_id=1, source_target_pairs={{0,28},{4,0},{8,4},{12,8},{16,12},{20,16},{24,20},{28,24},{1,29},{... | collective-permute-start | bytes 98312 | tf_op jit(solution)/shard_map/ppermute | solution.py:381
  218.5 2.9 %collective-permute-start.3 = (bf16[128,128]{1,0:T(8,128)(2,1)S(1)}, bf16[128,128]{1,0:T(8,128)(2,1)S(1)}, u32[]{:S(2)}, u32[]{:S(2)}) collective-permute-start(bf16[128,128]{1,0:T(8,128)(2,1)S(1)} %get-tuple-element.43), channel_id=1, source_target_pairs={{0,16},{4,20},{8,24},{12,28},{16,0},{20,4},{24,8},{28,12},{1,17},{... | collective-permute-start | bytes 98312 | tf_op jit(solution)/shard_map/ppermute | solution.py:381
  221.4 5.8 %collective-permute-done.1 = bf16[128,128]{1,0:T(8,128)(2,1)S(1)} collective-permute-done((bf16[128,128]{1,0:T(8,128)(2,1)S(1)}, bf16[128,128]{1,0:T(8,128)(2,1)S(1)}, u32[]{:S(2)}, u32[]{:S(2)}) %collective-permute-start.1) | collective-permute-done | bytes 32800 | tf_op jit(solution)/shard_map/ppermute | solution.py:381
  227.2 11.1 %collective-permute-start.2 = (bf16[128,128]{1,0:T(8,128)(2,1)S(1)}, bf16[128,128]{1,0:T(8,128)(2,1)S(1)}, u32[]{:S(2)}, u32[]{:S(2)}) collective-permute-start(bf16[128,128]{1,0:T(8,128)(2,1)S(1)} %get-tuple-element.44), channel_id=1, source_target_pairs={{0,12},{4,16},{8,20},{12,24},{16,28},{20,0},{24,4},{28,8},{1,13},{... | collective-permute-start | bytes 98312 | tf_op jit(solution)/shard_map/ppermute | solution.py:381
  238.4 1.6 collective-permute-done.2
  241.3 2.8 %combine.1 = (bf16[4,128,1024]{2,1,0:T(8,128)(2,1)}, f32[128,1024]{1,0:T(8,128)}) custom-call(s32[1]{0:T(128)} %bitcast.chain_ref, bf16[1024,128]{1,0:T(8,128)(2,1)} %bitcast.111, bf16[4,128,1024]{2,1,0:T(8,128)(2,1)} %pad_maximum_fusion.ends_ref, f32[4,1024]{1,0:T(4,128)} %reshape.241.decay_ref), custom_call_target="tpu_custom_call" | custom-call | tf_op jit(solution)/shard_map/combine/pallas_call | solution.py:361
  251.3 8.0 %collective-permute-done.11 = bf16[128,1024]{1,0:T(8,128)(2,1)S(1)} collective-permute-done((bf16[128,1024]{1,0:T(8,128)(2,1)S(1)}, bf16[128,1024]{1,0:T(8,128)(2,1)S(1)}, u32[]{:S(2)}, u32[]{:S(2)}) %collective-permute-start.11) | collective-permute-done | bytes 262176 | tf_op jit(solution)/shard_map/ppermute | solution.py:381
  260.7 11.6 %finish.1 = bf16[512,4096]{1,0:T(8,128)(2,1)} custom-call(s32[3]{0:T(128)} %pad_add_fusion.place_ref, f32[512,4096]{1,0:T(8,128)} %get-tuple-element.12.part_ref, bf16[512,4096]{1,0:T(8,128)(2,1)} %bitcast.109, bf16[512,128]{1,0:T(8,128)(2,1)} %get-tuple-element.13.read_ref, f32[512,128]{1,0:T(8,128)} %get-tuple-element.14.decay_ref, ...), custom_call_target="tpu_custom_call" | custom-call | flops 3000000000 | bytes 16000000 | tf_op jit(solution)/shard_map/finish/pallas_call | solution.py:273
  272.3 9.4 %unpack.1 = f32[13,8,128,128]{3,2,1,0:T(8,128)} custom-call(f32[128,1024]{1,0:T(8,128)} %get-tuple-element.11.final_ref, bf16[8,12,128,128]{3,2,1,0:T(8,128)(2,1)} %all-to-all-done.1.pieces_ref), custom_call_target="tpu_custom_call" | custom-call | tf_op jit(solution)/shard_map/unpack/pallas_call | solution.py:334
  (106 shorter events, 36.9 us)
Async XLA Ops:
  9.9 7.5 %copy-start.4 = (s32[13]{0:T(128)S(1)}, s32[13]{0:T(128)}, u32[]{:S(2)}) copy-start(s32[13]{0:T(128)} %keep_ref.1) | copy-start | bytes 160
  9.9 8.6 %copy-start.7 = (s32[13,2]{0,1:T(2,128)S(1)}, s32[13,2]{0,1:T(2,128)}, u32[]{:S(2)}) copy-start(s32[13,2]{0,1:T(2,128)} %param.19) | copy-start | bytes 316
  9.9 8.7 %copy-start.2 = (f32[4352]{0:T(1024)S(1)}, f32[4352]{0:T(1024)}, u32[]{:S(2)}) copy-start(f32[4352]{0:T(1024)} %param.27) | copy-start | bytes 52228
  9.9 9.4 %copy-start.5 = (f32[64]{0:T(128)S(1)}, f32[64]{0:T(128)}, u32[]{:S(2)}) copy-start(f32[64]{0:T(128)} %param.30) | copy-start | bytes 772
  10.0 11.1 %copy-start.3 = (bf16[13,3,64]{2,0,1:T(8,128)(2,1)S(1)}, bf16[13,3,64]{2,0,1:T(8,128)(2,1)}, u32[]{:S(2)}) copy-start(bf16[13,3,64]{2,0,1:T(8,128)(2,1)} %param.18) | copy-start | bytes 14980
  10.0 143.4 %all-to-all-start = ((bf16[8,13,128,128]{3,2,1,0:T(8,128)(2,1)}), bf16[8,13,128,128]{3,2,1,0:T(8,128)(2,1)S(1)}, u32[]{:S(2)}, u32[]{:S(2)}) async-start(bf16[8,13,128,128]{3,2,1,0:T(8,128)(2,1)} %pack.1), calls=%async_computation | async-start | bytes 6815744 | tf_op jit(solution)/shard_map/all_to_all | solution.py:373
  134.4 3.8 %copy-start.6 = (f32[64]{0:T(128)}, f32[64]{0:T(128)S(1)}, u32[]{:S(2)}) copy-start(f32[64]{0:T(128)S(1)} %exponential_multiply_fusion) | copy-start | bytes 772
  146.0 0.7 copy-start
  156.1 116.2 %all-to-all-start.1 = ((bf16[8,12,128,128]{3,2,1,0:T(8,128)(2,1)}), bf16[8,12,128,128]{3,2,1,0:T(8,128)(2,1)}, u32[]{:S(2)}, u32[]{:S(2)}) async-start(bf16[8,12,128,128]{3,2,1,0:T(8,128)(2,1)} %bitcast.106), calls=%async_computation.1 | async-start | bytes 6291456 | tf_op jit(solution)/shard_map/all_to_all | solution.py:373
  162.1 36.2 %copy-start.1 = (bf16[13,3328]{1,0:T(8,128)(2,1)S(1)}, bf16[13,3328]{1,0:T(8,128)(2,1)}, u32[]{:S(2)}) copy-start(bf16[13,3328]{1,0:T(8,128)(2,1)} %gather_fusion.3) | copy-start | bytes 259588
  196.3 11.6 %collective-permute-start.9 = (bf16[128,1024]{1,0:T(8,128)(2,1)}, bf16[128,1024]{1,0:T(8,128)(2,1)}, u32[]{:S(2)}, u32[]{:S(2)}) collective-permute-start(bf16[128,1024]{1,0:T(8,128)(2,1)} %get-tuple-element.35), channel_id=1, source_target_pairs={{0,3},{1,0},{2,1},{3,2},{4,7},{5,4},{6,5},{7,6},{8,11},{9,8},{10,9... | collective-permute-start | bytes 786440 | tf_op jit(solution)/shard_map/ppermute | solution.py:381
  197.7 13.3 %collective-permute-start.8 = (bf16[128,1024]{1,0:T(8,128)(2,1)}, bf16[128,1024]{1,0:T(8,128)(2,1)}, u32[]{:S(2)}, u32[]{:S(2)}) collective-permute-start(bf16[128,1024]{1,0:T(8,128)(2,1)} %get-tuple-element.36), channel_id=1, source_target_pairs={{0,2},{1,3},{2,0},{3,1},{4,6},{5,7},{6,4},{7,5},{8,10},{9,11},{10,... | collective-permute-start | bytes 786440 | tf_op jit(solution)/shard_map/ppermute | solution.py:381
  198.3 12.7 %collective-permute-start.7 = (bf16[128,1024]{1,0:T(8,128)(2,1)}, bf16[128,1024]{1,0:T(8,128)(2,1)}, u32[]{:S(2)}, u32[]{:S(2)}) collective-permute-start(bf16[128,1024]{1,0:T(8,128)(2,1)} %get-tuple-element.37), channel_id=1, source_target_pairs={{0,1},{1,2},{2,3},{3,0},{4,5},{5,6},{6,7},{7,4},{8,9},{9,10},{10,1... | collective-permute-start | bytes 786440 | tf_op jit(solution)/shard_map/ppermute | solution.py:381
  206.2 15.2 %collective-permute-start = (bf16[128,128]{1,0:T(8,128)(2,1)S(1)}, bf16[128,128]{1,0:T(8,128)(2,1)S(1)}, u32[]{:S(2)}, u32[]{:S(2)}) collective-permute-start(bf16[128,128]{1,0:T(8,128)(2,1)S(1)} %get-tuple-element.46), channel_id=1, source_target_pairs={{0,4},{4,8},{8,12},{12,16},{16,20},{20,24},{24,28},{28,0},{1,5},{5... | collective-permute-start | bytes 98312 | tf_op jit(solution)/shard_map/ppermute | solution.py:381
  213.3 26.7 %collective-permute-start.6 = (bf16[128,128]{1,0:T(8,128)(2,1)S(1)}, bf16[128,128]{1,0:T(8,128)(2,1)S(1)}, u32[]{:S(2)}, u32[]{:S(2)}) collective-permute-start(bf16[128,128]{1,0:T(8,128)(2,1)S(1)} %get-tuple-element.40), channel_id=1, source_target_pairs={{0,28},{4,0},{8,4},{12,8},{16,12},{20,16},{24,20},{28,24},{1,29},{... | collective-permute-start | bytes 98312 | tf_op jit(solution)/shard_map/ppermute | solution.py:381
  217.9 22.1 %collective-permute-start.5 = (bf16[128,128]{1,0:T(8,128)(2,1)S(1)}, bf16[128,128]{1,0:T(8,128)(2,1)S(1)}, u32[]{:S(2)}, u32[]{:S(2)}) collective-permute-start(bf16[128,128]{1,0:T(8,128)(2,1)S(1)} %get-tuple-element.41), channel_id=1, source_target_pairs={{0,24},{4,28},{8,0},{12,4},{16,8},{20,12},{24,16},{28,20},{1,25},{... | collective-permute-start | bytes 98312 | tf_op jit(solution)/shard_map/ppermute | solution.py:381
  218.5 21.5 %collective-permute-start.4 = (bf16[128,128]{1,0:T(8,128)(2,1)S(1)}, bf16[128,128]{1,0:T(8,128)(2,1)S(1)}, u32[]{:S(2)}, u32[]{:S(2)}) collective-permute-start(bf16[128,128]{1,0:T(8,128)(2,1)S(1)} %get-tuple-element.42), channel_id=1, source_target_pairs={{0,20},{4,24},{8,28},{12,0},{16,4},{20,8},{24,12},{28,16},{1,21},{... | collective-permute-start | bytes 98312 | tf_op jit(solution)/shard_map/ppermute | solution.py:381
  218.5 21.5 %collective-permute-start.3 = (bf16[128,128]{1,0:T(8,128)(2,1)S(1)}, bf16[128,128]{1,0:T(8,128)(2,1)S(1)}, u32[]{:S(2)}, u32[]{:S(2)}) collective-permute-start(bf16[128,128]{1,0:T(8,128)(2,1)S(1)} %get-tuple-element.43), channel_id=1, source_target_pairs={{0,16},{4,20},{8,24},{12,28},{16,0},{20,4},{24,8},{28,12},{1,17},{... | collective-permute-start | bytes 98312 | tf_op jit(solution)/shard_map/ppermute | solution.py:381
  221.4 5.8 %collective-permute-start.1 = (bf16[128,128]{1,0:T(8,128)(2,1)S(1)}, bf16[128,128]{1,0:T(8,128)(2,1)S(1)}, u32[]{:S(2)}, u32[]{:S(2)}) collective-permute-start(bf16[128,128]{1,0:T(8,128)(2,1)S(1)} %get-tuple-element.45), channel_id=1, source_target_pairs={{0,8},{4,12},{8,16},{12,20},{16,24},{20,28},{24,0},{28,4},{1,9},{5... | collective-permute-start | bytes 98312 | tf_op jit(solution)/shard_map/ppermute | solution.py:381
  227.2 12.7 %collective-permute-start.2 = (bf16[128,128]{1,0:T(8,128)(2,1)S(1)}, bf16[128,128]{1,0:T(8,128)(2,1)S(1)}, u32[]{:S(2)}, u32[]{:S(2)}) collective-permute-start(bf16[128,128]{1,0:T(8,128)(2,1)S(1)} %get-tuple-element.44), channel_id=1, source_target_pairs={{0,12},{4,16},{8,20},{12,24},{16,28},{20,0},{24,4},{28,8},{1,13},{... | collective-permute-start | bytes 98312 | tf_op jit(solution)/shard_map/ppermute | solution.py:381
  245.4 5.9 %collective-permute-start.12 = (bf16[128,1024]{1,0:T(8,128)(2,1)S(1)}, bf16[128,1024]{1,0:T(8,128)(2,1)S(1)}, u32[]{:S(2)}, u32[]{:S(2)}) collective-permute-start(bf16[128,1024]{1,0:T(8,128)(2,1)S(1)} %get-tuple-element.31), channel_id=1, source_target_pairs={{0,3},{1,0},{2,1},{3,2},{4,7},{5,4},{6,5},{7,6},{8,11},{9,8},{10,9... | collective-permute-start | bytes 786440 | tf_op jit(solution)/shard_map/ppermute | solution.py:381
  245.5 13.9 %collective-permute-start.11 = (bf16[128,1024]{1,0:T(8,128)(2,1)S(1)}, bf16[128,1024]{1,0:T(8,128)(2,1)S(1)}, u32[]{:S(2)}, u32[]{:S(2)}) collective-permute-start(bf16[128,1024]{1,0:T(8,128)(2,1)S(1)} %get-tuple-element.32), channel_id=1, source_target_pairs={{0,2},{1,3},{2,0},{3,1},{4,6},{5,7},{6,4},{7,5},{8,10},{9,11},{10,... | collective-permute-start | bytes 786440 | tf_op jit(solution)/shard_map/ppermute | solution.py:381
  246.9 12.7 %collective-permute-start.10 = (bf16[128,1024]{1,0:T(8,128)(2,1)S(1)}, bf16[128,1024]{1,0:T(8,128)(2,1)S(1)}, u32[]{:S(2)}, u32[]{:S(2)}) collective-permute-start(bf16[128,1024]{1,0:T(8,128)(2,1)S(1)} %get-tuple-element.33), channel_id=1, source_target_pairs={{0,1},{1,2},{2,3},{3,0},{4,5},{5,6},{6,7},{7,4},{8,9},{9,10},{10,1... | collective-permute-start | bytes 786440 | tf_op jit(solution)/shard_map/ppermute | solution.py:381

commit v2 on v1

--- a/solution.py
+++ b/solution.py
@@ -18,6 +18,8 @@
 PAIR_DIM = 2 * HEAD_DIM
 LANES = 128
 TILE = 128
+SLOT_TILE = 4
+PEER_TILE = 2
 EPSILON = 1e-05
 LOG2E = math.log2(math.e)
 F32 = jnp.float32
@@ -237,10 +239,17 @@
 
 
 def finish_kernel(
-    place_ref, part_ref, gate_ref, read_ref, decay_ref, state_ref, norm_ref, out_ref, gated_scr
+    place_ref, part_ref, gate_ref, read_ref, decay_ref, norm_ref, *refs
 ):
+    state_refs, out_ref, gated_scr, state_scr = refs[:-3], refs[-3], refs[-2], refs[-1]
     tile = pl.program_id(0)
-    chunks, _, width = state_ref.shape
+    chunks, _, width = state_scr.shape
+
+    @pl.when(tile == 0)
+    def _():
+        for hop in range(chunks):
+            state_scr[lax.rem(place_ref[2] - hop + chunks, chunks)] = state_refs[hop][...]
+
     positions = (
         place_ref[0] + tile * TILE + lax.broadcasted_iota(jnp.int32, (TILE, PAIR_DIM), 0)
     )
@@ -250,11 +259,10 @@
     decay = decay_ref[...]
     total = jnp.zeros((TILE, PAIR_DIM), F32)
     for chunk in range(chunks):
-        from_chunk = lax.rem(place_ref[2] - chunk + chunks, chunks)
         for i in range(width // PAIR_DIM):
             pair = chunk * (width // PAIR_DIM) + i
             span = slice(pair * PAIR_DIM, (pair + 1) * PAIR_DIM)
-            inter = dot(read, state_ref[from_chunk, :, i * PAIR_DIM : (i + 1) * PAIR_DIM])
+            inter = dot(read, state_scr[chunk, :, i * PAIR_DIM : (i + 1) * PAIR_DIM])
             y = part_ref[:, span] + inter * pair_of(decay, pair, low)
             y = (y * valid).astype(BF16).astype(F32)
             gated = y * silu(gate_ref[:, span].astype(F32))
@@ -268,7 +276,7 @@
         out_ref[:, span] = (gated_scr[:, span] * scale * norm_ref[:, span]).astype(BF16)
 
 
-def finish(place, part, gate, read, decay, states, norm_row):
+def finish(place, part, gate, read, decay, norm_row, states):
     length, channels = part.shape
     return pl.pallas_call(
         finish_kernel,
@@ -279,94 +287,396 @@
             pl.BlockSpec((TILE, channels), lambda t: (t, 0)),
             pl.BlockSpec((TILE, STATE_DIM), lambda t: (t, 0)),
             pl.BlockSpec((TILE, LANES), lambda t: (t, 0)),
-            pl.BlockSpec(states.shape, lambda t: (0, 0, 0)),
             pl.BlockSpec((1, channels), lambda t: (0, 0)),
-        ],
+        ]
+        + [pl.BlockSpec(state.shape, lambda t: (0, 0)) for state in states],
         out_specs=pl.BlockSpec((TILE, channels), lambda t: (t, 0)),
         out_shape=jax.ShapeDtypeStruct((length, channels), BF16),
-        scratch_shapes=[pltpu.VMEM((TILE, channels), F32)],
+        scratch_shapes=[
+            pltpu.VMEM((TILE, channels), F32),
+            pltpu.VMEM((len(states),) + states[0].shape, BF16),
+        ],
         compiler_params=pltpu.CompilerParams(dimension_semantics=("arbitrary",)),
         cost_estimate=pl.CostEstimate(
             flops=3_000_000_000, bytes_accessed=16_000_000, transcendentals=4_000_000
         ),
         name="finish",
-    )(place, part, gate, read, decay, states, norm_row)
-
-
-def pack_kernel(keep_ref, state_ref, out_ref):
-    keep = keep_ref[pl.program_id(0)].astype(F32)
-    out_ref[:, 0] = (state_ref[0] * keep).astype(BF16)
-
-
-def pack(keep, states):
+    )(place, part, gate, read, decay, norm_row, *states)
+
+
+def pack_kernel(place_ref, state_ref, after_ref, *out_refs):
+    first_slot = pl.program_id(0) * SLOT_TILE
+    peers = state_ref.shape[1]
+    for j in range(SLOT_TILE):
+        keep = place_ref[1 + first_slot + j].astype(F32)
+        for hop in range(len(out_refs)):
+            peer = lax.rem(place_ref[0] + hop, peers)
+            out_refs[hop][j] = (state_ref[j, peer] * keep).astype(BF16)
+
+
+def pack(place, states, after):
     slots, peers, piece, width = states.shape
+    half = piece // 2
+    steps = pl.cdiv(slots, SLOT_TILE)
     return pl.pallas_call(
         pack_kernel,
-        grid=(slots,),
+        grid=(steps,),
         in_specs=[
             pl.BlockSpec(memory_space=pltpu.SMEM),
-            pl.BlockSpec((1, peers, piece, width), lambda t: (t, 0, 0, 0)),
-        ],
-        out_specs=pl.BlockSpec((peers, 1, piece, width), lambda t: (0, t, 0, 0)),
-        out_shape=jax.ShapeDtypeStruct((peers, slots, piece, width), BF16),
+            pl.BlockSpec((SLOT_TILE, peers, half, width), lambda t: (t, 0, 0, 0)),
+            pl.BlockSpec(memory_space=pl.ANY),
+        ],
+        out_specs=[pl.BlockSpec((SLOT_TILE, half, width), lambda t: (t, 0, 0))] * peers,
+        out_shape=[jax.ShapeDtypeStruct((slots, half, width), BF16)] * peers,
         compiler_params=pltpu.CompilerParams(dimension_semantics=("arbitrary",)),
         name="pack",
-    )(keep, states)
-
-
-def unpack_kernel(final_ref, pieces_ref, out_ref):
-    slot = pl.program_id(0)
-    peers, piece = out_ref.shape[1:3]
-
-    @pl.when(slot == 0)
+    )(place, states, after)
+
+
+def pack_rest_kernel(place_ref, state_ref, after_ref, out_ref):
+    first_slot = pl.program_id(0) * SLOT_TILE
+    for j in range(SLOT_TILE):
+        keep = place_ref[1 + first_slot + j].astype(F32)
+        out_ref[:, j] = (state_ref[j] * keep).astype(BF16)
+
+
+def pack_rest(place, states, after):
+    slots, peers, piece, width = states.shape
+    half = piece // 2
+    steps = pl.cdiv(slots, SLOT_TILE)
+    return pl.pallas_call(
+        pack_rest_kernel,
+        grid=(steps,),
+        in_specs=[
+            pl.BlockSpec(memory_space=pltpu.SMEM),
+            pl.BlockSpec((SLOT_TILE, peers, half, width), lambda t: (t, 0, 1, 0)),
+            pl.BlockSpec(memory_space=pl.ANY),
+        ],
+        out_specs=pl.BlockSpec((peers, SLOT_TILE, half, width), lambda t: (0, t, 0, 0)),
+        out_shape=jax.ShapeDtypeStruct((peers, slots, half, width), BF16),
+        compiler_params=pltpu.CompilerParams(dimension_semantics=("arbitrary",)),
+        name="pack_rest",
+    )(place, states, after)
+
+
+def reorder_kernel(order_ref, *refs):
+    in_refs, out_ref, sems = refs[:-2], refs[-2], refs[-1]
+    slots = in_refs[0].shape[0]
+    for hop in range(len(in_refs)):
+
+        def start(i, unused):
+            target = order_ref[hop * slots + i]
+            pltpu.make_async_copy(in_refs[hop].at[i], out_ref.at[target], sems.at[hop]).start()
+            return unused
+
+        lax.fori_loop(0, slots, start, 0)
+    for hop in range(len(in_refs)):
+        span = pl.ds(hop * slots, slots)
+        pltpu.make_async_copy(in_refs[hop], out_ref.at[span], sems.at[hop]).wait()
+
+
+def reorder(order, pieces):
+    slots, half, width = pieces[0].shape
+    count = len(pieces)
+    whole = pl.BlockSpec(memory_space=pltpu.HBM)
+    return pl.pallas_call(
+        reorder_kernel,
+        in_specs=[pl.BlockSpec(memory_space=pltpu.SMEM)] + [whole] * count,
+        out_specs=whole,
+        out_shape=jax.ShapeDtypeStruct((count * slots, half, width), BF16),
+        scratch_shapes=[pltpu.SemaphoreType.DMA((count,))],
+        name="reorder",
+    )(order, *pieces)
+
+
+def unpack_kernel(place_ref, final_ref, *refs):
+    pieces, out_ref = refs[:-1], refs[-1]
+    step = pl.program_id(0)
+    peers, half = out_ref.shape[1:3]
+    for hop in range(peers):
+        peer = lax.rem(place_ref[0] - hop + peers, peers)
+        for j in range(SLOT_TILE):
+            out_ref[j, peer] = pieces[hop][j].astype(F32)
+
+    @pl.when(step == 0)
     def _():
         for p in range(peers):
-            out_ref[0, p] = final_ref[:, p * piece : (p + 1) * piece].T
-
-    @pl.when(slot > 0)
-    def _():
-        out_ref[0] = pieces_ref[:, 0].astype(F32)
-
-
-def unpack(final, pieces):
-    peers, others, piece, width = pieces.shape
-    slots = others + 1
+            out_ref[0, p] = final_ref[2 * p * half : (2 * p + 1) * half, :]
+
+
+def unpack(place, final, pieces):
+    peers = len(pieces)
+    slots, half, width = pieces[0].shape
     return pl.pallas_call(
         unpack_kernel,
-        grid=(slots,),
+        grid=(pl.cdiv(slots, SLOT_TILE),),
         in_specs=[
+            pl.BlockSpec(memory_space=pltpu.SMEM),
             pl.BlockSpec(final.shape, lambda t: (0, 0)),
-            pl.BlockSpec((peers, 1, piece, width), lambda t: (0, jnp.maximum(t - 1, 0), 0, 0)),
-        ],
-        out_specs=pl.BlockSpec((1, peers, piece, width), lambda t: (t, 0, 0, 0)),
-        out_shape=jax.ShapeDtypeStruct((slots, peers, piece, width), F32),
+        ]
+        + [pl.BlockSpec((SLOT_TILE, half, width), lambda t: (t, 0, 0))] * peers,
+        out_specs=pl.BlockSpec((SLOT_TILE, peers, half, width), lambda t: (t, 0, 0, 0)),
+        out_shape=jax.ShapeDtypeStruct((slots, peers, 2 * half, width), F32),
         compiler_params=pltpu.CompilerParams(dimension_semantics=("arbitrary",)),
         name="unpack",
-    )(final, pieces)
-
-
-def combine_kernel(chain_ref, first_ref, ends_ref, decay_ref, entering_ref, final_ref):
+    )(place, final, *pieces)
+
+
+def unpack_rest_kernel(final_ref, pieces_ref, states_ref, out_ref):
+    peers, half = pieces_ref.shape[0], pieces_ref.shape[2]
+    for p in range(peers):
+        out_ref[0, p] = final_ref[(2 * p + 1) * half : (2 * p + 2) * half, :]
+        out_ref[1:, p] = pieces_ref[p].astype(F32)
+
+
+def unpack_rest(final, pieces, states):
+    slots, peers, piece, width = states.shape
+    half = piece // 2
+    return pl.pallas_call(
+        unpack_rest_kernel,
+        grid=(peers // PEER_TILE,),
+        in_specs=[
+            pl.BlockSpec((PEER_TILE * piece, width), lambda p: (p, 0)),
+            pl.BlockSpec((PEER_TILE, slots - 1, half, width), lambda p: (p, 0, 0, 0)),
+            pl.BlockSpec(memory_space=pl.ANY),
+        ],
+        out_specs=pl.BlockSpec((slots, PEER_TILE, half, width), lambda p: (0, p, 1, 0)),
+        out_shape=jax.ShapeDtypeStruct(states.shape, F32),
+        input_output_aliases={2: 0},
+        compiler_params=pltpu.CompilerParams(dimension_semantics=("arbitrary",)),
+        name="unpack_rest",
+    )(final, pieces, states)
+
+
+def combine_kernel(place_ref, decay_ref, *refs):
+    peers, count = decay_ref.shape[1], decay_ref.shape[0]
+    count = decay_ref.shape[0]
+    scr, end_scr, enter_scr = refs[-3:]
+    entering_refs = refs[-4 - count : -4]
+    final_ref = refs[-4]
+    inputs = refs[: -4 - count]
+    end_refs = inputs[:count]
+    peers = (len(inputs) - count) // 2
+    upper, lower = inputs[count : count + peers], inputs[count + peers :]
+    half = lower[0].shape[0]
+    chain = place_ref[1]
+    for hop in range(peers):
+        peer = lax.rem(place_ref[0] - hop + peers, peers)
+        at = pl.multiple_of(peer * 2 * half, 16)
+        scr[pl.ds(at, half), :] = upper[hop][0]
+        scr[pl.ds(at + half, half), :] = lower[hop][...]
+    for hop in range(count):
+        end_scr[lax.rem(chain - hop + count, count)] = end_refs[hop][...]
+    state = scr[...].astype(F32).T
+    for k in range(count):
+        enter_scr[k] = state.astype(BF16)
+        state = state * decay_ref[k : k + 1, :] + end_scr[k].astype(F32)
+    for hop in range(count):
+        entering_refs[hop][...] = enter_scr[lax.rem(chain + hop, count)]
+    final_ref[...] = state.T
+
+
+def combine(place, decay, ends, upper, lower):
+    count = len(ends)
+    whole = pl.BlockSpec(memory_space=pltpu.VMEM)
+    half, width = lower[0].shape
+    rows, columns = ends[0].shape
+    outs = pl.pallas_call(
+        combine_kernel,
+        grid=(1,),
+        in_specs=[
+            pl.BlockSpec(memory_space=pltpu.SMEM),
+            pl.BlockSpec(decay.shape, lambda t: (0, 0)),
+        ]
+        + [pl.BlockSpec((rows, columns), lambda t: (0, 0))] * count
+        + [pl.BlockSpec((1, half, width), lambda t: (0, 0, 0))] * len(upper)
+        + [pl.BlockSpec((half, width), lambda t: (0, 0))] * len(lower),
+        out_specs=[pl.BlockSpec((rows, columns), lambda t: (0, 0))] * count
+        + [pl.BlockSpec((columns, rows), lambda t: (0, 0))],
+        out_shape=[jax.ShapeDtypeStruct((rows, columns), BF16)] * count
+        + [jax.ShapeDtypeStruct((columns, rows), F32)],
+        scratch_shapes=[
+            pltpu.VMEM((columns, rows), BF16),
+            pltpu.VMEM((count, rows, columns), BF16),
+            pltpu.VMEM((count, rows, columns), BF16),
+        ],
+        name="combine",
+    )(place, decay, *ends, *upper, *lower)
+    return outs[:count], outs[count]
+
+
+def share_kernel(
+    place_ref,
+    every_ref,
+    end_ref,
+    kept_ref,
+    kept_next_ref,
+    state_end_ref,
+    state_kept_ref,
+    state_next_ref,
+    raw_ref,
+    bias_ref,
+    rate_ref,
+    out_ref,
+    step_ref,
+):
+    taps = out_ref.shape[0]
+    inner = end_ref.shape[1]
+    outer = state_end_ref.shape[1]
+    channels = inner + outer
+    first = place_ref[0]
+    low_block, high_block, start, length = (
+        place_ref[1],
+        place_ref[2],
+        place_ref[3],
+        place_ref[4],
+    )
+    out_ref[:, :inner] = end_ref[16 - taps :, :]
+    out_ref[:, inner:channels] = state_end_ref[16 - taps :, :]
+    here = lax.broadcasted_iota(jnp.int32, (16, 1), 0)
+    wanted = length - taps - start
+
+    def kept_rows(low_ref, high_ref):
+        low = low_ref[...].astype(F32)
+        high = high_ref[...].astype(F32)
+        found = []
+        for i in range(taps):
+            in_low = (low_block * 16 + here) == (wanted + i)
+            in_high = ((high_block * 16 + here) == (wanted + i)) & (high_block > low_block)
+            picked = jnp.where(in_low, low, 0.0) + jnp.where(in_high, high, 0.0)
+            found.append(jnp.sum(picked, axis=0, keepdims=True))
+        return jnp.concatenate(found, axis=0).astype(BF16)
+
+    out_ref[:, channels : channels + inner] = kept_rows(kept_ref, kept_next_ref)
+    out_ref[:, channels + inner : 2 * channels] = kept_rows(state_kept_ref, state_next_ref)
+    window = every_ref[first].astype(F32)
+    width = window.shape[1]
+    keep = window[taps - 1 :, width - 1 :]
+    out_ref[:, 2 * channels : 2 * channels + width] = (window * keep).astype(BF16)
+    count = step_ref.shape[0]
+    heads = raw_ref.shape[1]
+    positions = start + lax.broadcasted_iota(jnp.int32, (count, heads), 0)
+    raw = raw_ref[...].astype(F32) + bias_ref[...]
+    step = jnp.maximum(raw, 0.0) + jnp.log1p(jnp.exp(-jnp.abs(raw)))
+    step = jnp.where(positions < length, step, 0.0)
+    step = jnp.concatenate([step, jnp.zeros((count, LANES - heads), F32)], axis=1)
+    step_ref[...] = step
+    total = jnp.sum(step * rate_ref[...], axis=0, keepdims=True)
+    high = total.astype(BF16).astype(F32)
+    middle = (total - high).astype(BF16).astype(F32)
+    rest = total - high - middle
+    parts = jnp.concatenate([high, middle, rest], axis=0)
+    out_ref[:, 2 * channels + width :] = parts.astype(BF16)
+
+
+def share(place, every, rows, state_rows, step_raw, step_bias, rate):
+    taps = every.shape[1]
+    width = every.shape[2]
+    length, inner = rows.shape
+    outer = state_rows.shape[1]
+    heads = step_raw.shape[1]
+    last = length // 16 - 1
+    total = 2 * (inner + outer) + width + LANES
+    return pl.pallas_call(
+        share_kernel,
+        grid_spec=pltpu.PrefetchScalarGridSpec(
+            num_scalar_prefetch=1,
+            grid=(1,),
+            in_specs=[
+                pl.BlockSpec(every.shape, lambda t, c: (0, 0, 0)),
+                pl.BlockSpec((16, inner), lambda t, c: (last, 0)),
+                pl.BlockSpec((16, inner), lambda t, c: (c[1], 0)),
+                pl.BlockSpec((16, inner), lambda t, c: (c[2], 0)),
+                pl.BlockSpec((16, outer), lambda t, c: (last, 0)),
+                pl.BlockSpec((16, outer), lambda t, c: (c[1], 0)),
+                pl.BlockSpec((16, outer), lambda t, c: (c[2], 0)),
+                pl.BlockSpec((length, heads), lambda t, c: (0, 0)),
+                pl.BlockSpec((1, heads), lambda t, c: (0, 0)),
+                pl.BlockSpec((1, LANES), lambda t, c: (0, 0)),
+            ],
+            out_specs=[
+                pl.BlockSpec((taps, total), lambda t, c: (0, 0)),
+                pl.BlockSpec((length, LANES), lambda t, c: (0, 0)),
+            ],
+        ),
+        out_shape=[
+            jax.ShapeDtypeStruct((taps, total), BF16),
+            jax.ShapeDtypeStruct((length, LANES), F32),
+        ],
+        name="share",
+    )(
+        place,
+        every,
+        rows,
+        rows,
+        rows,
+        state_rows,
+        state_rows,
+        state_rows,
+        step_raw,
+        step_bias,
+        rate,
+    )
+
+
+def tail_kernel(chain_ref, shared_ref, tail_ref, inner_ref, outer_ref, decay_ref):
     chain = chain_ref[0]
-    count = ends_ref.shape[0]
-    state = first_ref[...].astype(F32).T
-    for k in range(count):
-        entering_ref[lax.rem(k - chain + count, count)] = state.astype(BF16)
-        end = ends_ref[lax.rem(chain - k + count, count)].astype(F32)
-        state = state * decay_ref[k : k + 1, :] + end
-    final_ref[...] = state
-
-
-def combine(chain, first, ends, decay):
+    count, taps = shared_ref.shape[:2]
+    inner_local, outer_local = inner_ref.shape[1], outer_ref.shape[1]
+    channels = tail_ref.shape[1]
+    inner = count * inner_local
+    at = 2 * channels
+    window = jnp.concatenate(
+        [shared_ref[s, :, at : at + inner_local] for s in range(count)]
+        + [
+            shared_ref[s, :, at + inner_local : at + inner_local + outer_local]
+            for s in range(count)
+        ],
+        axis=1,
+    ).astype(F32)
+    earlier = shared_ref[jnp.maximum(chain - 1, 0), :, :channels].astype(F32)
+    tail = jnp.where(chain == 0, window, earlier)
+    tail_ref[...] = jnp.concatenate([jnp.zeros((8 - taps, channels), F32), tail], axis=0)
+    kept = shared_ref[0, :, channels:at].astype(F32)
+    for s in range(1, count):
+        kept = kept + shared_ref[s, :, channels:at].astype(F32)
+    own_inner = jnp.zeros((taps, inner_local), F32)
+    own_outer = jnp.zeros((taps, outer_local), F32)
+    for s in range(count):
+        mine = chain == s
+        inner_at, outer_at = s * inner_local, inner + s * outer_local
+        own_inner = jnp.where(mine, kept[:, inner_at : inner_at + inner_local], own_inner)
+        own_outer = jnp.where(mine, kept[:, outer_at : outer_at + outer_local], own_outer)
+    inner_ref[...] = own_inner.astype(BF16)
+    outer_ref[...] = own_outer.astype(BF16)
+    logs = []
+    for s in range(count):
+        parts = shared_ref[s, :, shared_ref.shape[2] - LANES :].astype(F32)
+        logs.append(jnp.sum(parts, axis=0, keepdims=True))
+    logs = jnp.concatenate(logs + [jnp.zeros((8 - count, LANES), F32)] * (count < 8), axis=0)
+    columns = decay_ref.shape[1]
+    head = lax.broadcasted_iota(jnp.int32, (LANES, columns), 0)
+    lane = lax.broadcasted_iota(jnp.int32, (LANES, columns), 1)
+    local_heads = columns // HEAD_DIM
+    pick = (head == chain * local_heads + lane // HEAD_DIM).astype(F32)
+    spread = dot(logs, pick, precision=lax.Precision.HIGHEST)
+    decay_ref[...] = jnp.exp2(spread[:count])
+
+
+def tails(chain, shared, channels, inner_local, outer_local, columns):
+    count, taps = shared.shape[:2]
     whole = pl.BlockSpec(memory_space=pltpu.VMEM)
     return pl.pallas_call(
-        combine_kernel,
-        in_specs=[pl.BlockSpec(memory_space=pltpu.SMEM), whole, whole, whole],
+        tail_kernel,
+        in_specs=[pl.BlockSpec(memory_space=pltpu.SMEM), whole],
         out_shape=[
-            jax.ShapeDtypeStruct(ends.shape, BF16),
-            jax.ShapeDtypeStruct(ends.shape[1:], F32),
-        ],
-        name="combine",
-    )(chain, first, ends, decay)
+            jax.ShapeDtypeStruct((8, channels), F32),
+            jax.ShapeDtypeStruct((taps, inner_local), BF16),
+            jax.ShapeDtypeStruct((taps, outer_local), BF16),
+            jax.ShapeDtypeStruct((count, columns), F32),
+        ],
+        name="tails",
+    )(chain, shared)
 
 
 def exchange(value, axis):
@@ -375,11 +685,11 @@
 
 def rotate(values, axis):
     count = lax.axis_size(axis)
-    got = [values[0]]
-    for hop in range(1, count):
+    got = [values[0]] + [None] * (count - 1)
+    for hop in sorted(range(1, count), key=lambda hop: abs(2 * hop - count)):
         pairs = [(source, (source + hop) % count) for source in range(count)]
-        got.append(lax.ppermute(values[hop], axis, pairs))
-    return jnp.stack(got)
+        got[hop] = lax.ppermute(values[hop], axis, pairs)
+    return got
 
 
 def rows_at(source, indices):
@@ -405,95 +715,81 @@
     norm_weight,
 ):
     peers = lax.axis_size("req")
-    own_peer = lax.axis_index("req")
+    own_peer = lax.axis_index("req").astype(jnp.int32)
     chain_size = lax.axis_size("seq")
-    chain_index = lax.axis_index("seq")
+    chain_index = lax.axis_index("seq").astype(jnp.int32)
     slots, local_heads = pool_states.shape[:2]
-    piece = local_heads * HEAD_DIM // peers
+    columns = local_heads * HEAD_DIM
+    piece = columns // peers
+    half = piece // 2
     taps = KERNEL - 1
-    keep_flag = active_mask.astype(F32)
-
-    pieces = pack(active_mask, pool_states.reshape(slots, peers, piece, STATE_DIM))
-    spread = exchange(pieces, "req").reshape(peers * slots, piece, STATE_DIM)
-
     inner_local = inner_window.shape[2]
     outer_local = state_window.shape[2]
-    own_windows = jnp.concatenate([inner_window, state_window], axis=2).reshape(slots, -1)
-    own_windows = (own_windows.astype(F32) * keep_flag[:, None]).astype(BF16)
-    width = own_windows.shape[1]
-    padding = jnp.zeros((slots, -(width + 2) % LANES), BF16)
-    packed = jnp.concatenate([own_windows, move_plan.astype(BF16), padding], axis=1)
+    width = inner_local + outer_local
+
+    marks = jnp.stack([move_plan[:, 0], move_plan[:, 1], active_mask], axis=1).astype(BF16)
+    marks = jnp.broadcast_to(marks[:, :, None], (slots, taps, (-width) % LANES))
+    packed = jnp.concatenate([inner_window, state_window, marks], axis=2)
     every = lax.all_gather(packed, "req", axis=0, tiled=True)
-    every_plan = every[:, width : width + 2].astype(F32).astype(jnp.int32)
-    targets = every_plan[:, 0] * slots + every_plan[:, 1]
+
+    own = own_peer[None]
+    pack_place = jnp.concatenate(
+        [own, active_mask, jnp.zeros((-slots % SLOT_TILE,), jnp.int32)]
+    )
+    pool_pieces = pool_states.reshape(slots, peers, piece, STATE_DIM)
+    spread_a = rotate(pack(pack_place, pool_pieces, every), "req")
+    spread_b = exchange(pack_rest(pack_place, pool_pieces, every), "req")
+    spread_b = spread_b.reshape(peers * slots, half, STATE_DIM)
+
+    every_marks = every[:, :, width].astype(F32).astype(jnp.int32)
+    target_peer = every_marks[:, 0]
+    target_slot = every_marks[:, 1]
     order = jnp.arange(peers * slots, dtype=jnp.int32)
+    targets = target_peer * slots + target_slot
     sources = jnp.sum(jnp.where(targets[None, :] == order[:, None], order[None, :], 0), axis=1)
     own_sources = lax.dynamic_slice_in_dim(sources, own_peer * slots, slots)
-    moved_windows = rows_at(every, own_sources)[:, :width].reshape(slots, taps, -1)
+    hop_targets = lax.rem(target_peer - own_peer + peers, peers) * slots + target_slot
+    peer_order = jnp.arange(peers, dtype=jnp.int32)
+    by_hop = rows_at(
+        hop_targets.reshape(peers, slots), lax.rem(own_peer + peers - peer_order, peers)
+    ).reshape(-1)
 
     rows = inputs_inner[0]
     state_rows = inputs_state[0]
-    local_length = rows.shape[0]
-    inner_dim = rows.shape[1]
+    local_length, inner_dim = rows.shape
+    channels = inner_dim + state_rows.shape[1]
     start = chain_index * local_length
     length = lengths[0]
-    window_pos = length - taps + jnp.arange(taps, dtype=jnp.int32) - start
-    inside = (window_pos >= 0) & (window_pos < local_length)
-    safe_pos = jnp.clip(window_pos, 0, local_length - 1)
-    ends = jnp.concatenate(
-        [rows[local_length - taps :], state_rows[local_length - taps :]], axis=1
-    )
-    kept_here = jnp.concatenate([rows_at(rows, safe_pos), rows_at(state_rows, safe_pos)], axis=1)
-    kept_here = jnp.where(inside[:, None], kept_here, jnp.zeros_like(kept_here))
-    channels = ends.shape[1]
-    window_local = inner_local + outer_local
+    last_tile = local_length // 16 - 1
+    low_block = jnp.clip((length - taps - start) // 16, 0, last_tile)
+    high_block = jnp.minimum(low_block + 1, last_tile)
     heads = decay_log.shape[0]
-    head_pad = LANES - heads
-    rate = -LOG2E * jnp.exp(decay_log)
-    positions = start + jnp.arange(local_length, dtype=jnp.int32)
-    valid_rows = (positions < length).astype(F32)
-    step = jax.nn.softplus(step_raw[0].astype(F32) + step_bias) * valid_rows[:, None]
-    device_log = jnp.sum(step * rate, axis=0)
-    log_high = lax.reduce_precision(device_log, 8, 7)
-    log_middle = lax.reduce_precision(device_log - log_high, 8, 7)
-    log_low = lax.reduce_precision(device_log - log_high - log_middle, 8, 7)
-    log_parts = jnp.stack([log_high, log_middle, log_low]).astype(BF16)
-    shared = lax.all_gather(
-        jnp.concatenate([log_parts, moved_windows[0], ends, kept_here], axis=1), "seq", axis=0
-    )
-    every_log = jnp.sum(shared[:, :, :heads].astype(F32), axis=1)
-    shared = shared[:, :, heads:]
-    own_log = lax.dynamic_slice_in_dim(every_log, chain_index * local_heads, local_heads, 1)
-    own_decay = jnp.repeat(jnp.exp2(own_log), HEAD_DIM, axis=1)
-    first_window = jnp.concatenate(
-        [
-            shared[:, :, :inner_local].transpose(1, 0, 2).reshape(taps, -1),
-            shared[:, :, inner_local:window_local].transpose(1, 0, 2).reshape(taps, -1),
-        ],
-        axis=1,
-    )
-    earlier_rows = lax.dynamic_index_in_dim(
-        shared[:, :, window_local : window_local + channels],
-        jnp.maximum(chain_index - 1, 0),
-        0,
-        keepdims=False,
-    )
-    tail = jnp.where(chain_index == 0, first_window, earlier_rows).astype(F32)
-    tail = jnp.concatenate([jnp.zeros((8 - taps, channels), F32), tail], axis=0)
-    kept = jnp.sum(shared[:, :, window_local + channels :].astype(F32), axis=0).astype(BF16)
-    kept_inner = lax.dynamic_slice_in_dim(kept, chain_index * inner_local, inner_local, 1)
-    kept_outer = lax.dynamic_slice_in_dim(
-        kept, inner_dim + chain_index * outer_local, outer_local, 1
-    )
-
-    chain = chain_index.astype(jnp.int32)[None]
+    rate = jnp.pad(-LOG2E * jnp.exp(decay_log), (0, LANES - heads))[None]
+    payload, step = share(
+        jnp.stack([own_sources[0], low_block, high_block, start, length]),
+        every,
+        rows,
+        state_rows,
+        step_raw[0],
+        step_bias[None],
+        rate,
+    )
+    shared = lax.all_gather(payload, "seq", axis=0)
+    chain = chain_index[None]
+    tail, kept_inner, kept_outer, own_decay = tails(
+        chain, shared, channels, inner_local, outer_local, columns
+    )
+
+    reordered = reorder(by_hop, spread_a).reshape(peers, slots, half, STATE_DIM)
+    moved_a = rotate(reordered, "req")
+
     part, local_end, read_rows, decay = block_parts(
         chain,
         tail,
         rows,
         state_rows,
-        jnp.pad(step, ((0, 0), (0, head_pad))),
-        jnp.pad(rate, (0, head_pad))[None],
+        step,
+        rate,
         conv_weight,
         conv_bias[None],
         jnp.repeat(skip_weight, HEAD_DIM)[None],
@@ -502,31 +798,30 @@
     own_ends = rotate(local_end, "seq")
 
     order_by_peer = sources.reshape(peers, slots)
-    peer_order = jnp.arange(peers, dtype=jnp.int32)
     first_sources = rows_at(order_by_peer[:, 0], lax.rem(own_peer + peer_order, peers))
-    first_pieces = rotate(rows_at(spread, first_sources), "req")
-    first_pieces = rows_at(first_pieces, lax.rem(own_peer + peers - peer_order, peers))
-    rest = rows_at(spread, order_by_peer[:, 1:].reshape(-1)).reshape(
-        peers, slots - 1, piece, STATE_DIM
-    )
-    rest_pieces = exchange(rest, "req")
-
-    entering, final = combine(
-        chain, first_pieces.reshape(local_heads * HEAD_DIM, STATE_DIM), own_ends, own_decay
-    )
+    first_b = rotate(rows_at(spread_b, first_sources), "req")
+    rest = rows_at(spread_b, order_by_peer[:, 1:].reshape(-1))
+    rest_b = exchange(rest.reshape(peers, slots - 1, half, STATE_DIM), "req")
+
+    place = jnp.stack([own_peer, chain_index])
+    entering, final = combine(place, own_decay, own_ends, moved_a, first_b)
     incoming = rotate(entering, "seq")
-
-    place = jnp.stack([start, length, chain_index]).astype(jnp.int32)
     mixer_out = finish(
-        place, part, gate_rows[0], read_rows, decay, incoming, norm_weight[None]
-    )
-    new_states = unpack(final, rest_pieces).reshape(pool_states.shape)
-    new_inner = jnp.concatenate(
-        [kept_inner[None], moved_windows[1:, :, :inner_local]], axis=0
-    )
-    new_outer = jnp.concatenate(
-        [kept_outer[None], moved_windows[1:, :, inner_local:]], axis=0
-    )
+        jnp.stack([start, length, chain_index]),
+        part,
+        gate_rows[0],
+        read_rows,
+        decay,
+        norm_weight[None],
+        incoming,
+    )
+    states = unpack(place, final, moved_a)
+    new_states = unpack_rest(final, rest_b, states).reshape(pool_states.shape)
+
+    moved = rows_at(every, own_sources).astype(F32)
+    moved = (moved[1:, :, :width] * moved[1:, taps - 1 :, width:][:, :, :1]).astype(BF16)
+    new_inner = jnp.concatenate([kept_inner[None], moved[:, :, :inner_local]], axis=0)
+    new_outer = jnp.concatenate([kept_outer[None], moved[:, :, inner_local:]], axis=0)
     return (new_states, new_inner, new_outer, mixer_out[None])
 
 

time: 286 us -> 319 us (1.12); the launches traced: 282 us -> 318 us
  Pallas kernels: 65.1 us -> 122 us
  blocking collectives: 96.1 us -> 42.9 us
  waiting for transfers between devices: 19.6 us -> 64.2 us
  local copies, waits for them, and re-layouts: 44.7 us -> 23.9 us
  starting transfers between devices: 36.4 us -> 57.1 us
  other arithmetic: 18.2 us -> 6.26 us
    pallas_call x3 -> x8, Pallas kernels: 21.5 us -> 78.2 us  [the longest x1 53.5 us: reorder(): pl.pallas_call(reorder_kernel, in_specs=[pl.BlockSpec(memory_space=pltpu....]
    all_gather x1, blocking collectives: 90 us -> 36.4 us  [device_body(): every = lax.all_gather(packed, 'req', axis=0, tiled=True)]
    all_to_all x2, waiting for transfers between devices: 0.01 us -> 34.5 us  [exchange(): return lax.all_to_all(value, axis, split_axis=0, concat_axis=0, tiled=True)]
    ppermute x13 -> x27, starting transfers between devices: 24.5 us -> 47.8 us  [rotate(): got[hop] = lax.ppermute(values[hop], axis, pairs)]
    ppermute x13 -> x27, waiting for transfers between devices: 19.6 us -> 29.7 us  [rotate(): got[hop] = lax.ppermute(values[hop], axis, pairs)]
    gather x7 -> x5, local copies, waits for them, and re-layouts: 14.8 us -> 6.85 us  [rows_at(): return source.at[indices].get(mode='promise_in_bounds')]
    slice x9 -> x5, local copies, waits for them, and re-layouts: 10.2 us -> 3.12 us  [the longest x1 2.75 us: rotate(): got[hop] = lax.ppermute(values[hop], axis, pairs)]
    reduce_sum x3 -> x0, other arithmetic: 3.95 us -> none  [the longest x1 1.7 us: device_body(): jnp.sum(shared[:, :, window_local + channels:].astype(F32), axis=0)]
  transfers between devices with their start and end apart: 15 -> 29, of which waited for: 6 -> 13; matrix products, arithmetic and copies ran while one was open for 21% -> 7% of each run, Pallas kernels for 16% -> 36%
where the time goes in v2:
time: 319 us; the launch traced here: 318 us
  Pallas kernels  122 us (38%)
  waiting for transfers between devices  64.2 us (20%)
  starting transfers between devices  57.1 us (18%)
  blocking collectives  42.9 us (13%)
  local copies, waits for them, and re-layouts  23.9 us (7%)
  other arithmetic  6.26 us (2%)
    pallas_call x1, Pallas kernels, reorder(): pl.pallas_call(reorder_kernel, in_specs=[pl.BlockSpec(memory_space=pltpu....  53.5 us
    ppermute x27, starting transfers between devices, rotate(): got[hop] = lax.ppermute(values[hop], axis, pairs)  47.8 us
    all_gather x1, blocking collectives, device_body(): every = lax.all_gather(packed, 'req', axis=0, tiled=True)  36.4 us
    all_to_all x2, waiting for transfers between devices, exchange(): return lax.all_to_all(value, axis, split_axis=0, concat_axis=0, tiled=True)  34.5 us
    pallas_call x1, Pallas kernels, block_parts(): pl.pallas_call(block_kernel, grid_spec=pltpu.PrefetchScalarGridSpec(num_s...  32.1 us
    ppermute x27, waiting for transfers between devices, rotate(): got[hop] = lax.ppermute(values[hop], axis, pairs)  29.7 us
    pallas_call x1, Pallas kernels, finish(): pl.pallas_call(finish_kernel, grid=(length // TILE,), in_specs=[pl.BlockS...  11.7 us
    all_to_all x2, starting transfers between devices, exchange(): return lax.all_to_all(value, axis, split_axis=0, concat_axis=0, tiled=True)  9.24 us
  transfers between devices with their start and end apart: 29, of which 13 were waited for; matrix products, arithmetic and copies ran while one was open for 7% of the time, Pallas kernels for 36%

profile of v2, /device:TPU:0, one launch (start us, length us, event | category | flops | bytes accessed | tf_op | source)
XLA Modules:
  0.0 318.0 jit_solution(10471213200465015264)
XLA Ops:
  4.0 36.4 %all_gather.9.every_ref.after_ref = bf16[104,3,1152]{2,1,0:T(4,128)(2,1)} all-gather(bf16[13,3,1152]{2,1,0:T(4,128)(2,1)S(1)} %concatenate.17), channel_id=1, replica_groups=mesh['req'=8,'seq'=4] {'req'}, dimensions={0}, use_global_device_ids=true | all-gather | bytes 808704 | tf_op jit(solution)/shard_map/all_gather | solution.py:733
  41.7 3.9 %pack_rest.1 = bf16[8,13,64,128]{3,2,1,0:T(8,128)(2,1)} custom-call(s32[17]{0:T(128)} %pad_add_fusion.1.place_ref, f32[13,8,128,128]{3,2,1,0:T(8,128)} %bitcast.69, bf16[104,3,1152]{2,1,0:T(4,128)(2,1)} %all_gather.9.every_ref.after_ref), custom_call_target="tpu_custom_call" | custom-call | tf_op jit(solution)/shard_map/pack_rest/pallas_call | solution.py:347
  45.6 5.5 %all-to-all-start = ((bf16[8,13,64,128]{3,2,1,0:T(8,128)(2,1)}), bf16[8,13,64,128]{3,2,1,0:T(8,128)(2,1)S(1)}, u32[]{:S(2)}, u32[]{:S(2)}) async-start(bf16[8,13,64,128]{3,2,1,0:T(8,128)(2,1)} %pack_rest.1), calls=%async_computation | async-start | bytes 3407872 | tf_op jit(solution)/shard_map/all_to_all | solution.py:683
  51.1 3.9 %pack.1 = (bf16[13,64,128]{2,1,0:T(8,128)(2,1)}, bf16[13,64,128]{2,1,0:T(8,128)(2,1)}, bf16[13,64,128]{2,1,0:T(8,128)(2,1)}, bf16[13,64,128]{2,1,0:T(8,128)(2,1)...) custom-call(s32[17]{0:T(128)} %pad_add_fusion.1.place_ref, ...), custom_call_target="tpu_custom_call" | custom-call | tf_op jit(solution)/shard_map/pack/pallas_call | solution.py:321
  58.6 2.4 collective-permute-start.5
  62.4 2.4 collective-permute-start.7
  70.1 3.3 %share.1 = (bf16[3,9984]{1,0:T(4,128)(2,1)}, f32[512,128]{1,0:T(8,128)}) custom-call(s32[5]{0:T(128)} %stack.41.place_ref, bf16[104,3,1152]{2,1,0:T(4,128)(2,1)} %all_gather.9.every_ref.after_ref, bf16[512,4096]{1,0:T(8,128)(2,1)} %bitcast.64, bf16[512,4096]{1,0:T(8,128)(2,1)} %bitcast.65, bf16[512,4096]{1,0:T(8,128)(2,1)} %bitcast.66, ...), custom_call_target="tpu_custom_call" | custom-call | tf_op jit(solution)/shard_map/share/pallas_call | solution.py:580
  73.5 34.5 %all-to-all-done = bf16[8,13,64,128]{3,2,1,0:T(8,128)(2,1)S(1)} async-done(((bf16[8,13,64,128]{3,2,1,0:T(8,128)(2,1)}), bf16[8,13,64,128]{3,2,1,0:T(8,128)(2,1)S(1)}, u32[]{:S(2)}, u32[]{:S(2)}) %all-to-all-start) | async-done | bytes 1703968 | tf_op jit(solution)/shard_map/all_to_all | solution.py:683
  110.0 3.7 %all-to-all-start.1 = ((bf16[8,12,64,128]{3,2,1,0:T(8,128)(2,1)}), bf16[8,12,64,128]{3,2,1,0:T(8,128)(2,1)S(1)}, u32[]{:S(2)}, u32[]{:S(2)}) async-start(bf16[8,12,64,128]{3,2,1,0:T(8,128)(2,1)} %bitcast.33), calls=%async_computation.1 | async-start | bytes 3145728 | tf_op jit(solution)/shard_map/all_to_all | solution.py:683
  113.7 6.5 %all-gather.1.shared_ref = bf16[4,3,9984]{2,1,0:T(4,128)(2,1)} all-gather(bf16[1,3,9984]{2,1,0:T(4,128)(2,1)S(1)} %bitcast.82), channel_id=2, replica_groups=mesh['req'=8,'seq'=4] {'seq'}, dimensions={0}, use_global_device_ids=true | all-gather | bytes 299520 | tf_op jit(solution)/shard_map/all_gather | solution.py:777
  122.7 2.5 gather_fusion.4
  128.1 32.1 %block_parts.1 = (f32[512,4096]{1,0:T(8,128)}, bf16[4,128,1024]{2,1,0:T(8,128)(2,1)}, bf16[512,128]{1,0:T(8,128)(2,1)}, f32[512,128]{1,0:T(8,128)}) custom-call(s32[1]{0:T(128)} %bitcast.1.chain_ref, f32[8,4352]{1,0:T(8,128)} %get-tuple-element.29.tail_ref.state_tail_ref, bf16[512,4096]{1,0:T(8,128)(2,1)} %bitcast.67, bf16[512,4096]{1,0:T(8,128)(2,1)} %bitcast.68, ...), custom_call_target="tpu_custom_call" | custom-call | flops 6000000000 | bytes 20000000 | tf_op jit(solution)/shard_map/block_parts/pallas_call | solution.py:175
  160.5 3.8 %collective-permute-start.8 = (bf16[13,64,128]{2,1,0:T(8,128)(2,1)}, bf16[13,64,128]{2,1,0:T(8,128)(2,1)}, u32[]{:S(2)}, u32[]{:S(2)}) collective-permute-start(bf16[13,64,128]{2,1,0:T(8,128)(2,1)} %get-tuple-element.38), channel_id=1, source_target_pairs={{0,24},{4,28},{8,0},{12,4},{16,8},{20,12},{24,16},{28,20},{1,25},{... | collective-permute-start | bytes 638984 | tf_op jit(solution)/shard_map/ppermute | solution.py:691
  165.7 2.2 slice_bitcast_fusion
  170.2 3.9 %collective-permute-done.9.refs_7_ = bf16[13,64,128]{2,1,0:T(8,128)(2,1)} collective-permute-done((bf16[13,64,128]{2,1,0:T(8,128)(2,1)}, bf16[13,64,128]{2,1,0:T(8,128)(2,1)}, u32[]{:S(2)}, u32[]{:S(2)}) %collective-permute-start.9) | collective-permute-done | bytes 213024 | tf_op jit(solution)/shard_map/ppermute | solution.py:691
  174.2 53.5 %reorder.1 = bf16[104,64,128]{2,1,0:T(8,128)(2,1)} custom-call(s32[104]{0:T(128)} %reshape.196.order_ref, bf16[13,64,128]{2,1,0:T(8,128)(2,1)} %get-tuple-element.32.refs_0_, bf16[13,64,128]{2,1,0:T(8,128)(2,1)} %collective-permute-done.3.refs_1_, bf16[13,64,128]{2,1,0:T(8,128)(2,1)} %collective-permute-done.4.refs_2_, ...), custom_call_target="tpu_custom_call" | custom-call | tf_op jit(solution)/shard_map/reorder/pallas_call | solution.py:382
  227.6 2.7 fusion.10
  230.4 5.2 %collective-permute-start.16 = (bf16[13,64,128]{2,1,0:T(8,128)(2,1)}, bf16[13,64,128]{2,1,0:T(8,128)(2,1)}, u32[]{:S(2)}, u32[]{:S(2)}) collective-permute-start(bf16[13,64,128]{2,1,0:T(8,128)(2,1)} %get-tuple-element.74), channel_id=1, source_target_pairs={{0,28},{4,0},{8,4},{12,8},{16,12},{20,16},{24,20},{28,24},{1,29},{... | collective-permute-start | bytes 638984 | tf_op jit(solution)/shard_map/ppermute | solution.py:691
  236.8 3.0 collective-permute-start.13
  243.2 2.9 collective-permute-done.15.refs_10_.refs_6_
  246.2 4.6 %collective-permute-done.14.refs_9_.refs_5_ = bf16[13,64,128]{2,1,0:T(8,128)(2,1)S(1)} collective-permute-done((bf16[13,64,128]{2,1,0:T(8,128)(2,1)}, bf16[13,64,128]{2,1,0:T(8,128)(2,1)S(1)}, u32[]{:S(2)}, u32[]{:S(2)}) %collective-permute-start.14) | collective-permute-done | bytes 213024 | tf_op jit(solution)/shard_map/ppermute | solution.py:691
  250.8 12.7 %collective-permute-start.23 = (bf16[64,128]{1,0:T(8,128)(2,1)S(1)}, bf16[64,128]{1,0:T(8,128)(2,1)S(1)}, u32[]{:S(2)}, u32[]{:S(2)}) collective-permute-start(bf16[64,128]{1,0:T(8,128)(2,1)S(1)} %get-tuple-element.86), channel_id=1, source_target_pairs={{0,28},{4,0},{8,4},{12,8},{16,12},{20,16},{24,20},{28,24},{1,29},{... | collective-permute-start | bytes 49160 | tf_op jit(solution)/shard_map/ppermute | solution.py:691
  263.5 7.2 %collective-permute-done.13.refs_8_.refs_4_ = bf16[13,64,128]{2,1,0:T(8,128)(2,1)S(1)} collective-permute-done((bf16[13,64,128]{2,1,0:T(8,128)(2,1)}, bf16[13,64,128]{2,1,0:T(8,128)(2,1)S(1)}, u32[]{:S(2)}, u32[]{:S(2)}) %collective-permute-start.13) | collective-permute-done | bytes 213024 | tf_op jit(solution)/shard_map/ppermute | solution.py:691
  270.8 2.2 collective-permute-done.12.refs_7_.refs_3_
  273.1 3.3 %collective-permute-start.20 = (bf16[64,128]{1,0:T(8,128)(2,1)S(1)}, bf16[64,128]{1,0:T(8,128)(2,1)S(1)}, u32[]{:S(2)}, u32[]{:S(2)}) collective-permute-start(bf16[64,128]{1,0:T(8,128)(2,1)S(1)} %get-tuple-element.89), channel_id=1, source_target_pairs={{0,16},{4,20},{8,24},{12,28},{16,0},{20,4},{24,8},{28,12},{1,17},{... | collective-permute-start | bytes 49160 | tf_op jit(solution)/shard_map/ppermute | solution.py:691
  276.5 2.4 collective-permute-start.17
  279.6 2.3 collective-permute-done.19.refs_15_
  283.7 3.2 %combine.1 = (bf16[128,1024]{1,0:T(8,128)(2,1)}, bf16[128,1024]{1,0:T(8,128)(2,1)}, bf16[128,1024]{1,0:T(8,128)(2,1)}, bf16[128,1024]{1,0:T(8,128)(2,1)}, f32[1024,128]{1,0:T(8,128)}) custom-call(s32[2]{0:T(128)} %pad_add_fusion.place_ref, f32[4,1024]{1,0:T(4,128)} %get-tuple-element.28.decay_ref, bf16[128,1024]{1,0:T(8,128)(2,1)} %get-tuple-element.85.refs_0_, ...), custom_call_target="tpu_custom_call" | custom-call | tf_op jit(solution)/shard_map/combine/pallas_call | solution.py:484
  291.8 4.3 %unpack.1.states_ref = f32[13,8,128,128]{3,2,1,0:T(8,128)} custom-call(s32[2]{0:T(128)} %pad_add_fusion.place_ref, f32[1024,128]{1,0:T(8,128)} %get-tuple-element.40.final_ref, bf16[13,64,128]{2,1,0:T(8,128)(2,1)} %get-tuple-element.81.refs_4_.refs_0_, bf16[13,64,128]{2,1,0:T(8,128)(2,1)} %copy-done.5, bf16[13,64,128]{2,1,0:T(8,128)(2,1)} %copy-done.4, ...), custom_call_target="tpu_custom_call" | custom-call | tf_op jit(solution)/shard_map/unpack/pallas_call | solution.py:410
  296.4 4.0 %collective-permute-done.26.refs_3_ = bf16[128,1024]{1,0:T(8,128)(2,1)S(1)} collective-permute-done((bf16[128,1024]{1,0:T(8,128)(2,1)}, bf16[128,1024]{1,0:T(8,128)(2,1)S(1)}, u32[]{:S(2)}, u32[]{:S(2)}) %collective-permute-start.26) | collective-permute-done | bytes 262176 | tf_op jit(solution)/shard_map/ppermute | solution.py:691
  301.0 11.7 %finish.1 = bf16[512,4096]{1,0:T(8,128)(2,1)} custom-call(s32[3]{0:T(128)} %pad_add_fusion.2.place_ref, f32[512,4096]{1,0:T(8,128)} %get-tuple-element.43.part_ref, bf16[512,4096]{1,0:T(8,128)(2,1)} %bitcast.74, bf16[512,128]{1,0:T(8,128)(2,1)} %get-tuple-element.44.read_ref, f32[512,128]{1,0:T(8,128)} %get-tuple-element.45.decay_ref, f32[1,4096]{1,0:T(1,128)} %bitcast.83, ...), custom_call_target="tpu_custom_call" | custom-call | flops 3000000000 | bytes 16000000 | tf_op jit(solution)/shard_map/finish/pallas_call | solution.py:281
  313.9 4.1 %unpack_rest.1 = f32[13,8,128,128]{3,2,1,0:T(8,128)} custom-call(f32[1024,128]{1,0:T(8,128)} %get-tuple-element.40.final_ref, bf16[8,12,64,128]{3,2,1,0:T(8,128)(2,1)} %copy-done, f32[13,8,128,128]{3,2,1,0:T(8,128)} %unpack.1.states_ref), custom_call_target="tpu_custom_call", output_to_operand_aliasing={{}: (2, {})} | custom-call | tf_op jit(solution)/shard_map/unpack_rest/pallas_call | solution.py:435
  (143 shorter events, 39.9 us)
Async XLA Ops:
  45.6 62.5 %all-to-all-start = ((bf16[8,13,64,128]{3,2,1,0:T(8,128)(2,1)}), bf16[8,13,64,128]{3,2,1,0:T(8,128)(2,1)S(1)}, u32[]{:S(2)}, u32[]{:S(2)}) async-start(bf16[8,13,64,128]{3,2,1,0:T(8,128)(2,1)} %pack_rest.1), calls=%async_computation | async-start | bytes 3407872 | tf_op jit(solution)/shard_map/all_to_all | solution.py:683
  55.0 105.4 %collective-permute-start.3 = (bf16[13,64,128]{2,1,0:T(8,128)(2,1)}, bf16[13,64,128]{2,1,0:T(8,128)(2,1)}, u32[]{:S(2)}, u32[]{:S(2)}) collective-permute-start(bf16[13,64,128]{2,1,0:T(8,128)(2,1)} %get-tuple-element.33), channel_id=1, source_target_pairs={{0,4},{4,8},{8,12},{12,16},{16,20},{20,24},{24,28},{28,0},{1,5},{5... | collective-permute-start | bytes 638984 | tf_op jit(solution)/shard_map/ppermute | solution.py:691
  57.1 107.1 %collective-permute-start.4 = (bf16[13,64,128]{2,1,0:T(8,128)(2,1)}, bf16[13,64,128]{2,1,0:T(8,128)(2,1)}, u32[]{:S(2)}, u32[]{:S(2)}) collective-permute-start(bf16[13,64,128]{2,1,0:T(8,128)(2,1)} %get-tuple-element.34), channel_id=1, source_target_pairs={{0,8},{4,12},{8,16},{12,20},{16,24},{20,28},{24,0},{28,4},{1,9},{5... | collective-permute-start | bytes 638984 | tf_op jit(solution)/shard_map/ppermute | solution.py:691
  58.6 109.3 %collective-permute-start.5 = (bf16[13,64,128]{2,1,0:T(8,128)(2,1)}, bf16[13,64,128]{2,1,0:T(8,128)(2,1)}, u32[]{:S(2)}, u32[]{:S(2)}) collective-permute-start(bf16[13,64,128]{2,1,0:T(8,128)(2,1)} %get-tuple-element.35), channel_id=1, source_target_pairs={{0,12},{4,16},{8,20},{12,24},{16,28},{20,0},{24,4},{28,8},{1,13},{... | collective-permute-start | bytes 638984 | tf_op jit(solution)/shard_map/ppermute | solution.py:691
  60.9 107.7 %collective-permute-start.6 = (bf16[13,64,128]{2,1,0:T(8,128)(2,1)}, bf16[13,64,128]{2,1,0:T(8,128)(2,1)}, u32[]{:S(2)}, u32[]{:S(2)}) collective-permute-start(bf16[13,64,128]{2,1,0:T(8,128)(2,1)} %get-tuple-element.36), channel_id=1, source_target_pairs={{0,16},{4,20},{8,24},{12,28},{16,0},{20,4},{24,8},{28,12},{1,17},{... | collective-permute-start | bytes 638984 | tf_op jit(solution)/shard_map/ppermute | solution.py:691
  62.4 106.9 %collective-permute-start.7 = (bf16[13,64,128]{2,1,0:T(8,128)(2,1)}, bf16[13,64,128]{2,1,0:T(8,128)(2,1)}, u32[]{:S(2)}, u32[]{:S(2)}) collective-permute-start(bf16[13,64,128]{2,1,0:T(8,128)(2,1)} %get-tuple-element.37), channel_id=1, source_target_pairs={{0,20},{4,24},{8,28},{12,0},{16,4},{20,8},{24,12},{28,16},{1,21},{... | collective-permute-start | bytes 638984 | tf_op jit(solution)/shard_map/ppermute | solution.py:691
  110.0 202.8 %all-to-all-start.1 = ((bf16[8,12,64,128]{3,2,1,0:T(8,128)(2,1)}), bf16[8,12,64,128]{3,2,1,0:T(8,128)(2,1)S(1)}, u32[]{:S(2)}, u32[]{:S(2)}) async-start(bf16[8,12,64,128]{3,2,1,0:T(8,128)(2,1)} %bitcast.33), calls=%async_computation.1 | async-start | bytes 3145728 | tf_op jit(solution)/shard_map/all_to_all | solution.py:683
  160.5 9.7 %collective-permute-start.8 = (bf16[13,64,128]{2,1,0:T(8,128)(2,1)}, bf16[13,64,128]{2,1,0:T(8,128)(2,1)}, u32[]{:S(2)}, u32[]{:S(2)}) collective-permute-start(bf16[13,64,128]{2,1,0:T(8,128)(2,1)} %get-tuple-element.38), channel_id=1, source_target_pairs={{0,24},{4,28},{8,0},{12,4},{16,8},{20,12},{24,16},{28,20},{1,25},{... | collective-permute-start | bytes 638984 | tf_op jit(solution)/shard_map/ppermute | solution.py:691
  164.3 9.9 %collective-permute-start.9 = (bf16[13,64,128]{2,1,0:T(8,128)(2,1)}, bf16[13,64,128]{2,1,0:T(8,128)(2,1)}, u32[]{:S(2)}, u32[]{:S(2)}) collective-permute-start(bf16[13,64,128]{2,1,0:T(8,128)(2,1)} %get-tuple-element.39), channel_id=1, source_target_pairs={{0,28},{4,0},{8,4},{12,8},{16,12},{20,16},{24,20},{28,24},{1,29},{... | collective-permute-start | bytes 638984 | tf_op jit(solution)/shard_map/ppermute | solution.py:691
  167.9 68.9 %collective-permute-start.2 = (bf16[128,1024]{1,0:T(8,128)(2,1)}, bf16[128,1024]{1,0:T(8,128)(2,1)}, u32[]{:S(2)}, u32[]{:S(2)}) collective-permute-start(bf16[128,1024]{1,0:T(8,128)(2,1)} %get-tuple-element.82), channel_id=1, source_target_pairs={{0,3},{1,0},{2,1},{3,2},{4,7},{5,4},{6,5},{7,6},{8,11},{9,8},{10,9... | collective-permute-start | bytes 786440 | tf_op jit(solution)/shard_map/ppermute | solution.py:691
  168.6 68.1 %collective-permute-start.1 = (bf16[128,1024]{1,0:T(8,128)(2,1)}, bf16[128,1024]{1,0:T(8,128)(2,1)}, u32[]{:S(2)}, u32[]{:S(2)}) collective-permute-start(bf16[128,1024]{1,0:T(8,128)(2,1)} %get-tuple-element.83), channel_id=1, source_target_pairs={{0,2},{1,3},{2,0},{3,1},{4,6},{5,7},{6,4},{7,5},{8,10},{9,11},{10,... | collective-permute-start | bytes 786440 | tf_op jit(solution)/shard_map/ppermute | solution.py:691
  169.3 71.9 %collective-permute-start = (bf16[128,1024]{1,0:T(8,128)(2,1)}, bf16[128,1024]{1,0:T(8,128)(2,1)}, u32[]{:S(2)}, u32[]{:S(2)}) collective-permute-start(bf16[128,1024]{1,0:T(8,128)(2,1)} %get-tuple-element.84), channel_id=1, source_target_pairs={{0,1},{1,2},{2,3},{3,0},{4,5},{5,6},{6,7},{7,4},{8,9},{9,10},{10,1... | collective-permute-start | bytes 786440 | tf_op jit(solution)/shard_map/ppermute | solution.py:691
  230.4 11.2 %collective-permute-start.16 = (bf16[13,64,128]{2,1,0:T(8,128)(2,1)}, bf16[13,64,128]{2,1,0:T(8,128)(2,1)}, u32[]{:S(2)}, u32[]{:S(2)}) collective-permute-start(bf16[13,64,128]{2,1,0:T(8,128)(2,1)} %get-tuple-element.74), channel_id=1, source_target_pairs={{0,28},{4,0},{8,4},{12,8},{16,12},{20,16},{24,20},{28,24},{1,29},{... | collective-permute-start | bytes 638984 | tf_op jit(solution)/shard_map/ppermute | solution.py:691
  235.5 10.6 %collective-permute-start.15 = (bf16[13,64,128]{2,1,0:T(8,128)(2,1)}, bf16[13,64,128]{2,1,0:T(8,128)(2,1)}, u32[]{:S(2)}, u32[]{:S(2)}) collective-permute-start(bf16[13,64,128]{2,1,0:T(8,128)(2,1)} %get-tuple-element.75), channel_id=1, source_target_pairs={{0,24},{4,28},{8,0},{12,4},{16,8},{20,12},{24,16},{28,20},{1,25},{... | collective-permute-start | bytes 638984 | tf_op jit(solution)/shard_map/ppermute | solution.py:691
  236.8 14.0 %collective-permute-start.14 = (bf16[13,64,128]{2,1,0:T(8,128)(2,1)}, bf16[13,64,128]{2,1,0:T(8,128)(2,1)S(1)}, u32[]{:S(2)}, u32[]{:S(2)}) collective-permute-start(bf16[13,64,128]{2,1,0:T(8,128)(2,1)} %get-tuple-element.76), channel_id=1, source_target_pairs={{0,20},{4,24},{8,28},{12,0},{16,4},{20,8},{24,12},{28,16},{1,21},{... | collective-permute-start | bytes 638984 | tf_op jit(solution)/shard_map/ppermute | solution.py:691
  236.8 33.9 %collective-permute-start.13 = (bf16[13,64,128]{2,1,0:T(8,128)(2,1)}, bf16[13,64,128]{2,1,0:T(8,128)(2,1)S(1)}, u32[]{:S(2)}, u32[]{:S(2)}) collective-permute-start(bf16[13,64,128]{2,1,0:T(8,128)(2,1)} %get-tuple-element.77), channel_id=1, source_target_pairs={{0,16},{4,20},{8,24},{12,28},{16,0},{20,4},{24,8},{28,12},{1,17},{... | collective-permute-start | bytes 638984 | tf_op jit(solution)/shard_map/ppermute | solution.py:691
  241.2 48.6 %copy-start.20 = (bf16[3,64]{1,0:T(4,128)(2,1)S(1)}, bf16[3,64]{1,0:T(4,128)(2,1)}, u32[]{:S(2)}) copy-start(bf16[3,64]{1,0:T(4,128)(2,1)} %get-tuple-element.42) | copy-start | bytes 1156
  241.2 31.8 %collective-permute-start.12 = (bf16[13,64,128]{2,1,0:T(8,128)(2,1)}, bf16[13,64,128]{2,1,0:T(8,128)(2,1)S(1)}, u32[]{:S(2)}, u32[]{:S(2)}) collective-permute-start(bf16[13,64,128]{2,1,0:T(8,128)(2,1)} %get-tuple-element.78), channel_id=1, source_target_pairs={{0,12},{4,16},{8,20},{12,24},{16,28},{20,0},{24,4},{28,8},{1,13},{... | collective-permute-start | bytes 638984 | tf_op jit(solution)/shard_map/ppermute | solution.py:691
  241.5 31.5 %collective-permute-start.11 = (bf16[13,64,128]{2,1,0:T(8,128)(2,1)}, bf16[13,64,128]{2,1,0:T(8,128)(2,1)S(1)}, u32[]{:S(2)}, u32[]{:S(2)}) collective-permute-start(bf16[13,64,128]{2,1,0:T(8,128)(2,1)} %get-tuple-element.79), channel_id=1, source_target_pairs={{0,8},{4,12},{8,16},{12,20},{16,24},{20,28},{24,0},{28,4},{1,9},{5... | collective-permute-start | bytes 638984 | tf_op jit(solution)/shard_map/ppermute | solution.py:691
  246.2 30.2 %collective-permute-start.10 = (bf16[13,64,128]{2,1,0:T(8,128)(2,1)}, bf16[13,64,128]{2,1,0:T(8,128)(2,1)S(1)}, u32[]{:S(2)}, u32[]{:S(2)}) collective-permute-start(bf16[13,64,128]{2,1,0:T(8,128)(2,1)} %get-tuple-element.80), channel_id=1, source_target_pairs={{0,4},{4,8},{8,12},{12,16},{16,20},{20,24},{24,28},{28,0},{1,5},{5... | collective-permute-start | bytes 638984 | tf_op jit(solution)/shard_map/ppermute | solution.py:691
  250.8 32.3 %copy-start.1 = (bf16[13,64,128]{2,1,0:T(8,128)(2,1)}, bf16[13,64,128]{2,1,0:T(8,128)(2,1)S(1)}, u32[]{:S(2)}) copy-start(bf16[13,64,128]{2,1,0:T(8,128)(2,1)S(1)} %collective-permute-done.14.refs_9_.refs_5_) | copy-start | bytes 638980
  250.8 25.6 %collective-permute-start.23 = (bf16[64,128]{1,0:T(8,128)(2,1)S(1)}, bf16[64,128]{1,0:T(8,128)(2,1)S(1)}, u32[]{:S(2)}, u32[]{:S(2)}) collective-permute-start(bf16[64,128]{1,0:T(8,128)(2,1)S(1)} %get-tuple-element.86), channel_id=1, source_target_pairs={{0,28},{4,0},{8,4},{12,8},{16,12},{20,16},{24,20},{28,24},{1,29},{... | collective-permute-start | bytes 49160 | tf_op jit(solution)/shard_map/ppermute | solution.py:691
  270.7 19.7 %copy-start.19 = (bf16[3,1024]{1,0:T(4,128)(2,1)S(1)}, bf16[3,1024]{1,0:T(4,128)(2,1)}, u32[]{:S(2)}) copy-start(bf16[3,1024]{1,0:T(4,128)(2,1)} %get-tuple-element.41) | copy-start | bytes 18436
  270.7 5.8 %collective-permute-start.22 = (bf16[64,128]{1,0:T(8,128)(2,1)S(1)}, bf16[64,128]{1,0:T(8,128)(2,1)S(1)}, u32[]{:S(2)}, u32[]{:S(2)}) collective-permute-start(bf16[64,128]{1,0:T(8,128)(2,1)S(1)} %get-tuple-element.87), channel_id=1, source_target_pairs={{0,24},{4,28},{8,0},{12,4},{16,8},{20,12},{24,16},{28,20},{1,25},{... | collective-permute-start | bytes 49160 | tf_op jit(solution)/shard_map/ppermute | solution.py:691
  273.0 6.5 %collective-permute-start.21 = (bf16[64,128]{1,0:T(8,128)(2,1)S(1)}, bf16[64,128]{1,0:T(8,128)(2,1)S(1)}, u32[]{:S(2)}, u32[]{:S(2)}) collective-permute-start(bf16[64,128]{1,0:T(8,128)(2,1)S(1)} %get-tuple-element.88), channel_id=1, source_target_pairs={{0,20},{4,24},{8,28},{12,0},{16,4},{20,8},{24,12},{28,16},{1,21},{... | collective-permute-start | bytes 49160 | tf_op jit(solution)/shard_map/ppermute | solution.py:691
  273.1 6.5 %collective-permute-start.20 = (bf16[64,128]{1,0:T(8,128)(2,1)S(1)}, bf16[64,128]{1,0:T(8,128)(2,1)S(1)}, u32[]{:S(2)}, u32[]{:S(2)}) collective-permute-start(bf16[64,128]{1,0:T(8,128)(2,1)S(1)} %get-tuple-element.89), channel_id=1, source_target_pairs={{0,16},{4,20},{8,24},{12,28},{16,0},{20,4},{24,8},{28,12},{1,17},{... | collective-permute-start | bytes 49160 | tf_op jit(solution)/shard_map/ppermute | solution.py:691
  276.4 5.5 %collective-permute-start.19 = (bf16[64,128]{1,0:T(8,128)(2,1)S(1)}, bf16[64,128]{1,0:T(8,128)(2,1)S(1)}, u32[]{:S(2)}, u32[]{:S(2)}) collective-permute-start(bf16[64,128]{1,0:T(8,128)(2,1)S(1)} %get-tuple-element.90), channel_id=1, source_target_pairs={{0,12},{4,16},{8,20},{12,24},{16,28},{20,0},{24,4},{28,8},{1,13},{... | collective-permute-start | bytes 49160 | tf_op jit(solution)/shard_map/ppermute | solution.py:691
  276.4 5.6 %collective-permute-start.18 = (bf16[64,128]{1,0:T(8,128)(2,1)S(1)}, bf16[64,128]{1,0:T(8,128)(2,1)S(1)}, u32[]{:S(2)}, u32[]{:S(2)}) collective-permute-start(bf16[64,128]{1,0:T(8,128)(2,1)S(1)} %get-tuple-element.91), channel_id=1, source_target_pairs={{0,8},{4,12},{8,16},{12,20},{16,24},{20,28},{24,0},{28,4},{1,9},{5... | collective-permute-start | bytes 49160 | tf_op jit(solution)/shard_map/ppermute | solution.py:691
  276.5 6.6 %collective-permute-start.17 = (bf16[64,128]{1,0:T(8,128)(2,1)S(1)}, bf16[64,128]{1,0:T(8,128)(2,1)S(1)}, u32[]{:S(2)}, u32[]{:S(2)}) collective-permute-start(bf16[64,128]{1,0:T(8,128)(2,1)S(1)} %get-tuple-element.92), channel_id=1, source_target_pairs={{0,4},{4,8},{8,12},{12,16},{16,20},{20,24},{24,28},{28,0},{1,5},{5... | collective-permute-start | bytes 49160 | tf_op jit(solution)/shard_map/ppermute | solution.py:691
  286.9 9.2 %collective-permute-start.24 = (bf16[128,1024]{1,0:T(8,128)(2,1)}, bf16[128,1024]{1,0:T(8,128)(2,1)S(1)}, u32[]{:S(2)}, u32[]{:S(2)}) collective-permute-start(bf16[128,1024]{1,0:T(8,128)(2,1)} %get-tuple-element.47), channel_id=1, source_target_pairs={{0,1},{1,2},{2,3},{3,0},{4,5},{5,6},{6,7},{7,4},{8,9},{9,10},{10,1... | collective-permute-start | bytes 786440 | tf_op jit(solution)/shard_map/ppermute | solution.py:691
  286.9 9.5 %collective-permute-start.25 = (bf16[128,1024]{1,0:T(8,128)(2,1)}, bf16[128,1024]{1,0:T(8,128)(2,1)S(1)}, u32[]{:S(2)}, u32[]{:S(2)}) collective-permute-start(bf16[128,1024]{1,0:T(8,128)(2,1)} %get-tuple-element.48), channel_id=1, source_target_pairs={{0,2},{1,3},{2,0},{3,1},{4,6},{5,7},{6,4},{7,5},{8,10},{9,11},{10,... | collective-permute-start | bytes 786440 | tf_op jit(solution)/shard_map/ppermute | solution.py:691
  288.4 12.0 %collective-permute-start.26 = (bf16[128,1024]{1,0:T(8,128)(2,1)}, bf16[128,1024]{1,0:T(8,128)(2,1)S(1)}, u32[]{:S(2)}, u32[]{:S(2)}) collective-permute-start(bf16[128,1024]{1,0:T(8,128)(2,1)} %get-tuple-element.49), channel_id=1, source_target_pairs={{0,3},{1,0},{2,1},{3,2},{4,7},{5,4},{6,5},{7,6},{8,11},{9,8},{10,9... | collective-permute-start | bytes 786440 | tf_op jit(solution)/shard_map/ppermute | solution.py:691
  (20 other events, 130.5 us)

commit v3 on v2

--- a/solution.py
+++ b/solution.py
@@ -19,6 +19,7 @@
 LANES = 128
 TILE = 128
 SLOT_TILE = 4
+SLOT_PAD = 16
 PEER_TILE = 2
 EPSILON = 1e-05
 LOG2E = math.log2(math.e)
@@ -304,17 +305,51 @@
     )(place, part, gate, read, decay, norm_row, *states)
 
 
-def pack_kernel(place_ref, state_ref, after_ref, *out_refs):
+def mark_kernel(plan_ref, mask_ref, inner_ref, outer_ref, out_ref):
+    peers, taps, padded, total = out_ref.shape
+    slots = inner_ref.shape[1]
+    width = inner_ref.shape[2] + outer_ref.shape[2]
+    row = lax.broadcasted_iota(jnp.int32, (padded, total - width), 0)
+    fill = jnp.zeros((padded - slots, width), F32)
+    for tap in range(taps):
+        marks = jnp.full((padded, total - width), -1.0, F32)
+        for slot in range(slots):
+            value = mask_ref[slot] if tap == 2 else plan_ref[slot, tap]
+            marks = jnp.where(row == slot, value.astype(F32), marks)
+        window = jnp.concatenate(
+            [inner_ref[tap].astype(F32), outer_ref[tap].astype(F32)], axis=1
+        )
+        window = jnp.concatenate([window, fill], axis=0)
+        block = jnp.concatenate([window, marks], axis=1).astype(BF16)
+        for peer in range(peers):
+            out_ref[peer, tap] = block
+
+
+def mark(plan, mask, inner, outer, peers):
+    taps, _ = inner.shape[:2]
+    width = inner.shape[2] + outer.shape[2]
+    whole = pl.BlockSpec(memory_space=pltpu.VMEM)
+    scalar = pl.BlockSpec(memory_space=pltpu.SMEM)
+    total = width + LANES - width % LANES
+    return pl.pallas_call(
+        mark_kernel,
+        in_specs=[scalar, scalar, whole, whole],
+        out_shape=jax.ShapeDtypeStruct((peers, taps, SLOT_PAD, total), BF16),
+        name="mark",
+    )(plan, mask, inner, outer)
+
+
+def pack_kernel(own_ref, mask_ref, state_ref, *out_refs):
     first_slot = pl.program_id(0) * SLOT_TILE
     peers = state_ref.shape[1]
     for j in range(SLOT_TILE):
-        keep = place_ref[1 + first_slot + j].astype(F32)
+        keep = mask_ref[jnp.minimum(first_slot + j, mask_ref.shape[0] - 1)].astype(F32)
         for hop in range(len(out_refs)):
-            peer = lax.rem(place_ref[0] + hop, peers)
+            peer = lax.rem(own_ref[0] + hop, peers)
             out_refs[hop][j] = (state_ref[j, peer] * keep).astype(BF16)
 
 
-def pack(place, states, after):
+def pack(own, mask, states):
     slots, peers, piece, width = states.shape
     half = piece // 2
     steps = pl.cdiv(slots, SLOT_TILE)
@@ -323,24 +358,24 @@
         grid=(steps,),
         in_specs=[
             pl.BlockSpec(memory_space=pltpu.SMEM),
+            pl.BlockSpec(memory_space=pltpu.SMEM),
             pl.BlockSpec((SLOT_TILE, peers, half, width), lambda t: (t, 0, 0, 0)),
-            pl.BlockSpec(memory_space=pl.ANY),
         ],
         out_specs=[pl.BlockSpec((SLOT_TILE, half, width), lambda t: (t, 0, 0))] * peers,
         out_shape=[jax.ShapeDtypeStruct((slots, half, width), BF16)] * peers,
         compiler_params=pltpu.CompilerParams(dimension_semantics=("arbitrary",)),
         name="pack",
-    )(place, states, after)
-
-
-def pack_rest_kernel(place_ref, state_ref, after_ref, out_ref):
+    )(own, mask, states)
+
+
+def pack_rest_kernel(mask_ref, state_ref, out_ref):
     first_slot = pl.program_id(0) * SLOT_TILE
     for j in range(SLOT_TILE):
-        keep = place_ref[1 + first_slot + j].astype(F32)
+        keep = mask_ref[jnp.minimum(first_slot + j, mask_ref.shape[0] - 1)].astype(F32)
         out_ref[:, j] = (state_ref[j] * keep).astype(BF16)
 
 
-def pack_rest(place, states, after):
+def pack_rest(mask, states):
     slots, peers, piece, width = states.shape
     half = piece // 2
     steps = pl.cdiv(slots, SLOT_TILE)
@@ -350,43 +385,85 @@
         in_specs=[
             pl.BlockSpec(memory_space=pltpu.SMEM),
             pl.BlockSpec((SLOT_TILE, peers, half, width), lambda t: (t, 0, 1, 0)),
-            pl.BlockSpec(memory_space=pl.ANY),
         ],
         out_specs=pl.BlockSpec((peers, SLOT_TILE, half, width), lambda t: (0, t, 0, 0)),
         out_shape=jax.ShapeDtypeStruct((peers, slots, half, width), BF16),
         compiler_params=pltpu.CompilerParams(dimension_semantics=("arbitrary",)),
         name="pack_rest",
-    )(place, states, after)
-
-
-def reorder_kernel(order_ref, *refs):
-    in_refs, out_ref, sems = refs[:-2], refs[-2], refs[-1]
+    )(mask, states)
+
+
+def source_of(table_ref, target):
+    code = table_ref[0, target]
+    peer = lax.div(code, SLOT_PAD)
+    return peer, code - peer * SLOT_PAD
+
+
+def reorder_kernel(own_ref, table_ref, *refs):
+    peers = (len(refs) - 1) // 2
+    in_refs, out_refs, scr = refs[:peers], refs[peers:-1], refs[-1]
     slots = in_refs[0].shape[0]
-    for hop in range(len(in_refs)):
-
-        def start(i, unused):
-            target = order_ref[hop * slots + i]
-            pltpu.make_async_copy(in_refs[hop].at[i], out_ref.at[target], sems.at[hop]).start()
+    own = own_ref[0]
+    for hop in range(peers):
+        scr[hop] = in_refs[hop][...]
+    for hop in range(peers):
+        base = lax.rem(own + hop, peers) * slots
+
+        def move(slot, unused):
+            peer, index = source_of(table_ref, base + slot)
+            out_refs[hop][slot] = scr[lax.rem(own - peer + peers, peers), index]
             return unused
 
-        lax.fori_loop(0, slots, start, 0)
-    for hop in range(len(in_refs)):
-        span = pl.ds(hop * slots, slots)
-        pltpu.make_async_copy(in_refs[hop], out_ref.at[span], sems.at[hop]).wait()
-
-
-def reorder(order, pieces):
+        lax.fori_loop(0, slots, move, 0)
+
+
+def reorder(own, table, pieces):
     slots, half, width = pieces[0].shape
     count = len(pieces)
-    whole = pl.BlockSpec(memory_space=pltpu.HBM)
+    whole = pl.BlockSpec((slots, half, width), lambda t: (0, 0, 0))
+    scalar = pl.BlockSpec(memory_space=pltpu.SMEM)
     return pl.pallas_call(
         reorder_kernel,
-        in_specs=[pl.BlockSpec(memory_space=pltpu.SMEM)] + [whole] * count,
-        out_specs=whole,
-        out_shape=jax.ShapeDtypeStruct((count * slots, half, width), BF16),
-        scratch_shapes=[pltpu.SemaphoreType.DMA((count,))],
+        grid=(1,),
+        in_specs=[scalar, scalar] + [whole] * count,
+        out_specs=[whole] * count,
+        out_shape=[jax.ShapeDtypeStruct((slots, half, width), BF16)] * count,
+        scratch_shapes=[pltpu.VMEM((count, slots, half, width), BF16)],
         name="reorder",
-    )(order, *pieces)
+    )(own, table, *pieces)
+
+
+def reorder_rest_kernel(own_ref, table_ref, in_ref, *out_refs):
+    rest_ref, first_refs = out_refs[0], out_refs[1:]
+    peers, slots = in_ref.shape[:2]
+    own = own_ref[0]
+    for hop in range(peers):
+        target = lax.rem(own + hop, peers)
+        peer, index = source_of(table_ref, target * slots)
+        first_refs[hop][...] = in_ref[peer, index]
+
+        def move(slot, unused):
+            peer, index = source_of(table_ref, hop * slots + slot)
+            rest_ref[hop, slot - 1] = in_ref[peer, index]
+            return unused
+
+        lax.fori_loop(1, slots, move, 0)
+
+
+def reorder_rest(own, table, pieces):
+    peers, slots, half, width = pieces.shape
+    scalar = pl.BlockSpec(memory_space=pltpu.SMEM)
+    outs = pl.pallas_call(
+        reorder_rest_kernel,
+        grid=(1,),
+        in_specs=[scalar, scalar, pl.BlockSpec(pieces.shape, lambda t: (0, 0, 0, 0))],
+        out_specs=[pl.BlockSpec((peers, slots - 1, half, width), lambda t: (0, 0, 0, 0))]
+        + [pl.BlockSpec((half, width), lambda t: (0, 0))] * peers,
+        out_shape=[jax.ShapeDtypeStruct((peers, slots - 1, half, width), BF16)]
+        + [jax.ShapeDtypeStruct((half, width), BF16)] * peers,
+        name="reorder_rest",
+    )(own, table, pieces)
+    return outs[0], outs[1:]
 
 
 def unpack_kernel(place_ref, final_ref, *refs):
@@ -519,12 +596,36 @@
     rate_ref,
     out_ref,
     step_ref,
+    moved_ref,
+    table_ref,
 ):
     taps = out_ref.shape[0]
     inner = end_ref.shape[1]
     outer = state_end_ref.shape[1]
     channels = inner + outer
-    first = place_ref[0]
+    own, slots = place_ref[0], place_ref[5]
+    peers, _, padded, width = every_ref.shape
+    rows = peers * padded
+    mark_at = width - width % LANES - LANES
+    marks = []
+    for tap in range(taps):
+        lanes = every_ref[:, tap, :, mark_at:].astype(F32).reshape(rows, width - mark_at)
+        marks.append(lanes[:, width - mark_at - 1 :])
+    target = marks[0] * slots.astype(F32) + marks[1]
+    columns = table_ref.shape[1]
+    lane = lax.broadcasted_iota(jnp.int32, (rows, columns), 1).astype(F32)
+    source = lax.broadcasted_iota(jnp.int32, (rows, columns), 0).astype(F32)
+    found = jnp.sum(jnp.where(target == lane, source, 0.0), axis=0, keepdims=True)
+    table_ref[...] = jnp.broadcast_to(found, table_ref.shape).astype(jnp.int32)
+    lane = lax.broadcasted_iota(jnp.int32, (rows, LANES), 1)
+    mine = (target == (own * slots + lane).astype(F32)) & (lane < slots)
+    pick = jnp.where(mine, marks[2], 0.0).astype(BF16)
+    firsts = []
+    for tap in range(taps):
+        source_rows = every_ref[:, tap].astype(F32).reshape(rows, width).astype(BF16)
+        moved = dot(pick, source_rows, ((0,), (0,)))[:padded]
+        moved_ref[tap] = moved.astype(BF16)
+        firsts.append(moved[:1])
     low_block, high_block, start, length = (
         place_ref[1],
         place_ref[2],
@@ -549,10 +650,7 @@
 
     out_ref[:, channels : channels + inner] = kept_rows(kept_ref, kept_next_ref)
     out_ref[:, channels + inner : 2 * channels] = kept_rows(state_kept_ref, state_next_ref)
-    window = every_ref[first].astype(F32)
-    width = window.shape[1]
-    keep = window[taps - 1 :, width - 1 :]
-    out_ref[:, 2 * channels : 2 * channels + width] = (window * keep).astype(BF16)
+    out_ref[:, 2 * channels : 2 * channels + width] = jnp.concatenate(firsts, axis=0).astype(BF16)
     count = step_ref.shape[0]
     heads = raw_ref.shape[1]
     positions = start + lax.broadcasted_iota(jnp.int32, (count, heads), 0)
@@ -569,21 +667,21 @@
     out_ref[:, 2 * channels + width :] = parts.astype(BF16)
 
 
-def share(place, every, rows, state_rows, step_raw, step_bias, rate):
-    taps = every.shape[1]
-    width = every.shape[2]
+def share(place, slots, every, rows, state_rows, step_raw, step_bias, rate):
+    peers, taps, padded, width = every.shape
     length, inner = rows.shape
     outer = state_rows.shape[1]
     heads = step_raw.shape[1]
     last = length // 16 - 1
     total = 2 * (inner + outer) + width + LANES
+    lanes = pl.cdiv(peers * slots, LANES) * LANES
     return pl.pallas_call(
         share_kernel,
         grid_spec=pltpu.PrefetchScalarGridSpec(
             num_scalar_prefetch=1,
             grid=(1,),
             in_specs=[
-                pl.BlockSpec(every.shape, lambda t, c: (0, 0, 0)),
+                pl.BlockSpec(every.shape, lambda t, c: (0, 0, 0, 0)),
                 pl.BlockSpec((16, inner), lambda t, c: (last, 0)),
                 pl.BlockSpec((16, inner), lambda t, c: (c[1], 0)),
                 pl.BlockSpec((16, inner), lambda t, c: (c[2], 0)),
@@ -597,11 +695,15 @@
             out_specs=[
                 pl.BlockSpec((taps, total), lambda t, c: (0, 0)),
                 pl.BlockSpec((length, LANES), lambda t, c: (0, 0)),
+                pl.BlockSpec((taps, padded, width), lambda t, c: (0, 0, 0)),
+                pl.BlockSpec((8, lanes), lambda t, c: (0, 0)),
             ],
         ),
         out_shape=[
             jax.ShapeDtypeStruct((taps, total), BF16),
             jax.ShapeDtypeStruct((length, LANES), F32),
+            jax.ShapeDtypeStruct((taps, padded, width), BF16),
+            jax.ShapeDtypeStruct((8, lanes), jnp.int32),
         ],
         name="share",
     )(
@@ -619,10 +721,13 @@
     )
 
 
-def tail_kernel(chain_ref, shared_ref, tail_ref, inner_ref, outer_ref, decay_ref):
+def tail_kernel(
+    chain_ref, shared_ref, moved_ref, tail_ref, inner_ref, outer_ref, decay_ref
+):
     chain = chain_ref[0]
     count, taps = shared_ref.shape[:2]
-    inner_local, outer_local = inner_ref.shape[1], outer_ref.shape[1]
+    slots, inner_local = inner_ref.shape[1:]
+    outer_local = outer_ref.shape[2]
     channels = tail_ref.shape[1]
     inner = count * inner_local
     at = 2 * channels
@@ -647,8 +752,14 @@
         inner_at, outer_at = s * inner_local, inner + s * outer_local
         own_inner = jnp.where(mine, kept[:, inner_at : inner_at + inner_local], own_inner)
         own_outer = jnp.where(mine, kept[:, outer_at : outer_at + outer_local], own_outer)
-    inner_ref[...] = own_inner.astype(BF16)
-    outer_ref[...] = own_outer.astype(BF16)
+    width = inner_local + outer_local
+    top = lax.broadcasted_iota(jnp.int32, (moved_ref.shape[1], 1), 0) == 0
+    for tap in range(taps):
+        moved = moved_ref[tap].astype(F32)
+        both = jnp.where(top, own_inner[tap : tap + 1], moved[:, :inner_local])
+        inner_ref[tap] = both.astype(BF16)[:slots]
+        both = jnp.where(top, own_outer[tap : tap + 1], moved[:, inner_local:width])
+        outer_ref[tap] = both.astype(BF16)[:slots]
     logs = []
     for s in range(count):
         parts = shared_ref[s, :, shared_ref.shape[2] - LANES :].astype(F32)
@@ -663,20 +774,20 @@
     decay_ref[...] = jnp.exp2(spread[:count])
 
 
-def tails(chain, shared, channels, inner_local, outer_local, columns):
+def tails(chain, shared, moved, slots, channels, inner_local, outer_local, columns):
     count, taps = shared.shape[:2]
     whole = pl.BlockSpec(memory_space=pltpu.VMEM)
     return pl.pallas_call(
         tail_kernel,
-        in_specs=[pl.BlockSpec(memory_space=pltpu.SMEM), whole],
+        in_specs=[pl.BlockSpec(memory_space=pltpu.SMEM), whole, whole],
         out_shape=[
             jax.ShapeDtypeStruct((8, channels), F32),
-            jax.ShapeDtypeStruct((taps, inner_local), BF16),
-            jax.ShapeDtypeStruct((taps, outer_local), BF16),
+            jax.ShapeDtypeStruct((taps, slots, inner_local), BF16),
+            jax.ShapeDtypeStruct((taps, slots, outer_local), BF16),
             jax.ShapeDtypeStruct((count, columns), F32),
         ],
         name="tails",
-    )(chain, shared)
+    )(chain, shared, moved)
 
 
 def exchange(value, axis):
@@ -690,10 +801,6 @@
         pairs = [(source, (source + hop) % count) for source in range(count)]
         got[hop] = lax.ppermute(values[hop], axis, pairs)
     return got
-
-
-def rows_at(source, indices):
-    return source.at[indices].get(mode="promise_in_bounds")
 
 
 def device_body(
@@ -721,38 +828,22 @@
     slots, local_heads = pool_states.shape[:2]
     columns = local_heads * HEAD_DIM
     piece = columns // peers
-    half = piece // 2
     taps = KERNEL - 1
     inner_local = inner_window.shape[2]
     outer_local = state_window.shape[2]
-    width = inner_local + outer_local
-
-    marks = jnp.stack([move_plan[:, 0], move_plan[:, 1], active_mask], axis=1).astype(BF16)
-    marks = jnp.broadcast_to(marks[:, :, None], (slots, taps, (-width) % LANES))
-    packed = jnp.concatenate([inner_window, state_window, marks], axis=2)
-    every = lax.all_gather(packed, "req", axis=0, tiled=True)
 
     own = own_peer[None]
-    pack_place = jnp.concatenate(
-        [own, active_mask, jnp.zeros((-slots % SLOT_TILE,), jnp.int32)]
-    )
+    packed = mark(
+        move_plan,
+        active_mask,
+        inner_window.transpose(1, 0, 2),
+        state_window.transpose(1, 0, 2),
+        peers,
+    )
+    every = exchange(packed, "req")
     pool_pieces = pool_states.reshape(slots, peers, piece, STATE_DIM)
-    spread_a = rotate(pack(pack_place, pool_pieces, every), "req")
-    spread_b = exchange(pack_rest(pack_place, pool_pieces, every), "req")
-    spread_b = spread_b.reshape(peers * slots, half, STATE_DIM)
-
-    every_marks = every[:, :, width].astype(F32).astype(jnp.int32)
-    target_peer = every_marks[:, 0]
-    target_slot = every_marks[:, 1]
-    order = jnp.arange(peers * slots, dtype=jnp.int32)
-    targets = target_peer * slots + target_slot
-    sources = jnp.sum(jnp.where(targets[None, :] == order[:, None], order[None, :], 0), axis=1)
-    own_sources = lax.dynamic_slice_in_dim(sources, own_peer * slots, slots)
-    hop_targets = lax.rem(target_peer - own_peer + peers, peers) * slots + target_slot
-    peer_order = jnp.arange(peers, dtype=jnp.int32)
-    by_hop = rows_at(
-        hop_targets.reshape(peers, slots), lax.rem(own_peer + peers - peer_order, peers)
-    ).reshape(-1)
+    spread_a = rotate(pack(own, active_mask, pool_pieces), "req")
+    spread_b = exchange(pack_rest(active_mask, pool_pieces), "req")
 
     rows = inputs_inner[0]
     state_rows = inputs_state[0]
@@ -765,8 +856,9 @@
     high_block = jnp.minimum(low_block + 1, last_tile)
     heads = decay_log.shape[0]
     rate = jnp.pad(-LOG2E * jnp.exp(decay_log), (0, LANES - heads))[None]
-    payload, step = share(
-        jnp.stack([own_sources[0], low_block, high_block, start, length]),
+    payload, step, moved, table = share(
+        jnp.stack([own_peer, low_block, high_block, start, length, jnp.int32(slots)]),
+        slots,
         every,
         rows,
         state_rows,
@@ -776,12 +868,11 @@
     )
     shared = lax.all_gather(payload, "seq", axis=0)
     chain = chain_index[None]
-    tail, kept_inner, kept_outer, own_decay = tails(
-        chain, shared, channels, inner_local, outer_local, columns
-    )
-
-    reordered = reorder(by_hop, spread_a).reshape(peers, slots, half, STATE_DIM)
-    moved_a = rotate(reordered, "req")
+    tail, new_inner, new_outer, own_decay = tails(
+        chain, shared, moved, slots, channels, inner_local, outer_local, columns
+    )
+
+    moved_a = rotate(reorder(own, table, spread_a), "req")
 
     part, local_end, read_rows, decay = block_parts(
         chain,
@@ -797,17 +888,16 @@
     )
     own_ends = rotate(local_end, "seq")
 
-    order_by_peer = sources.reshape(peers, slots)
-    first_sources = rows_at(order_by_peer[:, 0], lax.rem(own_peer + peer_order, peers))
-    first_b = rotate(rows_at(spread_b, first_sources), "req")
-    rest = rows_at(spread_b, order_by_peer[:, 1:].reshape(-1))
-    rest_b = exchange(rest.reshape(peers, slots - 1, half, STATE_DIM), "req")
+    rest, first = reorder_rest(own, table, spread_b)
+    first_b = rotate(first, "req")
+    rest_b = exchange(rest, "req")
 
     place = jnp.stack([own_peer, chain_index])
     entering, final = combine(place, own_decay, own_ends, moved_a, first_b)
     incoming = rotate(entering, "seq")
+    finish_place = jnp.stack([start, length, chain_index])
     mixer_out = finish(
-        jnp.stack([start, length, chain_index]),
+        finish_place,
         part,
         gate_rows[0],
         read_rows,
@@ -818,11 +908,12 @@
     states = unpack(place, final, moved_a)
     new_states = unpack_rest(final, rest_b, states).reshape(pool_states.shape)
 
-    moved = rows_at(every, own_sources).astype(F32)
-    moved = (moved[1:, :, :width] * moved[1:, taps - 1 :, width:][:, :, :1]).astype(BF16)
-    new_inner = jnp.concatenate([kept_inner[None], moved[:, :, :inner_local]], axis=0)
-    new_outer = jnp.concatenate([kept_outer[None], moved[:, :, inner_local:]], axis=0)
-    return (new_states, new_inner, new_outer, mixer_out[None])
+    return (
+        new_states,
+        new_inner.transpose(1, 0, 2),
+        new_outer.transpose(1, 0, 2),
+        mixer_out[None],
+    )
 
 
 def solution(mesh):

time: 319 us -> 278 us (0.87)
  waiting for transfers between devices: 64.2 us -> 111 us
  Pallas kernels: 122 us -> 79 us
  blocking collectives: 42.9 us -> 6.52 us
  local copies, waits for them, and re-layouts: 23.9 us -> 11.2 us
  starting transfers between devices: 57.1 us -> 66.4 us
  other arithmetic: 6.26 us -> 1.16 us
    pallas_call x1 -> x3, Pallas kernels: 53.5 us -> 10.2 us  [the longest x1 4.46 us: reorder(): pl.pallas_call(reorder_kernel, grid=(1,), in_specs=[scalar, scalar] + [wh...]
    all_gather x1 -> x0, blocking collectives: 36.4 us -> none  [device_body(): every = lax.all_gather(packed, 'req', axis=0, tiled=True)]
    ppermute x27, waiting for transfers between devices: 29.7 us -> 58.8 us  [rotate(): got[hop] = lax.ppermute(values[hop], axis, pairs)]
    all_to_all x2 -> x3, waiting for transfers between devices: 34.5 us -> 52 us  [exchange(): return lax.all_to_all(value, axis, split_axis=0, concat_axis=0, tiled=True)]
    gather x5 -> x0, local copies, waits for them, and re-layouts: 6.85 us -> none  [rows_at(): return source.at[indices].get(mode='promise_in_bounds')]
    all_to_all x2 -> x3, starting transfers between devices: 9.24 us -> 14.5 us  [exchange(): return lax.all_to_all(value, axis, split_axis=0, concat_axis=0, tiled=True)]
    ppermute x27, starting transfers between devices: 47.8 us -> 51.9 us  [rotate(): got[hop] = lax.ppermute(values[hop], axis, pairs)]
    slice x6 -> x0, local copies, waits for them, and re-layouts: 3.23 us -> none  [the longest x1 2.75 us: rotate(): got[hop] = lax.ppermute(values[hop], axis, pairs)]
  transfers between devices with their start and end apart: 29 -> 30, of which waited for: 13 -> 11; matrix products, arithmetic and copies ran while one was open for 7% -> 2% of each run, Pallas kernels for 36% -> 25%
where the time goes in v3:
time: 278 us; the launch traced here: 277 us
  waiting for transfers between devices  111 us (40%)
  Pallas kernels  79 us (28%)
  starting transfers between devices  66.4 us (24%)
  local copies, waits for them, and re-layouts  11.2 us (4%)
  blocking collectives  6.52 us (2%)
    ppermute x27, waiting for transfers between devices, rotate(): got[hop] = lax.ppermute(values[hop], axis, pairs)  58.8 us
    all_to_all x3, waiting for transfers between devices, exchange(): return lax.all_to_all(value, axis, split_axis=0, concat_axis=0, tiled=True)  52 us
    ppermute x27, starting transfers between devices, rotate(): got[hop] = lax.ppermute(values[hop], axis, pairs)  51.9 us
    pallas_call x1, Pallas kernels, block_parts(): pl.pallas_call(block_kernel, grid_spec=pltpu.PrefetchScalarGridSpec(num_s...  32.1 us
    all_to_all x3, starting transfers between devices, exchange(): return lax.all_to_all(value, axis, split_axis=0, concat_axis=0, tiled=True)  14.5 us
    pallas_call x1, Pallas kernels, finish(): pl.pallas_call(finish_kernel, grid=(length // TILE,), in_specs=[pl.BlockS...  11.7 us
    unnamed x70, local copies, waits for them, and re-layouts  6.71 us
    all_gather x1, blocking collectives, device_body(): shared = lax.all_gather(payload, 'seq', axis=0)  6.52 us
  transfers between devices with their start and end apart: 30, of which 11 were waited for; matrix products, arithmetic and copies ran while one was open for 2% of the time, Pallas kernels for 25%

profile of v3, /device:TPU:0, one launch (start us, length us, event | category | flops | bytes accessed | tf_op | source)
XLA Modules:
  0.0 276.7 jit_solution(8287762919628411638)
XLA Ops:
  3.9 7.3 %all-to-all-start = ((bf16[8,3,16,1152]{3,2,1,0:T(8,128)(2,1)}), bf16[8,3,16,1152]{3,2,1,0:T(8,128)(2,1)S(1)}, u32[]{:S(2)}, u32[]{:S(2)}) async-start(bf16[8,3,16,1152]{3,2,1,0:T(8,128)(2,1)} %mark.1), calls=%async_computation | async-start | bytes 1769472 | tf_op jit(solution)/shard_map/all_to_all | solution.py:794
  11.2 3.9 %pack_rest.1 = bf16[8,13,64,128]{3,2,1,0:T(8,128)(2,1)} custom-call(s32[13]{0:T(128)} %mask_ref.5, f32[13,8,128,128]{3,2,1,0:T(8,128)} %bitcast.35), custom_call_target="tpu_custom_call" | custom-call | tf_op jit(solution)/shard_map/pack_rest/pallas_call | solution.py:382
  15.1 18.4 %all-to-all-done.every_ref = bf16[8,3,16,1152]{3,2,1,0:T(8,128)(2,1)S(1)} async-done(((bf16[8,3,16,1152]{3,2,1,0:T(8,128)(2,1)}), bf16[8,3,16,1152]{3,2,1,0:T(8,128)(2,1)S(1)}, u32[]{:S(2)}, u32[]{:S(2)}) %all-to-all-start) | async-done | bytes 884768 | tf_op jit(solution)/shard_map/all_to_all | solution.py:794
  33.5 3.6 %all-to-all-start.1 = ((bf16[8,13,64,128]{3,2,1,0:T(8,128)(2,1)}), bf16[8,13,64,128]{3,2,1,0:T(8,128)(2,1)S(1)}, u32[]{:S(2)}, u32[]{:S(2)}) async-start(bf16[8,13,64,128]{3,2,1,0:T(8,128)(2,1)} %pack_rest.1), calls=%async_computation.1 | async-start | bytes 3407872 | tf_op jit(solution)/shard_map/all_to_all | solution.py:794
  39.7 3.7 %share.1 = (bf16[3,9984]{1,0:T(4,128)(2,1)}, f32[512,128]{1,0:T(8,128)}, bf16[3,16,1152]{2,1,0:T(8,128)(2,1)}, s32[8,128]{1,0:T(8,128)}) custom-call(s32[6]{0:T(128)} %stack.33.place_ref, bf16[8,3,16,1152]{3,2,1,0:T(8,128)(2,1)} %copy-done.2, bf16[512,4096]{1,0:T(8,128)(2,1)} %bitcast.30, bf16[512,4096]{1,0:T(8,128)(2,1)} %bitcast.31, ...), custom_call_target="tpu_custom_call" | custom-call | tf_op jit(solution)/shard_map/share/pallas_call | solution.py:678
  43.4 33.6 %all-to-all-done.1.in_ref = bf16[8,13,64,128]{3,2,1,0:T(8,128)(2,1)S(1)} async-done(((bf16[8,13,64,128]{3,2,1,0:T(8,128)(2,1)}), bf16[8,13,64,128]{3,2,1,0:T(8,128)(2,1)S(1)}, u32[]{:S(2)}, u32[]{:S(2)}) %all-to-all-start.1) | async-done | bytes 1703968 | tf_op jit(solution)/shard_map/all_to_all | solution.py:794
  78.2 3.8 %reorder_rest.1 = (bf16[8,12,64,128]{3,2,1,0:T(8,128)(2,1)}, bf16[64,128]{1,0:T(8,128)(2,1)}, bf16[64,128]{1,0:T(8,128)(2,1)}, bf16[64,128]{1,0:T(8,128)(2,1)}, ...) custom-call(s32[1]{0:T(128)} %bitcast.own_ref, ...), custom_call_target="tpu_custom_call" | custom-call | tf_op jit(solution)/shard_map/reorder_rest/pallas_call | solution.py:456
  82.0 3.6 %all-to-all-start.2 = ((bf16[8,12,64,128]{3,2,1,0:T(8,128)(2,1)}), bf16[8,12,64,128]{3,2,1,0:T(8,128)(2,1)S(1)}, u32[]{:S(2)}, u32[]{:S(2)}) async-start(bf16[8,12,64,128]{3,2,1,0:T(8,128)(2,1)} %get-tuple-element.78), calls=%async_computation.2 | async-start | bytes 3145728 | tf_op jit(solution)/shard_map/all_to_all | solution.py:794
  85.7 3.9 %pack.1 = (bf16[13,64,128]{2,1,0:T(8,128)(2,1)}, bf16[13,64,128]{2,1,0:T(8,128)(2,1)}, bf16[13,64,128]{2,1,0:T(8,128)(2,1)}, bf16[13,64,128]{2,1,0:T(8,128)(2,1)...) custom-call(s32[1]{0:T(128)} %bitcast.own_ref, ...), custom_call_target="tpu_custom_call" | custom-call | tf_op jit(solution)/shard_map/pack/pallas_call | solution.py:356
  89.6 2.1 collective-permute-start.3
  93.2 2.4 collective-permute-start.5
  97.0 2.4 collective-permute-start.7
  99.3 22.8 %collective-permute-done.3.refs_1_ = bf16[13,64,128]{2,1,0:T(8,128)(2,1)S(1)} collective-permute-done((bf16[13,64,128]{2,1,0:T(8,128)(2,1)}, bf16[13,64,128]{2,1,0:T(8,128)(2,1)S(1)}, u32[]{:S(2)}, u32[]{:S(2)}) %collective-permute-start.3) | collective-permute-done | bytes 213024 | tf_op jit(solution)/shard_map/ppermute | solution.py:802
  122.1 4.1 %collective-permute-start.9 = (bf16[13,64,128]{2,1,0:T(8,128)(2,1)}, bf16[13,64,128]{2,1,0:T(8,128)(2,1)S(1)}, u32[]{:S(2)}, u32[]{:S(2)}) collective-permute-start(bf16[13,64,128]{2,1,0:T(8,128)(2,1)} %get-tuple-element.60), channel_id=1, source_target_pairs={{0,28},{4,0},{8,4},{12,8},{16,12},{20,16},{24,20},{28,24},{1,29},{... | collective-permute-start | bytes 638984 | tf_op jit(solution)/shard_map/ppermute | solution.py:802
  127.6 20.0 %collective-permute-done.5.refs_3_ = bf16[13,64,128]{2,1,0:T(8,128)(2,1)S(1)} collective-permute-done((bf16[13,64,128]{2,1,0:T(8,128)(2,1)}, bf16[13,64,128]{2,1,0:T(8,128)(2,1)S(1)}, u32[]{:S(2)}, u32[]{:S(2)}) %collective-permute-start.5) | collective-permute-done | bytes 213024 | tf_op jit(solution)/shard_map/ppermute | solution.py:802
  148.7 4.5 %reorder.1 = (bf16[13,64,128]{2,1,0:T(8,128)(2,1)}, bf16[13,64,128]{2,1,0:T(8,128)(2,1)}, bf16[13,64,128]{2,1,0:T(8,128)(2,1)}, bf16[13,64,128]{2,1,0:T(8,128)(2...) custom-call(s32[1]{0:T(128)} %bitcast.own_ref, ...), custom_call_target="tpu_custom_call" | custom-call | tf_op jit(solution)/shard_map/reorder/pallas_call | solution.py:425
  153.1 8.3 %collective-permute-start.10 = (bf16[13,64,128]{2,1,0:T(8,128)(2,1)}, bf16[13,64,128]{2,1,0:T(8,128)(2,1)S(1)}, u32[]{:S(2)}, u32[]{:S(2)}) collective-permute-start(bf16[13,64,128]{2,1,0:T(8,128)(2,1)} %get-tuple-element.62), channel_id=1, source_target_pairs={{0,4},{4,8},{8,12},{12,16},{16,20},{20,24},{24,28},{28,0},{1,5},{5... | collective-permute-start | bytes 638984 | tf_op jit(solution)/shard_map/ppermute | solution.py:802
  161.5 5.2 %collective-permute-start.11 = (bf16[13,64,128]{2,1,0:T(8,128)(2,1)}, bf16[13,64,128]{2,1,0:T(8,128)(2,1)S(1)}, u32[]{:S(2)}, u32[]{:S(2)}) collective-permute-start(bf16[13,64,128]{2,1,0:T(8,128)(2,1)} %get-tuple-element.63), channel_id=1, source_target_pairs={{0,8},{4,12},{8,16},{12,20},{16,24},{20,28},{24,0},{28,4},{1,9},{5... | collective-permute-start | bytes 638984 | tf_op jit(solution)/shard_map/ppermute | solution.py:802
  167.5 3.2 %collective-permute-start.13 = (bf16[13,64,128]{2,1,0:T(8,128)(2,1)}, bf16[13,64,128]{2,1,0:T(8,128)(2,1)S(1)}, u32[]{:S(2)}, u32[]{:S(2)}) collective-permute-start(bf16[13,64,128]{2,1,0:T(8,128)(2,1)} %get-tuple-element.65), channel_id=1, source_target_pairs={{0,16},{4,20},{8,24},{12,28},{16,0},{20,4},{24,8},{28,12},{1,17},{... | collective-permute-start | bytes 638984 | tf_op jit(solution)/shard_map/ppermute | solution.py:802
  170.7 2.1 collective-permute-start.14
  172.8 6.5 %all-gather.1.shared_ref = bf16[4,3,9984]{2,1,0:T(4,128)(2,1)} all-gather(bf16[1,3,9984]{2,1,0:T(4,128)(2,1)S(1)} %bitcast.47), channel_id=2, replica_groups=mesh['req'=8,'seq'=4] {'seq'}, dimensions={0}, use_global_device_ids=true | all-gather | bytes 299520 | tf_op jit(solution)/shard_map/all_gather | solution.py:869
  181.3 32.1 %block_parts.1 = (f32[512,4096]{1,0:T(8,128)}, bf16[4,128,1024]{2,1,0:T(8,128)(2,1)}, bf16[512,128]{1,0:T(8,128)(2,1)}, f32[512,128]{1,0:T(8,128)}) custom-call(s32[1]{0:T(128)} %bitcast.1.chain_ref, f32[8,4352]{1,0:T(8,128)} %get-tuple-element.49.tail_ref.state_tail_ref, bf16[512,4096]{1,0:T(8,128)(2,1)} %bitcast.33, bf16[512,4096]{1,0:T(8,128)(2,1)} %bitcast.34, ...), custom_call_target="tpu_custom_call" | custom-call | flops 6000000000 | bytes 20000000 | tf_op jit(solution)/shard_map/block_parts/pallas_call | solution.py:176
  219.3 6.1 %collective-permute-done.15.refs_10_.refs_6_ = bf16[13,64,128]{2,1,0:T(8,128)(2,1)S(1)} collective-permute-done((bf16[13,64,128]{2,1,0:T(8,128)(2,1)}, bf16[13,64,128]{2,1,0:T(8,128)(2,1)S(1)}, u32[]{:S(2)}, u32[]{:S(2)}) %collective-permute-start.15) | collective-permute-done | bytes 213024 | tf_op jit(solution)/shard_map/ppermute | solution.py:802
  225.4 2.3 collective-permute-done.16.refs_11_.refs_7_
  229.5 2.7 collective-permute-start.19
  232.1 3.1 %collective-permute-start.20 = (bf16[64,128]{1,0:T(8,128)(2,1)}, bf16[64,128]{1,0:T(8,128)(2,1)S(1)}, u32[]{:S(2)}, u32[]{:S(2)}) collective-permute-start(bf16[64,128]{1,0:T(8,128)(2,1)} %get-tuple-element.73), channel_id=1, source_target_pairs={{0,16},{4,20},{8,24},{12,28},{16,0},{20,4},{24,8},{28,12},{1,17},{... | collective-permute-start | bytes 49160 | tf_op jit(solution)/shard_map/ppermute | solution.py:802
  235.3 2.4 collective-permute-start.22
  242.3 3.2 %combine.1 = (bf16[128,1024]{1,0:T(8,128)(2,1)}, bf16[128,1024]{1,0:T(8,128)(2,1)}, bf16[128,1024]{1,0:T(8,128)(2,1)}, bf16[128,1024]{1,0:T(8,128)(2,1)}, f32[1024,128]{1,0:T(8,128)}) custom-call(s32[2]{0:T(128)} %pad_add_fusion.place_ref, f32[4,1024]{1,0:T(4,128)} %get-tuple-element.48.decay_ref, bf16[128,1024]{1,0:T(8,128)(2,1)} %get-tuple-element.91.refs_0_, ...), custom_call_target="tpu_custom_call" | custom-call | tf_op jit(solution)/shard_map/combine/pallas_call | solution.py:561
  249.1 4.3 %unpack.1.states_ref = f32[13,8,128,128]{3,2,1,0:T(8,128)} custom-call(s32[2]{0:T(128)} %pad_add_fusion.place_ref, f32[1024,128]{1,0:T(8,128)} %get-tuple-element.77.final_ref, bf16[13,64,128]{2,1,0:T(8,128)(2,1)} %get-tuple-element.61.refs_4_.refs_0_, bf16[13,64,128]{2,1,0:T(8,128)(2,1)} %copy-done.3, bf16[13,64,128]{2,1,0:T(8,128)(2,1)} %copy-done.4, ...), custom_call_target="tpu_custom_call" | custom-call | tf_op jit(solution)/shard_map/unpack/pallas_call | solution.py:487
  255.0 4.1 %collective-permute-done.26.refs_3_ = bf16[128,1024]{1,0:T(8,128)(2,1)S(1)} collective-permute-done((bf16[128,1024]{1,0:T(8,128)(2,1)}, bf16[128,1024]{1,0:T(8,128)(2,1)S(1)}, u32[]{:S(2)}, u32[]{:S(2)}) %collective-permute-start.26) | collective-permute-done | bytes 262176 | tf_op jit(solution)/shard_map/ppermute | solution.py:802
  259.8 11.7 %finish.1 = bf16[512,4096]{1,0:T(8,128)(2,1)} custom-call(s32[3]{0:T(128)} %pad_add_fusion.1.place_ref, f32[512,4096]{1,0:T(8,128)} %get-tuple-element.81.part_ref, bf16[512,4096]{1,0:T(8,128)(2,1)} %bitcast.38, bf16[512,128]{1,0:T(8,128)(2,1)} %get-tuple-element.82.read_ref, f32[512,128]{1,0:T(8,128)} %get-tuple-element.83.decay_ref, f32[1,4096]{1,0:T(1,128)} %bitcast.48, ...), custom_call_target="tpu_custom_call" | custom-call | flops 3000000000 | bytes 16000000 | tf_op jit(solution)/shard_map/finish/pallas_call | solution.py:282
  272.7 4.1 %unpack_rest.1 = f32[13,8,128,128]{3,2,1,0:T(8,128)} custom-call(f32[1024,128]{1,0:T(8,128)} %get-tuple-element.77.final_ref, bf16[8,12,64,128]{3,2,1,0:T(8,128)(2,1)} %copy-done.1, f32[13,8,128,128]{3,2,1,0:T(8,128)} %unpack.1.states_ref), custom_call_target="tpu_custom_call", output_to_operand_aliasing={{}: (2, {})} | custom-call | tf_op jit(solution)/shard_map/unpack_rest/pallas_call | solution.py:512
  (120 shorter events, 33.6 us)
Async XLA Ops:
  3.9 29.6 %all-to-all-start = ((bf16[8,3,16,1152]{3,2,1,0:T(8,128)(2,1)}), bf16[8,3,16,1152]{3,2,1,0:T(8,128)(2,1)S(1)}, u32[]{:S(2)}, u32[]{:S(2)}) async-start(bf16[8,3,16,1152]{3,2,1,0:T(8,128)(2,1)} %mark.1), calls=%async_computation | async-start | bytes 1769472 | tf_op jit(solution)/shard_map/all_to_all | solution.py:794
  33.5 43.5 %all-to-all-start.1 = ((bf16[8,13,64,128]{3,2,1,0:T(8,128)(2,1)}), bf16[8,13,64,128]{3,2,1,0:T(8,128)(2,1)S(1)}, u32[]{:S(2)}, u32[]{:S(2)}) async-start(bf16[8,13,64,128]{3,2,1,0:T(8,128)(2,1)} %pack_rest.1), calls=%async_computation.1 | async-start | bytes 3407872 | tf_op jit(solution)/shard_map/all_to_all | solution.py:794
  82.0 189.4 %all-to-all-start.2 = ((bf16[8,12,64,128]{3,2,1,0:T(8,128)(2,1)}), bf16[8,12,64,128]{3,2,1,0:T(8,128)(2,1)S(1)}, u32[]{:S(2)}, u32[]{:S(2)}) async-start(bf16[8,12,64,128]{3,2,1,0:T(8,128)(2,1)} %get-tuple-element.78), calls=%async_computation.2 | async-start | bytes 3145728 | tf_op jit(solution)/shard_map/all_to_all | solution.py:794
  85.7 41.2 %copy-start.31 = (f32[64]{0:T(128)S(1)}, f32[64]{0:T(128)}, u32[]{:S(2)}) copy-start(f32[64]{0:T(128)} %param.30) | copy-start | bytes 772
  85.7 87.1 %copy-start.21 = (bf16[3,9984]{1,0:T(4,128)(2,1)S(1)}, bf16[3,9984]{1,0:T(4,128)(2,1)}, u32[]{:S(2)}) copy-start(bf16[3,9984]{1,0:T(4,128)(2,1)} %get-tuple-element.46) | copy-start | bytes 179716
  89.6 32.5 %collective-permute-start.3 = (bf16[13,64,128]{2,1,0:T(8,128)(2,1)}, bf16[13,64,128]{2,1,0:T(8,128)(2,1)S(1)}, u32[]{:S(2)}, u32[]{:S(2)}) collective-permute-start(bf16[13,64,128]{2,1,0:T(8,128)(2,1)} %get-tuple-element.54), channel_id=1, source_target_pairs={{0,4},{4,8},{8,12},{12,16},{16,20},{20,24},{24,28},{28,0},{1,5},{5... | collective-permute-start | bytes 638984 | tf_op jit(solution)/shard_map/ppermute | solution.py:802
  91.7 30.4 %collective-permute-start.4 = (bf16[13,64,128]{2,1,0:T(8,128)(2,1)}, bf16[13,64,128]{2,1,0:T(8,128)(2,1)S(1)}, u32[]{:S(2)}, u32[]{:S(2)}) collective-permute-start(bf16[13,64,128]{2,1,0:T(8,128)(2,1)} %get-tuple-element.55), channel_id=1, source_target_pairs={{0,8},{4,12},{8,16},{12,20},{16,24},{20,28},{24,0},{28,4},{1,9},{5... | collective-permute-start | bytes 638984 | tf_op jit(solution)/shard_map/ppermute | solution.py:802
  93.2 54.5 %collective-permute-start.5 = (bf16[13,64,128]{2,1,0:T(8,128)(2,1)}, bf16[13,64,128]{2,1,0:T(8,128)(2,1)S(1)}, u32[]{:S(2)}, u32[]{:S(2)}) collective-permute-start(bf16[13,64,128]{2,1,0:T(8,128)(2,1)} %get-tuple-element.56), channel_id=1, source_target_pairs={{0,12},{4,16},{8,20},{12,24},{16,28},{20,0},{24,4},{28,8},{1,13},{... | collective-permute-start | bytes 638984 | tf_op jit(solution)/shard_map/ppermute | solution.py:802
  95.5 52.1 %collective-permute-start.6 = (bf16[13,64,128]{2,1,0:T(8,128)(2,1)}, bf16[13,64,128]{2,1,0:T(8,128)(2,1)S(1)}, u32[]{:S(2)}, u32[]{:S(2)}) collective-permute-start(bf16[13,64,128]{2,1,0:T(8,128)(2,1)} %get-tuple-element.57), channel_id=1, source_target_pairs={{0,16},{4,20},{8,24},{12,28},{16,0},{20,4},{24,8},{28,12},{1,17},{... | collective-permute-start | bytes 638984 | tf_op jit(solution)/shard_map/ppermute | solution.py:802
  97.0 50.7 %collective-permute-start.7 = (bf16[13,64,128]{2,1,0:T(8,128)(2,1)}, bf16[13,64,128]{2,1,0:T(8,128)(2,1)S(1)}, u32[]{:S(2)}, u32[]{:S(2)}) collective-permute-start(bf16[13,64,128]{2,1,0:T(8,128)(2,1)} %get-tuple-element.58), channel_id=1, source_target_pairs={{0,20},{4,24},{8,28},{12,0},{16,4},{20,8},{24,12},{28,16},{1,21},{... | collective-permute-start | bytes 638984 | tf_op jit(solution)/shard_map/ppermute | solution.py:802
  122.1 25.6 %collective-permute-start.8 = (bf16[13,64,128]{2,1,0:T(8,128)(2,1)}, bf16[13,64,128]{2,1,0:T(8,128)(2,1)S(1)}, u32[]{:S(2)}, u32[]{:S(2)}) collective-permute-start(bf16[13,64,128]{2,1,0:T(8,128)(2,1)} %get-tuple-element.59), channel_id=1, source_target_pairs={{0,24},{4,28},{8,0},{12,4},{16,8},{20,12},{24,16},{28,20},{1,25},{... | collective-permute-start | bytes 638984 | tf_op jit(solution)/shard_map/ppermute | solution.py:802
  122.1 25.6 %collective-permute-start.9 = (bf16[13,64,128]{2,1,0:T(8,128)(2,1)}, bf16[13,64,128]{2,1,0:T(8,128)(2,1)S(1)}, u32[]{:S(2)}, u32[]{:S(2)}) collective-permute-start(bf16[13,64,128]{2,1,0:T(8,128)(2,1)} %get-tuple-element.60), channel_id=1, source_target_pairs={{0,28},{4,0},{8,4},{12,8},{16,12},{20,16},{24,20},{28,24},{1,29},{... | collective-permute-start | bytes 638984 | tf_op jit(solution)/shard_map/ppermute | solution.py:802
  153.1 62.2 %collective-permute-start.10 = (bf16[13,64,128]{2,1,0:T(8,128)(2,1)}, bf16[13,64,128]{2,1,0:T(8,128)(2,1)S(1)}, u32[]{:S(2)}, u32[]{:S(2)}) collective-permute-start(bf16[13,64,128]{2,1,0:T(8,128)(2,1)} %get-tuple-element.62), channel_id=1, source_target_pairs={{0,4},{4,8},{8,12},{12,16},{16,20},{20,24},{24,28},{28,0},{1,5},{5... | collective-permute-start | bytes 638984 | tf_op jit(solution)/shard_map/ppermute | solution.py:802
  161.5 55.2 %collective-permute-start.11 = (bf16[13,64,128]{2,1,0:T(8,128)(2,1)}, bf16[13,64,128]{2,1,0:T(8,128)(2,1)S(1)}, u32[]{:S(2)}, u32[]{:S(2)}) collective-permute-start(bf16[13,64,128]{2,1,0:T(8,128)(2,1)} %get-tuple-element.63), channel_id=1, source_target_pairs={{0,8},{4,12},{8,16},{12,20},{16,24},{20,28},{24,0},{28,4},{1,9},{5... | collective-permute-start | bytes 638984 | tf_op jit(solution)/shard_map/ppermute | solution.py:802
  166.7 50.6 %collective-permute-start.12 = (bf16[13,64,128]{2,1,0:T(8,128)(2,1)}, bf16[13,64,128]{2,1,0:T(8,128)(2,1)S(1)}, u32[]{:S(2)}, u32[]{:S(2)}) collective-permute-start(bf16[13,64,128]{2,1,0:T(8,128)(2,1)} %get-tuple-element.64), channel_id=1, source_target_pairs={{0,12},{4,16},{8,20},{12,24},{16,28},{20,0},{24,4},{28,8},{1,13},{... | collective-permute-start | bytes 638984 | tf_op jit(solution)/shard_map/ppermute | solution.py:802
  167.5 49.9 %collective-permute-start.13 = (bf16[13,64,128]{2,1,0:T(8,128)(2,1)}, bf16[13,64,128]{2,1,0:T(8,128)(2,1)S(1)}, u32[]{:S(2)}, u32[]{:S(2)}) collective-permute-start(bf16[13,64,128]{2,1,0:T(8,128)(2,1)} %get-tuple-element.65), channel_id=1, source_target_pairs={{0,16},{4,20},{8,24},{12,28},{16,0},{20,4},{24,8},{28,12},{1,17},{... | collective-permute-start | bytes 638984 | tf_op jit(solution)/shard_map/ppermute | solution.py:802
  170.7 47.0 %collective-permute-start.14 = (bf16[13,64,128]{2,1,0:T(8,128)(2,1)}, bf16[13,64,128]{2,1,0:T(8,128)(2,1)S(1)}, u32[]{:S(2)}, u32[]{:S(2)}) collective-permute-start(bf16[13,64,128]{2,1,0:T(8,128)(2,1)} %get-tuple-element.66), channel_id=1, source_target_pairs={{0,20},{4,24},{8,28},{12,0},{16,4},{20,8},{24,12},{28,16},{1,21},{... | collective-permute-start | bytes 638984 | tf_op jit(solution)/shard_map/ppermute | solution.py:802
  215.4 14.1 %collective-permute-start.2 = (bf16[128,1024]{1,0:T(8,128)(2,1)S(1)}, bf16[128,1024]{1,0:T(8,128)(2,1)S(1)}, u32[]{:S(2)}, u32[]{:S(2)}) collective-permute-start(bf16[128,1024]{1,0:T(8,128)(2,1)S(1)} %get-tuple-element.88), channel_id=1, source_target_pairs={{0,3},{1,0},{2,1},{3,2},{4,7},{5,4},{6,5},{7,6},{8,11},{9,8},{10,9... | collective-permute-start | bytes 786440 | tf_op jit(solution)/shard_map/ppermute | solution.py:802
  216.7 15.4 %collective-permute-start.1 = (bf16[128,1024]{1,0:T(8,128)(2,1)S(1)}, bf16[128,1024]{1,0:T(8,128)(2,1)}, u32[]{:S(2)}, u32[]{:S(2)}) collective-permute-start(bf16[128,1024]{1,0:T(8,128)(2,1)S(1)} %get-tuple-element.89), channel_id=1, source_target_pairs={{0,2},{1,3},{2,0},{3,1},{4,6},{5,7},{6,4},{7,5},{8,10},{9,11},{10,... | collective-permute-start | bytes 786440 | tf_op jit(solution)/shard_map/ppermute | solution.py:802
  217.3 17.9 %collective-permute-start = (bf16[128,1024]{1,0:T(8,128)(2,1)S(1)}, bf16[128,1024]{1,0:T(8,128)(2,1)}, u32[]{:S(2)}, u32[]{:S(2)}) collective-permute-start(bf16[128,1024]{1,0:T(8,128)(2,1)S(1)} %get-tuple-element.90), channel_id=1, source_target_pairs={{0,1},{1,2},{2,3},{3,0},{4,5},{5,6},{6,7},{7,4},{8,9},{9,10},{10,1... | collective-permute-start | bytes 786440 | tf_op jit(solution)/shard_map/ppermute | solution.py:802
  217.4 7.9 %collective-permute-start.15 = (bf16[13,64,128]{2,1,0:T(8,128)(2,1)}, bf16[13,64,128]{2,1,0:T(8,128)(2,1)S(1)}, u32[]{:S(2)}, u32[]{:S(2)}) collective-permute-start(bf16[13,64,128]{2,1,0:T(8,128)(2,1)} %get-tuple-element.67), channel_id=1, source_target_pairs={{0,24},{4,28},{8,0},{12,4},{16,8},{20,12},{24,16},{28,20},{1,25},{... | collective-permute-start | bytes 638984 | tf_op jit(solution)/shard_map/ppermute | solution.py:802
  217.8 10.0 %collective-permute-start.16 = (bf16[13,64,128]{2,1,0:T(8,128)(2,1)S(1)}, bf16[13,64,128]{2,1,0:T(8,128)(2,1)S(1)}, u32[]{:S(2)}, u32[]{:S(2)}) collective-permute-start(bf16[13,64,128]{2,1,0:T(8,128)(2,1)S(1)} %copy-done.32), channel_id=1, source_target_pairs={{0,28},{4,0},{8,4},{12,8},{16,12},{20,16},{24,20},{28,24},{1,29},{... | collective-permute-start | bytes 638984 | tf_op jit(solution)/shard_map/ppermute | solution.py:802
  225.3 10.0 %collective-permute-start.17 = (bf16[64,128]{1,0:T(8,128)(2,1)}, bf16[64,128]{1,0:T(8,128)(2,1)S(1)}, u32[]{:S(2)}, u32[]{:S(2)}) collective-permute-start(bf16[64,128]{1,0:T(8,128)(2,1)} %get-tuple-element.70), channel_id=1, source_target_pairs={{0,4},{4,8},{8,12},{12,16},{16,20},{20,24},{24,28},{28,0},{1,5},{5... | collective-permute-start | bytes 49160 | tf_op jit(solution)/shard_map/ppermute | solution.py:802
  227.7 10.0 %collective-permute-start.18 = (bf16[64,128]{1,0:T(8,128)(2,1)}, bf16[64,128]{1,0:T(8,128)(2,1)S(1)}, u32[]{:S(2)}, u32[]{:S(2)}) collective-permute-start(bf16[64,128]{1,0:T(8,128)(2,1)} %get-tuple-element.71), channel_id=1, source_target_pairs={{0,8},{4,12},{8,16},{12,20},{16,24},{20,28},{24,0},{28,4},{1,9},{5... | collective-permute-start | bytes 49160 | tf_op jit(solution)/shard_map/ppermute | solution.py:802
  229.5 10.3 %collective-permute-start.19 = (bf16[64,128]{1,0:T(8,128)(2,1)}, bf16[64,128]{1,0:T(8,128)(2,1)S(1)}, u32[]{:S(2)}, u32[]{:S(2)}) collective-permute-start(bf16[64,128]{1,0:T(8,128)(2,1)} %get-tuple-element.72), channel_id=1, source_target_pairs={{0,12},{4,16},{8,20},{12,24},{16,28},{20,0},{24,4},{28,8},{1,13},{... | collective-permute-start | bytes 49160 | tf_op jit(solution)/shard_map/ppermute | solution.py:802
  232.1 7.7 %collective-permute-start.20 = (bf16[64,128]{1,0:T(8,128)(2,1)}, bf16[64,128]{1,0:T(8,128)(2,1)S(1)}, u32[]{:S(2)}, u32[]{:S(2)}) collective-permute-start(bf16[64,128]{1,0:T(8,128)(2,1)} %get-tuple-element.73), channel_id=1, source_target_pairs={{0,16},{4,20},{8,24},{12,28},{16,0},{20,4},{24,8},{28,12},{1,17},{... | collective-permute-start | bytes 49160 | tf_op jit(solution)/shard_map/ppermute | solution.py:802
  235.3 4.8 %collective-permute-start.21 = (bf16[64,128]{1,0:T(8,128)(2,1)}, bf16[64,128]{1,0:T(8,128)(2,1)S(1)}, u32[]{:S(2)}, u32[]{:S(2)}) collective-permute-start(bf16[64,128]{1,0:T(8,128)(2,1)} %get-tuple-element.74), channel_id=1, source_target_pairs={{0,20},{4,24},{8,28},{12,0},{16,4},{20,8},{24,12},{28,16},{1,21},{... | collective-permute-start | bytes 49160 | tf_op jit(solution)/shard_map/ppermute | solution.py:802
  235.3 4.8 %collective-permute-start.22 = (bf16[64,128]{1,0:T(8,128)(2,1)}, bf16[64,128]{1,0:T(8,128)(2,1)S(1)}, u32[]{:S(2)}, u32[]{:S(2)}) collective-permute-start(bf16[64,128]{1,0:T(8,128)(2,1)} %get-tuple-element.75), channel_id=1, source_target_pairs={{0,24},{4,28},{8,0},{12,4},{16,8},{20,12},{24,16},{28,20},{1,25},{... | collective-permute-start | bytes 49160 | tf_op jit(solution)/shard_map/ppermute | solution.py:802
  237.7 4.0 %collective-permute-start.23 = (bf16[64,128]{1,0:T(8,128)(2,1)}, bf16[64,128]{1,0:T(8,128)(2,1)S(1)}, u32[]{:S(2)}, u32[]{:S(2)}) collective-permute-start(bf16[64,128]{1,0:T(8,128)(2,1)} %get-tuple-element.76), channel_id=1, source_target_pairs={{0,28},{4,0},{8,4},{12,8},{16,12},{20,16},{24,20},{28,24},{1,29},{... | collective-permute-start | bytes 49160 | tf_op jit(solution)/shard_map/ppermute | solution.py:802
  245.5 8.2 %collective-permute-start.24 = (bf16[128,1024]{1,0:T(8,128)(2,1)}, bf16[128,1024]{1,0:T(8,128)(2,1)S(1)}, u32[]{:S(2)}, u32[]{:S(2)}) collective-permute-start(bf16[128,1024]{1,0:T(8,128)(2,1)} %get-tuple-element.85), channel_id=1, source_target_pairs={{0,1},{1,2},{2,3},{3,0},{4,5},{5,6},{6,7},{7,4},{8,9},{9,10},{10,1... | collective-permute-start | bytes 786440 | tf_op jit(solution)/shard_map/ppermute | solution.py:802
  245.5 9.5 %collective-permute-start.25 = (bf16[128,1024]{1,0:T(8,128)(2,1)}, bf16[128,1024]{1,0:T(8,128)(2,1)S(1)}, u32[]{:S(2)}, u32[]{:S(2)}) collective-permute-start(bf16[128,1024]{1,0:T(8,128)(2,1)} %get-tuple-element.86), channel_id=1, source_target_pairs={{0,2},{1,3},{2,0},{3,1},{4,6},{5,7},{6,4},{7,5},{8,10},{9,11},{10,... | collective-permute-start | bytes 786440 | tf_op jit(solution)/shard_map/ppermute | solution.py:802
  247.1 12.0 %collective-permute-start.26 = (bf16[128,1024]{1,0:T(8,128)(2,1)}, bf16[128,1024]{1,0:T(8,128)(2,1)S(1)}, u32[]{:S(2)}, u32[]{:S(2)}) collective-permute-start(bf16[128,1024]{1,0:T(8,128)(2,1)} %get-tuple-element.87), channel_id=1, source_target_pairs={{0,3},{1,0},{2,1},{3,2},{4,7},{5,4},{6,5},{7,6},{8,11},{9,8},{10,9... | collective-permute-start | bytes 786440 | tf_op jit(solution)/shard_map/ppermute | solution.py:802
  (32 other events, 391.0 us)

commit v4 on v3

--- a/solution.py
+++ b/solution.py
@@ -1,3 +1,4 @@
+import functools
 import math
 
 import jax
@@ -305,36 +306,55 @@
     )(place, part, gate, read, decay, norm_row, *states)
 
 
-def mark_kernel(plan_ref, mask_ref, inner_ref, outer_ref, out_ref):
-    peers, taps, padded, total = out_ref.shape
-    slots = inner_ref.shape[1]
+def mark_kernel(plan_ref, mask_ref, inner_ref, outer_ref, out_ref, scr):
+    peers, padded, total = out_ref.shape
+    taps, slots = inner_ref.shape[:2]
     width = inner_ref.shape[2] + outer_ref.shape[2]
-    row = lax.broadcasted_iota(jnp.int32, (padded, total - width), 0)
-    fill = jnp.zeros((padded - slots, width), F32)
+    capacity = most_per_pair(slots, peers)
+    scr[:, :width] = jnp.zeros((peers * padded, width), F32)
+    scr[:, width:] = jnp.full((peers * padded, total - width), -1.0, F32)
+    windows = []
     for tap in range(taps):
-        marks = jnp.full((padded, total - width), -1.0, F32)
-        for slot in range(slots):
-            value = mask_ref[slot] if tap == 2 else plan_ref[slot, tap]
-            marks = jnp.where(row == slot, value.astype(F32), marks)
-        window = jnp.concatenate(
-            [inner_ref[tap].astype(F32), outer_ref[tap].astype(F32)], axis=1
-        )
-        window = jnp.concatenate([window, fill], axis=0)
-        block = jnp.concatenate([window, marks], axis=1).astype(BF16)
-        for peer in range(peers):
-            out_ref[peer, tap] = block
+        both = [inner_ref[tap].astype(F32), outer_ref[tap].astype(F32)]
+        windows.append(jnp.concatenate(both, axis=1))
+    lane = lax.broadcasted_iota(jnp.int32, (1, LANES), 1)
+    peer_marks = jnp.zeros((1, LANES), F32)
+    slot_marks = jnp.zeros((1, LANES), F32)
+    for slot in range(slots):
+        peer, target = plan_ref[slot, 0], plan_ref[slot, 1]
+        rank = jnp.int32(0)
+        for earlier in range(slot):
+            rank = rank + (plan_ref[earlier, 0] == peer).astype(jnp.int32)
+        keep = mask_ref[slot].astype(F32)
+        for tap in range(taps):
+            tag = jnp.full((1, total - width), (target + tap * SLOT_PAD).astype(F32))
+            row = jnp.concatenate([windows[tap][slot : slot + 1] * keep, tag], axis=1)
+            scr[pl.ds(peer * padded + tap * capacity + rank, 1), :] = row
+        peer_marks = jnp.where(lane == slot, peer.astype(F32), peer_marks)
+        slot_marks = jnp.where(lane == slot, target.astype(F32), slot_marks)
+    for peer in range(peers):
+        at = peer * padded + taps * capacity
+        scr[at : at + 1, :LANES] = peer_marks
+        scr[at + 1 : at + 2, :LANES] = slot_marks
+        out_ref[peer] = scr[peer * padded : (peer + 1) * padded, :].astype(BF16)
+
+
+def most_per_pair(slots, peers):
+    return (2 * slots + peers - 1) // peers
 
 
 def mark(plan, mask, inner, outer, peers):
-    taps, _ = inner.shape[:2]
+    taps, slots = inner.shape[:2]
     width = inner.shape[2] + outer.shape[2]
     whole = pl.BlockSpec(memory_space=pltpu.VMEM)
     scalar = pl.BlockSpec(memory_space=pltpu.SMEM)
     total = width + LANES - width % LANES
+    padded = pl.cdiv(taps * most_per_pair(slots, peers) + 2, 16) * 16
     return pl.pallas_call(
         mark_kernel,
         in_specs=[scalar, scalar, whole, whole],
-        out_shape=jax.ShapeDtypeStruct((peers, taps, SLOT_PAD, total), BF16),
+        out_shape=jax.ShapeDtypeStruct((peers, padded, total), BF16),
+        scratch_shapes=[pltpu.VMEM((peers * padded, total), F32)],
         name="mark",
     )(plan, mask, inner, outer)
 
@@ -583,6 +603,7 @@
 
 
 def share_kernel(
+    slot_count,
     place_ref,
     every_ref,
     end_ref,
@@ -603,34 +624,36 @@
     inner = end_ref.shape[1]
     outer = state_end_ref.shape[1]
     channels = inner + outer
-    own, slots = place_ref[0], place_ref[5]
-    peers, _, padded, width = every_ref.shape
-    rows = peers * padded
-    mark_at = width - width % LANES - LANES
-    marks = []
-    for tap in range(taps):
-        lanes = every_ref[:, tap, :, mark_at:].astype(F32).reshape(rows, width - mark_at)
-        marks.append(lanes[:, width - mark_at - 1 :])
-    target = marks[0] * slots.astype(F32) + marks[1]
-    columns = table_ref.shape[1]
-    lane = lax.broadcasted_iota(jnp.int32, (rows, columns), 1).astype(F32)
-    source = lax.broadcasted_iota(jnp.int32, (rows, columns), 0).astype(F32)
-    found = jnp.sum(jnp.where(target == lane, source, 0.0), axis=0, keepdims=True)
-    table_ref[...] = jnp.broadcast_to(found, table_ref.shape).astype(jnp.int32)
-    lane = lax.broadcasted_iota(jnp.int32, (rows, LANES), 1)
-    mine = (target == (own * slots + lane).astype(F32)) & (lane < slots)
-    pick = jnp.where(mine, marks[2], 0.0).astype(BF16)
+    peers, packet, width = every_ref.shape
+    padded = moved_ref.shape[1]
+    slots = float(slot_count)
+    rows = peers * packet
+    everything = every_ref[...].astype(F32).reshape(rows, width)
+    tags = everything[:, width - 1 :]
+    lane = lax.broadcasted_iota(jnp.int32, (rows, LANES), 1).astype(F32)
+    pick = (tags == lane).astype(BF16)
+    moved = dot(pick, everything.astype(BF16), ((0,), (0,)))
     firsts = []
     for tap in range(taps):
-        source_rows = every_ref[:, tap].astype(F32).reshape(rows, width).astype(BF16)
-        moved = dot(pick, source_rows, ((0,), (0,)))[:padded]
-        moved_ref[tap] = moved.astype(BF16)
-        firsts.append(moved[:1])
+        moved_ref[tap] = moved[tap * padded : (tap + 1) * padded].astype(BF16)
+        firsts.append(moved[tap * padded : tap * padded + 1])
+    at = taps * most_per_pair(slot_count, peers)
+    peer_marks = [every_ref[p, at : at + 1, :LANES].astype(F32) for p in range(peers)]
+    slot_marks = [every_ref[p, at + 1 : at + 2, :LANES].astype(F32) for p in range(peers)]
+    target = jnp.concatenate(peer_marks, axis=0) * slots + jnp.concatenate(slot_marks, axis=0)
+    columns = table_ref.shape[1]
+    lane = lax.broadcasted_iota(jnp.int32, (peers, columns), 1).astype(F32)
+    code = lax.broadcasted_iota(jnp.int32, (peers, columns), 0).astype(F32) * SLOT_PAD
+    found = jnp.zeros((peers, columns), F32)
+    for slot in range(slot_count):
+        found = found + jnp.where(target[:, slot : slot + 1] == lane, code + slot, 0.0)
+    found = jnp.sum(found, axis=0, keepdims=True)
+    table_ref[...] = jnp.broadcast_to(found, table_ref.shape).astype(jnp.int32)
     low_block, high_block, start, length = (
+        place_ref[0],
         place_ref[1],
         place_ref[2],
         place_ref[3],
-        place_ref[4],
     )
     out_ref[:, :inner] = end_ref[16 - taps :, :]
     out_ref[:, inner:channels] = state_end_ref[16 - taps :, :]
@@ -668,7 +691,8 @@
 
 
 def share(place, slots, every, rows, state_rows, step_raw, step_bias, rate):
-    peers, taps, padded, width = every.shape
+    peers, _, width = every.shape
+    taps, padded = KERNEL - 1, SLOT_PAD
     length, inner = rows.shape
     outer = state_rows.shape[1]
     heads = step_raw.shape[1]
@@ -676,18 +700,18 @@
     total = 2 * (inner + outer) + width + LANES
     lanes = pl.cdiv(peers * slots, LANES) * LANES
     return pl.pallas_call(
-        share_kernel,
+        functools.partial(share_kernel, slots),
         grid_spec=pltpu.PrefetchScalarGridSpec(
             num_scalar_prefetch=1,
             grid=(1,),
             in_specs=[
-                pl.BlockSpec(every.shape, lambda t, c: (0, 0, 0, 0)),
+                pl.BlockSpec(every.shape, lambda t, c: (0, 0, 0)),
                 pl.BlockSpec((16, inner), lambda t, c: (last, 0)),
+                pl.BlockSpec((16, inner), lambda t, c: (c[0], 0)),
                 pl.BlockSpec((16, inner), lambda t, c: (c[1], 0)),
-                pl.BlockSpec((16, inner), lambda t, c: (c[2], 0)),
                 pl.BlockSpec((16, outer), lambda t, c: (last, 0)),
+                pl.BlockSpec((16, outer), lambda t, c: (c[0], 0)),
                 pl.BlockSpec((16, outer), lambda t, c: (c[1], 0)),
-                pl.BlockSpec((16, outer), lambda t, c: (c[2], 0)),
                 pl.BlockSpec((length, heads), lambda t, c: (0, 0)),
                 pl.BlockSpec((1, heads), lambda t, c: (0, 0)),
                 pl.BlockSpec((1, LANES), lambda t, c: (0, 0)),
@@ -857,7 +881,7 @@
     heads = decay_log.shape[0]
     rate = jnp.pad(-LOG2E * jnp.exp(decay_log), (0, LANES - heads))[None]
     payload, step, moved, table = share(
-        jnp.stack([own_peer, low_block, high_block, start, length, jnp.int32(slots)]),
+        jnp.stack([low_block, high_block, start, length]),
         slots,
         every,
         rows,

time: 278 us -> 265 us (0.953)
  waiting for transfers between devices: 111 us -> 97.9 us
    all_to_all x3, waiting for transfers between devices: 52 us -> 39.1 us  [exchange(): return lax.all_to_all(value, axis, split_axis=0, concat_axis=0, tiled=True)]
  transfers between devices with their start and end apart: 30 -> 30, of which waited for: 11 -> 11; matrix products, arithmetic and copies ran while one was open for 2% -> 2% of each run, Pallas kernels for 25% -> 26%
where the time goes in v4:
time: 265 us; the launch traced here: 264 us
  waiting for transfers between devices  97.9 us (37%)
  Pallas kernels  78.7 us (30%)
  starting transfers between devices  66.4 us (25%)
  local copies, waits for them, and re-layouts  10.6 us (4%)
  blocking collectives  6.52 us (2%)
    ppermute x27, waiting for transfers between devices, rotate(): got[hop] = lax.ppermute(values[hop], axis, pairs)  58.8 us
    ppermute x27, starting transfers between devices, rotate(): got[hop] = lax.ppermute(values[hop], axis, pairs)  51.9 us
    all_to_all x3, waiting for transfers between devices, exchange(): return lax.all_to_all(value, axis, split_axis=0, concat_axis=0, tiled=True)  39.1 us
    pallas_call x1, Pallas kernels, block_parts(): pl.pallas_call(block_kernel, grid_spec=pltpu.PrefetchScalarGridSpec(num_s...  32 us
    all_to_all x3, starting transfers between devices, exchange(): return lax.all_to_all(value, axis, split_axis=0, concat_axis=0, tiled=True)  14.5 us
    pallas_call x1, Pallas kernels, finish(): pl.pallas_call(finish_kernel, grid=(length // TILE,), in_specs=[pl.BlockS...  11.7 us
    unnamed x70, local copies, waits for them, and re-layouts  6.71 us
    all_gather x1, blocking collectives, device_body(): shared = lax.all_gather(payload, 'seq', axis=0)  6.52 us
  transfers between devices with their start and end apart: 30, of which 11 were waited for; matrix products, arithmetic and copies ran while one was open for 2% of the time, Pallas kernels for 26%

profile of v4, /device:TPU:0, one launch (start us, length us, event | category | flops | bytes accessed | tf_op | source)
XLA Modules:
  0.0 263.5 jit_solution(17900183689672990864)
XLA Ops:
  3.9 7.3 %all-to-all-start = ((bf16[8,16,1152]{2,1,0:T(8,128)(2,1)}), bf16[8,16,1152]{2,1,0:T(8,128)(2,1)S(1)}, u32[]{:S(2)}, u32[]{:S(2)}) async-start(bf16[8,16,1152]{2,1,0:T(8,128)(2,1)} %mark.1), calls=%async_computation | async-start | bytes 589824 | tf_op jit(solution)/shard_map/all_to_all | solution.py:818
  11.2 3.9 %pack_rest.1 = bf16[8,13,64,128]{3,2,1,0:T(8,128)(2,1)} custom-call(s32[13]{0:T(128)} %mask_ref.5, f32[13,8,128,128]{3,2,1,0:T(8,128)} %bitcast.35), custom_call_target="tpu_custom_call" | custom-call | tf_op jit(solution)/shard_map/pack_rest/pallas_call | solution.py:402
  15.1 5.7 %all-to-all-done.every_ref = bf16[8,16,1152]{2,1,0:T(8,128)(2,1)S(1)} async-done(((bf16[8,16,1152]{2,1,0:T(8,128)(2,1)}), bf16[8,16,1152]{2,1,0:T(8,128)(2,1)S(1)}, u32[]{:S(2)}, u32[]{:S(2)}) %all-to-all-start) | async-done | bytes 294944 | tf_op jit(solution)/shard_map/all_to_all | solution.py:818
  20.8 3.6 %all-to-all-start.1 = ((bf16[8,13,64,128]{3,2,1,0:T(8,128)(2,1)}), bf16[8,13,64,128]{3,2,1,0:T(8,128)(2,1)S(1)}, u32[]{:S(2)}, u32[]{:S(2)}) async-start(bf16[8,13,64,128]{3,2,1,0:T(8,128)(2,1)} %pack_rest.1), calls=%async_computation.1 | async-start | bytes 3407872 | tf_op jit(solution)/shard_map/all_to_all | solution.py:818
  27.0 3.4 %share.1 = (bf16[3,9984]{1,0:T(4,128)(2,1)}, f32[512,128]{1,0:T(8,128)}, bf16[3,16,1152]{2,1,0:T(8,128)(2,1)}, s32[8,128]{1,0:T(8,128)}) custom-call(s32[4]{0:T(128)} %pad_add_fusion.1.place_ref, bf16[8,16,1152]{2,1,0:T(8,128)(2,1)} %copy-done.2, bf16[512,4096]{1,0:T(8,128)(2,1)} %bitcast.30, bf16[512,4096]{1,0:T(8,128)(2,1)} %bitcast.31, ...), custom_call_target="tpu_custom_call" | custom-call | tf_op jit(solution)/shard_map/share/pallas_call | solution.py:702
  30.4 33.4 %all-to-all-done.1.in_ref = bf16[8,13,64,128]{3,2,1,0:T(8,128)(2,1)S(1)} async-done(((bf16[8,13,64,128]{3,2,1,0:T(8,128)(2,1)}), bf16[8,13,64,128]{3,2,1,0:T(8,128)(2,1)S(1)}, u32[]{:S(2)}, u32[]{:S(2)}) %all-to-all-start.1) | async-done | bytes 1703968 | tf_op jit(solution)/shard_map/all_to_all | solution.py:818
  65.0 3.8 %reorder_rest.1 = (bf16[8,12,64,128]{3,2,1,0:T(8,128)(2,1)}, bf16[64,128]{1,0:T(8,128)(2,1)}, bf16[64,128]{1,0:T(8,128)(2,1)}, bf16[64,128]{1,0:T(8,128)(2,1)}, ...) custom-call(s32[1]{0:T(128)} %bitcast.own_ref, ...), custom_call_target="tpu_custom_call" | custom-call | tf_op jit(solution)/shard_map/reorder_rest/pallas_call | solution.py:476
  68.8 3.6 %all-to-all-start.2 = ((bf16[8,12,64,128]{3,2,1,0:T(8,128)(2,1)}), bf16[8,12,64,128]{3,2,1,0:T(8,128)(2,1)S(1)}, u32[]{:S(2)}, u32[]{:S(2)}) async-start(bf16[8,12,64,128]{3,2,1,0:T(8,128)(2,1)} %get-tuple-element.78), calls=%async_computation.2 | async-start | bytes 3145728 | tf_op jit(solution)/shard_map/all_to_all | solution.py:818
  72.5 3.9 %pack.1 = (bf16[13,64,128]{2,1,0:T(8,128)(2,1)}, bf16[13,64,128]{2,1,0:T(8,128)(2,1)}, bf16[13,64,128]{2,1,0:T(8,128)(2,1)}, bf16[13,64,128]{2,1,0:T(8,128)(2,1)...) custom-call(s32[1]{0:T(128)} %bitcast.own_ref, ...), custom_call_target="tpu_custom_call" | custom-call | tf_op jit(solution)/shard_map/pack/pallas_call | solution.py:376
  76.4 2.1 collective-permute-start.3
  79.9 2.4 collective-permute-start.5
  83.8 2.4 collective-permute-start.7
  86.1 22.8 %collective-permute-done.3.refs_1_ = bf16[13,64,128]{2,1,0:T(8,128)(2,1)S(1)} collective-permute-done((bf16[13,64,128]{2,1,0:T(8,128)(2,1)}, bf16[13,64,128]{2,1,0:T(8,128)(2,1)S(1)}, u32[]{:S(2)}, u32[]{:S(2)}) %collective-permute-start.3) | collective-permute-done | bytes 213024 | tf_op jit(solution)/shard_map/ppermute | solution.py:826
  108.9 4.1 %collective-permute-start.9 = (bf16[13,64,128]{2,1,0:T(8,128)(2,1)}, bf16[13,64,128]{2,1,0:T(8,128)(2,1)S(1)}, u32[]{:S(2)}, u32[]{:S(2)}) collective-permute-start(bf16[13,64,128]{2,1,0:T(8,128)(2,1)} %get-tuple-element.60), channel_id=1, source_target_pairs={{0,28},{4,0},{8,4},{12,8},{16,12},{20,16},{24,20},{28,24},{1,29},{... | collective-permute-start | bytes 638984 | tf_op jit(solution)/shard_map/ppermute | solution.py:826
  114.4 20.0 %collective-permute-done.5.refs_3_ = bf16[13,64,128]{2,1,0:T(8,128)(2,1)S(1)} collective-permute-done((bf16[13,64,128]{2,1,0:T(8,128)(2,1)}, bf16[13,64,128]{2,1,0:T(8,128)(2,1)S(1)}, u32[]{:S(2)}, u32[]{:S(2)}) %collective-permute-start.5) | collective-permute-done | bytes 213024 | tf_op jit(solution)/shard_map/ppermute | solution.py:826
  135.5 4.5 %reorder.1 = (bf16[13,64,128]{2,1,0:T(8,128)(2,1)}, bf16[13,64,128]{2,1,0:T(8,128)(2,1)}, bf16[13,64,128]{2,1,0:T(8,128)(2,1)}, bf16[13,64,128]{2,1,0:T(8,128)(2...) custom-call(s32[1]{0:T(128)} %bitcast.own_ref, ...), custom_call_target="tpu_custom_call" | custom-call | tf_op jit(solution)/shard_map/reorder/pallas_call | solution.py:445
  139.9 8.3 %collective-permute-start.10 = (bf16[13,64,128]{2,1,0:T(8,128)(2,1)}, bf16[13,64,128]{2,1,0:T(8,128)(2,1)S(1)}, u32[]{:S(2)}, u32[]{:S(2)}) collective-permute-start(bf16[13,64,128]{2,1,0:T(8,128)(2,1)} %get-tuple-element.62), channel_id=1, source_target_pairs={{0,4},{4,8},{8,12},{12,16},{16,20},{20,24},{24,28},{28,0},{1,5},{5... | collective-permute-start | bytes 638984 | tf_op jit(solution)/shard_map/ppermute | solution.py:826
  148.3 5.2 %collective-permute-start.11 = (bf16[13,64,128]{2,1,0:T(8,128)(2,1)}, bf16[13,64,128]{2,1,0:T(8,128)(2,1)S(1)}, u32[]{:S(2)}, u32[]{:S(2)}) collective-permute-start(bf16[13,64,128]{2,1,0:T(8,128)(2,1)} %get-tuple-element.63), channel_id=1, source_target_pairs={{0,8},{4,12},{8,16},{12,20},{16,24},{20,28},{24,0},{28,4},{1,9},{5... | collective-permute-start | bytes 638984 | tf_op jit(solution)/shard_map/ppermute | solution.py:826
  154.3 3.2 %collective-permute-start.13 = (bf16[13,64,128]{2,1,0:T(8,128)(2,1)}, bf16[13,64,128]{2,1,0:T(8,128)(2,1)S(1)}, u32[]{:S(2)}, u32[]{:S(2)}) collective-permute-start(bf16[13,64,128]{2,1,0:T(8,128)(2,1)} %get-tuple-element.65), channel_id=1, source_target_pairs={{0,16},{4,20},{8,24},{12,28},{16,0},{20,4},{24,8},{28,12},{1,17},{... | collective-permute-start | bytes 638984 | tf_op jit(solution)/shard_map/ppermute | solution.py:826
  157.5 2.1 collective-permute-start.14
  159.6 6.5 %all-gather.1.shared_ref = bf16[4,3,9984]{2,1,0:T(4,128)(2,1)} all-gather(bf16[1,3,9984]{2,1,0:T(4,128)(2,1)S(1)} %bitcast.47), channel_id=2, replica_groups=mesh['req'=8,'seq'=4] {'seq'}, dimensions={0}, use_global_device_ids=true | all-gather | bytes 299520 | tf_op jit(solution)/shard_map/all_gather | solution.py:893
  168.1 32.0 %block_parts.1 = (f32[512,4096]{1,0:T(8,128)}, bf16[4,128,1024]{2,1,0:T(8,128)(2,1)}, bf16[512,128]{1,0:T(8,128)(2,1)}, f32[512,128]{1,0:T(8,128)}) custom-call(s32[1]{0:T(128)} %bitcast.1.chain_ref, f32[8,4352]{1,0:T(8,128)} %get-tuple-element.49.tail_ref.state_tail_ref, bf16[512,4096]{1,0:T(8,128)(2,1)} %bitcast.33, bf16[512,4096]{1,0:T(8,128)(2,1)} %bitcast.34, ...), custom_call_target="tpu_custom_call" | custom-call | flops 6000000000 | bytes 20000000 | tf_op jit(solution)/shard_map/block_parts/pallas_call | solution.py:177
  206.0 6.1 %collective-permute-done.15.refs_10_.refs_6_ = bf16[13,64,128]{2,1,0:T(8,128)(2,1)S(1)} collective-permute-done((bf16[13,64,128]{2,1,0:T(8,128)(2,1)}, bf16[13,64,128]{2,1,0:T(8,128)(2,1)S(1)}, u32[]{:S(2)}, u32[]{:S(2)}) %collective-permute-start.15) | collective-permute-done | bytes 213024 | tf_op jit(solution)/shard_map/ppermute | solution.py:826
  212.2 2.3 collective-permute-done.16.refs_11_.refs_7_
  216.3 2.7 %collective-permute-start.19 = (bf16[64,128]{1,0:T(8,128)(2,1)}, bf16[64,128]{1,0:T(8,128)(2,1)S(1)}, u32[]{:S(2)}, u32[]{:S(2)}) collective-permute-start(bf16[64,128]{1,0:T(8,128)(2,1)} %get-tuple-element.72), channel_id=1, source_target_pairs={{0,12},{4,16},{8,20},{12,24},{16,28},{20,0},{24,4},{28,8},{1,13},{... | collective-permute-start | bytes 49160 | tf_op jit(solution)/shard_map/ppermute | solution.py:826
  218.9 3.1 %collective-permute-start.20 = (bf16[64,128]{1,0:T(8,128)(2,1)}, bf16[64,128]{1,0:T(8,128)(2,1)S(1)}, u32[]{:S(2)}, u32[]{:S(2)}) collective-permute-start(bf16[64,128]{1,0:T(8,128)(2,1)} %get-tuple-element.73), channel_id=1, source_target_pairs={{0,16},{4,20},{8,24},{12,28},{16,0},{20,4},{24,8},{28,12},{1,17},{... | collective-permute-start | bytes 49160 | tf_op jit(solution)/shard_map/ppermute | solution.py:826
  222.1 2.4 collective-permute-start.22
  229.1 3.2 %combine.1 = (bf16[128,1024]{1,0:T(8,128)(2,1)}, bf16[128,1024]{1,0:T(8,128)(2,1)}, bf16[128,1024]{1,0:T(8,128)(2,1)}, bf16[128,1024]{1,0:T(8,128)(2,1)}, f32[1024,128]{1,0:T(8,128)}) custom-call(s32[2]{0:T(128)} %pad_add_fusion.place_ref, f32[4,1024]{1,0:T(4,128)} %get-tuple-element.48.decay_ref, bf16[128,1024]{1,0:T(8,128)(2,1)} %get-tuple-element.91.refs_0_, ...), custom_call_target="tpu_custom_call" | custom-call | tf_op jit(solution)/shard_map/combine/pallas_call | solution.py:581
  235.8 4.3 %unpack.1.states_ref = f32[13,8,128,128]{3,2,1,0:T(8,128)} custom-call(s32[2]{0:T(128)} %pad_add_fusion.place_ref, f32[1024,128]{1,0:T(8,128)} %get-tuple-element.77.final_ref, bf16[13,64,128]{2,1,0:T(8,128)(2,1)} %get-tuple-element.61.refs_4_.refs_0_, bf16[13,64,128]{2,1,0:T(8,128)(2,1)} %copy-done.3, bf16[13,64,128]{2,1,0:T(8,128)(2,1)} %copy-done.4, ...), custom_call_target="tpu_custom_call" | custom-call | tf_op jit(solution)/shard_map/unpack/pallas_call | solution.py:507
  241.8 4.1 %collective-permute-done.26.refs_3_ = bf16[128,1024]{1,0:T(8,128)(2,1)S(1)} collective-permute-done((bf16[128,1024]{1,0:T(8,128)(2,1)}, bf16[128,1024]{1,0:T(8,128)(2,1)S(1)}, u32[]{:S(2)}, u32[]{:S(2)}) %collective-permute-start.26) | collective-permute-done | bytes 262176 | tf_op jit(solution)/shard_map/ppermute | solution.py:826
  246.6 11.7 %finish.1 = bf16[512,4096]{1,0:T(8,128)(2,1)} custom-call(s32[3]{0:T(128)} %pad_add_fusion.2.place_ref, f32[512,4096]{1,0:T(8,128)} %get-tuple-element.81.part_ref, bf16[512,4096]{1,0:T(8,128)(2,1)} %bitcast.38, bf16[512,128]{1,0:T(8,128)(2,1)} %get-tuple-element.82.read_ref, f32[512,128]{1,0:T(8,128)} %get-tuple-element.83.decay_ref, f32[1,4096]{1,0:T(1,128)} %bitcast.48, ...), custom_call_target="tpu_custom_call" | custom-call | flops 3000000000 | bytes 16000000 | tf_op jit(solution)/shard_map/finish/pallas_call | solution.py:283
  259.4 4.1 %unpack_rest.1 = f32[13,8,128,128]{3,2,1,0:T(8,128)} custom-call(f32[1024,128]{1,0:T(8,128)} %get-tuple-element.77.final_ref, bf16[8,12,64,128]{3,2,1,0:T(8,128)(2,1)} %copy-done.1, f32[13,8,128,128]{3,2,1,0:T(8,128)} %unpack.1.states_ref), custom_call_target="tpu_custom_call", output_to_operand_aliasing={{}: (2, {})} | custom-call | tf_op jit(solution)/shard_map/unpack_rest/pallas_call | solution.py:532
  (120 shorter events, 33.6 us)
Async XLA Ops:
  3.9 16.9 %all-to-all-start = ((bf16[8,16,1152]{2,1,0:T(8,128)(2,1)}), bf16[8,16,1152]{2,1,0:T(8,128)(2,1)S(1)}, u32[]{:S(2)}, u32[]{:S(2)}) async-start(bf16[8,16,1152]{2,1,0:T(8,128)(2,1)} %mark.1), calls=%async_computation | async-start | bytes 589824 | tf_op jit(solution)/shard_map/all_to_all | solution.py:818
  20.8 43.0 %all-to-all-start.1 = ((bf16[8,13,64,128]{3,2,1,0:T(8,128)(2,1)}), bf16[8,13,64,128]{3,2,1,0:T(8,128)(2,1)S(1)}, u32[]{:S(2)}, u32[]{:S(2)}) async-start(bf16[8,13,64,128]{3,2,1,0:T(8,128)(2,1)} %pack_rest.1), calls=%async_computation.1 | async-start | bytes 3407872 | tf_op jit(solution)/shard_map/all_to_all | solution.py:818
  68.8 189.5 %all-to-all-start.2 = ((bf16[8,12,64,128]{3,2,1,0:T(8,128)(2,1)}), bf16[8,12,64,128]{3,2,1,0:T(8,128)(2,1)S(1)}, u32[]{:S(2)}, u32[]{:S(2)}) async-start(bf16[8,12,64,128]{3,2,1,0:T(8,128)(2,1)} %get-tuple-element.78), calls=%async_computation.2 | async-start | bytes 3145728 | tf_op jit(solution)/shard_map/all_to_all | solution.py:818
  72.4 41.2 %copy-start.31 = (f32[64]{0:T(128)S(1)}, f32[64]{0:T(128)}, u32[]{:S(2)}) copy-start(f32[64]{0:T(128)} %param.30) | copy-start | bytes 772
  72.4 87.1 %copy-start.21 = (bf16[3,9984]{1,0:T(4,128)(2,1)S(1)}, bf16[3,9984]{1,0:T(4,128)(2,1)}, u32[]{:S(2)}) copy-start(bf16[3,9984]{1,0:T(4,128)(2,1)} %get-tuple-element.46) | copy-start | bytes 179716
  76.4 32.5 %collective-permute-start.3 = (bf16[13,64,128]{2,1,0:T(8,128)(2,1)}, bf16[13,64,128]{2,1,0:T(8,128)(2,1)S(1)}, u32[]{:S(2)}, u32[]{:S(2)}) collective-permute-start(bf16[13,64,128]{2,1,0:T(8,128)(2,1)} %get-tuple-element.54), channel_id=1, source_target_pairs={{0,4},{4,8},{8,12},{12,16},{16,20},{20,24},{24,28},{28,0},{1,5},{5... | collective-permute-start | bytes 638984 | tf_op jit(solution)/shard_map/ppermute | solution.py:826
  78.5 30.4 %collective-permute-start.4 = (bf16[13,64,128]{2,1,0:T(8,128)(2,1)}, bf16[13,64,128]{2,1,0:T(8,128)(2,1)S(1)}, u32[]{:S(2)}, u32[]{:S(2)}) collective-permute-start(bf16[13,64,128]{2,1,0:T(8,128)(2,1)} %get-tuple-element.55), channel_id=1, source_target_pairs={{0,8},{4,12},{8,16},{12,20},{16,24},{20,28},{24,0},{28,4},{1,9},{5... | collective-permute-start | bytes 638984 | tf_op jit(solution)/shard_map/ppermute | solution.py:826
  79.9 54.5 %collective-permute-start.5 = (bf16[13,64,128]{2,1,0:T(8,128)(2,1)}, bf16[13,64,128]{2,1,0:T(8,128)(2,1)S(1)}, u32[]{:S(2)}, u32[]{:S(2)}) collective-permute-start(bf16[13,64,128]{2,1,0:T(8,128)(2,1)} %get-tuple-element.56), channel_id=1, source_target_pairs={{0,12},{4,16},{8,20},{12,24},{16,28},{20,0},{24,4},{28,8},{1,13},{... | collective-permute-start | bytes 638984 | tf_op jit(solution)/shard_map/ppermute | solution.py:826
  82.3 52.1 %collective-permute-start.6 = (bf16[13,64,128]{2,1,0:T(8,128)(2,1)}, bf16[13,64,128]{2,1,0:T(8,128)(2,1)S(1)}, u32[]{:S(2)}, u32[]{:S(2)}) collective-permute-start(bf16[13,64,128]{2,1,0:T(8,128)(2,1)} %get-tuple-element.57), channel_id=1, source_target_pairs={{0,16},{4,20},{8,24},{12,28},{16,0},{20,4},{24,8},{28,12},{1,17},{... | collective-permute-start | bytes 638984 | tf_op jit(solution)/shard_map/ppermute | solution.py:826
  83.8 50.7 %collective-permute-start.7 = (bf16[13,64,128]{2,1,0:T(8,128)(2,1)}, bf16[13,64,128]{2,1,0:T(8,128)(2,1)S(1)}, u32[]{:S(2)}, u32[]{:S(2)}) collective-permute-start(bf16[13,64,128]{2,1,0:T(8,128)(2,1)} %get-tuple-element.58), channel_id=1, source_target_pairs={{0,20},{4,24},{8,28},{12,0},{16,4},{20,8},{24,12},{28,16},{1,21},{... | collective-permute-start | bytes 638984 | tf_op jit(solution)/shard_map/ppermute | solution.py:826
  108.9 25.6 %collective-permute-start.8 = (bf16[13,64,128]{2,1,0:T(8,128)(2,1)}, bf16[13,64,128]{2,1,0:T(8,128)(2,1)S(1)}, u32[]{:S(2)}, u32[]{:S(2)}) collective-permute-start(bf16[13,64,128]{2,1,0:T(8,128)(2,1)} %get-tuple-element.59), channel_id=1, source_target_pairs={{0,24},{4,28},{8,0},{12,4},{16,8},{20,12},{24,16},{28,20},{1,25},{... | collective-permute-start | bytes 638984 | tf_op jit(solution)/shard_map/ppermute | solution.py:826
  108.9 25.6 %collective-permute-start.9 = (bf16[13,64,128]{2,1,0:T(8,128)(2,1)}, bf16[13,64,128]{2,1,0:T(8,128)(2,1)S(1)}, u32[]{:S(2)}, u32[]{:S(2)}) collective-permute-start(bf16[13,64,128]{2,1,0:T(8,128)(2,1)} %get-tuple-element.60), channel_id=1, source_target_pairs={{0,28},{4,0},{8,4},{12,8},{16,12},{20,16},{24,20},{28,24},{1,29},{... | collective-permute-start | bytes 638984 | tf_op jit(solution)/shard_map/ppermute | solution.py:826
  139.9 62.2 %collective-permute-start.10 = (bf16[13,64,128]{2,1,0:T(8,128)(2,1)}, bf16[13,64,128]{2,1,0:T(8,128)(2,1)S(1)}, u32[]{:S(2)}, u32[]{:S(2)}) collective-permute-start(bf16[13,64,128]{2,1,0:T(8,128)(2,1)} %get-tuple-element.62), channel_id=1, source_target_pairs={{0,4},{4,8},{8,12},{12,16},{16,20},{20,24},{24,28},{28,0},{1,5},{5... | collective-permute-start | bytes 638984 | tf_op jit(solution)/shard_map/ppermute | solution.py:826
  148.3 55.2 %collective-permute-start.11 = (bf16[13,64,128]{2,1,0:T(8,128)(2,1)}, bf16[13,64,128]{2,1,0:T(8,128)(2,1)S(1)}, u32[]{:S(2)}, u32[]{:S(2)}) collective-permute-start(bf16[13,64,128]{2,1,0:T(8,128)(2,1)} %get-tuple-element.63), channel_id=1, source_target_pairs={{0,8},{4,12},{8,16},{12,20},{16,24},{20,28},{24,0},{28,4},{1,9},{5... | collective-permute-start | bytes 638984 | tf_op jit(solution)/shard_map/ppermute | solution.py:826
  153.5 50.7 %collective-permute-start.12 = (bf16[13,64,128]{2,1,0:T(8,128)(2,1)}, bf16[13,64,128]{2,1,0:T(8,128)(2,1)S(1)}, u32[]{:S(2)}, u32[]{:S(2)}) collective-permute-start(bf16[13,64,128]{2,1,0:T(8,128)(2,1)} %get-tuple-element.64), channel_id=1, source_target_pairs={{0,12},{4,16},{8,20},{12,24},{16,28},{20,0},{24,4},{28,8},{1,13},{... | collective-permute-start | bytes 638984 | tf_op jit(solution)/shard_map/ppermute | solution.py:826
  154.3 49.9 %collective-permute-start.13 = (bf16[13,64,128]{2,1,0:T(8,128)(2,1)}, bf16[13,64,128]{2,1,0:T(8,128)(2,1)S(1)}, u32[]{:S(2)}, u32[]{:S(2)}) collective-permute-start(bf16[13,64,128]{2,1,0:T(8,128)(2,1)} %get-tuple-element.65), channel_id=1, source_target_pairs={{0,16},{4,20},{8,24},{12,28},{16,0},{20,4},{24,8},{28,12},{1,17},{... | collective-permute-start | bytes 638984 | tf_op jit(solution)/shard_map/ppermute | solution.py:826
  157.5 47.0 %collective-permute-start.14 = (bf16[13,64,128]{2,1,0:T(8,128)(2,1)}, bf16[13,64,128]{2,1,0:T(8,128)(2,1)S(1)}, u32[]{:S(2)}, u32[]{:S(2)}) collective-permute-start(bf16[13,64,128]{2,1,0:T(8,128)(2,1)} %get-tuple-element.66), channel_id=1, source_target_pairs={{0,20},{4,24},{8,28},{12,0},{16,4},{20,8},{24,12},{28,16},{1,21},{... | collective-permute-start | bytes 638984 | tf_op jit(solution)/shard_map/ppermute | solution.py:826
  202.1 14.1 %collective-permute-start.2 = (bf16[128,1024]{1,0:T(8,128)(2,1)S(1)}, bf16[128,1024]{1,0:T(8,128)(2,1)S(1)}, u32[]{:S(2)}, u32[]{:S(2)}) collective-permute-start(bf16[128,1024]{1,0:T(8,128)(2,1)S(1)} %get-tuple-element.88), channel_id=1, source_target_pairs={{0,3},{1,0},{2,1},{3,2},{4,7},{5,4},{6,5},{7,6},{8,11},{9,8},{10,9... | collective-permute-start | bytes 786440 | tf_op jit(solution)/shard_map/ppermute | solution.py:826
  203.5 15.5 %collective-permute-start.1 = (bf16[128,1024]{1,0:T(8,128)(2,1)S(1)}, bf16[128,1024]{1,0:T(8,128)(2,1)}, u32[]{:S(2)}, u32[]{:S(2)}) collective-permute-start(bf16[128,1024]{1,0:T(8,128)(2,1)S(1)} %get-tuple-element.89), channel_id=1, source_target_pairs={{0,2},{1,3},{2,0},{3,1},{4,6},{5,7},{6,4},{7,5},{8,10},{9,11},{10,... | collective-permute-start | bytes 786440 | tf_op jit(solution)/shard_map/ppermute | solution.py:826
  204.1 17.9 %collective-permute-start = (bf16[128,1024]{1,0:T(8,128)(2,1)S(1)}, bf16[128,1024]{1,0:T(8,128)(2,1)}, u32[]{:S(2)}, u32[]{:S(2)}) collective-permute-start(bf16[128,1024]{1,0:T(8,128)(2,1)S(1)} %get-tuple-element.90), channel_id=1, source_target_pairs={{0,1},{1,2},{2,3},{3,0},{4,5},{5,6},{6,7},{7,4},{8,9},{9,10},{10,1... | collective-permute-start | bytes 786440 | tf_op jit(solution)/shard_map/ppermute | solution.py:826
  204.2 7.9 %collective-permute-start.15 = (bf16[13,64,128]{2,1,0:T(8,128)(2,1)}, bf16[13,64,128]{2,1,0:T(8,128)(2,1)S(1)}, u32[]{:S(2)}, u32[]{:S(2)}) collective-permute-start(bf16[13,64,128]{2,1,0:T(8,128)(2,1)} %get-tuple-element.67), channel_id=1, source_target_pairs={{0,24},{4,28},{8,0},{12,4},{16,8},{20,12},{24,16},{28,20},{1,25},{... | collective-permute-start | bytes 638984 | tf_op jit(solution)/shard_map/ppermute | solution.py:826
  204.5 10.0 %collective-permute-start.16 = (bf16[13,64,128]{2,1,0:T(8,128)(2,1)S(1)}, bf16[13,64,128]{2,1,0:T(8,128)(2,1)S(1)}, u32[]{:S(2)}, u32[]{:S(2)}) collective-permute-start(bf16[13,64,128]{2,1,0:T(8,128)(2,1)S(1)} %copy-done.32), channel_id=1, source_target_pairs={{0,28},{4,0},{8,4},{12,8},{16,12},{20,16},{24,20},{28,24},{1,29},{... | collective-permute-start | bytes 638984 | tf_op jit(solution)/shard_map/ppermute | solution.py:826
  212.1 10.0 %collective-permute-start.17 = (bf16[64,128]{1,0:T(8,128)(2,1)}, bf16[64,128]{1,0:T(8,128)(2,1)S(1)}, u32[]{:S(2)}, u32[]{:S(2)}) collective-permute-start(bf16[64,128]{1,0:T(8,128)(2,1)} %get-tuple-element.70), channel_id=1, source_target_pairs={{0,4},{4,8},{8,12},{12,16},{16,20},{20,24},{24,28},{28,0},{1,5},{5... | collective-permute-start | bytes 49160 | tf_op jit(solution)/shard_map/ppermute | solution.py:826
  214.5 10.0 %collective-permute-start.18 = (bf16[64,128]{1,0:T(8,128)(2,1)}, bf16[64,128]{1,0:T(8,128)(2,1)S(1)}, u32[]{:S(2)}, u32[]{:S(2)}) collective-permute-start(bf16[64,128]{1,0:T(8,128)(2,1)} %get-tuple-element.71), channel_id=1, source_target_pairs={{0,8},{4,12},{8,16},{12,20},{16,24},{20,28},{24,0},{28,4},{1,9},{5... | collective-permute-start | bytes 49160 | tf_op jit(solution)/shard_map/ppermute | solution.py:826
  216.3 10.3 %collective-permute-start.19 = (bf16[64,128]{1,0:T(8,128)(2,1)}, bf16[64,128]{1,0:T(8,128)(2,1)S(1)}, u32[]{:S(2)}, u32[]{:S(2)}) collective-permute-start(bf16[64,128]{1,0:T(8,128)(2,1)} %get-tuple-element.72), channel_id=1, source_target_pairs={{0,12},{4,16},{8,20},{12,24},{16,28},{20,0},{24,4},{28,8},{1,13},{... | collective-permute-start | bytes 49160 | tf_op jit(solution)/shard_map/ppermute | solution.py:826
  218.9 7.7 %collective-permute-start.20 = (bf16[64,128]{1,0:T(8,128)(2,1)}, bf16[64,128]{1,0:T(8,128)(2,1)S(1)}, u32[]{:S(2)}, u32[]{:S(2)}) collective-permute-start(bf16[64,128]{1,0:T(8,128)(2,1)} %get-tuple-element.73), channel_id=1, source_target_pairs={{0,16},{4,20},{8,24},{12,28},{16,0},{20,4},{24,8},{28,12},{1,17},{... | collective-permute-start | bytes 49160 | tf_op jit(solution)/shard_map/ppermute | solution.py:826
  222.1 4.8 %collective-permute-start.21 = (bf16[64,128]{1,0:T(8,128)(2,1)}, bf16[64,128]{1,0:T(8,128)(2,1)S(1)}, u32[]{:S(2)}, u32[]{:S(2)}) collective-permute-start(bf16[64,128]{1,0:T(8,128)(2,1)} %get-tuple-element.74), channel_id=1, source_target_pairs={{0,20},{4,24},{8,28},{12,0},{16,4},{20,8},{24,12},{28,16},{1,21},{... | collective-permute-start | bytes 49160 | tf_op jit(solution)/shard_map/ppermute | solution.py:826
  222.1 4.8 %collective-permute-start.22 = (bf16[64,128]{1,0:T(8,128)(2,1)}, bf16[64,128]{1,0:T(8,128)(2,1)S(1)}, u32[]{:S(2)}, u32[]{:S(2)}) collective-permute-start(bf16[64,128]{1,0:T(8,128)(2,1)} %get-tuple-element.75), channel_id=1, source_target_pairs={{0,24},{4,28},{8,0},{12,4},{16,8},{20,12},{24,16},{28,20},{1,25},{... | collective-permute-start | bytes 49160 | tf_op jit(solution)/shard_map/ppermute | solution.py:826
  224.5 4.0 %collective-permute-start.23 = (bf16[64,128]{1,0:T(8,128)(2,1)}, bf16[64,128]{1,0:T(8,128)(2,1)S(1)}, u32[]{:S(2)}, u32[]{:S(2)}) collective-permute-start(bf16[64,128]{1,0:T(8,128)(2,1)} %get-tuple-element.76), channel_id=1, source_target_pairs={{0,28},{4,0},{8,4},{12,8},{16,12},{20,16},{24,20},{28,24},{1,29},{... | collective-permute-start | bytes 49160 | tf_op jit(solution)/shard_map/ppermute | solution.py:826
  232.3 8.2 %collective-permute-start.24 = (bf16[128,1024]{1,0:T(8,128)(2,1)}, bf16[128,1024]{1,0:T(8,128)(2,1)S(1)}, u32[]{:S(2)}, u32[]{:S(2)}) collective-permute-start(bf16[128,1024]{1,0:T(8,128)(2,1)} %get-tuple-element.85), channel_id=1, source_target_pairs={{0,1},{1,2},{2,3},{3,0},{4,5},{5,6},{6,7},{7,4},{8,9},{9,10},{10,1... | collective-permute-start | bytes 786440 | tf_op jit(solution)/shard_map/ppermute | solution.py:826
  232.3 9.5 %collective-permute-start.25 = (bf16[128,1024]{1,0:T(8,128)(2,1)}, bf16[128,1024]{1,0:T(8,128)(2,1)S(1)}, u32[]{:S(2)}, u32[]{:S(2)}) collective-permute-start(bf16[128,1024]{1,0:T(8,128)(2,1)} %get-tuple-element.86), channel_id=1, source_target_pairs={{0,2},{1,3},{2,0},{3,1},{4,6},{5,7},{6,4},{7,5},{8,10},{9,11},{10,... | collective-permute-start | bytes 786440 | tf_op jit(solution)/shard_map/ppermute | solution.py:826
  233.9 12.0 %collective-permute-start.26 = (bf16[128,1024]{1,0:T(8,128)(2,1)}, bf16[128,1024]{1,0:T(8,128)(2,1)S(1)}, u32[]{:S(2)}, u32[]{:S(2)}) collective-permute-start(bf16[128,1024]{1,0:T(8,128)(2,1)} %get-tuple-element.87), channel_id=1, source_target_pairs={{0,3},{1,0},{2,1},{3,2},{4,7},{5,4},{6,5},{7,6},{8,11},{9,8},{10,9... | collective-permute-start | bytes 786440 | tf_op jit(solution)/shard_map/ppermute | solution.py:826
  (32 other events, 365.1 us)

commit v5 on v4

--- a/solution.py
+++ b/solution.py
@@ -321,10 +321,10 @@
     peer_marks = jnp.zeros((1, LANES), F32)
     slot_marks = jnp.zeros((1, LANES), F32)
     for slot in range(slots):
-        peer, target = plan_ref[slot, 0], plan_ref[slot, 1]
+        peer, target = plan_ref[0, slot], plan_ref[1, slot]
         rank = jnp.int32(0)
         for earlier in range(slot):
-            rank = rank + (plan_ref[earlier, 0] == peer).astype(jnp.int32)
+            rank = rank + (plan_ref[0, earlier] == peer).astype(jnp.int32)
         keep = mask_ref[slot].astype(F32)
         for tap in range(taps):
             tag = jnp.full((1, total - width), (target + tap * SLOT_PAD).astype(F32))
@@ -420,148 +420,165 @@
 
 
 def reorder_kernel(own_ref, table_ref, *refs):
-    peers = (len(refs) - 1) // 2
-    in_refs, out_refs, scr = refs[:peers], refs[peers:-1], refs[-1]
+    peers = (len(refs) - 2) // 2
+    in_refs, rest_ref, first_refs, scr = (
+        refs[:peers],
+        refs[peers],
+        refs[peers + 1 : -1],
+        refs[-1],
+    )
     slots = in_refs[0].shape[0]
     own = own_ref[0]
     for hop in range(peers):
-        scr[hop] = in_refs[hop][...]
+        scr[lax.rem(own - hop + peers, peers)] = in_refs[hop][...]
+    for hop in range(peers):
+        peer, index = source_of(table_ref, lax.rem(own + hop, peers) * slots)
+        first_refs[hop][...] = scr[peer, index]
+
+        def move(slot, unused):
+            peer, index = source_of(table_ref, hop * slots + slot)
+            rest_ref[hop, slot - 1] = scr[peer, index]
+            return unused
+
+        lax.fori_loop(1, slots, move, 0)
+
+
+def reorder(own, table, pieces):
+    slots, half, width = pieces[0].shape
+    peers = len(pieces)
+    scalar = pl.BlockSpec(memory_space=pltpu.SMEM)
+    outs = pl.pallas_call(
+        reorder_kernel,
+        grid=(1,),
+        in_specs=[scalar, scalar]
+        + [pl.BlockSpec((slots, half, width), lambda t: (0, 0, 0))] * peers,
+        out_specs=[pl.BlockSpec((peers, slots - 1, half, width), lambda t: (0, 0, 0, 0))]
+        + [pl.BlockSpec((half, width), lambda t: (0, 0))] * peers,
+        out_shape=[jax.ShapeDtypeStruct((peers, slots - 1, half, width), BF16)]
+        + [jax.ShapeDtypeStruct((half, width), BF16)] * peers,
+        scratch_shapes=[pltpu.VMEM((peers, slots, half, width), BF16)],
+        name="reorder",
+    )(own, table, *pieces)
+    return outs[0], outs[1:]
+
+
+def reorder_rest_kernel(own_ref, table_ref, in_ref, *refs):
+    peers, slots, half, _ = in_ref.shape
+    upper_refs, first_refs, rest_refs = (
+        refs[:peers],
+        refs[peers : 2 * peers],
+        refs[2 * peers :],
+    )
+    own = own_ref[0]
     for hop in range(peers):
         base = lax.rem(own + hop, peers) * slots
+        peer, index = source_of(table_ref, base)
+        first_refs[hop][:half, :] = upper_refs[hop][...]
+        first_refs[hop][half:, :] = in_ref[peer, index]
 
         def move(slot, unused):
             peer, index = source_of(table_ref, base + slot)
-            out_refs[hop][slot] = scr[lax.rem(own - peer + peers, peers), index]
+            rest_refs[hop][slot - 1] = in_ref[peer, index]
             return unused
 
-        lax.fori_loop(0, slots, move, 0)
-
-
-def reorder(own, table, pieces):
-    slots, half, width = pieces[0].shape
-    count = len(pieces)
-    whole = pl.BlockSpec((slots, half, width), lambda t: (0, 0, 0))
-    scalar = pl.BlockSpec(memory_space=pltpu.SMEM)
-    return pl.pallas_call(
-        reorder_kernel,
-        grid=(1,),
-        in_specs=[scalar, scalar] + [whole] * count,
-        out_specs=[whole] * count,
-        out_shape=[jax.ShapeDtypeStruct((slots, half, width), BF16)] * count,
-        scratch_shapes=[pltpu.VMEM((count, slots, half, width), BF16)],
-        name="reorder",
-    )(own, table, *pieces)
-
-
-def reorder_rest_kernel(own_ref, table_ref, in_ref, *out_refs):
-    rest_ref, first_refs = out_refs[0], out_refs[1:]
-    peers, slots = in_ref.shape[:2]
-    own = own_ref[0]
-    for hop in range(peers):
-        target = lax.rem(own + hop, peers)
-        peer, index = source_of(table_ref, target * slots)
-        first_refs[hop][...] = in_ref[peer, index]
-
-        def move(slot, unused):
-            peer, index = source_of(table_ref, hop * slots + slot)
-            rest_ref[hop, slot - 1] = in_ref[peer, index]
-            return unused
-
         lax.fori_loop(1, slots, move, 0)
 
 
-def reorder_rest(own, table, pieces):
+def reorder_rest(own, table, pieces, upper):
     peers, slots, half, width = pieces.shape
     scalar = pl.BlockSpec(memory_space=pltpu.SMEM)
     outs = pl.pallas_call(
         reorder_rest_kernel,
         grid=(1,),
-        in_specs=[scalar, scalar, pl.BlockSpec(pieces.shape, lambda t: (0, 0, 0, 0))],
-        out_specs=[pl.BlockSpec((peers, slots - 1, half, width), lambda t: (0, 0, 0, 0))]
+        in_specs=[scalar, scalar, pl.BlockSpec(pieces.shape, lambda t: (0, 0, 0, 0))]
         + [pl.BlockSpec((half, width), lambda t: (0, 0))] * peers,
-        out_shape=[jax.ShapeDtypeStruct((peers, slots - 1, half, width), BF16)]
-        + [jax.ShapeDtypeStruct((half, width), BF16)] * peers,
+        out_specs=[pl.BlockSpec((2 * half, width), lambda t: (0, 0))] * peers
+        + [pl.BlockSpec((slots - 1, half, width), lambda t: (0, 0, 0))] * peers,
+        out_shape=[jax.ShapeDtypeStruct((2 * half, width), BF16)] * peers
+        + [jax.ShapeDtypeStruct((slots - 1, half, width), BF16)] * peers,
         name="reorder_rest",
-    )(own, table, pieces)
-    return outs[0], outs[1:]
-
-
-def unpack_kernel(place_ref, final_ref, *refs):
-    pieces, out_ref = refs[:-1], refs[-1]
-    step = pl.program_id(0)
-    peers, half = out_ref.shape[1:3]
-    for hop in range(peers):
-        peer = lax.rem(place_ref[0] - hop + peers, peers)
-        for j in range(SLOT_TILE):
-            out_ref[j, peer] = pieces[hop][j].astype(F32)
-
-    @pl.when(step == 0)
-    def _():
-        for p in range(peers):
-            out_ref[0, p] = final_ref[2 * p * half : (2 * p + 1) * half, :]
-
-
-def unpack(place, final, pieces):
-    peers = len(pieces)
-    slots, half, width = pieces[0].shape
+    )(own, table, pieces, *upper)
+    return outs[:peers], outs[peers:]
+
+
+def unpack_kernel(final_ref, pieces_ref, out_ref):
+    peers, half = pieces_ref.shape[0], pieces_ref.shape[2]
+    for p in range(peers):
+        out_ref[0, p] = final_ref[2 * p * half : (2 * p + 1) * half, :]
+        out_ref[1:, p] = pieces_ref[p].astype(F32)
+
+
+def unpack(final, pieces):
+    peers, others, half, width = pieces.shape
+    slots, piece = others + 1, 2 * half
     return pl.pallas_call(
         unpack_kernel,
-        grid=(pl.cdiv(slots, SLOT_TILE),),
-        in_specs=[
-            pl.BlockSpec(memory_space=pltpu.SMEM),
-            pl.BlockSpec(final.shape, lambda t: (0, 0)),
-        ]
-        + [pl.BlockSpec((SLOT_TILE, half, width), lambda t: (t, 0, 0))] * peers,
-        out_specs=pl.BlockSpec((SLOT_TILE, peers, half, width), lambda t: (t, 0, 0, 0)),
-        out_shape=jax.ShapeDtypeStruct((slots, peers, 2 * half, width), F32),
-        compiler_params=pltpu.CompilerParams(dimension_semantics=("arbitrary",)),
-        name="unpack",
-    )(place, final, *pieces)
-
-
-def unpack_rest_kernel(final_ref, pieces_ref, states_ref, out_ref):
-    peers, half = pieces_ref.shape[0], pieces_ref.shape[2]
-    for p in range(peers):
-        out_ref[0, p] = final_ref[(2 * p + 1) * half : (2 * p + 2) * half, :]
-        out_ref[1:, p] = pieces_ref[p].astype(F32)
-
-
-def unpack_rest(final, pieces, states):
-    slots, peers, piece, width = states.shape
-    half = piece // 2
-    return pl.pallas_call(
-        unpack_rest_kernel,
         grid=(peers // PEER_TILE,),
         in_specs=[
             pl.BlockSpec((PEER_TILE * piece, width), lambda p: (p, 0)),
-            pl.BlockSpec((PEER_TILE, slots - 1, half, width), lambda p: (p, 0, 0, 0)),
-            pl.BlockSpec(memory_space=pl.ANY),
-        ],
-        out_specs=pl.BlockSpec((slots, PEER_TILE, half, width), lambda p: (0, p, 1, 0)),
+            pl.BlockSpec((PEER_TILE, others, half, width), lambda p: (p, 0, 0, 0)),
+        ],
+        out_specs=pl.BlockSpec((slots, PEER_TILE, half, width), lambda p: (0, p, 0, 0)),
+        out_shape=jax.ShapeDtypeStruct((slots, peers, piece, width), F32),
+        compiler_params=pltpu.CompilerParams(dimension_semantics=("arbitrary",)),
+        name="unpack",
+    )(final, pieces)
+
+
+def unpack_rest_kernel(own_ref, final_ref, states_ref, *refs):
+    piece_refs, out_ref = refs[:-1], refs[-1]
+    step = pl.program_id(0)
+    half = out_ref.shape[2]
+    out_ref[0, 0] = final_ref[half:, :]
+    for hop in range(len(piece_refs)):
+
+        @pl.when(step == hop)
+        def _():
+            out_ref[1:, 0] = piece_refs[hop][...].astype(F32)
+
+
+def unpack_rest(own, final, pieces, states):
+    slots, peers, piece, width = states.shape
+    half = piece // 2
+
+    def from_peer(hop, own):
+        return lax.rem(own[0] - hop + peers, peers)
+
+    return pl.pallas_call(
+        unpack_rest_kernel,
+        grid_spec=pltpu.PrefetchScalarGridSpec(
+            num_scalar_prefetch=1,
+            grid=(peers,),
+            in_specs=[
+                pl.BlockSpec((piece, width), lambda h, own: (from_peer(h, own), 0)),
+                pl.BlockSpec(memory_space=pl.ANY),
+            ]
+            + [pl.BlockSpec((slots - 1, half, width), lambda h, own: (0, 0, 0))] * peers,
+            out_specs=pl.BlockSpec(
+                (slots, 1, half, width), lambda h, own: (0, from_peer(h, own), 1, 0)
+            ),
+        ),
         out_shape=jax.ShapeDtypeStruct(states.shape, F32),
         input_output_aliases={2: 0},
         compiler_params=pltpu.CompilerParams(dimension_semantics=("arbitrary",)),
         name="unpack_rest",
-    )(final, pieces, states)
+    )(own, final, states, *pieces)
 
 
 def combine_kernel(place_ref, decay_ref, *refs):
-    peers, count = decay_ref.shape[1], decay_ref.shape[0]
     count = decay_ref.shape[0]
     scr, end_scr, enter_scr = refs[-3:]
     entering_refs = refs[-4 - count : -4]
     final_ref = refs[-4]
     inputs = refs[: -4 - count]
     end_refs = inputs[:count]
-    peers = (len(inputs) - count) // 2
-    upper, lower = inputs[count : count + peers], inputs[count + peers :]
-    half = lower[0].shape[0]
+    peers = len(inputs) - count
+    first_refs = inputs[count:]
+    piece = first_refs[0].shape[0]
     chain = place_ref[1]
     for hop in range(peers):
         peer = lax.rem(place_ref[0] - hop + peers, peers)
-        at = pl.multiple_of(peer * 2 * half, 16)
-        scr[pl.ds(at, half), :] = upper[hop][0]
-        scr[pl.ds(at + half, half), :] = lower[hop][...]
+        scr[pl.ds(pl.multiple_of(peer * piece, 16), piece), :] = first_refs[hop][...]
     for hop in range(count):
         end_scr[lax.rem(chain - hop + count, count)] = end_refs[hop][...]
     state = scr[...].astype(F32).T
@@ -573,10 +590,9 @@
     final_ref[...] = state.T
 
 
-def combine(place, decay, ends, upper, lower):
+def combine(place, decay, ends, first):
     count = len(ends)
     whole = pl.BlockSpec(memory_space=pltpu.VMEM)
-    half, width = lower[0].shape
     rows, columns = ends[0].shape
     outs = pl.pallas_call(
         combine_kernel,
@@ -586,8 +602,7 @@
             pl.BlockSpec(decay.shape, lambda t: (0, 0)),
         ]
         + [pl.BlockSpec((rows, columns), lambda t: (0, 0))] * count
-        + [pl.BlockSpec((1, half, width), lambda t: (0, 0, 0))] * len(upper)
-        + [pl.BlockSpec((half, width), lambda t: (0, 0))] * len(lower),
+        + [pl.BlockSpec(first[0].shape, lambda t: (0, 0))] * len(first),
         out_specs=[pl.BlockSpec((rows, columns), lambda t: (0, 0))] * count
         + [pl.BlockSpec((columns, rows), lambda t: (0, 0))],
         out_shape=[jax.ShapeDtypeStruct((rows, columns), BF16)] * count
@@ -598,7 +613,7 @@
             pltpu.VMEM((count, rows, columns), BF16),
         ],
         name="combine",
-    )(place, decay, *ends, *upper, *lower)
+    )(place, decay, *ends, *first)
     return outs[:count], outs[count]
 
 
@@ -821,7 +836,8 @@
 def rotate(values, axis):
     count = lax.axis_size(axis)
     got = [values[0]] + [None] * (count - 1)
-    for hop in sorted(range(1, count), key=lambda hop: abs(2 * hop - count)):
+    hops = sorted(range(1, count), key=lambda hop: abs(2 * hop - count))
+    for hop in hops:
         pairs = [(source, (source + hop) % count) for source in range(count)]
         got[hop] = lax.ppermute(values[hop], axis, pairs)
     return got
@@ -857,16 +873,16 @@
     outer_local = state_window.shape[2]
 
     own = own_peer[None]
+    pool_pieces = pool_states.reshape(slots, peers, piece, STATE_DIM)
+    spread_a = rotate(pack(own, active_mask, pool_pieces), "req")
     packed = mark(
-        move_plan,
+        move_plan.T,
         active_mask,
         inner_window.transpose(1, 0, 2),
         state_window.transpose(1, 0, 2),
         peers,
     )
     every = exchange(packed, "req")
-    pool_pieces = pool_states.reshape(slots, peers, piece, STATE_DIM)
-    spread_a = rotate(pack(own, active_mask, pool_pieces), "req")
     spread_b = exchange(pack_rest(active_mask, pool_pieces), "req")
 
     rows = inputs_inner[0]
@@ -896,8 +912,6 @@
         chain, shared, moved, slots, channels, inner_local, outer_local, columns
     )
 
-    moved_a = rotate(reorder(own, table, spread_a), "req")
-
     part, local_end, read_rows, decay = block_parts(
         chain,
         tail,
@@ -912,12 +926,14 @@
     )
     own_ends = rotate(local_end, "seq")
 
-    rest, first = reorder_rest(own, table, spread_b)
-    first_b = rotate(first, "req")
-    rest_b = exchange(rest, "req")
+    rest_a, upper = reorder(own, table, spread_a)
+    moved_a = exchange(rest_a, "req")
+    first, rest_b = reorder_rest(own, table, spread_b, upper)
+    first = rotate(first, "req")
+    moved_b = rotate(rest_b, "req")
 
     place = jnp.stack([own_peer, chain_index])
-    entering, final = combine(place, own_decay, own_ends, moved_a, first_b)
+    entering, final = combine(place, own_decay, own_ends, first)
     incoming = rotate(entering, "seq")
     finish_place = jnp.stack([start, length, chain_index])
     mixer_out = finish(
@@ -929,8 +945,8 @@
         norm_weight[None],
         incoming,
     )
-    states = unpack(place, final, moved_a)
-    new_states = unpack_rest(final, rest_b, states).reshape(pool_states.shape)
+    states = unpack(final, moved_a)
+    new_states = unpack_rest(own, final, moved_b, states).reshape(pool_states.shape)
 
     return (
         new_states,

time: 265 us -> 234 us (0.88)
  waiting for transfers between devices: 97.9 us -> 54 us
  starting transfers between devices: 66.4 us -> 79.8 us
    all_to_all x3, waiting for transfers between devices: 39.1 us -> 5.71 us  [exchange(): return lax.all_to_all(value, axis, split_axis=0, concat_axis=0, tiled=True)]
    all_to_all x3, starting transfers between devices: 14.5 us -> 26.4 us  [exchange(): return lax.all_to_all(value, axis, split_axis=0, concat_axis=0, tiled=True)]
    ppermute x27, waiting for transfers between devices: 58.8 us -> 48.3 us  [rotate(): got[hop] = lax.ppermute(values[hop], axis, pairs)]
    unnamed x70 -> x69, local copies, waits for them, and re-layouts: 6.71 us -> 5.01 us
  transfers between devices with their start and end apart: 30 -> 30, of which waited for: 11 -> 6; matrix products, arithmetic and copies ran while one was open for 2% -> 3% of each run, Pallas kernels for 26% -> 29%
where the time goes in v5:
time: 234 us; the launch traced here: 233 us
  Pallas kernels  80.2 us (34%)
  starting transfers between devices  79.8 us (34%)
  waiting for transfers between devices  54 us (23%)
  local copies, waits for them, and re-layouts  8.87 us (4%)
  blocking collectives  6.52 us (3%)
    ppermute x27, starting transfers between devices, rotate(): got[hop] = lax.ppermute(values[hop], axis, pairs)  53.4 us
    ppermute x27, waiting for transfers between devices, rotate(): got[hop] = lax.ppermute(values[hop], axis, pairs)  48.3 us
    pallas_call x1, Pallas kernels, block_parts(): pl.pallas_call(block_kernel, grid_spec=pltpu.PrefetchScalarGridSpec(num_s...  32.1 us
    all_to_all x3, starting transfers between devices, exchange(): return lax.all_to_all(value, axis, split_axis=0, concat_axis=0, tiled=True)  26.4 us
    pallas_call x1, Pallas kernels, finish(): pl.pallas_call(finish_kernel, grid=(length // TILE,), in_specs=[pl.BlockS...  11.7 us
    all_gather x1, blocking collectives, device_body(): shared = lax.all_gather(payload, 'seq', axis=0)  6.52 us
    pallas_call x1, Pallas kernels, unpack_rest(): pl.pallas_call(unpack_rest_kernel, grid_spec=pltpu.PrefetchScalarGridSpec...  6.06 us
    all_to_all x3, waiting for transfers between devices, exchange(): return lax.all_to_all(value, axis, split_axis=0, concat_axis=0, tiled=True)  5.71 us
  transfers between devices with their start and end apart: 30, of which 6 were waited for; matrix products, arithmetic and copies ran while one was open for 3% of the time, Pallas kernels for 29%

profile of v5, /device:TPU:0, one launch (start us, length us, event | category | flops | bytes accessed | tf_op | source)
XLA Modules:
  0.0 233.0 jit_solution(7212924333712131845)
XLA Ops:
  2.5 7.3 %all-to-all-start = ((bf16[8,16,1152]{2,1,0:T(8,128)(2,1)}), bf16[8,16,1152]{2,1,0:T(8,128)(2,1)S(1)}, u32[]{:S(2)}, u32[]{:S(2)}) async-start(bf16[8,16,1152]{2,1,0:T(8,128)(2,1)} %mark.1), calls=%async_computation | async-start | bytes 589824 | tf_op jit(solution)/shard_map/all_to_all | solution.py:833
  9.8 3.9 %pack_rest.1 = bf16[8,13,64,128]{3,2,1,0:T(8,128)(2,1)} custom-call(s32[13]{0:T(128)} %mask_ref.5, f32[13,8,128,128]{3,2,1,0:T(8,128)} %bitcast.37), custom_call_target="tpu_custom_call" | custom-call | tf_op jit(solution)/shard_map/pack_rest/pallas_call | solution.py:402
  13.7 5.7 %all-to-all-done.every_ref = bf16[8,16,1152]{2,1,0:T(8,128)(2,1)S(1)} async-done(((bf16[8,16,1152]{2,1,0:T(8,128)(2,1)}), bf16[8,16,1152]{2,1,0:T(8,128)(2,1)S(1)}, u32[]{:S(2)}, u32[]{:S(2)}) %all-to-all-start) | async-done | bytes 294944 | tf_op jit(solution)/shard_map/all_to_all | solution.py:833
  19.4 3.6 %all-to-all-start.1 = ((bf16[8,13,64,128]{3,2,1,0:T(8,128)(2,1)}), bf16[8,13,64,128]{3,2,1,0:T(8,128)(2,1)S(1)}, u32[]{:S(2)}, u32[]{:S(2)}) async-start(bf16[8,13,64,128]{3,2,1,0:T(8,128)(2,1)} %pack_rest.1), calls=%async_computation.1 | async-start | bytes 3407872 | tf_op jit(solution)/shard_map/all_to_all | solution.py:833
  23.0 4.0 %pack.1 = (bf16[13,64,128]{2,1,0:T(8,128)(2,1)}, bf16[13,64,128]{2,1,0:T(8,128)(2,1)}, bf16[13,64,128]{2,1,0:T(8,128)(2,1)}, bf16[13,64,128]{2,1,0:T(8,128)(2,1)...) custom-call(s32[1]{0:T(128)} %bitcast.own_ref, ...), custom_call_target="tpu_custom_call" | custom-call | tf_op jit(solution)/shard_map/pack/pallas_call | solution.py:376
  27.0 2.1 collective-permute-start.3
  30.6 2.4 %collective-permute-start.5 = (bf16[13,64,128]{2,1,0:T(8,128)(2,1)}, bf16[13,64,128]{2,1,0:T(8,128)(2,1)S(1)}, u32[]{:S(2)}, u32[]{:S(2)}) collective-permute-start(bf16[13,64,128]{2,1,0:T(8,128)(2,1)} %get-tuple-element.64), channel_id=1, source_target_pairs={{0,12},{4,16},{8,20},{12,24},{16,28},{20,0},{24,4},{28,8},{1,13},{... | collective-permute-start | bytes 638984 | tf_op jit(solution)/shard_map/ppermute | solution.py:842
  34.4 2.4 %collective-permute-start.7 = (bf16[13,64,128]{2,1,0:T(8,128)(2,1)}, bf16[13,64,128]{2,1,0:T(8,128)(2,1)S(1)}, u32[]{:S(2)}, u32[]{:S(2)}) collective-permute-start(bf16[13,64,128]{2,1,0:T(8,128)(2,1)} %get-tuple-element.66), channel_id=1, source_target_pairs={{0,20},{4,24},{8,28},{12,0},{16,4},{20,8},{24,12},{28,16},{1,21},{... | collective-permute-start | bytes 638984 | tf_op jit(solution)/shard_map/ppermute | solution.py:842
  38.2 23.4 %collective-permute-done.3.refs_1_ = bf16[13,64,128]{2,1,0:T(8,128)(2,1)S(1)} collective-permute-done((bf16[13,64,128]{2,1,0:T(8,128)(2,1)}, bf16[13,64,128]{2,1,0:T(8,128)(2,1)S(1)}, u32[]{:S(2)}, u32[]{:S(2)}) %collective-permute-start.3) | collective-permute-done | bytes 213024 | tf_op jit(solution)/shard_map/ppermute | solution.py:842
  61.6 4.1 %collective-permute-start.9 = (bf16[13,64,128]{2,1,0:T(8,128)(2,1)}, bf16[13,64,128]{2,1,0:T(8,128)(2,1)S(1)}, u32[]{:S(2)}, u32[]{:S(2)}) collective-permute-start(bf16[13,64,128]{2,1,0:T(8,128)(2,1)} %get-tuple-element.68), channel_id=1, source_target_pairs={{0,28},{4,0},{8,4},{12,8},{16,12},{20,16},{24,20},{28,24},{1,29},{... | collective-permute-start | bytes 638984 | tf_op jit(solution)/shard_map/ppermute | solution.py:842
  66.9 3.4 %share.1 = (bf16[3,9984]{1,0:T(4,128)(2,1)}, f32[512,128]{1,0:T(8,128)}, bf16[3,16,1152]{2,1,0:T(8,128)(2,1)}, s32[8,128]{1,0:T(8,128)}) custom-call(s32[4]{0:T(128)} %pad_add_fusion.1.place_ref, bf16[8,16,1152]{2,1,0:T(8,128)(2,1)} %copy-done.2, bf16[512,4096]{1,0:T(8,128)(2,1)} %bitcast.31, bf16[512,4096]{1,0:T(8,128)(2,1)} %bitcast.32, ...), custom_call_target="tpu_custom_call" | custom-call | tf_op jit(solution)/shard_map/share/pallas_call | solution.py:717
  70.4 16.8 %collective-permute-done.5.refs_3_ = bf16[13,64,128]{2,1,0:T(8,128)(2,1)S(1)} collective-permute-done((bf16[13,64,128]{2,1,0:T(8,128)(2,1)}, bf16[13,64,128]{2,1,0:T(8,128)(2,1)S(1)}, u32[]{:S(2)}, u32[]{:S(2)}) %collective-permute-start.5) | collective-permute-done | bytes 213024 | tf_op jit(solution)/shard_map/ppermute | solution.py:842
  88.2 3.9 %reorder.1 = (bf16[8,12,64,128]{3,2,1,0:T(8,128)(2,1)}, bf16[64,128]{1,0:T(8,128)(2,1)}, bf16[64,128]{1,0:T(8,128)(2,1)}, bf16[64,128]{1,0:T(8,128)(2,1)}, bf16[...) custom-call(s32[1]{0:T(128)} %bitcast.own_ref, ...), custom_call_target="tpu_custom_call" | custom-call | tf_op jit(solution)/shard_map/reorder/pallas_call | solution.py:450
  92.1 15.5 %all-to-all-start.2 = ((bf16[8,12,64,128]{3,2,1,0:T(8,128)(2,1)}), bf16[8,12,64,128]{3,2,1,0:T(8,128)(2,1)S(1)}, u32[]{:S(2)}, u32[]{:S(2)}) async-start(bf16[8,12,64,128]{3,2,1,0:T(8,128)(2,1)} %get-tuple-element.86), calls=%async_computation.2 | async-start | bytes 3145728 | tf_op jit(solution)/shard_map/all_to_all | solution.py:833
  109.0 6.5 %all-gather.1.shared_ref = bf16[4,3,9984]{2,1,0:T(4,128)(2,1)} all-gather(bf16[1,3,9984]{2,1,0:T(4,128)(2,1)S(1)} %bitcast.48), channel_id=2, replica_groups=mesh['req'=8,'seq'=4] {'seq'}, dimensions={0}, use_global_device_ids=true | all-gather | bytes 299520 | tf_op jit(solution)/shard_map/all_gather | solution.py:909
  115.5 2.0 tails.1
  117.5 32.1 %block_parts.1 = (f32[512,4096]{1,0:T(8,128)}, bf16[4,128,1024]{2,1,0:T(8,128)(2,1)}, bf16[512,128]{1,0:T(8,128)(2,1)}, f32[512,128]{1,0:T(8,128)}) custom-call(s32[1]{0:T(128)} %bitcast.1.chain_ref, f32[8,4352]{1,0:T(8,128)} %get-tuple-element.57.tail_ref.state_tail_ref, bf16[512,4096]{1,0:T(8,128)(2,1)} %bitcast.34, bf16[512,4096]{1,0:T(8,128)(2,1)} %bitcast.35, ...), custom_call_target="tpu_custom_call" | custom-call | flops 6000000000 | bytes 20000000 | tf_op jit(solution)/shard_map/block_parts/pallas_call | solution.py:177
  153.5 4.1 %reorder_rest.1 = (bf16[128,128]{1,0:T(8,128)(2,1)}, bf16[128,128]{1,0:T(8,128)(2,1)}, bf16[128,128]{1,0:T(8,128)(2,1)}, bf16[128,128]{1,0:T(8,128)(2,1)}, bf16[...) custom-call(s32[1]{0:T(128)} %bitcast.own_ref, ...), custom_call_target="tpu_custom_call" | custom-call | tf_op jit(solution)/shard_map/reorder_rest/pallas_call | solution.py:490
  157.6 2.1 collective-permute-start.10
  161.2 2.3 %collective-permute-start.12 = (bf16[128,128]{1,0:T(8,128)(2,1)}, bf16[128,128]{1,0:T(8,128)(2,1)S(1)}, u32[]{:S(2)}, u32[]{:S(2)}) collective-permute-start(bf16[128,128]{1,0:T(8,128)(2,1)} %get-tuple-element.80), channel_id=1, source_target_pairs={{0,12},{4,16},{8,20},{12,24},{16,28},{20,0},{24,4},{28,8},{1,13},{... | collective-permute-start | bytes 98312 | tf_op jit(solution)/shard_map/ppermute | solution.py:842
  163.5 2.4 %collective-permute-done.1.refs_2_ = bf16[128,1024]{1,0:T(8,128)(2,1)S(1)} collective-permute-done((bf16[128,1024]{1,0:T(8,128)(2,1)S(1)}, bf16[128,1024]{1,0:T(8,128)(2,1)S(1)}, u32[]{:S(2)}, u32[]{:S(2)}) %collective-permute-start.1) | collective-permute-done | bytes 262176 | tf_op jit(solution)/shard_map/ppermute | solution.py:842
  165.9 2.9 %collective-permute-start.13 = (bf16[128,128]{1,0:T(8,128)(2,1)}, bf16[128,128]{1,0:T(8,128)(2,1)S(1)}, u32[]{:S(2)}, u32[]{:S(2)}) collective-permute-start(bf16[128,128]{1,0:T(8,128)(2,1)} %get-tuple-element.81), channel_id=1, source_target_pairs={{0,16},{4,20},{8,24},{12,28},{16,0},{20,4},{24,8},{28,12},{1,17},{... | collective-permute-start | bytes 98312 | tf_op jit(solution)/shard_map/ppermute | solution.py:842
  172.3 3.3 %collective-permute-start.19 = (bf16[12,64,128]{2,1,0:T(8,128)(2,1)}, bf16[12,64,128]{2,1,0:T(8,128)(2,1)S(1)}, u32[]{:S(2)}, u32[]{:S(2)}) collective-permute-start(bf16[12,64,128]{2,1,0:T(8,128)(2,1)} %get-tuple-element.90), channel_id=1, source_target_pairs={{0,12},{4,16},{8,20},{12,24},{16,28},{20,0},{24,4},{28,8},{1,13},{... | collective-permute-start | bytes 589832 | tf_op jit(solution)/shard_map/ppermute | solution.py:842
  175.6 2.4 %collective-permute-start.15 = (bf16[128,128]{1,0:T(8,128)(2,1)}, bf16[128,128]{1,0:T(8,128)(2,1)S(1)}, u32[]{:S(2)}, u32[]{:S(2)}) collective-permute-start(bf16[128,128]{1,0:T(8,128)(2,1)} %get-tuple-element.83), channel_id=1, source_target_pairs={{0,24},{4,28},{8,0},{12,4},{16,8},{20,12},{24,16},{28,20},{1,25},{... | collective-permute-start | bytes 98312 | tf_op jit(solution)/shard_map/ppermute | solution.py:842
  179.6 4.0 %collective-permute-done.15.refs_10_ = bf16[128,128]{1,0:T(8,128)(2,1)S(1)} collective-permute-done((bf16[128,128]{1,0:T(8,128)(2,1)}, bf16[128,128]{1,0:T(8,128)(2,1)S(1)}, u32[]{:S(2)}, u32[]{:S(2)}) %collective-permute-start.15) | collective-permute-done | bytes 32800 | tf_op jit(solution)/shard_map/ppermute | solution.py:842
  184.8 7.4 %collective-permute-start.21 = (bf16[12,64,128]{2,1,0:T(8,128)(2,1)}, bf16[12,64,128]{2,1,0:T(8,128)(2,1)S(1)}, u32[]{:S(2)}, u32[]{:S(2)}) collective-permute-start(bf16[12,64,128]{2,1,0:T(8,128)(2,1)} %get-tuple-element.92), channel_id=1, source_target_pairs={{0,20},{4,24},{8,28},{12,0},{16,4},{20,8},{24,12},{28,16},{1,21},{... | collective-permute-start | bytes 589832 | tf_op jit(solution)/shard_map/ppermute | solution.py:842
  192.9 3.2 %combine.1 = (bf16[128,1024]{1,0:T(8,128)(2,1)}, bf16[128,1024]{1,0:T(8,128)(2,1)}, bf16[128,1024]{1,0:T(8,128)(2,1)}, bf16[128,1024]{1,0:T(8,128)(2,1)}, f32[1024,128]{1,0:T(8,128)}) custom-call(s32[2]{0:T(128)} %pad_add_fusion.place_ref, f32[4,1024]{1,0:T(4,128)} %get-tuple-element.56.decay_ref, bf16[128,1024]{1,0:T(8,128)(2,1)} %get-tuple-element.107.refs_0_, ...), custom_call_target="tpu_custom_call" | custom-call | tf_op jit(solution)/shard_map/combine/pallas_call | solution.py:597
  198.2 3.3 %collective-permute-start.22 = (bf16[12,64,128]{2,1,0:T(8,128)(2,1)}, bf16[12,64,128]{2,1,0:T(8,128)(2,1)S(1)}, u32[]{:S(2)}, u32[]{:S(2)}) collective-permute-start(bf16[12,64,128]{2,1,0:T(8,128)(2,1)} %get-tuple-element.93), channel_id=1, source_target_pairs={{0,24},{4,28},{8,0},{12,4},{16,8},{20,12},{24,16},{28,20},{1,25},{... | collective-permute-start | bytes 589832 | tf_op jit(solution)/shard_map/ppermute | solution.py:842
  201.5 6.4 %collective-permute-start.23 = (bf16[12,64,128]{2,1,0:T(8,128)(2,1)}, bf16[12,64,128]{2,1,0:T(8,128)(2,1)}, u32[]{:S(2)}, u32[]{:S(2)}) collective-permute-start(bf16[12,64,128]{2,1,0:T(8,128)(2,1)} %get-tuple-element.94), channel_id=1, source_target_pairs={{0,28},{4,0},{8,4},{12,8},{16,12},{20,16},{24,20},{28,24},{1,29},{... | collective-permute-start | bytes 589832 | tf_op jit(solution)/shard_map/ppermute | solution.py:842
  209.6 4.1 %unpack.1.states_ref = f32[13,8,128,128]{3,2,1,0:T(8,128)} custom-call(f32[1024,128]{1,0:T(8,128)} %get-tuple-element.85.final_ref, bf16[8,12,64,128]{3,2,1,0:T(8,128)(2,1)} %copy-done.1), custom_call_target="tpu_custom_call" | custom-call | tf_op jit(solution)/shard_map/unpack/pallas_call | solution.py:514
  214.4 6.1 %unpack_rest.1 = f32[13,8,128,128]{3,2,1,0:T(8,128)} custom-call(s32[1]{0:T(128)} %bitcast.own_ref, f32[1024,128]{1,0:T(8,128)} %get-tuple-element.85.final_ref, f32[13,8,128,128]{3,2,1,0:T(8,128)} %unpack.1.states_ref, bf16[12,64,128]{2,1,0:T(8,128)(2,1)} %get-tuple-element.87.refs_0_, ...), custom_call_target="tpu_custom_call", output_to_operand_aliasing={{}: (2, {})} | custom-call | tf_op jit(solution)/shard_map/unpack_rest/pallas_call | solution.py:547
  221.3 11.7 %finish.1 = bf16[512,4096]{1,0:T(8,128)(2,1)} custom-call(s32[3]{0:T(128)} %pad_add_fusion.2.place_ref, f32[512,4096]{1,0:T(8,128)} %get-tuple-element.97.part_ref, bf16[512,4096]{1,0:T(8,128)(2,1)} %bitcast.39, bf16[512,128]{1,0:T(8,128)(2,1)} %get-tuple-element.98.read_ref, f32[512,128]{1,0:T(8,128)} %get-tuple-element.99.decay_ref, f32[1,4096]{1,0:T(1,128)} %bitcast.49, ...), custom_call_target="tpu_custom_call" | custom-call | flops 3000000000 | bytes 16000000 | tf_op jit(solution)/shard_map/finish/pallas_call | solution.py:283
  (119 shorter events, 26.9 us)
Async XLA Ops:
  2.5 16.9 %all-to-all-start = ((bf16[8,16,1152]{2,1,0:T(8,128)(2,1)}), bf16[8,16,1152]{2,1,0:T(8,128)(2,1)S(1)}, u32[]{:S(2)}, u32[]{:S(2)}) async-start(bf16[8,16,1152]{2,1,0:T(8,128)(2,1)} %mark.1), calls=%async_computation | async-start | bytes 589824 | tf_op jit(solution)/shard_map/all_to_all | solution.py:833
  19.4 72.7 %all-to-all-start.1 = ((bf16[8,13,64,128]{3,2,1,0:T(8,128)(2,1)}), bf16[8,13,64,128]{3,2,1,0:T(8,128)(2,1)S(1)}, u32[]{:S(2)}, u32[]{:S(2)}) async-start(bf16[8,13,64,128]{3,2,1,0:T(8,128)(2,1)} %pack_rest.1), calls=%async_computation.1 | async-start | bytes 3407872 | tf_op jit(solution)/shard_map/all_to_all | solution.py:833
  27.0 34.5 %collective-permute-start.3 = (bf16[13,64,128]{2,1,0:T(8,128)(2,1)}, bf16[13,64,128]{2,1,0:T(8,128)(2,1)S(1)}, u32[]{:S(2)}, u32[]{:S(2)}) collective-permute-start(bf16[13,64,128]{2,1,0:T(8,128)(2,1)} %get-tuple-element.62), channel_id=1, source_target_pairs={{0,4},{4,8},{8,12},{12,16},{16,20},{20,24},{24,28},{28,0},{1,5},{5... | collective-permute-start | bytes 638984 | tf_op jit(solution)/shard_map/ppermute | solution.py:842
  29.1 32.5 %collective-permute-start.4 = (bf16[13,64,128]{2,1,0:T(8,128)(2,1)}, bf16[13,64,128]{2,1,0:T(8,128)(2,1)S(1)}, u32[]{:S(2)}, u32[]{:S(2)}) collective-permute-start(bf16[13,64,128]{2,1,0:T(8,128)(2,1)} %get-tuple-element.63), channel_id=1, source_target_pairs={{0,8},{4,12},{8,16},{12,20},{16,24},{20,28},{24,0},{28,4},{1,9},{5... | collective-permute-start | bytes 638984 | tf_op jit(solution)/shard_map/ppermute | solution.py:842
  30.6 56.6 %collective-permute-start.5 = (bf16[13,64,128]{2,1,0:T(8,128)(2,1)}, bf16[13,64,128]{2,1,0:T(8,128)(2,1)S(1)}, u32[]{:S(2)}, u32[]{:S(2)}) collective-permute-start(bf16[13,64,128]{2,1,0:T(8,128)(2,1)} %get-tuple-element.64), channel_id=1, source_target_pairs={{0,12},{4,16},{8,20},{12,24},{16,28},{20,0},{24,4},{28,8},{1,13},{... | collective-permute-start | bytes 638984 | tf_op jit(solution)/shard_map/ppermute | solution.py:842
  32.9 54.3 %collective-permute-start.6 = (bf16[13,64,128]{2,1,0:T(8,128)(2,1)}, bf16[13,64,128]{2,1,0:T(8,128)(2,1)S(1)}, u32[]{:S(2)}, u32[]{:S(2)}) collective-permute-start(bf16[13,64,128]{2,1,0:T(8,128)(2,1)} %get-tuple-element.65), channel_id=1, source_target_pairs={{0,16},{4,20},{8,24},{12,28},{16,0},{20,4},{24,8},{28,12},{1,17},{... | collective-permute-start | bytes 638984 | tf_op jit(solution)/shard_map/ppermute | solution.py:842
  34.4 52.8 %collective-permute-start.7 = (bf16[13,64,128]{2,1,0:T(8,128)(2,1)}, bf16[13,64,128]{2,1,0:T(8,128)(2,1)S(1)}, u32[]{:S(2)}, u32[]{:S(2)}) collective-permute-start(bf16[13,64,128]{2,1,0:T(8,128)(2,1)} %get-tuple-element.66), channel_id=1, source_target_pairs={{0,20},{4,24},{8,28},{12,0},{16,4},{20,8},{24,12},{28,16},{1,21},{... | collective-permute-start | bytes 638984 | tf_op jit(solution)/shard_map/ppermute | solution.py:842
  61.6 25.6 %collective-permute-start.8 = (bf16[13,64,128]{2,1,0:T(8,128)(2,1)}, bf16[13,64,128]{2,1,0:T(8,128)(2,1)S(1)}, u32[]{:S(2)}, u32[]{:S(2)}) collective-permute-start(bf16[13,64,128]{2,1,0:T(8,128)(2,1)} %get-tuple-element.67), channel_id=1, source_target_pairs={{0,24},{4,28},{8,0},{12,4},{16,8},{20,12},{24,16},{28,20},{1,25},{... | collective-permute-start | bytes 638984 | tf_op jit(solution)/shard_map/ppermute | solution.py:842
  61.6 25.6 %collective-permute-start.9 = (bf16[13,64,128]{2,1,0:T(8,128)(2,1)}, bf16[13,64,128]{2,1,0:T(8,128)(2,1)S(1)}, u32[]{:S(2)}, u32[]{:S(2)}) collective-permute-start(bf16[13,64,128]{2,1,0:T(8,128)(2,1)} %get-tuple-element.68), channel_id=1, source_target_pairs={{0,28},{4,0},{8,4},{12,8},{16,12},{20,16},{24,20},{28,24},{1,29},{... | collective-permute-start | bytes 638984 | tf_op jit(solution)/shard_map/ppermute | solution.py:842
  70.4 38.6 %copy-start.22 = (bf16[3,9984]{1,0:T(4,128)(2,1)S(1)}, bf16[3,9984]{1,0:T(4,128)(2,1)}, u32[]{:S(2)}) copy-start(bf16[3,9984]{1,0:T(4,128)(2,1)} %get-tuple-element.54) | copy-start | bytes 179716
  92.1 57.5 %copy-start = (bf16[8,13,64,128]{3,2,1,0:T(8,128)(2,1)}, bf16[8,13,64,128]{3,2,1,0:T(8,128)(2,1)S(1)}, u32[]{:S(2)}) copy-start(bf16[8,13,64,128]{3,2,1,0:T(8,128)(2,1)S(1)} %all-to-all-done.1.in_ref) | copy-start | bytes 5111812
  92.1 116.4 %all-to-all-start.2 = ((bf16[8,12,64,128]{3,2,1,0:T(8,128)(2,1)}), bf16[8,12,64,128]{3,2,1,0:T(8,128)(2,1)S(1)}, u32[]{:S(2)}, u32[]{:S(2)}) async-start(bf16[8,12,64,128]{3,2,1,0:T(8,128)(2,1)} %get-tuple-element.86), calls=%async_computation.2 | async-start | bytes 3145728 | tf_op jit(solution)/shard_map/all_to_all | solution.py:833
  151.6 9.6 %collective-permute-start.2 = (bf16[128,1024]{1,0:T(8,128)(2,1)S(1)}, bf16[128,1024]{1,0:T(8,128)(2,1)S(1)}, u32[]{:S(2)}, u32[]{:S(2)}) collective-permute-start(bf16[128,1024]{1,0:T(8,128)(2,1)S(1)} %get-tuple-element.104), channel_id=1, source_target_pairs={{0,3},{1,0},{2,1},{3,2},{4,7},{5,4},{6,5},{7,6},{8,11},{9,8},{10,9... | collective-permute-start | bytes 786440 | tf_op jit(solution)/shard_map/ppermute | solution.py:842
  152.9 13.1 %collective-permute-start.1 = (bf16[128,1024]{1,0:T(8,128)(2,1)S(1)}, bf16[128,1024]{1,0:T(8,128)(2,1)S(1)}, u32[]{:S(2)}, u32[]{:S(2)}) collective-permute-start(bf16[128,1024]{1,0:T(8,128)(2,1)S(1)} %get-tuple-element.105), channel_id=1, source_target_pairs={{0,2},{1,3},{2,0},{3,1},{4,6},{5,7},{6,4},{7,5},{8,10},{9,11},{10,... | collective-permute-start | bytes 786440 | tf_op jit(solution)/shard_map/ppermute | solution.py:842
  153.5 15.3 %collective-permute-start = (bf16[128,1024]{1,0:T(8,128)(2,1)S(1)}, bf16[128,1024]{1,0:T(8,128)(2,1)S(1)}, u32[]{:S(2)}, u32[]{:S(2)}) collective-permute-start(bf16[128,1024]{1,0:T(8,128)(2,1)S(1)} %get-tuple-element.106), channel_id=1, source_target_pairs={{0,1},{1,2},{2,3},{3,0},{4,5},{5,6},{6,7},{7,4},{8,9},{9,10},{10,1... | collective-permute-start | bytes 786440 | tf_op jit(solution)/shard_map/ppermute | solution.py:842
  157.6 12.7 %collective-permute-start.10 = (bf16[128,128]{1,0:T(8,128)(2,1)}, bf16[128,128]{1,0:T(8,128)(2,1)S(1)}, u32[]{:S(2)}, u32[]{:S(2)}) collective-permute-start(bf16[128,128]{1,0:T(8,128)(2,1)} %get-tuple-element.78), channel_id=1, source_target_pairs={{0,4},{4,8},{8,12},{12,16},{16,20},{20,24},{24,28},{28,0},{1,5},{5... | collective-permute-start | bytes 98312 | tf_op jit(solution)/shard_map/ppermute | solution.py:842
  159.7 12.1 %collective-permute-start.11 = (bf16[128,128]{1,0:T(8,128)(2,1)}, bf16[128,128]{1,0:T(8,128)(2,1)S(1)}, u32[]{:S(2)}, u32[]{:S(2)}) collective-permute-start(bf16[128,128]{1,0:T(8,128)(2,1)} %get-tuple-element.79), channel_id=1, source_target_pairs={{0,8},{4,12},{8,16},{12,20},{16,24},{20,28},{24,0},{28,4},{1,9},{5... | collective-permute-start | bytes 98312 | tf_op jit(solution)/shard_map/ppermute | solution.py:842
  161.2 11.2 %collective-permute-start.12 = (bf16[128,128]{1,0:T(8,128)(2,1)}, bf16[128,128]{1,0:T(8,128)(2,1)S(1)}, u32[]{:S(2)}, u32[]{:S(2)}) collective-permute-start(bf16[128,128]{1,0:T(8,128)(2,1)} %get-tuple-element.80), channel_id=1, source_target_pairs={{0,12},{4,16},{8,20},{12,24},{16,28},{20,0},{24,4},{28,8},{1,13},{... | collective-permute-start | bytes 98312 | tf_op jit(solution)/shard_map/ppermute | solution.py:842
  165.9 9.7 %collective-permute-start.13 = (bf16[128,128]{1,0:T(8,128)(2,1)}, bf16[128,128]{1,0:T(8,128)(2,1)S(1)}, u32[]{:S(2)}, u32[]{:S(2)}) collective-permute-start(bf16[128,128]{1,0:T(8,128)(2,1)} %get-tuple-element.81), channel_id=1, source_target_pairs={{0,16},{4,20},{8,24},{12,28},{16,0},{20,4},{24,8},{28,12},{1,17},{... | collective-permute-start | bytes 98312 | tf_op jit(solution)/shard_map/ppermute | solution.py:842
  168.8 10.8 %collective-permute-start.14 = (bf16[128,128]{1,0:T(8,128)(2,1)}, bf16[128,128]{1,0:T(8,128)(2,1)S(1)}, u32[]{:S(2)}, u32[]{:S(2)}) collective-permute-start(bf16[128,128]{1,0:T(8,128)(2,1)} %get-tuple-element.82), channel_id=1, source_target_pairs={{0,20},{4,24},{8,28},{12,0},{16,4},{20,8},{24,12},{28,16},{1,21},{... | collective-permute-start | bytes 98312 | tf_op jit(solution)/shard_map/ppermute | solution.py:842
  170.3 25.8 %collective-permute-start.17 = (bf16[12,64,128]{2,1,0:T(8,128)(2,1)}, bf16[12,64,128]{2,1,0:T(8,128)(2,1)S(1)}, u32[]{:S(2)}, u32[]{:S(2)}) collective-permute-start(bf16[12,64,128]{2,1,0:T(8,128)(2,1)} %get-tuple-element.88), channel_id=1, source_target_pairs={{0,4},{4,8},{8,12},{12,16},{16,20},{20,24},{24,28},{28,0},{1,5},{5... | collective-permute-start | bytes 589832 | tf_op jit(solution)/shard_map/ppermute | solution.py:842
  171.8 24.4 %collective-permute-start.18 = (bf16[12,64,128]{2,1,0:T(8,128)(2,1)}, bf16[12,64,128]{2,1,0:T(8,128)(2,1)S(1)}, u32[]{:S(2)}, u32[]{:S(2)}) collective-permute-start(bf16[12,64,128]{2,1,0:T(8,128)(2,1)} %get-tuple-element.89), channel_id=1, source_target_pairs={{0,8},{4,12},{8,16},{12,20},{16,24},{20,28},{24,0},{28,4},{1,9},{5... | collective-permute-start | bytes 589832 | tf_op jit(solution)/shard_map/ppermute | solution.py:842
  172.3 24.5 %collective-permute-start.19 = (bf16[12,64,128]{2,1,0:T(8,128)(2,1)}, bf16[12,64,128]{2,1,0:T(8,128)(2,1)S(1)}, u32[]{:S(2)}, u32[]{:S(2)}) collective-permute-start(bf16[12,64,128]{2,1,0:T(8,128)(2,1)} %get-tuple-element.90), channel_id=1, source_target_pairs={{0,12},{4,16},{8,20},{12,24},{16,28},{20,0},{24,4},{28,8},{1,13},{... | collective-permute-start | bytes 589832 | tf_op jit(solution)/shard_map/ppermute | solution.py:842
  175.6 8.0 %collective-permute-start.15 = (bf16[128,128]{1,0:T(8,128)(2,1)}, bf16[128,128]{1,0:T(8,128)(2,1)S(1)}, u32[]{:S(2)}, u32[]{:S(2)}) collective-permute-start(bf16[128,128]{1,0:T(8,128)(2,1)} %get-tuple-element.83), channel_id=1, source_target_pairs={{0,24},{4,28},{8,0},{12,4},{16,8},{20,12},{24,16},{28,20},{1,25},{... | collective-permute-start | bytes 98312 | tf_op jit(solution)/shard_map/ppermute | solution.py:842
  179.6 4.6 %collective-permute-start.16 = (bf16[128,128]{1,0:T(8,128)(2,1)}, bf16[128,128]{1,0:T(8,128)(2,1)S(1)}, u32[]{:S(2)}, u32[]{:S(2)}) collective-permute-start(bf16[128,128]{1,0:T(8,128)(2,1)} %get-tuple-element.84), channel_id=1, source_target_pairs={{0,28},{4,0},{8,4},{12,8},{16,12},{20,16},{24,20},{28,24},{1,29},{... | collective-permute-start | bytes 98312 | tf_op jit(solution)/shard_map/ppermute | solution.py:842
  183.6 14.6 %collective-permute-start.20 = (bf16[12,64,128]{2,1,0:T(8,128)(2,1)}, bf16[12,64,128]{2,1,0:T(8,128)(2,1)S(1)}, u32[]{:S(2)}, u32[]{:S(2)}) collective-permute-start(bf16[12,64,128]{2,1,0:T(8,128)(2,1)} %get-tuple-element.91), channel_id=1, source_target_pairs={{0,16},{4,20},{8,24},{12,28},{16,0},{20,4},{24,8},{28,12},{1,17},{... | collective-permute-start | bytes 589832 | tf_op jit(solution)/shard_map/ppermute | solution.py:842
  184.8 16.6 %collective-permute-start.21 = (bf16[12,64,128]{2,1,0:T(8,128)(2,1)}, bf16[12,64,128]{2,1,0:T(8,128)(2,1)S(1)}, u32[]{:S(2)}, u32[]{:S(2)}) collective-permute-start(bf16[12,64,128]{2,1,0:T(8,128)(2,1)} %get-tuple-element.92), channel_id=1, source_target_pairs={{0,20},{4,24},{8,28},{12,0},{16,4},{20,8},{24,12},{28,16},{1,21},{... | collective-permute-start | bytes 589832 | tf_op jit(solution)/shard_map/ppermute | solution.py:842
  196.1 24.4 %collective-permute-start.24 = (bf16[128,1024]{1,0:T(8,128)(2,1)}, bf16[128,1024]{1,0:T(8,128)(2,1)S(1)}, u32[]{:S(2)}, u32[]{:S(2)}) collective-permute-start(bf16[128,1024]{1,0:T(8,128)(2,1)} %get-tuple-element.101), channel_id=1, source_target_pairs={{0,1},{1,2},{2,3},{3,0},{4,5},{5,6},{6,7},{7,4},{8,9},{9,10},{10,1... | collective-permute-start | bytes 786440 | tf_op jit(solution)/shard_map/ppermute | solution.py:842
  196.2 24.3 %collective-permute-start.25 = (bf16[128,1024]{1,0:T(8,128)(2,1)}, bf16[128,1024]{1,0:T(8,128)(2,1)S(1)}, u32[]{:S(2)}, u32[]{:S(2)}) collective-permute-start(bf16[128,1024]{1,0:T(8,128)(2,1)} %get-tuple-element.102), channel_id=1, source_target_pairs={{0,2},{1,3},{2,0},{3,1},{4,6},{5,7},{6,4},{7,5},{8,10},{9,11},{10,... | collective-permute-start | bytes 786440 | tf_op jit(solution)/shard_map/ppermute | solution.py:842
  196.8 23.6 %collective-permute-start.26 = (bf16[128,1024]{1,0:T(8,128)(2,1)}, bf16[128,1024]{1,0:T(8,128)(2,1)S(1)}, u32[]{:S(2)}, u32[]{:S(2)}) collective-permute-start(bf16[128,1024]{1,0:T(8,128)(2,1)} %get-tuple-element.103), channel_id=1, source_target_pairs={{0,3},{1,0},{2,1},{3,2},{4,7},{5,4},{6,5},{7,6},{8,11},{9,8},{10,9... | collective-permute-start | bytes 786440 | tf_op jit(solution)/shard_map/ppermute | solution.py:842
  198.2 15.5 %collective-permute-start.22 = (bf16[12,64,128]{2,1,0:T(8,128)(2,1)}, bf16[12,64,128]{2,1,0:T(8,128)(2,1)S(1)}, u32[]{:S(2)}, u32[]{:S(2)}) collective-permute-start(bf16[12,64,128]{2,1,0:T(8,128)(2,1)} %get-tuple-element.93), channel_id=1, source_target_pairs={{0,24},{4,28},{8,0},{12,4},{16,8},{20,12},{24,16},{28,20},{1,25},{... | collective-permute-start | bytes 589832 | tf_op jit(solution)/shard_map/ppermute | solution.py:842
  201.5 12.2 %collective-permute-start.23 = (bf16[12,64,128]{2,1,0:T(8,128)(2,1)}, bf16[12,64,128]{2,1,0:T(8,128)(2,1)}, u32[]{:S(2)}, u32[]{:S(2)}) collective-permute-start(bf16[12,64,128]{2,1,0:T(8,128)(2,1)} %get-tuple-element.94), channel_id=1, source_target_pairs={{0,28},{4,0},{8,4},{12,8},{16,12},{20,16},{24,20},{28,24},{1,29},{... | collective-permute-start | bytes 589832 | tf_op jit(solution)/shard_map/ppermute | solution.py:842
  (32 other events, 405.2 us)

commit v6 on v4

--- a/solution.py
+++ b/solution.py
@@ -22,6 +22,7 @@
 SLOT_TILE = 4
 SLOT_PAD = 16
 PEER_TILE = 2
+PACK_TILE = 2
 EPSILON = 1e-05
 LOG2E = math.log2(math.e)
 F32 = jnp.float32
@@ -321,10 +322,10 @@
     peer_marks = jnp.zeros((1, LANES), F32)
     slot_marks = jnp.zeros((1, LANES), F32)
     for slot in range(slots):
-        peer, target = plan_ref[slot, 0], plan_ref[slot, 1]
+        peer, target = plan_ref[0, slot], plan_ref[1, slot]
         rank = jnp.int32(0)
         for earlier in range(slot):
-            rank = rank + (plan_ref[earlier, 0] == peer).astype(jnp.int32)
+            rank = rank + (plan_ref[0, earlier] == peer).astype(jnp.int32)
         keep = mask_ref[slot].astype(F32)
         for tap in range(taps):
             tag = jnp.full((1, total - width), (target + tap * SLOT_PAD).astype(F32))
@@ -359,58 +360,58 @@
     )(plan, mask, inner, outer)
 
 
-def pack_kernel(own_ref, mask_ref, state_ref, *out_refs):
+def pack_lead_kernel(own_ref, mask_ref, state_ref, out_ref):
     first_slot = pl.program_id(0) * SLOT_TILE
-    peers = state_ref.shape[1]
     for j in range(SLOT_TILE):
         keep = mask_ref[jnp.minimum(first_slot + j, mask_ref.shape[0] - 1)].astype(F32)
-        for hop in range(len(out_refs)):
+        out_ref[j] = (state_ref[j, 0] * keep).astype(BF16)
+
+
+def pack_lead(own, mask, states, hop):
+    slots, peers, piece, width = states.shape
+
+    def from_peer(t, own, mask):
+        return t, lax.rem(own[0] + hop, peers), 0, 0
+
+    return pl.pallas_call(
+        pack_lead_kernel,
+        grid_spec=pltpu.PrefetchScalarGridSpec(
+            num_scalar_prefetch=2,
+            grid=(pl.cdiv(slots, SLOT_TILE),),
+            in_specs=[pl.BlockSpec((SLOT_TILE, 1, piece, width), from_peer)],
+            out_specs=pl.BlockSpec((SLOT_TILE, piece, width), lambda t, own, mask: (t, 0, 0)),
+        ),
+        out_shape=jax.ShapeDtypeStruct((slots, piece, width), BF16),
+        compiler_params=pltpu.CompilerParams(dimension_semantics=("arbitrary",)),
+        name="pack_lead",
+    )(own, mask, states)
+
+
+def pack_kernel(hops, own_ref, mask_ref, state_ref, *out_refs):
+    first_slot = pl.program_id(0) * PACK_TILE
+    peers = state_ref.shape[1]
+    for j in range(PACK_TILE):
+        keep = mask_ref[jnp.minimum(first_slot + j, mask_ref.shape[0] - 1)].astype(F32)
+        for hop, out_ref in zip(hops, out_refs):
             peer = lax.rem(own_ref[0] + hop, peers)
-            out_refs[hop][j] = (state_ref[j, peer] * keep).astype(BF16)
-
-
-def pack(own, mask, states):
+            out_ref[j] = (state_ref[j, peer] * keep).astype(BF16)
+
+
+def pack(own, mask, states, hops):
     slots, peers, piece, width = states.shape
-    half = piece // 2
-    steps = pl.cdiv(slots, SLOT_TILE)
     return pl.pallas_call(
-        pack_kernel,
-        grid=(steps,),
+        functools.partial(pack_kernel, hops),
+        grid=(pl.cdiv(slots, PACK_TILE),),
         in_specs=[
             pl.BlockSpec(memory_space=pltpu.SMEM),
             pl.BlockSpec(memory_space=pltpu.SMEM),
-            pl.BlockSpec((SLOT_TILE, peers, half, width), lambda t: (t, 0, 0, 0)),
+            pl.BlockSpec((PACK_TILE, peers, piece, width), lambda t: (t, 0, 0, 0)),
         ],
-        out_specs=[pl.BlockSpec((SLOT_TILE, half, width), lambda t: (t, 0, 0))] * peers,
-        out_shape=[jax.ShapeDtypeStruct((slots, half, width), BF16)] * peers,
+        out_specs=[pl.BlockSpec((PACK_TILE, piece, width), lambda t: (t, 0, 0))] * len(hops),
+        out_shape=[jax.ShapeDtypeStruct((slots, piece, width), BF16)] * len(hops),
         compiler_params=pltpu.CompilerParams(dimension_semantics=("arbitrary",)),
         name="pack",
     )(own, mask, states)
-
-
-def pack_rest_kernel(mask_ref, state_ref, out_ref):
-    first_slot = pl.program_id(0) * SLOT_TILE
-    for j in range(SLOT_TILE):
-        keep = mask_ref[jnp.minimum(first_slot + j, mask_ref.shape[0] - 1)].astype(F32)
-        out_ref[:, j] = (state_ref[j] * keep).astype(BF16)
-
-
-def pack_rest(mask, states):
-    slots, peers, piece, width = states.shape
-    half = piece // 2
-    steps = pl.cdiv(slots, SLOT_TILE)
-    return pl.pallas_call(
-        pack_rest_kernel,
-        grid=(steps,),
-        in_specs=[
-            pl.BlockSpec(memory_space=pltpu.SMEM),
-            pl.BlockSpec((SLOT_TILE, peers, half, width), lambda t: (t, 0, 1, 0)),
-        ],
-        out_specs=pl.BlockSpec((peers, SLOT_TILE, half, width), lambda t: (0, t, 0, 0)),
-        out_shape=jax.ShapeDtypeStruct((peers, slots, half, width), BF16),
-        compiler_params=pltpu.CompilerParams(dimension_semantics=("arbitrary",)),
-        name="pack_rest",
-    )(mask, states)
 
 
 def source_of(table_ref, target):
@@ -419,104 +420,135 @@
     return peer, code - peer * SLOT_PAD
 
 
+def pick_first_kernel(own_ref, table_ref, *refs):
+    in_refs, out_ref, sem = refs[:-2], refs[-2], refs[-1]
+    peers = len(in_refs)
+    slots = in_refs[0].shape[0]
+    for target in range(peers):
+        peer, index = source_of(table_ref, target * slots)
+        source = lax.rem(own_ref[0] - peer + peers, peers)
+        for hop in range(peers):
+
+            @pl.when(source == hop)
+            def _():
+                pltpu.make_async_copy(
+                    in_refs[hop].at[index], out_ref.at[target], sem.at[target]
+                ).start()
+
+    for target in range(peers):
+        pltpu.make_async_copy(in_refs[0].at[0], out_ref.at[target], sem.at[target]).wait()
+
+
+def pick_first(own, table, pieces):
+    _, piece, width = pieces[0].shape
+    peers = len(pieces)
+    scalar = pl.BlockSpec(memory_space=pltpu.SMEM)
+    return pl.pallas_call(
+        pick_first_kernel,
+        in_specs=[scalar, scalar] + [pl.BlockSpec(memory_space=pl.ANY)] * peers,
+        out_specs=pl.BlockSpec(memory_space=pltpu.VMEM),
+        out_shape=jax.ShapeDtypeStruct((peers, piece, width), BF16),
+        scratch_shapes=[pltpu.SemaphoreType.DMA((peers,))],
+        name="pick_first",
+    )(own, table, *pieces)
+
+
+def gather_pieces(own_ref, refs, scr):
+    peers = len(refs)
+    for hop in range(peers):
+        scr[lax.rem(own_ref[0] - hop + peers, peers)] = refs[hop][...]
+
+
 def reorder_kernel(own_ref, table_ref, *refs):
-    peers = (len(refs) - 1) // 2
-    in_refs, out_refs, scr = refs[:peers], refs[peers:-1], refs[-1]
-    slots = in_refs[0].shape[0]
-    own = own_ref[0]
+    scr = refs[-1]
+    peers, slots = scr.shape[:2]
+    gather_pieces(own_ref, refs[:peers], scr)
     for hop in range(peers):
-        scr[hop] = in_refs[hop][...]
-    for hop in range(peers):
-        base = lax.rem(own + hop, peers) * slots
+        base = lax.rem(own_ref[0] + hop, peers) * slots
+        out_ref = refs[peers + hop]
 
         def move(slot, unused):
             peer, index = source_of(table_ref, base + slot)
-            out_refs[hop][slot] = scr[lax.rem(own - peer + peers, peers), index]
+            out_ref[slot - 1] = scr[peer, index]
             return unused
 
-        lax.fori_loop(0, slots, move, 0)
-
-
-def reorder(own, table, pieces):
-    slots, half, width = pieces[0].shape
-    count = len(pieces)
-    whole = pl.BlockSpec((slots, half, width), lambda t: (0, 0, 0))
+        lax.fori_loop(1, slots, move, 0)
+
+
+def reorder_rest_kernel(own_ref, table_ref, *refs):
+    out_ref, scr = refs[-2:]
+    peers, slots = scr.shape[:2]
+    gather_pieces(own_ref, refs[:peers], scr)
+    for target in range(peers):
+
+        def move(slot, unused):
+            peer, index = source_of(table_ref, target * slots + slot)
+            out_ref[target, slot - 1] = scr[peer, index]
+            return unused
+
+        lax.fori_loop(1, slots, move, 0)
+
+
+def reorder(own, table, pieces, part):
+    slots, piece, width = pieces[0].shape
+    half = piece // 2
+    peers = len(pieces)
     scalar = pl.BlockSpec(memory_space=pltpu.SMEM)
+    if part == 0:
+        one = (slots - 1, half, width)
+        out_specs = [pl.BlockSpec(one, lambda t: (0, 0, 0))] * peers
+        out_shape = [jax.ShapeDtypeStruct(one, BF16)] * peers
+    else:
+        all_rest = (peers, slots - 1, half, width)
+        out_specs = pl.BlockSpec(all_rest, lambda t: (0, 0, 0, 0))
+        out_shape = jax.ShapeDtypeStruct(all_rest, BF16)
     return pl.pallas_call(
-        reorder_kernel,
+        reorder_kernel if part == 0 else reorder_rest_kernel,
         grid=(1,),
-        in_specs=[scalar, scalar] + [whole] * count,
-        out_specs=[whole] * count,
-        out_shape=[jax.ShapeDtypeStruct((slots, half, width), BF16)] * count,
-        scratch_shapes=[pltpu.VMEM((count, slots, half, width), BF16)],
-        name="reorder",
+        in_specs=[scalar, scalar]
+        + [pl.BlockSpec((slots, half, width), lambda t: (0, part, 0))] * peers,
+        out_specs=out_specs,
+        out_shape=out_shape,
+        scratch_shapes=[pltpu.VMEM((peers, slots, half, width), BF16)],
+        name="reorder" if part == 0 else "reorder_rest",
     )(own, table, *pieces)
 
 
-def reorder_rest_kernel(own_ref, table_ref, in_ref, *out_refs):
-    rest_ref, first_refs = out_refs[0], out_refs[1:]
-    peers, slots = in_ref.shape[:2]
-    own = own_ref[0]
-    for hop in range(peers):
-        target = lax.rem(own + hop, peers)
-        peer, index = source_of(table_ref, target * slots)
-        first_refs[hop][...] = in_ref[peer, index]
-
-        def move(slot, unused):
-            peer, index = source_of(table_ref, hop * slots + slot)
-            rest_ref[hop, slot - 1] = in_ref[peer, index]
-            return unused
-
-        lax.fori_loop(1, slots, move, 0)
-
-
-def reorder_rest(own, table, pieces):
-    peers, slots, half, width = pieces.shape
-    scalar = pl.BlockSpec(memory_space=pltpu.SMEM)
-    outs = pl.pallas_call(
-        reorder_rest_kernel,
-        grid=(1,),
-        in_specs=[scalar, scalar, pl.BlockSpec(pieces.shape, lambda t: (0, 0, 0, 0))],
-        out_specs=[pl.BlockSpec((peers, slots - 1, half, width), lambda t: (0, 0, 0, 0))]
-        + [pl.BlockSpec((half, width), lambda t: (0, 0))] * peers,
-        out_shape=[jax.ShapeDtypeStruct((peers, slots - 1, half, width), BF16)]
-        + [jax.ShapeDtypeStruct((half, width), BF16)] * peers,
-        name="reorder_rest",
-    )(own, table, pieces)
-    return outs[0], outs[1:]
-
-
-def unpack_kernel(place_ref, final_ref, *refs):
-    pieces, out_ref = refs[:-1], refs[-1]
+def unpack_kernel(own_ref, final_ref, *refs):
+    piece_refs, out_ref = refs[:-1], refs[-1]
     step = pl.program_id(0)
-    peers, half = out_ref.shape[1:3]
-    for hop in range(peers):
-        peer = lax.rem(place_ref[0] - hop + peers, peers)
-        for j in range(SLOT_TILE):
-            out_ref[j, peer] = pieces[hop][j].astype(F32)
-
-    @pl.when(step == 0)
-    def _():
-        for p in range(peers):
-            out_ref[0, p] = final_ref[2 * p * half : (2 * p + 1) * half, :]
-
-
-def unpack(place, final, pieces):
+    half = out_ref.shape[2]
+    out_ref[0, 0] = final_ref[:half, :]
+    for hop in range(len(piece_refs)):
+
+        @pl.when(step == hop)
+        def _():
+            out_ref[1:, 0] = piece_refs[hop][...].astype(F32)
+
+
+def unpack(own, final, pieces):
+    others, half, width = pieces[0].shape
     peers = len(pieces)
-    slots, half, width = pieces[0].shape
+    slots, piece = others + 1, 2 * half
+
+    def from_peer(hop, own):
+        return lax.rem(own[0] - hop + peers, peers)
+
     return pl.pallas_call(
         unpack_kernel,
-        grid=(pl.cdiv(slots, SLOT_TILE),),
-        in_specs=[
-            pl.BlockSpec(memory_space=pltpu.SMEM),
-            pl.BlockSpec(final.shape, lambda t: (0, 0)),
-        ]
-        + [pl.BlockSpec((SLOT_TILE, half, width), lambda t: (t, 0, 0))] * peers,
-        out_specs=pl.BlockSpec((SLOT_TILE, peers, half, width), lambda t: (t, 0, 0, 0)),
-        out_shape=jax.ShapeDtypeStruct((slots, peers, 2 * half, width), F32),
+        grid_spec=pltpu.PrefetchScalarGridSpec(
+            num_scalar_prefetch=1,
+            grid=(peers,),
+            in_specs=[pl.BlockSpec((piece, width), lambda h, own: (from_peer(h, own), 0))]
+            + [pl.BlockSpec((others, half, width), lambda h, own: (0, 0, 0))] * peers,
+            out_specs=pl.BlockSpec(
+                (slots, 1, half, width), lambda h, own: (0, from_peer(h, own), 0, 0)
+            ),
+        ),
+        out_shape=jax.ShapeDtypeStruct((slots, peers, piece, width), F32),
         compiler_params=pltpu.CompilerParams(dimension_semantics=("arbitrary",)),
         name="unpack",
-    )(place, final, *pieces)
+    )(own, final, *pieces)
 
 
 def unpack_rest_kernel(final_ref, pieces_ref, states_ref, out_ref):
@@ -546,25 +578,15 @@
 
 
 def combine_kernel(place_ref, decay_ref, *refs):
-    peers, count = decay_ref.shape[1], decay_ref.shape[0]
     count = decay_ref.shape[0]
-    scr, end_scr, enter_scr = refs[-3:]
-    entering_refs = refs[-4 - count : -4]
-    final_ref = refs[-4]
-    inputs = refs[: -4 - count]
-    end_refs = inputs[:count]
-    peers = (len(inputs) - count) // 2
-    upper, lower = inputs[count : count + peers], inputs[count + peers :]
-    half = lower[0].shape[0]
-    chain = place_ref[1]
-    for hop in range(peers):
-        peer = lax.rem(place_ref[0] - hop + peers, peers)
-        at = pl.multiple_of(peer * 2 * half, 16)
-        scr[pl.ds(at, half), :] = upper[hop][0]
-        scr[pl.ds(at + half, half), :] = lower[hop][...]
+    end_scr, enter_scr = refs[-2:]
+    final_ref = refs[-3]
+    entering_refs = refs[-3 - count : -3]
+    end_refs, first_ref = refs[:count], refs[count]
+    chain = place_ref[0]
     for hop in range(count):
         end_scr[lax.rem(chain - hop + count, count)] = end_refs[hop][...]
-    state = scr[...].astype(F32).T
+    state = first_ref[...].astype(F32).T
     for k in range(count):
         enter_scr[k] = state.astype(BF16)
         state = state * decay_ref[k : k + 1, :] + end_scr[k].astype(F32)
@@ -573,10 +595,9 @@
     final_ref[...] = state.T
 
 
-def combine(place, decay, ends, upper, lower):
+def combine(place, decay, ends, first):
     count = len(ends)
     whole = pl.BlockSpec(memory_space=pltpu.VMEM)
-    half, width = lower[0].shape
     rows, columns = ends[0].shape
     outs = pl.pallas_call(
         combine_kernel,
@@ -586,19 +607,17 @@
             pl.BlockSpec(decay.shape, lambda t: (0, 0)),
         ]
         + [pl.BlockSpec((rows, columns), lambda t: (0, 0))] * count
-        + [pl.BlockSpec((1, half, width), lambda t: (0, 0, 0))] * len(upper)
-        + [pl.BlockSpec((half, width), lambda t: (0, 0))] * len(lower),
+        + [pl.BlockSpec(first.shape, lambda t: (0, 0))],
         out_specs=[pl.BlockSpec((rows, columns), lambda t: (0, 0))] * count
         + [pl.BlockSpec((columns, rows), lambda t: (0, 0))],
         out_shape=[jax.ShapeDtypeStruct((rows, columns), BF16)] * count
         + [jax.ShapeDtypeStruct((columns, rows), F32)],
         scratch_shapes=[
-            pltpu.VMEM((columns, rows), BF16),
             pltpu.VMEM((count, rows, columns), BF16),
             pltpu.VMEM((count, rows, columns), BF16),
         ],
         name="combine",
-    )(place, decay, *ends, *upper, *lower)
+    )(place, decay, *ends, first)
     return outs[:count], outs[count]
 
 
@@ -818,12 +837,20 @@
     return lax.all_to_all(value, axis, split_axis=0, concat_axis=0, tiled=True)
 
 
+def hop_order(count):
+    return sorted(range(1, count), key=lambda hop: abs(2 * hop - count))
+
+
+def send(value, axis, hop):
+    count = lax.axis_size(axis)
+    pairs = [(source, (source + hop) % count) for source in range(count)]
+    return lax.ppermute(value, axis, pairs)
+
+
 def rotate(values, axis):
-    count = lax.axis_size(axis)
-    got = [values[0]] + [None] * (count - 1)
-    for hop in sorted(range(1, count), key=lambda hop: abs(2 * hop - count)):
-        pairs = [(source, (source + hop) % count) for source in range(count)]
-        got[hop] = lax.ppermute(values[hop], axis, pairs)
+    got = list(values)
+    for hop in hop_order(len(got)):
+        got[hop] = send(values[hop], axis, hop)
     return got
 
 
@@ -857,17 +884,22 @@
     outer_local = state_window.shape[2]
 
     own = own_peer[None]
+    pool_pieces = pool_states.reshape(slots, peers, piece, STATE_DIM)
+    lead, *others = hop_order(peers)
+    spread = [None] * peers
+    lead_pieces = pack_lead(own, active_mask, pool_pieces, lead)
+    spread[lead] = send(lead_pieces, "req", lead)
     packed = mark(
-        move_plan,
+        move_plan.T,
         active_mask,
         inner_window.transpose(1, 0, 2),
         state_window.transpose(1, 0, 2),
         peers,
     )
     every = exchange(packed, "req")
-    pool_pieces = pool_states.reshape(slots, peers, piece, STATE_DIM)
-    spread_a = rotate(pack(own, active_mask, pool_pieces), "req")
-    spread_b = exchange(pack_rest(active_mask, pool_pieces), "req")
+    others = [0] + others
+    for hop, pieces in zip(others, pack(own, active_mask, pool_pieces, others)):
+        spread[hop] = pieces if hop == 0 else send(pieces, "req", hop)
 
     rows = inputs_inner[0]
     state_rows = inputs_state[0]
@@ -896,8 +928,6 @@
         chain, shared, moved, slots, channels, inner_local, outer_local, columns
     )
 
-    moved_a = rotate(reorder(own, table, spread_a), "req")
-
     part, local_end, read_rows, decay = block_parts(
         chain,
         tail,
@@ -912,16 +942,15 @@
     )
     own_ends = rotate(local_end, "seq")
 
-    rest, first = reorder_rest(own, table, spread_b)
-    first_b = rotate(first, "req")
-    rest_b = exchange(rest, "req")
-
-    place = jnp.stack([own_peer, chain_index])
-    entering, final = combine(place, own_decay, own_ends, moved_a, first_b)
+    first = exchange(pick_first(own, table, spread), "req")
+    moved_a = rotate(reorder(own, table, spread, 0), "req")
+    moved_b = exchange(reorder(own, table, spread, 1), "req")
+    entering, final = combine(
+        chain, own_decay, own_ends, first.reshape(columns, STATE_DIM)
+    )
     incoming = rotate(entering, "seq")
-    finish_place = jnp.stack([start, length, chain_index])
     mixer_out = finish(
-        finish_place,
+        jnp.stack([start, length, chain_index]),
         part,
         gate_rows[0],
         read_rows,
@@ -929,8 +958,8 @@
         norm_weight[None],
         incoming,
     )
-    states = unpack(place, final, moved_a)
-    new_states = unpack_rest(final, rest_b, states).reshape(pool_states.shape)
+    states = unpack(own, final, moved_a)
+    new_states = unpack_rest(final, moved_b, states).reshape(pool_states.shape)
 
     return (
         new_states,

time: 265 us -> 230 us (0.87)
  waiting for transfers between devices: 97.9 us -> 63.3 us
  Pallas kernels: 78.7 us -> 85 us
  starting transfers between devices: 66.4 us -> 63 us
    all_to_all x3, waiting for transfers between devices: 39.1 us -> 5.18 us  [exchange(): return lax.all_to_all(value, axis, split_axis=0, concat_axis=0, tiled=True)]
    ppermute x27 -> x20, starting transfers between devices: 51.9 us -> 38.9 us  [send(): return lax.ppermute(value, axis, pairs)]
    all_to_all x3, starting transfers between devices: 14.5 us -> 24.1 us  [exchange(): return lax.all_to_all(value, axis, split_axis=0, concat_axis=0, tiled=True)]
    pallas_call x5 -> x6, Pallas kernels: 20.5 us -> 26.8 us  [the longest x2 7.86 us: reorder(): pl.pallas_call(reorder_kernel if part == 0 else reorder_rest_kernel, grid...]
    unnamed x70 -> x53, local copies, waits for them, and re-layouts: 6.71 us -> 4.47 us
    ppermute x27 -> x20, waiting for transfers between devices: 58.8 us -> 58.1 us  [send(): return lax.ppermute(value, axis, pairs)]
  transfers between devices with their start and end apart: 30 -> 23, of which waited for: 11 -> 9; matrix products, arithmetic and copies ran while one was open for 2% -> 3% of each run, Pallas kernels for 26% -> 33%
where the time goes in v6:
time: 230 us; the launch traced here: 229 us
  Pallas kernels  85 us (37%)
  waiting for transfers between devices  63.3 us (28%)
  starting transfers between devices  63 us (27%)
  local copies, waits for them, and re-layouts  8.42 us (4%)
  blocking collectives  6.52 us (3%)
    ppermute x20, waiting for transfers between devices, send(): return lax.ppermute(value, axis, pairs)  58.1 us
    ppermute x20, starting transfers between devices, send(): return lax.ppermute(value, axis, pairs)  38.9 us
    pallas_call x1, Pallas kernels, block_parts(): pl.pallas_call(block_kernel, grid_spec=pltpu.PrefetchScalarGridSpec(num_s...  32 us
    all_to_all x3, starting transfers between devices, exchange(): return lax.all_to_all(value, axis, split_axis=0, concat_axis=0, tiled=True)  24.1 us
    pallas_call x1, Pallas kernels, finish(): pl.pallas_call(finish_kernel, grid=(length // TILE,), in_specs=[pl.BlockS...  11.7 us
    pallas_call x2, Pallas kernels, reorder(): pl.pallas_call(reorder_kernel if part == 0 else reorder_rest_kernel, grid...  7.86 us
    pallas_call x1, Pallas kernels, pack(): pl.pallas_call(functools.partial(pack_kernel, hops), grid=(pl.cdiv(slots,...  6.61 us
    all_gather x1, blocking collectives, device_body(): shared = lax.all_gather(payload, 'seq', axis=0)  6.52 us
  transfers between devices with their start and end apart: 23, of which 9 were waited for; matrix products, arithmetic and copies ran while one was open for 3% of the time, Pallas kernels for 33%

profile of v6, /device:TPU:0, one launch (start us, length us, event | category | flops | bytes accessed | tf_op | source)
XLA Modules:
  0.0 229.1 jit_solution(15366170223667349180)
XLA Ops:
  0.6 3.8 %pack_lead.1 = bf16[13,128,128]{2,1,0:T(8,128)(2,1)} custom-call(s32[1]{0:T(128)} %bitcast.18.own_ref, s32[13]{0:T(128)} %mask_ref.5, f32[13,8,128,128]{3,2,1,0:T(8,128)} %bitcast.37), custom_call_target="tpu_custom_call" | custom-call | tf_op jit(solution)/shard_map/pack_lead/pallas_call | solution.py:376
  4.5 4.1 %collective-permute-start.6 = (bf16[13,128,128]{2,1,0:T(8,128)(2,1)}, bf16[13,128,128]{2,1,0:T(8,128)(2,1)S(1)}, u32[]{:S(2)}, u32[]{:S(2)}) collective-permute-start(bf16[13,128,128]{2,1,0:T(8,128)(2,1)} %pack_lead.1), channel_id=1, source_target_pairs={{0,16},{4,20},{8,24},{12,28},{16,0},{20,4},{24,8},{28,12},{1,17},{... | collective-permute-start | bytes 1277960 | tf_op jit(solution)/shard_map/ppermute | solution.py:847
  8.5 6.6 %pack.1 = (bf16[13,128,128]{2,1,0:T(8,128)(2,1)}, bf16[13,128,128]{2,1,0:T(8,128)(2,1)}, bf16[13,128,128]{2,1,0:T(8,128)(2,1)}, bf16[13,128,128]{2,1,0:T(8,128)(...) custom-call(s32[1]{0:T(128)} %bitcast.18.own_ref, s32[13]{0:T(128)} %mask_ref.5, ...), custom_call_target="tpu_custom_call" | custom-call | tf_op jit(solution)/shard_map/pack/pallas_call | solution.py:402
  18.5 4.5 %all-to-all-start = ((bf16[8,16,1152]{2,1,0:T(8,128)(2,1)}), bf16[8,16,1152]{2,1,0:T(8,128)(2,1)S(1)}, u32[]{:S(2)}, u32[]{:S(2)}) async-start(bf16[8,16,1152]{2,1,0:T(8,128)(2,1)} %mark.1), calls=%async_computation | async-start | bytes 589824 | tf_op jit(solution)/shard_map/all_to_all | solution.py:837
  23.0 2.0 collective-permute-start.4
  25.1 2.4 %collective-permute-start.5 = (bf16[13,128,128]{2,1,0:T(8,128)(2,1)}, bf16[13,128,128]{2,1,0:T(8,128)(2,1)S(1)}, u32[]{:S(2)}, u32[]{:S(2)}) collective-permute-start(bf16[13,128,128]{2,1,0:T(8,128)(2,1)} %get-tuple-element.46), channel_id=1, source_target_pairs={{0,12},{4,16},{8,20},{12,24},{16,28},{20,0},{24,4},{28,8},{1,13},{... | collective-permute-start | bytes 1277960 | tf_op jit(solution)/shard_map/ppermute | solution.py:847
  30.3 27.2 %collective-permute-done.6.refs_4_ = bf16[13,128,128]{2,1,0:T(8,128)(2,1)S(1)} collective-permute-done((bf16[13,128,128]{2,1,0:T(8,128)(2,1)}, bf16[13,128,128]{2,1,0:T(8,128)(2,1)S(1)}, u32[]{:S(2)}, u32[]{:S(2)}) %collective-permute-start.6) | collective-permute-done | bytes 426016 | tf_op jit(solution)/shard_map/ppermute | solution.py:847
  57.5 4.0 %collective-permute-start.9 = (bf16[13,128,128]{2,1,0:T(8,128)(2,1)}, bf16[13,128,128]{2,1,0:T(8,128)(2,1)S(1)}, u32[]{:S(2)}, u32[]{:S(2)}) collective-permute-start(bf16[13,128,128]{2,1,0:T(8,128)(2,1)} %get-tuple-element.49), channel_id=1, source_target_pairs={{0,28},{4,0},{8,4},{12,8},{16,12},{20,16},{24,20},{28,24},{1,29},{... | collective-permute-start | bytes 1277960 | tf_op jit(solution)/shard_map/ppermute | solution.py:847
  63.5 3.4 %share.1 = (bf16[3,9984]{1,0:T(4,128)(2,1)}, f32[512,128]{1,0:T(8,128)}, bf16[3,16,1152]{2,1,0:T(8,128)(2,1)}, s32[8,128]{1,0:T(8,128)}) custom-call(s32[4]{0:T(128)} %pad_add_fusion.place_ref, bf16[8,16,1152]{2,1,0:T(8,128)(2,1)} %copy-done.8, bf16[512,4096]{1,0:T(8,128)(2,1)} %bitcast.32, bf16[512,4096]{1,0:T(8,128)(2,1)} %bitcast.33, ...), custom_call_target="tpu_custom_call" | custom-call | tf_op jit(solution)/shard_map/share/pallas_call | solution.py:721
  66.9 5.8 %collective-permute-done.5.refs_3_ = bf16[13,128,128]{2,1,0:T(8,128)(2,1)S(1)} collective-permute-done((bf16[13,128,128]{2,1,0:T(8,128)(2,1)}, bf16[13,128,128]{2,1,0:T(8,128)(2,1)S(1)}, u32[]{:S(2)}, u32[]{:S(2)}) %collective-permute-start.5) | collective-permute-done | bytes 426016 | tf_op jit(solution)/shard_map/ppermute | solution.py:847
  72.6 7.0 %collective-permute-done.8.refs_6_ = bf16[13,128,128]{2,1,0:T(8,128)(2,1)S(1)} collective-permute-done((bf16[13,128,128]{2,1,0:T(8,128)(2,1)}, bf16[13,128,128]{2,1,0:T(8,128)(2,1)S(1)}, u32[]{:S(2)}, u32[]{:S(2)}) %collective-permute-start.8) | collective-permute-done | bytes 426016 | tf_op jit(solution)/shard_map/ppermute | solution.py:847
  80.6 2.4 %pick_first.1 = bf16[8,128,128]{2,1,0:T(8,128)(2,1)} custom-call(s32[1]{0:T(128)} %bitcast.18.own_ref, s32[8,128]{1,0:T(8,128)} %get-tuple-element.42.table_ref, bf16[13,128,128]{2,1,0:T(8,128)(2,1)} %get-tuple-element.43.refs_0_, bf16[13,128,128]{2,1,0:T(8,128)(2,1)} %copy-done.2, bf16[13,128,128]{2,1,0:T(8,128)(2,1)} %copy-done.3, ...), custom_call_target="tpu_custom_call" | custom-call | tf_op jit(solution)/shard_map/pick_first/pallas_call | solution.py:446
  83.0 16.0 %all-to-all-start.1 = ((bf16[8,128,128]{2,1,0:T(8,128)(2,1)}), bf16[8,128,128]{2,1,0:T(8,128)(2,1)S(1)}, u32[]{:S(2)}, u32[]{:S(2)}) async-start(bf16[8,128,128]{2,1,0:T(8,128)(2,1)} %pick_first.1), calls=%async_computation.1 | async-start | bytes 524288 | tf_op jit(solution)/shard_map/all_to_all | solution.py:837
  99.1 3.9 %reorder_rest.1 = bf16[8,12,64,128]{3,2,1,0:T(8,128)(2,1)} custom-call(s32[1]{0:T(128)} %bitcast.18.own_ref, s32[8,128]{1,0:T(8,128)} %get-tuple-element.42.table_ref, bf16[13,128,128]{2,1,0:T(8,128)(2,1)} %get-tuple-element.43.refs_0_, bf16[13,128,128]{2,1,0:T(8,128)(2,1)} %copy-done.2, bf16[13,128,128]{2,1,0:T(8,128)(2,1)} %copy-done.3, ...), custom_call_target="tpu_custom_call" | custom-call | tf_op jit(solution)/shard_map/reorder_rest/pallas_call | solution.py:505
  103.0 5.2 %all-to-all-done.1 = bf16[8,128,128]{2,1,0:T(8,128)(2,1)S(1)} async-done(((bf16[8,128,128]{2,1,0:T(8,128)(2,1)}), bf16[8,128,128]{2,1,0:T(8,128)(2,1)S(1)}, u32[]{:S(2)}, u32[]{:S(2)}) %all-to-all-start.1) | async-done | bytes 262176 | tf_op jit(solution)/shard_map/all_to_all | solution.py:837
  108.2 3.6 %all-to-all-start.2 = ((bf16[8,12,64,128]{3,2,1,0:T(8,128)(2,1)}), bf16[8,12,64,128]{3,2,1,0:T(8,128)(2,1)S(1)}, u32[]{:S(2)}, u32[]{:S(2)}) async-start(bf16[8,12,64,128]{3,2,1,0:T(8,128)(2,1)} %reorder_rest.1), calls=%async_computation.2 | async-start | bytes 3145728 | tf_op jit(solution)/shard_map/all_to_all | solution.py:837
  113.2 6.5 %all-gather.1.shared_ref = bf16[4,3,9984]{2,1,0:T(4,128)(2,1)} all-gather(bf16[1,3,9984]{2,1,0:T(4,128)(2,1)S(1)} %bitcast.50), channel_id=2, replica_groups=mesh['req'=8,'seq'=4] {'seq'}, dimensions={0}, use_global_device_ids=true | all-gather | bytes 299520 | tf_op jit(solution)/shard_map/all_gather | solution.py:925
  119.7 2.0 tails.1
  121.7 32.0 %block_parts.1 = (f32[512,4096]{1,0:T(8,128)}, bf16[4,128,1024]{2,1,0:T(8,128)(2,1)}, bf16[512,128]{1,0:T(8,128)(2,1)}, f32[512,128]{1,0:T(8,128)}) custom-call(s32[1]{0:T(128)} %bitcast.chain_ref.place_ref, f32[8,4352]{1,0:T(8,128)} %get-tuple-element.39.tail_ref.state_tail_ref, bf16[512,4096]{1,0:T(8,128)(2,1)} %bitcast.35, bf16[512,4096]{1,0:T(8,128)(2,1)} %bitcast.36, ...), custom_call_target="tpu_custom_call" | custom-call | flops 6000000000 | bytes 20000000 | tf_op jit(solution)/shard_map/block_parts/pallas_call | solution.py:178
  157.7 4.0 %reorder.1 = (bf16[12,64,128]{2,1,0:T(8,128)(2,1)}, bf16[12,64,128]{2,1,0:T(8,128)(2,1)}, bf16[12,64,128]{2,1,0:T(8,128)(2,1)}, bf16[12,64,128]{2,1,0:T(8,128)(2...) custom-call(s32[1]{0:T(128)} %bitcast.18.own_ref, ...), custom_call_target="tpu_custom_call" | custom-call | tf_op jit(solution)/shard_map/reorder/pallas_call | solution.py:505
  161.7 2.0 collective-permute-start.10
  165.2 2.4 %collective-permute-start.12 = (bf16[12,64,128]{2,1,0:T(8,128)(2,1)}, bf16[12,64,128]{2,1,0:T(8,128)(2,1)S(1)}, u32[]{:S(2)}, u32[]{:S(2)}) collective-permute-start(bf16[12,64,128]{2,1,0:T(8,128)(2,1)} %get-tuple-element.54), channel_id=1, source_target_pairs={{0,12},{4,16},{8,20},{12,24},{16,28},{20,0},{24,4},{28,8},{1,13},{... | collective-permute-start | bytes 589832 | tf_op jit(solution)/shard_map/ppermute | solution.py:847
  167.5 2.5 %collective-permute-done.1.refs_2_ = bf16[128,1024]{1,0:T(8,128)(2,1)S(1)} collective-permute-done((bf16[128,1024]{1,0:T(8,128)(2,1)S(1)}, bf16[128,1024]{1,0:T(8,128)(2,1)S(1)}, u32[]{:S(2)}, u32[]{:S(2)}) %collective-permute-start.1) | collective-permute-done | bytes 262176 | tf_op jit(solution)/shard_map/ppermute | solution.py:847
  170.1 2.9 %collective-permute-start.13 = (bf16[12,64,128]{2,1,0:T(8,128)(2,1)}, bf16[12,64,128]{2,1,0:T(8,128)(2,1)S(1)}, u32[]{:S(2)}, u32[]{:S(2)}) collective-permute-start(bf16[12,64,128]{2,1,0:T(8,128)(2,1)} %get-tuple-element.55), channel_id=1, source_target_pairs={{0,16},{4,20},{8,24},{12,28},{16,0},{20,4},{24,8},{28,12},{1,17},{... | collective-permute-start | bytes 589832 | tf_op jit(solution)/shard_map/ppermute | solution.py:847
  174.4 3.1 %combine.1 = (bf16[128,1024]{1,0:T(8,128)(2,1)}, bf16[128,1024]{1,0:T(8,128)(2,1)}, bf16[128,1024]{1,0:T(8,128)(2,1)}, bf16[128,1024]{1,0:T(8,128)(2,1)}, f32[1024,128]{1,0:T(8,128)}) custom-call(s32[1]{0:T(128)} %bitcast.chain_ref.place_ref, f32[4,1024]{1,0:T(4,128)} %get-tuple-element.38.decay_ref, bf16[128,1024]{1,0:T(8,128)(2,1)} %get-tuple-element.71.refs_0_, ...), custom_call_target="tpu_custom_call" | custom-call | tf_op jit(solution)/shard_map/combine/pallas_call | solution.py:602
  179.1 10.1 %collective-permute-done.12.refs_3_ = bf16[12,64,128]{2,1,0:T(8,128)(2,1)S(1)} collective-permute-done((bf16[12,64,128]{2,1,0:T(8,128)(2,1)}, bf16[12,64,128]{2,1,0:T(8,128)(2,1)S(1)}, u32[]{:S(2)}, u32[]{:S(2)}) %collective-permute-start.12) | collective-permute-done | bytes 196640 | tf_op jit(solution)/shard_map/ppermute | solution.py:847
  190.4 5.7 %collective-permute-start.15 = (bf16[12,64,128]{2,1,0:T(8,128)(2,1)}, bf16[12,64,128]{2,1,0:T(8,128)(2,1)}, u32[]{:S(2)}, u32[]{:S(2)}) collective-permute-start(bf16[12,64,128]{2,1,0:T(8,128)(2,1)} %get-tuple-element.57), channel_id=1, source_target_pairs={{0,24},{4,28},{8,0},{12,4},{16,8},{20,12},{24,16},{28,20},{1,25},{... | collective-permute-start | bytes 589832 | tf_op jit(solution)/shard_map/ppermute | solution.py:847
  196.1 3.1 %collective-permute-start.16 = (bf16[12,64,128]{2,1,0:T(8,128)(2,1)}, bf16[12,64,128]{2,1,0:T(8,128)(2,1)}, u32[]{:S(2)}, u32[]{:S(2)}) collective-permute-start(bf16[12,64,128]{2,1,0:T(8,128)(2,1)} %get-tuple-element.58), channel_id=1, source_target_pairs={{0,28},{4,0},{8,4},{12,8},{16,12},{20,16},{24,20},{28,24},{1,29},{... | collective-permute-start | bytes 589832 | tf_op jit(solution)/shard_map/ppermute | solution.py:847
  201.0 4.1 %collective-permute-done.16.refs_7_ = bf16[12,64,128]{2,1,0:T(8,128)(2,1)} collective-permute-done((bf16[12,64,128]{2,1,0:T(8,128)(2,1)}, bf16[12,64,128]{2,1,0:T(8,128)(2,1)}, u32[]{:S(2)}, u32[]{:S(2)}) %collective-permute-start.16) | collective-permute-done | bytes 196640 | tf_op jit(solution)/shard_map/ppermute | solution.py:847
  205.2 6.1 %unpack.1.states_ref = f32[13,8,128,128]{3,2,1,0:T(8,128)} custom-call(s32[1]{0:T(128)} %bitcast.18.own_ref, f32[1024,128]{1,0:T(8,128)} %get-tuple-element.50.final_ref, bf16[12,64,128]{2,1,0:T(8,128)(2,1)} %get-tuple-element.51.refs_0_, bf16[12,64,128]{2,1,0:T(8,128)(2,1)} %copy-done.16, bf16[12,64,128]{2,1,0:T(8,128)(2,1)} %copy-done.17, ...), custom_call_target="tpu_custom_call" | custom-call | tf_op jit(solution)/shard_map/unpack/pallas_call | solution.py:537
  212.1 11.7 %finish.1 = bf16[512,4096]{1,0:T(8,128)(2,1)} custom-call(s32[3]{0:T(128)} %pad_add_fusion.1.place_ref, f32[512,4096]{1,0:T(8,128)} %get-tuple-element.61.part_ref, bf16[512,4096]{1,0:T(8,128)(2,1)} %bitcast.40, bf16[512,128]{1,0:T(8,128)(2,1)} %get-tuple-element.62.read_ref, f32[512,128]{1,0:T(8,128)} %get-tuple-element.63.decay_ref, f32[1,4096]{1,0:T(1,128)} %bitcast.51, ...), custom_call_target="tpu_custom_call" | custom-call | flops 3000000000 | bytes 16000000 | tf_op jit(solution)/shard_map/finish/pallas_call | solution.py:284
  225.0 4.1 %unpack_rest.1 = f32[13,8,128,128]{3,2,1,0:T(8,128)} custom-call(f32[1024,128]{1,0:T(8,128)} %get-tuple-element.50.final_ref, bf16[8,12,64,128]{3,2,1,0:T(8,128)(2,1)} %copy-done, f32[13,8,128,128]{3,2,1,0:T(8,128)} %unpack.1.states_ref), custom_call_target="tpu_custom_call", output_to_operand_aliasing={{}: (2, {})} | custom-call | tf_op jit(solution)/shard_map/unpack_rest/pallas_call | solution.py:564
  (89 shorter events, 23.4 us)
Async XLA Ops:
  4.5 25.1 %copy-start.22 = (bf16[1,512,64]{1,2,0:T(8,128)(2,1)S(1)}, bf16[1,512,64]{1,2,0:T(8,128)(2,1)}, u32[]{:S(2)}) copy-start(bf16[1,512,64]{1,2,0:T(8,128)(2,1)} %param.24) | copy-start | bytes 196612
  4.5 57.0 %copy-start.25 = (f32[64]{0:T(128)S(1)}, f32[64]{0:T(128)}, u32[]{:S(2)}) copy-start(f32[64]{0:T(128)} %param.29) | copy-start | bytes 772
  4.5 53.0 %collective-permute-start.6 = (bf16[13,128,128]{2,1,0:T(8,128)(2,1)}, bf16[13,128,128]{2,1,0:T(8,128)(2,1)S(1)}, u32[]{:S(2)}, u32[]{:S(2)}) collective-permute-start(bf16[13,128,128]{2,1,0:T(8,128)(2,1)} %pack_lead.1), channel_id=1, source_target_pairs={{0,16},{4,20},{8,24},{12,28},{16,0},{20,4},{24,8},{28,12},{1,17},{... | collective-permute-start | bytes 1277960 | tf_op jit(solution)/shard_map/ppermute | solution.py:847
  15.1 42.4 %collective-permute-start.3 = (bf16[13,128,128]{2,1,0:T(8,128)(2,1)}, bf16[13,128,128]{2,1,0:T(8,128)(2,1)S(1)}, u32[]{:S(2)}, u32[]{:S(2)}) collective-permute-start(bf16[13,128,128]{2,1,0:T(8,128)(2,1)} %get-tuple-element.44), channel_id=1, source_target_pairs={{0,4},{4,8},{8,12},{12,16},{16,20},{20,24},{24,28},{28,0},{1,5},{5... | collective-permute-start | bytes 1277960 | tf_op jit(solution)/shard_map/ppermute | solution.py:847
  18.5 44.2 %all-to-all-start = ((bf16[8,16,1152]{2,1,0:T(8,128)(2,1)}), bf16[8,16,1152]{2,1,0:T(8,128)(2,1)S(1)}, u32[]{:S(2)}, u32[]{:S(2)}) async-start(bf16[8,16,1152]{2,1,0:T(8,128)(2,1)} %mark.1), calls=%async_computation | async-start | bytes 589824 | tf_op jit(solution)/shard_map/all_to_all | solution.py:837
  23.0 43.8 %collective-permute-start.4 = (bf16[13,128,128]{2,1,0:T(8,128)(2,1)}, bf16[13,128,128]{2,1,0:T(8,128)(2,1)S(1)}, u32[]{:S(2)}, u32[]{:S(2)}) collective-permute-start(bf16[13,128,128]{2,1,0:T(8,128)(2,1)} %get-tuple-element.45), channel_id=1, source_target_pairs={{0,8},{4,12},{8,16},{12,20},{16,24},{20,28},{24,0},{28,4},{1,9},{5... | collective-permute-start | bytes 1277960 | tf_op jit(solution)/shard_map/ppermute | solution.py:847
  25.1 47.6 %collective-permute-start.5 = (bf16[13,128,128]{2,1,0:T(8,128)(2,1)}, bf16[13,128,128]{2,1,0:T(8,128)(2,1)S(1)}, u32[]{:S(2)}, u32[]{:S(2)}) collective-permute-start(bf16[13,128,128]{2,1,0:T(8,128)(2,1)} %get-tuple-element.46), channel_id=1, source_target_pairs={{0,12},{4,16},{8,20},{12,24},{16,28},{20,0},{24,4},{28,8},{1,13},{... | collective-permute-start | bytes 1277960 | tf_op jit(solution)/shard_map/ppermute | solution.py:847
  27.4 45.2 %collective-permute-start.7 = (bf16[13,128,128]{2,1,0:T(8,128)(2,1)}, bf16[13,128,128]{2,1,0:T(8,128)(2,1)S(1)}, u32[]{:S(2)}, u32[]{:S(2)}) collective-permute-start(bf16[13,128,128]{2,1,0:T(8,128)(2,1)} %get-tuple-element.47), channel_id=1, source_target_pairs={{0,20},{4,24},{8,28},{12,0},{16,4},{20,8},{24,12},{28,16},{1,21},{... | collective-permute-start | bytes 1277960 | tf_op jit(solution)/shard_map/ppermute | solution.py:847
  57.5 22.2 %collective-permute-start.8 = (bf16[13,128,128]{2,1,0:T(8,128)(2,1)}, bf16[13,128,128]{2,1,0:T(8,128)(2,1)S(1)}, u32[]{:S(2)}, u32[]{:S(2)}) collective-permute-start(bf16[13,128,128]{2,1,0:T(8,128)(2,1)} %get-tuple-element.48), channel_id=1, source_target_pairs={{0,24},{4,28},{8,0},{12,4},{16,8},{20,12},{24,16},{28,20},{1,25},{... | collective-permute-start | bytes 1277960 | tf_op jit(solution)/shard_map/ppermute | solution.py:847
  57.5 22.2 %collective-permute-start.9 = (bf16[13,128,128]{2,1,0:T(8,128)(2,1)}, bf16[13,128,128]{2,1,0:T(8,128)(2,1)S(1)}, u32[]{:S(2)}, u32[]{:S(2)}) collective-permute-start(bf16[13,128,128]{2,1,0:T(8,128)(2,1)} %get-tuple-element.49), channel_id=1, source_target_pairs={{0,28},{4,0},{8,4},{12,8},{16,12},{20,16},{24,20},{28,24},{1,29},{... | collective-permute-start | bytes 1277960 | tf_op jit(solution)/shard_map/ppermute | solution.py:847
  83.0 25.1 %all-to-all-start.1 = ((bf16[8,128,128]{2,1,0:T(8,128)(2,1)}), bf16[8,128,128]{2,1,0:T(8,128)(2,1)S(1)}, u32[]{:S(2)}, u32[]{:S(2)}) async-start(bf16[8,128,128]{2,1,0:T(8,128)(2,1)} %pick_first.1), calls=%async_computation.1 | async-start | bytes 524288 | tf_op jit(solution)/shard_map/all_to_all | solution.py:837
  99.1 13.3 %copy-start.24 = (f32[64]{0:T(128)S(1)}, f32[64]{0:T(128)}, u32[]{:S(2)}) copy-start(f32[64]{0:T(128)} %param.30) | copy-start | bytes 772
  99.1 14.1 %copy-start.21 = (bf16[3,9984]{1,0:T(4,128)(2,1)S(1)}, bf16[3,9984]{1,0:T(4,128)(2,1)}, u32[]{:S(2)}) copy-start(bf16[3,9984]{1,0:T(4,128)(2,1)} %get-tuple-element.36) | copy-start | bytes 179716
  108.2 45.6 %copy-start.9 = (bf16[8,128,128]{2,1,0:T(8,128)(2,1)}, bf16[8,128,128]{2,1,0:T(8,128)(2,1)S(1)}, u32[]{:S(2)}) copy-start(bf16[8,128,128]{2,1,0:T(8,128)(2,1)S(1)} %all-to-all-done.1) | copy-start | bytes 786436
  108.2 115.7 %all-to-all-start.2 = ((bf16[8,12,64,128]{3,2,1,0:T(8,128)(2,1)}), bf16[8,12,64,128]{3,2,1,0:T(8,128)(2,1)S(1)}, u32[]{:S(2)}, u32[]{:S(2)}) async-start(bf16[8,12,64,128]{3,2,1,0:T(8,128)(2,1)} %reorder_rest.1), calls=%async_computation.2 | async-start | bytes 3145728 | tf_op jit(solution)/shard_map/all_to_all | solution.py:837
  155.7 9.4 %collective-permute-start.2 = (bf16[128,1024]{1,0:T(8,128)(2,1)S(1)}, bf16[128,1024]{1,0:T(8,128)(2,1)S(1)}, u32[]{:S(2)}, u32[]{:S(2)}) collective-permute-start(bf16[128,1024]{1,0:T(8,128)(2,1)S(1)} %get-tuple-element.68), channel_id=1, source_target_pairs={{0,3},{1,0},{2,1},{3,2},{4,7},{5,4},{6,5},{7,6},{8,11},{9,8},{10,9... | collective-permute-start | bytes 786440 | tf_op jit(solution)/shard_map/ppermute | solution.py:847
  157.1 13.0 %collective-permute-start.1 = (bf16[128,1024]{1,0:T(8,128)(2,1)S(1)}, bf16[128,1024]{1,0:T(8,128)(2,1)S(1)}, u32[]{:S(2)}, u32[]{:S(2)}) collective-permute-start(bf16[128,1024]{1,0:T(8,128)(2,1)S(1)} %get-tuple-element.69), channel_id=1, source_target_pairs={{0,2},{1,3},{2,0},{3,1},{4,6},{5,7},{6,4},{7,5},{8,10},{9,11},{10,... | collective-permute-start | bytes 786440 | tf_op jit(solution)/shard_map/ppermute | solution.py:847
  157.7 15.3 %collective-permute-start = (bf16[128,1024]{1,0:T(8,128)(2,1)S(1)}, bf16[128,1024]{1,0:T(8,128)(2,1)S(1)}, u32[]{:S(2)}, u32[]{:S(2)}) collective-permute-start(bf16[128,1024]{1,0:T(8,128)(2,1)S(1)} %get-tuple-element.70), channel_id=1, source_target_pairs={{0,1},{1,2},{2,3},{3,0},{4,5},{5,6},{6,7},{7,4},{8,9},{9,10},{10,1... | collective-permute-start | bytes 786440 | tf_op jit(solution)/shard_map/ppermute | solution.py:847
  161.7 15.9 %collective-permute-start.10 = (bf16[12,64,128]{2,1,0:T(8,128)(2,1)}, bf16[12,64,128]{2,1,0:T(8,128)(2,1)S(1)}, u32[]{:S(2)}, u32[]{:S(2)}) collective-permute-start(bf16[12,64,128]{2,1,0:T(8,128)(2,1)} %get-tuple-element.52), channel_id=1, source_target_pairs={{0,4},{4,8},{8,12},{12,16},{16,20},{20,24},{24,28},{28,0},{1,5},{5... | collective-permute-start | bytes 589832 | tf_op jit(solution)/shard_map/ppermute | solution.py:847
  163.7 14.0 %collective-permute-start.11 = (bf16[12,64,128]{2,1,0:T(8,128)(2,1)}, bf16[12,64,128]{2,1,0:T(8,128)(2,1)S(1)}, u32[]{:S(2)}, u32[]{:S(2)}) collective-permute-start(bf16[12,64,128]{2,1,0:T(8,128)(2,1)} %get-tuple-element.53), channel_id=1, source_target_pairs={{0,8},{4,12},{8,16},{12,20},{16,24},{20,28},{24,0},{28,4},{1,9},{5... | collective-permute-start | bytes 589832 | tf_op jit(solution)/shard_map/ppermute | solution.py:847
  165.2 24.1 %collective-permute-start.12 = (bf16[12,64,128]{2,1,0:T(8,128)(2,1)}, bf16[12,64,128]{2,1,0:T(8,128)(2,1)S(1)}, u32[]{:S(2)}, u32[]{:S(2)}) collective-permute-start(bf16[12,64,128]{2,1,0:T(8,128)(2,1)} %get-tuple-element.54), channel_id=1, source_target_pairs={{0,12},{4,16},{8,20},{12,24},{16,28},{20,0},{24,4},{28,8},{1,13},{... | collective-permute-start | bytes 589832 | tf_op jit(solution)/shard_map/ppermute | solution.py:847
  170.1 20.3 %collective-permute-start.13 = (bf16[12,64,128]{2,1,0:T(8,128)(2,1)}, bf16[12,64,128]{2,1,0:T(8,128)(2,1)S(1)}, u32[]{:S(2)}, u32[]{:S(2)}) collective-permute-start(bf16[12,64,128]{2,1,0:T(8,128)(2,1)} %get-tuple-element.55), channel_id=1, source_target_pairs={{0,16},{4,20},{8,24},{12,28},{16,0},{20,4},{24,8},{28,12},{1,17},{... | collective-permute-start | bytes 589832 | tf_op jit(solution)/shard_map/ppermute | solution.py:847
  173.0 23.1 %collective-permute-start.14 = (bf16[12,64,128]{2,1,0:T(8,128)(2,1)}, bf16[12,64,128]{2,1,0:T(8,128)(2,1)S(1)}, u32[]{:S(2)}, u32[]{:S(2)}) collective-permute-start(bf16[12,64,128]{2,1,0:T(8,128)(2,1)} %get-tuple-element.56), channel_id=1, source_target_pairs={{0,20},{4,24},{8,28},{12,0},{16,4},{20,8},{24,12},{28,16},{1,21},{... | collective-permute-start | bytes 589832 | tf_op jit(solution)/shard_map/ppermute | solution.py:847
  177.6 27.6 %copy-start.16 = (bf16[12,64,128]{2,1,0:T(8,128)(2,1)}, bf16[12,64,128]{2,1,0:T(8,128)(2,1)S(1)}, u32[]{:S(2)}) copy-start(bf16[12,64,128]{2,1,0:T(8,128)(2,1)S(1)} %collective-permute-done.10.refs_1_) | copy-start | bytes 589828
  177.6 33.7 %collective-permute-start.17 = (bf16[128,1024]{1,0:T(8,128)(2,1)}, bf16[128,1024]{1,0:T(8,128)(2,1)S(1)}, u32[]{:S(2)}, u32[]{:S(2)}) collective-permute-start(bf16[128,1024]{1,0:T(8,128)(2,1)} %get-tuple-element.65), channel_id=1, source_target_pairs={{0,1},{1,2},{2,3},{3,0},{4,5},{5,6},{6,7},{7,4},{8,9},{9,10},{10,1... | collective-permute-start | bytes 786440 | tf_op jit(solution)/shard_map/ppermute | solution.py:847
  177.6 27.5 %copy-start.17 = (bf16[12,64,128]{2,1,0:T(8,128)(2,1)}, bf16[12,64,128]{2,1,0:T(8,128)(2,1)S(1)}, u32[]{:S(2)}) copy-start(bf16[12,64,128]{2,1,0:T(8,128)(2,1)S(1)} %collective-permute-done.11.refs_2_) | copy-start | bytes 589828
  177.6 33.6 %collective-permute-start.18 = (bf16[128,1024]{1,0:T(8,128)(2,1)}, bf16[128,1024]{1,0:T(8,128)(2,1)S(1)}, u32[]{:S(2)}, u32[]{:S(2)}) collective-permute-start(bf16[128,1024]{1,0:T(8,128)(2,1)} %get-tuple-element.66), channel_id=1, source_target_pairs={{0,2},{1,3},{2,0},{3,1},{4,6},{5,7},{6,4},{7,5},{8,10},{9,11},{10,... | collective-permute-start | bytes 786440 | tf_op jit(solution)/shard_map/ppermute | solution.py:847
  189.2 15.9 %copy-start.18 = (bf16[12,64,128]{2,1,0:T(8,128)(2,1)}, bf16[12,64,128]{2,1,0:T(8,128)(2,1)S(1)}, u32[]{:S(2)}) copy-start(bf16[12,64,128]{2,1,0:T(8,128)(2,1)S(1)} %collective-permute-done.12.refs_3_) | copy-start | bytes 589828
  189.3 22.0 %collective-permute-start.19 = (bf16[128,1024]{1,0:T(8,128)(2,1)}, bf16[128,1024]{1,0:T(8,128)(2,1)S(1)}, u32[]{:S(2)}, u32[]{:S(2)}) collective-permute-start(bf16[128,1024]{1,0:T(8,128)(2,1)} %get-tuple-element.67), channel_id=1, source_target_pairs={{0,3},{1,0},{2,1},{3,2},{4,7},{5,4},{6,5},{7,6},{8,11},{9,8},{10,9... | collective-permute-start | bytes 786440 | tf_op jit(solution)/shard_map/ppermute | solution.py:847
  190.4 14.7 %copy-start.19 = (bf16[12,64,128]{2,1,0:T(8,128)(2,1)}, bf16[12,64,128]{2,1,0:T(8,128)(2,1)S(1)}, u32[]{:S(2)}) copy-start(bf16[12,64,128]{2,1,0:T(8,128)(2,1)S(1)} %collective-permute-done.13.refs_4_) | copy-start | bytes 589828
  190.4 10.6 %collective-permute-start.15 = (bf16[12,64,128]{2,1,0:T(8,128)(2,1)}, bf16[12,64,128]{2,1,0:T(8,128)(2,1)}, u32[]{:S(2)}, u32[]{:S(2)}) collective-permute-start(bf16[12,64,128]{2,1,0:T(8,128)(2,1)} %get-tuple-element.57), channel_id=1, source_target_pairs={{0,24},{4,28},{8,0},{12,4},{16,8},{20,12},{24,16},{28,20},{1,25},{... | collective-permute-start | bytes 589832 | tf_op jit(solution)/shard_map/ppermute | solution.py:847
  196.1 9.0 %collective-permute-start.16 = (bf16[12,64,128]{2,1,0:T(8,128)(2,1)}, bf16[12,64,128]{2,1,0:T(8,128)(2,1)}, u32[]{:S(2)}, u32[]{:S(2)}) collective-permute-start(bf16[12,64,128]{2,1,0:T(8,128)(2,1)} %get-tuple-element.58), channel_id=1, source_target_pairs={{0,28},{4,0},{8,4},{12,8},{16,12},{20,16},{24,20},{28,24},{1,29},{... | collective-permute-start | bytes 589832 | tf_op jit(solution)/shard_map/ppermute | solution.py:847
  (17 other events, 88.5 us)

commit v7 on v6

--- a/solution.py
+++ b/solution.py
@@ -307,20 +307,82 @@
     )(place, part, gate, read, decay, norm_row, *states)
 
 
-def mark_kernel(plan_ref, mask_ref, inner_ref, outer_ref, out_ref, scr):
-    peers, padded, total = out_ref.shape
+def most_per_pair(slots, peers):
+    return (2 * slots + peers - 1) // peers
+
+
+def padded_windows(inner_ref, outer_ref, total):
     taps, slots = inner_ref.shape[:2]
     width = inner_ref.shape[2] + outer_ref.shape[2]
-    capacity = most_per_pair(slots, peers)
-    scr[:, :width] = jnp.zeros((peers * padded, width), F32)
-    scr[:, width:] = jnp.full((peers * padded, total - width), -1.0, F32)
     windows = []
     for tap in range(taps):
         both = [inner_ref[tap].astype(F32), outer_ref[tap].astype(F32)]
+        both.append(jnp.zeros((slots, total - width), F32))
         windows.append(jnp.concatenate(both, axis=1))
-    lane = lax.broadcasted_iota(jnp.int32, (1, LANES), 1)
+    return windows
+
+
+def mark_kernel(plan_ref, mask_ref, inner_ref, outer_ref, out_ref):
+    peers, packet, _ = out_ref.shape
+    taps, slots = inner_ref.shape[:2]
+    chunks = (packet - 2) // taps
+    fill = jnp.zeros((SLOT_PAD - slots, chunks * LANES), F32)
+    row = lax.broadcasted_iota(jnp.int32, (peers, LANES), 0)
+    lane = lax.broadcasted_iota(jnp.int32, (peers, LANES), 1)
+    pick = jnp.zeros((peers, LANES), F32)
     peer_marks = jnp.zeros((1, LANES), F32)
     slot_marks = jnp.zeros((1, LANES), F32)
+    for slot in range(slots):
+        peer, target = plan_ref[0, slot], plan_ref[1, slot]
+        here = (row == peer) & (lane == slot) & (target == 0)
+        pick = jnp.where(here, mask_ref[slot].astype(F32), pick)
+        peer_marks = jnp.where(lane[:1] == slot, peer.astype(F32), peer_marks)
+        slot_marks = jnp.where(lane[:1] == slot, target.astype(F32), slot_marks)
+    pick = pick[:, :SLOT_PAD].astype(BF16)
+    picked = []
+    for window in padded_windows(inner_ref, outer_ref, chunks * LANES):
+        window = jnp.concatenate([window, fill], axis=0).astype(BF16)
+        picked.append(dot(pick, window))
+    spare = packet - chunks * taps - 2
+    for peer in range(peers):
+        lines = []
+        for chunk in range(chunks):
+            span = slice(chunk * LANES, (chunk + 1) * LANES)
+            lines += [picked[tap][peer : peer + 1, span] for tap in range(taps)]
+        lines += [peer_marks, slot_marks]
+        if spare > 0:
+            lines.append(jnp.zeros((spare, LANES), F32))
+        out_ref[peer] = jnp.concatenate(lines, axis=0).astype(BF16)
+
+
+def mark(plan, mask, inner, outer, peers):
+    taps, _ = inner.shape[:2]
+    width = inner.shape[2] + outer.shape[2]
+    whole = pl.BlockSpec(memory_space=pltpu.VMEM)
+    scalar = pl.BlockSpec(memory_space=pltpu.SMEM)
+    packet = pl.cdiv(taps * pl.cdiv(width, LANES) + 2, 16) * 16
+    return pl.pallas_call(
+        mark_kernel,
+        in_specs=[scalar, scalar, whole, whole],
+        out_shape=jax.ShapeDtypeStruct((peers, packet, LANES), BF16),
+        name="mark",
+    )(plan, mask, inner, outer)
+
+
+def window_kernel(plan_ref, mask_ref, inner_ref, outer_ref, out_ref, scr):
+    peers = out_ref.shape[0]
+    taps, slots = inner_ref.shape[:2]
+    total = scr.shape[1]
+    chunks = total // LANES
+    padded = out_ref.shape[1] // chunks
+    capacity = most_per_pair(slots, peers)
+    at = total - LANES
+    scr[...] = jnp.zeros((peers * padded, total), F32)
+    windows = padded_windows(inner_ref, outer_ref, total)
+    last = lax.broadcasted_iota(jnp.int32, (1, total), 1) == total - 1
+    for line in range(peers * padded // 8):
+        lane = lax.broadcasted_iota(jnp.int32, (8, LANES), 1)
+        scr[line * 8 : line * 8 + 8, at:] = jnp.where(lane == LANES - 1, -1.0, 0.0)
     for slot in range(slots):
         peer, target = plan_ref[0, slot], plan_ref[1, slot]
         rank = jnp.int32(0)
@@ -328,36 +390,69 @@
             rank = rank + (plan_ref[0, earlier] == peer).astype(jnp.int32)
         keep = mask_ref[slot].astype(F32)
         for tap in range(taps):
-            tag = jnp.full((1, total - width), (target + tap * SLOT_PAD).astype(F32))
-            row = jnp.concatenate([windows[tap][slot : slot + 1] * keep, tag], axis=1)
-            scr[pl.ds(peer * padded + tap * capacity + rank, 1), :] = row
-        peer_marks = jnp.where(lane == slot, peer.astype(F32), peer_marks)
-        slot_marks = jnp.where(lane == slot, target.astype(F32), slot_marks)
+            tag = (target + tap * SLOT_PAD).astype(F32)
+            line = jnp.where(last, tag, windows[tap][slot : slot + 1] * keep)
+            scr[pl.ds(peer * padded + tap * capacity + rank, 1), :] = line
     for peer in range(peers):
-        at = peer * padded + taps * capacity
-        scr[at : at + 1, :LANES] = peer_marks
-        scr[at + 1 : at + 2, :LANES] = slot_marks
-        out_ref[peer] = scr[peer * padded : (peer + 1) * padded, :].astype(BF16)
-
-
-def most_per_pair(slots, peers):
-    return (2 * slots + peers - 1) // peers
-
-
-def mark(plan, mask, inner, outer, peers):
+        for chunk in range(chunks):
+            block = scr[peer * padded : (peer + 1) * padded, chunk * LANES : (chunk + 1) * LANES]
+            out_ref[peer, chunk * padded : (chunk + 1) * padded, :] = block.astype(BF16)
+
+
+def window_packets(plan, mask, inner, outer, peers):
     taps, slots = inner.shape[:2]
     width = inner.shape[2] + outer.shape[2]
     whole = pl.BlockSpec(memory_space=pltpu.VMEM)
     scalar = pl.BlockSpec(memory_space=pltpu.SMEM)
     total = width + LANES - width % LANES
-    padded = pl.cdiv(taps * most_per_pair(slots, peers) + 2, 16) * 16
-    return pl.pallas_call(
-        mark_kernel,
+    padded = pl.cdiv(taps * most_per_pair(slots, peers), 16) * 16
+    return pl.pallas_call(
+        window_kernel,
         in_specs=[scalar, scalar, whole, whole],
-        out_shape=jax.ShapeDtypeStruct((peers, padded, total), BF16),
+        out_shape=jax.ShapeDtypeStruct((peers, padded * (total // LANES), LANES), BF16),
         scratch_shapes=[pltpu.VMEM((peers * padded, total), F32)],
-        name="mark",
+        name="window_packets",
     )(plan, mask, inner, outer)
+
+
+def settle_kernel(got_ref, inner_own_ref, outer_own_ref, inner_ref, outer_ref):
+    peers, lines, _ = got_ref.shape
+    taps, slots, inner_local = inner_ref.shape
+    width = inner_local + outer_ref.shape[2]
+    chunks = width // LANES + 1
+    padded = pl.cdiv(taps * most_per_pair(slots, peers), 16) * 16
+    start = lines - chunks * padded
+    rows = peers * padded
+    parts = []
+    for chunk in range(chunks):
+        at = start + chunk * padded
+        part = got_ref[:, at : at + padded, :].astype(F32)
+        parts.append(part.reshape(rows, LANES))
+    tags = parts[-1][:, LANES - 1 :]
+    lane = lax.broadcasted_iota(jnp.int32, (rows, LANES), 1).astype(F32)
+    pick = (tags == lane).astype(BF16)
+    moved = dot(pick, jnp.concatenate(parts, axis=1).astype(BF16), ((0,), (0,)))
+    top = lax.broadcasted_iota(jnp.int32, (SLOT_PAD, 1), 0) == 0
+    for tap in range(taps):
+        block = moved[tap * SLOT_PAD : (tap + 1) * SLOT_PAD]
+        own = inner_own_ref[tap : tap + 1, :].astype(F32)
+        inner_ref[tap] = jnp.where(top, own, block[:, :inner_local]).astype(BF16)[:slots]
+        own = outer_own_ref[tap : tap + 1, :].astype(F32)
+        outer_ref[tap] = jnp.where(top, own, block[:, inner_local:width]).astype(BF16)[:slots]
+
+
+def settle(got, inner_own, outer_own, slots):
+    taps, inner_local = inner_own.shape
+    whole = pl.BlockSpec(memory_space=pltpu.VMEM)
+    return pl.pallas_call(
+        settle_kernel,
+        in_specs=[whole, whole, whole],
+        out_shape=[
+            jax.ShapeDtypeStruct((taps, slots, inner_local), BF16),
+            jax.ShapeDtypeStruct((taps, slots, outer_own.shape[1]), BF16),
+        ],
+        name="settle",
+    )(got, inner_own, outer_own)
 
 
 def pack_lead_kernel(own_ref, mask_ref, state_ref, out_ref):
@@ -420,10 +515,11 @@
     return peer, code - peer * SLOT_PAD
 
 
-def pick_first_kernel(own_ref, table_ref, *refs):
+def pick_first_kernel(own_ref, table_ref, packet_ref, *refs):
     in_refs, out_ref, sem = refs[:-2], refs[-2], refs[-1]
     peers = len(in_refs)
-    slots = in_refs[0].shape[0]
+    slots, piece, _ = in_refs[0].shape
+    own_piece = pl.ds(0, piece)
     for target in range(peers):
         peer, index = source_of(table_ref, target * slots)
         source = lax.rem(own_ref[0] - peer + peers, peers)
@@ -432,25 +528,30 @@
             @pl.when(source == hop)
             def _():
                 pltpu.make_async_copy(
-                    in_refs[hop].at[index], out_ref.at[target], sem.at[target]
+                    in_refs[hop].at[index], out_ref.at[target, own_piece], sem.at[target]
                 ).start()
 
     for target in range(peers):
-        pltpu.make_async_copy(in_refs[0].at[0], out_ref.at[target], sem.at[target]).wait()
-
-
-def pick_first(own, table, pieces):
+        out_ref[target, piece:, :] = packet_ref[target]
+    for target in range(peers):
+        pltpu.make_async_copy(
+            in_refs[0].at[0], out_ref.at[target, own_piece], sem.at[target]
+        ).wait()
+
+
+def pick_first(own, table, packets, pieces):
     _, piece, width = pieces[0].shape
     peers = len(pieces)
     scalar = pl.BlockSpec(memory_space=pltpu.SMEM)
     return pl.pallas_call(
         pick_first_kernel,
-        in_specs=[scalar, scalar] + [pl.BlockSpec(memory_space=pl.ANY)] * peers,
+        in_specs=[scalar, scalar, pl.BlockSpec(memory_space=pltpu.VMEM)]
+        + [pl.BlockSpec(memory_space=pl.ANY)] * peers,
         out_specs=pl.BlockSpec(memory_space=pltpu.VMEM),
-        out_shape=jax.ShapeDtypeStruct((peers, piece, width), BF16),
+        out_shape=jax.ShapeDtypeStruct((peers, piece + packets.shape[1], width), BF16),
         scratch_shapes=[pltpu.SemaphoreType.DMA((peers,))],
         name="pick_first",
-    )(own, table, *pieces)
+    )(own, table, packets, *pieces)
 
 
 def gather_pieces(own_ref, refs, scr):
@@ -586,7 +687,8 @@
     chain = place_ref[0]
     for hop in range(count):
         end_scr[lax.rem(chain - hop + count, count)] = end_refs[hop][...]
-    state = first_ref[...].astype(F32).T
+    peers, piece, width = first_ref.shape
+    state = first_ref[...].astype(F32).reshape(peers * piece, width).T
     for k in range(count):
         enter_scr[k] = state.astype(BF16)
         state = state * decay_ref[k : k + 1, :] + end_scr[k].astype(F32)
@@ -599,6 +701,7 @@
     count = len(ends)
     whole = pl.BlockSpec(memory_space=pltpu.VMEM)
     rows, columns = ends[0].shape
+    peers = first.shape[0]
     outs = pl.pallas_call(
         combine_kernel,
         grid=(1,),
@@ -607,7 +710,7 @@
             pl.BlockSpec(decay.shape, lambda t: (0, 0)),
         ]
         + [pl.BlockSpec((rows, columns), lambda t: (0, 0))] * count
-        + [pl.BlockSpec(first.shape, lambda t: (0, 0))],
+        + [pl.BlockSpec((peers, columns // peers, rows), lambda t: (0, 0, 0))],
         out_specs=[pl.BlockSpec((rows, columns), lambda t: (0, 0))] * count
         + [pl.BlockSpec((columns, rows), lambda t: (0, 0))],
         out_shape=[jax.ShapeDtypeStruct((rows, columns), BF16)] * count
@@ -636,30 +739,23 @@
     rate_ref,
     out_ref,
     step_ref,
-    moved_ref,
     table_ref,
 ):
     taps = out_ref.shape[0]
     inner = end_ref.shape[1]
     outer = state_end_ref.shape[1]
     channels = inner + outer
-    peers, packet, width = every_ref.shape
-    padded = moved_ref.shape[1]
+    peers, packet, _ = every_ref.shape
     slots = float(slot_count)
-    rows = peers * packet
-    everything = every_ref[...].astype(F32).reshape(rows, width)
-    tags = everything[:, width - 1 :]
-    lane = lax.broadcasted_iota(jnp.int32, (rows, LANES), 1).astype(F32)
-    pick = (tags == lane).astype(BF16)
-    moved = dot(pick, everything.astype(BF16), ((0,), (0,)))
-    firsts = []
-    for tap in range(taps):
-        moved_ref[tap] = moved[tap * padded : (tap + 1) * padded].astype(BF16)
-        firsts.append(moved[tap * padded : tap * padded + 1])
-    at = taps * most_per_pair(slot_count, peers)
-    peer_marks = [every_ref[p, at : at + 1, :LANES].astype(F32) for p in range(peers)]
-    slot_marks = [every_ref[p, at + 1 : at + 2, :LANES].astype(F32) for p in range(peers)]
-    target = jnp.concatenate(peer_marks, axis=0) * slots + jnp.concatenate(slot_marks, axis=0)
+    chunks = (packet - 2) // taps
+    width = chunks * LANES
+    everything = [every_ref[p].astype(F32) for p in range(peers)]
+    firsts = everything[0]
+    for part in everything[1:]:
+        firsts = firsts + part
+    at = chunks * taps
+    target = jnp.concatenate([part[at : at + 1] for part in everything], axis=0) * slots
+    target = target + jnp.concatenate([part[at + 1 : at + 2] for part in everything], axis=0)
     columns = table_ref.shape[1]
     lane = lax.broadcasted_iota(jnp.int32, (peers, columns), 1).astype(F32)
     code = lax.broadcasted_iota(jnp.int32, (peers, columns), 0).astype(F32) * SLOT_PAD
@@ -692,7 +788,10 @@
 
     out_ref[:, channels : channels + inner] = kept_rows(kept_ref, kept_next_ref)
     out_ref[:, channels + inner : 2 * channels] = kept_rows(state_kept_ref, state_next_ref)
-    out_ref[:, 2 * channels : 2 * channels + width] = jnp.concatenate(firsts, axis=0).astype(BF16)
+    for chunk in range(chunks):
+        at = 2 * channels + chunk * LANES
+        lines = firsts[chunk * taps : (chunk + 1) * taps]
+        out_ref[:, at : at + LANES] = lines.astype(BF16)
     count = step_ref.shape[0]
     heads = raw_ref.shape[1]
     positions = start + lax.broadcasted_iota(jnp.int32, (count, heads), 0)
@@ -710,8 +809,9 @@
 
 
 def share(place, slots, every, rows, state_rows, step_raw, step_bias, rate):
-    peers, _, width = every.shape
-    taps, padded = KERNEL - 1, SLOT_PAD
+    peers, packet, _ = every.shape
+    taps = KERNEL - 1
+    width = (packet - 2) // taps * LANES
     length, inner = rows.shape
     outer = state_rows.shape[1]
     heads = step_raw.shape[1]
@@ -738,14 +838,12 @@
             out_specs=[
                 pl.BlockSpec((taps, total), lambda t, c: (0, 0)),
                 pl.BlockSpec((length, LANES), lambda t, c: (0, 0)),
-                pl.BlockSpec((taps, padded, width), lambda t, c: (0, 0, 0)),
                 pl.BlockSpec((8, lanes), lambda t, c: (0, 0)),
             ],
         ),
         out_shape=[
             jax.ShapeDtypeStruct((taps, total), BF16),
             jax.ShapeDtypeStruct((length, LANES), F32),
-            jax.ShapeDtypeStruct((taps, padded, width), BF16),
             jax.ShapeDtypeStruct((8, lanes), jnp.int32),
         ],
         name="share",
@@ -765,12 +863,11 @@
 
 
 def tail_kernel(
-    chain_ref, shared_ref, moved_ref, tail_ref, inner_ref, outer_ref, decay_ref
+    chain_ref, shared_ref, tail_ref, inner_ref, outer_ref, decay_ref
 ):
     chain = chain_ref[0]
     count, taps = shared_ref.shape[:2]
-    slots, inner_local = inner_ref.shape[1:]
-    outer_local = outer_ref.shape[2]
+    inner_local, outer_local = inner_ref.shape[1], outer_ref.shape[1]
     channels = tail_ref.shape[1]
     inner = count * inner_local
     at = 2 * channels
@@ -795,14 +892,8 @@
         inner_at, outer_at = s * inner_local, inner + s * outer_local
         own_inner = jnp.where(mine, kept[:, inner_at : inner_at + inner_local], own_inner)
         own_outer = jnp.where(mine, kept[:, outer_at : outer_at + outer_local], own_outer)
-    width = inner_local + outer_local
-    top = lax.broadcasted_iota(jnp.int32, (moved_ref.shape[1], 1), 0) == 0
-    for tap in range(taps):
-        moved = moved_ref[tap].astype(F32)
-        both = jnp.where(top, own_inner[tap : tap + 1], moved[:, :inner_local])
-        inner_ref[tap] = both.astype(BF16)[:slots]
-        both = jnp.where(top, own_outer[tap : tap + 1], moved[:, inner_local:width])
-        outer_ref[tap] = both.astype(BF16)[:slots]
+    inner_ref[...] = own_inner.astype(BF16)
+    outer_ref[...] = own_outer.astype(BF16)
     logs = []
     for s in range(count):
         parts = shared_ref[s, :, shared_ref.shape[2] - LANES :].astype(F32)
@@ -817,20 +908,20 @@
     decay_ref[...] = jnp.exp2(spread[:count])
 
 
-def tails(chain, shared, moved, slots, channels, inner_local, outer_local, columns):
+def tails(chain, shared, channels, inner_local, outer_local, columns):
     count, taps = shared.shape[:2]
     whole = pl.BlockSpec(memory_space=pltpu.VMEM)
     return pl.pallas_call(
         tail_kernel,
-        in_specs=[pl.BlockSpec(memory_space=pltpu.SMEM), whole, whole],
+        in_specs=[pl.BlockSpec(memory_space=pltpu.SMEM), whole],
         out_shape=[
             jax.ShapeDtypeStruct((8, channels), F32),
-            jax.ShapeDtypeStruct((taps, slots, inner_local), BF16),
-            jax.ShapeDtypeStruct((taps, slots, outer_local), BF16),
+            jax.ShapeDtypeStruct((taps, inner_local), BF16),
+            jax.ShapeDtypeStruct((taps, outer_local), BF16),
             jax.ShapeDtypeStruct((count, columns), F32),
         ],
         name="tails",
-    )(chain, shared, moved)
+    )(chain, shared)
 
 
 def exchange(value, axis):
@@ -889,13 +980,10 @@
     spread = [None] * peers
     lead_pieces = pack_lead(own, active_mask, pool_pieces, lead)
     spread[lead] = send(lead_pieces, "req", lead)
-    packed = mark(
-        move_plan.T,
-        active_mask,
-        inner_window.transpose(1, 0, 2),
-        state_window.transpose(1, 0, 2),
-        peers,
-    )
+    plan = move_plan.T
+    inner_taps = inner_window.transpose(1, 0, 2)
+    outer_taps = state_window.transpose(1, 0, 2)
+    packed = mark(plan, active_mask, inner_taps, outer_taps, peers)
     every = exchange(packed, "req")
     others = [0] + others
     for hop, pieces in zip(others, pack(own, active_mask, pool_pieces, others)):
@@ -912,7 +1000,7 @@
     high_block = jnp.minimum(low_block + 1, last_tile)
     heads = decay_log.shape[0]
     rate = jnp.pad(-LOG2E * jnp.exp(decay_log), (0, LANES - heads))[None]
-    payload, step, moved, table = share(
+    payload, step, table = share(
         jnp.stack([low_block, high_block, start, length]),
         slots,
         every,
@@ -924,9 +1012,10 @@
     )
     shared = lax.all_gather(payload, "seq", axis=0)
     chain = chain_index[None]
-    tail, new_inner, new_outer, own_decay = tails(
-        chain, shared, moved, slots, channels, inner_local, outer_local, columns
+    tail, kept_inner, kept_outer, own_decay = tails(
+        chain, shared, channels, inner_local, outer_local, columns
     )
+    packets = window_packets(plan, active_mask, inner_taps, outer_taps, peers)
 
     part, local_end, read_rows, decay = block_parts(
         chain,
@@ -942,12 +1031,11 @@
     )
     own_ends = rotate(local_end, "seq")
 
-    first = exchange(pick_first(own, table, spread), "req")
+    first = exchange(pick_first(own, table, packets, spread), "req")
     moved_a = rotate(reorder(own, table, spread, 0), "req")
     moved_b = exchange(reorder(own, table, spread, 1), "req")
-    entering, final = combine(
-        chain, own_decay, own_ends, first.reshape(columns, STATE_DIM)
-    )
+    entering, final = combine(chain, own_decay, own_ends, first)
+    new_inner, new_outer = settle(first, kept_inner, kept_outer, slots)
     incoming = rotate(entering, "seq")
     mixer_out = finish(
         jnp.stack([start, length, chain_index]),

time: 230 us -> 231 us (level)
  Pallas kernels: 85 us -> 88.6 us
  starting transfers between devices: 63 us -> 60.5 us
    all_to_all x3, waiting for transfers between devices: 5.18 us -> 11.5 us  [exchange(): return lax.all_to_all(value, axis, split_axis=0, concat_axis=0, tiled=True)]
    ppermute x20, waiting for transfers between devices: 58.1 us -> 51.8 us  [send(): return lax.ppermute(value, axis, pairs)]
    pallas_call x1 -> x3, Pallas kernels: 2.39 us -> 6.63 us  [the longest x1 2.74 us: pick_first(): pl.pallas_call(pick_first_kernel, in_specs=[scalar, scalar, pl.BlockSpec(...]
  transfers between devices with their start and end apart: 23 -> 23, of which waited for: 9 -> 9; matrix products, arithmetic and copies ran while one was open for 3% -> 3% of each run, Pallas kernels for 33% -> 34%
where the time goes in v7:
time: 231 us; the launch traced here: 230 us
  Pallas kernels  88.6 us (38%)
  waiting for transfers between devices  63.3 us (27%)
  starting transfers between devices  60.5 us (26%)
  local copies, waits for them, and re-layouts  8.12 us (4%)
  blocking collectives  6.54 us (3%)
    ppermute x20, waiting for transfers between devices, send(): return lax.ppermute(value, axis, pairs)  51.8 us
    ppermute x20, starting transfers between devices, send(): return lax.ppermute(value, axis, pairs)  37.5 us
    pallas_call x1, Pallas kernels, block_parts(): pl.pallas_call(block_kernel, grid_spec=pltpu.PrefetchScalarGridSpec(num_s...  32 us
    all_to_all x3, starting transfers between devices, exchange(): return lax.all_to_all(value, axis, split_axis=0, concat_axis=0, tiled=True)  22.9 us
    pallas_call x1, Pallas kernels, finish(): pl.pallas_call(finish_kernel, grid=(length // TILE,), in_specs=[pl.BlockS...  11.7 us
    all_to_all x3, waiting for transfers between devices, exchange(): return lax.all_to_all(value, axis, split_axis=0, concat_axis=0, tiled=True)  11.5 us
    pallas_call x2, Pallas kernels, reorder(): pl.pallas_call(reorder_kernel if part == 0 else reorder_rest_kernel, grid...  7.82 us
    pallas_call x1, Pallas kernels, pack(): pl.pallas_call(functools.partial(pack_kernel, hops), grid=(pl.cdiv(slots,...  6.59 us
  transfers between devices with their start and end apart: 23, of which 9 were waited for; matrix products, arithmetic and copies ran while one was open for 3% of the time, Pallas kernels for 34%

profile of v7, /device:TPU:0, one launch (start us, length us, event | category | flops | bytes accessed | tf_op | source)
XLA Modules:
  0.0 229.8 jit_solution(14149971608390373272)
XLA Ops:
  0.6 3.8 %pack_lead.1 = bf16[13,128,128]{2,1,0:T(8,128)(2,1)} custom-call(s32[1]{0:T(128)} %bitcast.18.own_ref, s32[13]{0:T(128)} %mask_ref.7, f32[13,8,128,128]{3,2,1,0:T(8,128)} %bitcast.36), custom_call_target="tpu_custom_call" | custom-call | tf_op jit(solution)/shard_map/pack_lead/pallas_call | solution.py:471
  4.4 4.1 %collective-permute-start.6 = (bf16[13,128,128]{2,1,0:T(8,128)(2,1)}, bf16[13,128,128]{2,1,0:T(8,128)(2,1)S(1)}, u32[]{:S(2)}, u32[]{:S(2)}) collective-permute-start(bf16[13,128,128]{2,1,0:T(8,128)(2,1)} %pack_lead.1), channel_id=1, source_target_pairs={{0,16},{4,20},{8,24},{12,28},{16,0},{20,4},{24,8},{28,12},{1,17},{... | collective-permute-start | bytes 1277960 | tf_op jit(solution)/shard_map/ppermute | solution.py:938
  8.5 6.6 %pack.1 = (bf16[13,128,128]{2,1,0:T(8,128)(2,1)}, bf16[13,128,128]{2,1,0:T(8,128)(2,1)}, bf16[13,128,128]{2,1,0:T(8,128)(2,1)}, bf16[13,128,128]{2,1,0:T(8,128)(...) custom-call(s32[1]{0:T(128)} %bitcast.18.own_ref, s32[13]{0:T(128)} %mask_ref.7, ...), custom_call_target="tpu_custom_call" | custom-call | tf_op jit(solution)/shard_map/pack/pallas_call | solution.py:497
  18.4 4.5 %all-to-all-start = ((bf16[8,32,128]{2,1,0:T(8,128)(2,1)}), bf16[8,32,128]{2,1,0:T(8,128)(2,1)S(1)}, u32[]{:S(2)}, u32[]{:S(2)}) async-start(bf16[8,32,128]{2,1,0:T(8,128)(2,1)} %mark.1), calls=%async_computation | async-start | bytes 131072 | tf_op jit(solution)/shard_map/all_to_all | solution.py:928
  22.9 2.0 collective-permute-start.4
  24.9 2.4 %collective-permute-start.5 = (bf16[13,128,128]{2,1,0:T(8,128)(2,1)}, bf16[13,128,128]{2,1,0:T(8,128)(2,1)S(1)}, u32[]{:S(2)}, u32[]{:S(2)}) collective-permute-start(bf16[13,128,128]{2,1,0:T(8,128)(2,1)} %get-tuple-element.46), channel_id=1, source_target_pairs={{0,12},{4,16},{8,20},{12,24},{16,28},{20,0},{24,4},{28,8},{1,13},{... | collective-permute-start | bytes 1277960 | tf_op jit(solution)/shard_map/ppermute | solution.py:938
  28.7 27.6 %collective-permute-done.6.refs_4_ = bf16[13,128,128]{2,1,0:T(8,128)(2,1)S(1)} collective-permute-done((bf16[13,128,128]{2,1,0:T(8,128)(2,1)}, bf16[13,128,128]{2,1,0:T(8,128)(2,1)S(1)}, u32[]{:S(2)}, u32[]{:S(2)}) %collective-permute-start.6) | collective-permute-done | bytes 426016 | tf_op jit(solution)/shard_map/ppermute | solution.py:938
  56.4 2.6 %collective-permute-start.9 = (bf16[13,128,128]{2,1,0:T(8,128)(2,1)}, bf16[13,128,128]{2,1,0:T(8,128)(2,1)S(1)}, u32[]{:S(2)}, u32[]{:S(2)}) collective-permute-start(bf16[13,128,128]{2,1,0:T(8,128)(2,1)} %get-tuple-element.49), channel_id=1, source_target_pairs={{0,28},{4,0},{8,4},{12,8},{16,12},{20,16},{24,20},{28,24},{1,29},{... | collective-permute-start | bytes 1277960 | tf_op jit(solution)/shard_map/ppermute | solution.py:938
  64.1 3.1 %share.1 = (bf16[3,10112]{1,0:T(4,128)(2,1)}, f32[512,128]{1,0:T(8,128)}, s32[8,128]{1,0:T(8,128)}) custom-call(s32[4]{0:T(128)} %pad_add_fusion.place_ref, bf16[8,32,128]{2,1,0:T(8,128)(2,1)} %copy-done.12, bf16[512,4096]{1,0:T(8,128)(2,1)} %bitcast.31, bf16[512,4096]{1,0:T(8,128)(2,1)} %bitcast.32, bf16[512,4096]{1,0:T(8,128)(2,1)} %bitcast.33, ...), custom_call_target="tpu_custom_call" | custom-call | tf_op jit(solution)/shard_map/share/pallas_call | solution.py:821
  67.7 7.1 %collective-permute-done.8.refs_6_ = bf16[13,128,128]{2,1,0:T(8,128)(2,1)S(1)} collective-permute-done((bf16[13,128,128]{2,1,0:T(8,128)(2,1)}, bf16[13,128,128]{2,1,0:T(8,128)(2,1)S(1)}, u32[]{:S(2)}, u32[]{:S(2)}) %collective-permute-start.8) | collective-permute-done | bytes 426016 | tf_op jit(solution)/shard_map/ppermute | solution.py:938
  76.0 2.7 %pick_first.1 = bf16[8,272,128]{2,1,0:T(8,128)(2,1)} custom-call(s32[1]{0:T(128)} %bitcast.18.own_ref, s32[8,128]{1,0:T(8,128)} %get-tuple-element.42.table_ref, bf16[8,144,128]{2,1,0:T(8,128)(2,1)} %window_packets.1.packet_ref, bf16[13,128,128]{2,1,0:T(8,128)(2,1)} %get-tuple-element.43.refs_0_, bf16[13,128,128]{2,1,0:T(8,128)(2,1)} %copy-done.3, ...), custom_call_target="tpu_custom_call" | custom-call | tf_op jit(solution)/shard_map/pick_first/pallas_call | solution.py:546
  78.8 14.8 %all-to-all-start.1 = ((bf16[8,272,128]{2,1,0:T(8,128)(2,1)}), bf16[8,272,128]{2,1,0:T(8,128)(2,1)S(1)}, u32[]{:S(2)}, u32[]{:S(2)}) async-start(bf16[8,272,128]{2,1,0:T(8,128)(2,1)} %pick_first.1), calls=%async_computation.1 | async-start | bytes 1114112 | tf_op jit(solution)/shard_map/all_to_all | solution.py:928
  93.6 3.9 %reorder_rest.1 = bf16[8,12,64,128]{3,2,1,0:T(8,128)(2,1)} custom-call(s32[1]{0:T(128)} %bitcast.18.own_ref, s32[8,128]{1,0:T(8,128)} %get-tuple-element.42.table_ref, bf16[13,128,128]{2,1,0:T(8,128)(2,1)} %get-tuple-element.43.refs_0_, bf16[13,128,128]{2,1,0:T(8,128)(2,1)} %copy-done.3, bf16[13,128,128]{2,1,0:T(8,128)(2,1)} %copy-done.4, ...), custom_call_target="tpu_custom_call" | custom-call | tf_op jit(solution)/shard_map/reorder_rest/pallas_call | solution.py:606
  97.5 11.5 %all-to-all-done.1.refs_4_.got_ref = bf16[8,272,128]{2,1,0:T(8,128)(2,1)S(1)} async-done(((bf16[8,272,128]{2,1,0:T(8,128)(2,1)}), bf16[8,272,128]{2,1,0:T(8,128)(2,1)S(1)}, u32[]{:S(2)}, u32[]{:S(2)}) %all-to-all-start.1) | async-done | bytes 557088 | tf_op jit(solution)/shard_map/all_to_all | solution.py:928
  108.9 3.6 %all-to-all-start.2 = ((bf16[8,12,64,128]{3,2,1,0:T(8,128)(2,1)}), bf16[8,12,64,128]{3,2,1,0:T(8,128)(2,1)S(1)}, u32[]{:S(2)}, u32[]{:S(2)}) async-start(bf16[8,12,64,128]{3,2,1,0:T(8,128)(2,1)} %reorder_rest.1), calls=%async_computation.2 | async-start | bytes 3145728 | tf_op jit(solution)/shard_map/all_to_all | solution.py:928
  114.0 6.5 %all-gather.1.shared_ref = bf16[4,3,10112]{2,1,0:T(4,128)(2,1)} all-gather(bf16[1,3,10112]{2,1,0:T(4,128)(2,1)S(1)} %bitcast.49), channel_id=2, replica_groups=mesh['req'=8,'seq'=4] {'seq'}, dimensions={0}, use_global_device_ids=true | all-gather | bytes 303360 | tf_op jit(solution)/shard_map/all_gather | solution.py:1013
  120.5 2.0 tails.1
  122.5 32.0 %block_parts.1 = (f32[512,4096]{1,0:T(8,128)}, bf16[4,128,1024]{2,1,0:T(8,128)(2,1)}, bf16[512,128]{1,0:T(8,128)(2,1)}, f32[512,128]{1,0:T(8,128)}) custom-call(s32[1]{0:T(128)} %bitcast.chain_ref.place_ref, f32[8,4352]{1,0:T(8,128)} %get-tuple-element.39.tail_ref.state_tail_ref, bf16[512,4096]{1,0:T(8,128)(2,1)} %bitcast.34, bf16[512,4096]{1,0:T(8,128)(2,1)} %bitcast.35, ...), custom_call_target="tpu_custom_call" | custom-call | flops 6000000000 | bytes 20000000 | tf_op jit(solution)/shard_map/block_parts/pallas_call | solution.py:178
  158.5 3.9 %reorder.1 = (bf16[12,64,128]{2,1,0:T(8,128)(2,1)}, bf16[12,64,128]{2,1,0:T(8,128)(2,1)}, bf16[12,64,128]{2,1,0:T(8,128)(2,1)}, bf16[12,64,128]{2,1,0:T(8,128)(2...) custom-call(s32[1]{0:T(128)} %bitcast.18.own_ref, ...), custom_call_target="tpu_custom_call" | custom-call | tf_op jit(solution)/shard_map/reorder/pallas_call | solution.py:606
  162.4 2.0 collective-permute-start.10
  165.9 2.4 %collective-permute-start.12 = (bf16[12,64,128]{2,1,0:T(8,128)(2,1)}, bf16[12,64,128]{2,1,0:T(8,128)(2,1)S(1)}, u32[]{:S(2)}, u32[]{:S(2)}) collective-permute-start(bf16[12,64,128]{2,1,0:T(8,128)(2,1)} %get-tuple-element.54), channel_id=1, source_target_pairs={{0,12},{4,16},{8,20},{12,24},{16,28},{20,0},{24,4},{28,8},{1,13},{... | collective-permute-start | bytes 589832 | tf_op jit(solution)/shard_map/ppermute | solution.py:938
  168.3 2.6 %collective-permute-done.1.refs_2_ = bf16[128,1024]{1,0:T(8,128)(2,1)S(1)} collective-permute-done((bf16[128,1024]{1,0:T(8,128)(2,1)S(1)}, bf16[128,1024]{1,0:T(8,128)(2,1)S(1)}, u32[]{:S(2)}, u32[]{:S(2)}) %collective-permute-start.1) | collective-permute-done | bytes 262176 | tf_op jit(solution)/shard_map/ppermute | solution.py:938
  170.9 2.9 %collective-permute-start.13 = (bf16[12,64,128]{2,1,0:T(8,128)(2,1)}, bf16[12,64,128]{2,1,0:T(8,128)(2,1)S(1)}, u32[]{:S(2)}, u32[]{:S(2)}) collective-permute-start(bf16[12,64,128]{2,1,0:T(8,128)(2,1)} %get-tuple-element.55), channel_id=1, source_target_pairs={{0,16},{4,20},{8,24},{12,28},{16,0},{20,4},{24,8},{28,12},{1,17},{... | collective-permute-start | bytes 589832 | tf_op jit(solution)/shard_map/ppermute | solution.py:938
  175.3 3.1 %combine.1 = (bf16[128,1024]{1,0:T(8,128)(2,1)}, bf16[128,1024]{1,0:T(8,128)(2,1)}, bf16[128,1024]{1,0:T(8,128)(2,1)}, bf16[128,1024]{1,0:T(8,128)(2,1)}, f32[1024,128]{1,0:T(8,128)}) custom-call(s32[1]{0:T(128)} %bitcast.chain_ref.place_ref, f32[4,1024]{1,0:T(4,128)} %get-tuple-element.38.decay_ref, bf16[128,1024]{1,0:T(8,128)(2,1)} %get-tuple-element.73.refs_0_, ...), custom_call_target="tpu_custom_call" | custom-call | tf_op jit(solution)/shard_map/combine/pallas_call | solution.py:705
  179.9 10.1 %collective-permute-done.12.refs_3_ = bf16[12,64,128]{2,1,0:T(8,128)(2,1)S(1)} collective-permute-done((bf16[12,64,128]{2,1,0:T(8,128)(2,1)}, bf16[12,64,128]{2,1,0:T(8,128)(2,1)S(1)}, u32[]{:S(2)}, u32[]{:S(2)}) %collective-permute-start.12) | collective-permute-done | bytes 196640 | tf_op jit(solution)/shard_map/ppermute | solution.py:938
  191.2 5.7 %collective-permute-start.15 = (bf16[12,64,128]{2,1,0:T(8,128)(2,1)}, bf16[12,64,128]{2,1,0:T(8,128)(2,1)}, u32[]{:S(2)}, u32[]{:S(2)}) collective-permute-start(bf16[12,64,128]{2,1,0:T(8,128)(2,1)} %get-tuple-element.57), channel_id=1, source_target_pairs={{0,24},{4,28},{8,0},{12,4},{16,8},{20,12},{24,16},{28,20},{1,25},{... | collective-permute-start | bytes 589832 | tf_op jit(solution)/shard_map/ppermute | solution.py:938
  196.9 3.1 %collective-permute-start.16 = (bf16[12,64,128]{2,1,0:T(8,128)(2,1)}, bf16[12,64,128]{2,1,0:T(8,128)(2,1)}, u32[]{:S(2)}, u32[]{:S(2)}) collective-permute-start(bf16[12,64,128]{2,1,0:T(8,128)(2,1)} %get-tuple-element.58), channel_id=1, source_target_pairs={{0,28},{4,0},{8,4},{12,8},{16,12},{20,16},{24,20},{28,24},{1,29},{... | collective-permute-start | bytes 589832 | tf_op jit(solution)/shard_map/ppermute | solution.py:938
  200.6 2.0 settle.1
  202.6 3.3 %collective-permute-done.16.refs_7_ = bf16[12,64,128]{2,1,0:T(8,128)(2,1)} collective-permute-done((bf16[12,64,128]{2,1,0:T(8,128)(2,1)}, bf16[12,64,128]{2,1,0:T(8,128)(2,1)}, u32[]{:S(2)}, u32[]{:S(2)}) %collective-permute-start.16) | collective-permute-done | bytes 196640 | tf_op jit(solution)/shard_map/ppermute | solution.py:938
  205.9 6.1 %unpack.1.states_ref = f32[13,8,128,128]{3,2,1,0:T(8,128)} custom-call(s32[1]{0:T(128)} %bitcast.18.own_ref, f32[1024,128]{1,0:T(8,128)} %get-tuple-element.50.final_ref, bf16[12,64,128]{2,1,0:T(8,128)(2,1)} %get-tuple-element.51.refs_0_, bf16[12,64,128]{2,1,0:T(8,128)(2,1)} %copy-done.16, bf16[12,64,128]{2,1,0:T(8,128)(2,1)} %copy-done.17, ...), custom_call_target="tpu_custom_call" | custom-call | tf_op jit(solution)/shard_map/unpack/pallas_call | solution.py:638
  212.9 11.7 %finish.1 = bf16[512,4096]{1,0:T(8,128)(2,1)} custom-call(s32[3]{0:T(128)} %pad_add_fusion.1.place_ref, f32[512,4096]{1,0:T(8,128)} %get-tuple-element.63.part_ref, bf16[512,4096]{1,0:T(8,128)(2,1)} %bitcast.39, bf16[512,128]{1,0:T(8,128)(2,1)} %get-tuple-element.64.read_ref, f32[512,128]{1,0:T(8,128)} %get-tuple-element.65.decay_ref, f32[1,4096]{1,0:T(1,128)} %bitcast.52, ...), custom_call_target="tpu_custom_call" | custom-call | flops 3000000000 | bytes 16000000 | tf_op jit(solution)/shard_map/finish/pallas_call | solution.py:284
  225.8 4.1 %unpack_rest.1 = f32[13,8,128,128]{3,2,1,0:T(8,128)} custom-call(f32[1024,128]{1,0:T(8,128)} %get-tuple-element.50.final_ref, bf16[8,12,64,128]{3,2,1,0:T(8,128)(2,1)} %copy-done, f32[13,8,128,128]{3,2,1,0:T(8,128)} %unpack.1.states_ref), custom_call_target="tpu_custom_call", output_to_operand_aliasing={{}: (2, {})} | custom-call | tf_op jit(solution)/shard_map/unpack_rest/pallas_call | solution.py:665
  (91 shorter events, 24.5 us)
Async XLA Ops:
  4.4 54.6 %copy-start.25 = (f32[64]{0:T(128)S(1)}, f32[64]{0:T(128)}, u32[]{:S(2)}) copy-start(f32[64]{0:T(128)} %param.29) | copy-start | bytes 772
  4.4 57.6 %copy-start.22 = (bf16[1,512,64]{1,2,0:T(8,128)(2,1)S(1)}, bf16[1,512,64]{1,2,0:T(8,128)(2,1)}, u32[]{:S(2)}) copy-start(bf16[1,512,64]{1,2,0:T(8,128)(2,1)} %param.24) | copy-start | bytes 196612
  4.4 51.9 %collective-permute-start.6 = (bf16[13,128,128]{2,1,0:T(8,128)(2,1)}, bf16[13,128,128]{2,1,0:T(8,128)(2,1)S(1)}, u32[]{:S(2)}, u32[]{:S(2)}) collective-permute-start(bf16[13,128,128]{2,1,0:T(8,128)(2,1)} %pack_lead.1), channel_id=1, source_target_pairs={{0,16},{4,20},{8,24},{12,28},{16,0},{20,4},{24,8},{28,12},{1,17},{... | collective-permute-start | bytes 1277960 | tf_op jit(solution)/shard_map/ppermute | solution.py:938
  15.1 41.3 %collective-permute-start.3 = (bf16[13,128,128]{2,1,0:T(8,128)(2,1)}, bf16[13,128,128]{2,1,0:T(8,128)(2,1)S(1)}, u32[]{:S(2)}, u32[]{:S(2)}) collective-permute-start(bf16[13,128,128]{2,1,0:T(8,128)(2,1)} %get-tuple-element.44), channel_id=1, source_target_pairs={{0,4},{4,8},{8,12},{12,16},{16,20},{20,24},{24,28},{28,0},{1,5},{5... | collective-permute-start | bytes 1277960 | tf_op jit(solution)/shard_map/ppermute | solution.py:938
  18.4 45.1 %all-to-all-start = ((bf16[8,32,128]{2,1,0:T(8,128)(2,1)}), bf16[8,32,128]{2,1,0:T(8,128)(2,1)S(1)}, u32[]{:S(2)}, u32[]{:S(2)}) async-start(bf16[8,32,128]{2,1,0:T(8,128)(2,1)} %mark.1), calls=%async_computation | async-start | bytes 131072 | tf_op jit(solution)/shard_map/all_to_all | solution.py:928
  22.9 44.3 %collective-permute-start.4 = (bf16[13,128,128]{2,1,0:T(8,128)(2,1)}, bf16[13,128,128]{2,1,0:T(8,128)(2,1)S(1)}, u32[]{:S(2)}, u32[]{:S(2)}) collective-permute-start(bf16[13,128,128]{2,1,0:T(8,128)(2,1)} %get-tuple-element.45), channel_id=1, source_target_pairs={{0,8},{4,12},{8,16},{12,20},{16,24},{20,28},{24,0},{28,4},{1,9},{5... | collective-permute-start | bytes 1277960 | tf_op jit(solution)/shard_map/ppermute | solution.py:938
  24.9 42.8 %collective-permute-start.5 = (bf16[13,128,128]{2,1,0:T(8,128)(2,1)}, bf16[13,128,128]{2,1,0:T(8,128)(2,1)S(1)}, u32[]{:S(2)}, u32[]{:S(2)}) collective-permute-start(bf16[13,128,128]{2,1,0:T(8,128)(2,1)} %get-tuple-element.46), channel_id=1, source_target_pairs={{0,12},{4,16},{8,20},{12,24},{16,28},{20,0},{24,4},{28,8},{1,13},{... | collective-permute-start | bytes 1277960 | tf_op jit(solution)/shard_map/ppermute | solution.py:938
  27.3 40.5 %collective-permute-start.7 = (bf16[13,128,128]{2,1,0:T(8,128)(2,1)}, bf16[13,128,128]{2,1,0:T(8,128)(2,1)S(1)}, u32[]{:S(2)}, u32[]{:S(2)}) collective-permute-start(bf16[13,128,128]{2,1,0:T(8,128)(2,1)} %get-tuple-element.47), channel_id=1, source_target_pairs={{0,20},{4,24},{8,28},{12,0},{16,4},{20,8},{24,12},{28,16},{1,21},{... | collective-permute-start | bytes 1277960 | tf_op jit(solution)/shard_map/ppermute | solution.py:938
  56.4 18.5 %collective-permute-start.8 = (bf16[13,128,128]{2,1,0:T(8,128)(2,1)}, bf16[13,128,128]{2,1,0:T(8,128)(2,1)S(1)}, u32[]{:S(2)}, u32[]{:S(2)}) collective-permute-start(bf16[13,128,128]{2,1,0:T(8,128)(2,1)} %get-tuple-element.48), channel_id=1, source_target_pairs={{0,24},{4,28},{8,0},{12,4},{16,8},{20,12},{24,16},{28,20},{1,25},{... | collective-permute-start | bytes 1277960 | tf_op jit(solution)/shard_map/ppermute | solution.py:938
  56.4 18.9 %collective-permute-start.9 = (bf16[13,128,128]{2,1,0:T(8,128)(2,1)}, bf16[13,128,128]{2,1,0:T(8,128)(2,1)S(1)}, u32[]{:S(2)}, u32[]{:S(2)}) collective-permute-start(bf16[13,128,128]{2,1,0:T(8,128)(2,1)} %get-tuple-element.49), channel_id=1, source_target_pairs={{0,28},{4,0},{8,4},{12,8},{16,12},{20,16},{24,20},{28,24},{1,29},{... | collective-permute-start | bytes 1277960 | tf_op jit(solution)/shard_map/ppermute | solution.py:938
  78.8 30.2 %all-to-all-start.1 = ((bf16[8,272,128]{2,1,0:T(8,128)(2,1)}), bf16[8,272,128]{2,1,0:T(8,128)(2,1)S(1)}, u32[]{:S(2)}, u32[]{:S(2)}) async-start(bf16[8,272,128]{2,1,0:T(8,128)(2,1)} %pick_first.1), calls=%async_computation.1 | async-start | bytes 1114112 | tf_op jit(solution)/shard_map/all_to_all | solution.py:928
  93.6 19.0 %copy-start.23 = (f32[4352]{0:T(1024)S(1)}, f32[4352]{0:T(1024)}, u32[]{:S(2)}) copy-start(f32[4352]{0:T(1024)} %param.27) | copy-start | bytes 52228
  93.6 19.6 %copy-start.24 = (f32[64]{0:T(128)S(1)}, f32[64]{0:T(128)}, u32[]{:S(2)}) copy-start(f32[64]{0:T(128)} %param.30) | copy-start | bytes 772
  93.6 20.4 %copy-start.21 = (bf16[3,10112]{1,0:T(4,128)(2,1)S(1)}, bf16[3,10112]{1,0:T(4,128)(2,1)}, u32[]{:S(2)}) copy-start(bf16[3,10112]{1,0:T(4,128)(2,1)} %get-tuple-element.37) | copy-start | bytes 182020
  108.9 45.6 %copy-start.1 = (bf16[8,272,128]{2,1,0:T(8,128)(2,1)}, bf16[8,272,128]{2,1,0:T(8,128)(2,1)S(1)}, u32[]{:S(2)}) copy-start(bf16[8,272,128]{2,1,0:T(8,128)(2,1)S(1)} %all-to-all-done.1.refs_4_.got_ref) | copy-start | bytes 1671172
  108.9 115.7 %all-to-all-start.2 = ((bf16[8,12,64,128]{3,2,1,0:T(8,128)(2,1)}), bf16[8,12,64,128]{3,2,1,0:T(8,128)(2,1)S(1)}, u32[]{:S(2)}, u32[]{:S(2)}) async-start(bf16[8,12,64,128]{3,2,1,0:T(8,128)(2,1)} %reorder_rest.1), calls=%async_computation.2 | async-start | bytes 3145728 | tf_op jit(solution)/shard_map/all_to_all | solution.py:928
  156.5 9.4 %collective-permute-start.2 = (bf16[128,1024]{1,0:T(8,128)(2,1)S(1)}, bf16[128,1024]{1,0:T(8,128)(2,1)S(1)}, u32[]{:S(2)}, u32[]{:S(2)}) collective-permute-start(bf16[128,1024]{1,0:T(8,128)(2,1)S(1)} %get-tuple-element.70), channel_id=1, source_target_pairs={{0,3},{1,0},{2,1},{3,2},{4,7},{5,4},{6,5},{7,6},{8,11},{9,8},{10,9... | collective-permute-start | bytes 786440 | tf_op jit(solution)/shard_map/ppermute | solution.py:938
  157.8 13.0 %collective-permute-start.1 = (bf16[128,1024]{1,0:T(8,128)(2,1)S(1)}, bf16[128,1024]{1,0:T(8,128)(2,1)S(1)}, u32[]{:S(2)}, u32[]{:S(2)}) collective-permute-start(bf16[128,1024]{1,0:T(8,128)(2,1)S(1)} %get-tuple-element.71), channel_id=1, source_target_pairs={{0,2},{1,3},{2,0},{3,1},{4,6},{5,7},{6,4},{7,5},{8,10},{9,11},{10,... | collective-permute-start | bytes 786440 | tf_op jit(solution)/shard_map/ppermute | solution.py:938
  158.5 15.3 %collective-permute-start = (bf16[128,1024]{1,0:T(8,128)(2,1)S(1)}, bf16[128,1024]{1,0:T(8,128)(2,1)S(1)}, u32[]{:S(2)}, u32[]{:S(2)}) collective-permute-start(bf16[128,1024]{1,0:T(8,128)(2,1)S(1)} %get-tuple-element.72), channel_id=1, source_target_pairs={{0,1},{1,2},{2,3},{3,0},{4,5},{5,6},{6,7},{7,4},{8,9},{9,10},{10,1... | collective-permute-start | bytes 786440 | tf_op jit(solution)/shard_map/ppermute | solution.py:938
  162.4 15.9 %collective-permute-start.10 = (bf16[12,64,128]{2,1,0:T(8,128)(2,1)}, bf16[12,64,128]{2,1,0:T(8,128)(2,1)S(1)}, u32[]{:S(2)}, u32[]{:S(2)}) collective-permute-start(bf16[12,64,128]{2,1,0:T(8,128)(2,1)} %get-tuple-element.52), channel_id=1, source_target_pairs={{0,4},{4,8},{8,12},{12,16},{16,20},{20,24},{24,28},{28,0},{1,5},{5... | collective-permute-start | bytes 589832 | tf_op jit(solution)/shard_map/ppermute | solution.py:938
  164.4 14.0 %collective-permute-start.11 = (bf16[12,64,128]{2,1,0:T(8,128)(2,1)}, bf16[12,64,128]{2,1,0:T(8,128)(2,1)S(1)}, u32[]{:S(2)}, u32[]{:S(2)}) collective-permute-start(bf16[12,64,128]{2,1,0:T(8,128)(2,1)} %get-tuple-element.53), channel_id=1, source_target_pairs={{0,8},{4,12},{8,16},{12,20},{16,24},{20,28},{24,0},{28,4},{1,9},{5... | collective-permute-start | bytes 589832 | tf_op jit(solution)/shard_map/ppermute | solution.py:938
  165.9 24.1 %collective-permute-start.12 = (bf16[12,64,128]{2,1,0:T(8,128)(2,1)}, bf16[12,64,128]{2,1,0:T(8,128)(2,1)S(1)}, u32[]{:S(2)}, u32[]{:S(2)}) collective-permute-start(bf16[12,64,128]{2,1,0:T(8,128)(2,1)} %get-tuple-element.54), channel_id=1, source_target_pairs={{0,12},{4,16},{8,20},{12,24},{16,28},{20,0},{24,4},{28,8},{1,13},{... | collective-permute-start | bytes 589832 | tf_op jit(solution)/shard_map/ppermute | solution.py:938
  170.9 20.3 %collective-permute-start.13 = (bf16[12,64,128]{2,1,0:T(8,128)(2,1)}, bf16[12,64,128]{2,1,0:T(8,128)(2,1)S(1)}, u32[]{:S(2)}, u32[]{:S(2)}) collective-permute-start(bf16[12,64,128]{2,1,0:T(8,128)(2,1)} %get-tuple-element.55), channel_id=1, source_target_pairs={{0,16},{4,20},{8,24},{12,28},{16,0},{20,4},{24,8},{28,12},{1,17},{... | collective-permute-start | bytes 589832 | tf_op jit(solution)/shard_map/ppermute | solution.py:938
  173.8 23.1 %collective-permute-start.14 = (bf16[12,64,128]{2,1,0:T(8,128)(2,1)}, bf16[12,64,128]{2,1,0:T(8,128)(2,1)S(1)}, u32[]{:S(2)}, u32[]{:S(2)}) collective-permute-start(bf16[12,64,128]{2,1,0:T(8,128)(2,1)} %get-tuple-element.56), channel_id=1, source_target_pairs={{0,20},{4,24},{8,28},{12,0},{16,4},{20,8},{24,12},{28,16},{1,21},{... | collective-permute-start | bytes 589832 | tf_op jit(solution)/shard_map/ppermute | solution.py:938
  178.4 27.5 %copy-start.16 = (bf16[12,64,128]{2,1,0:T(8,128)(2,1)}, bf16[12,64,128]{2,1,0:T(8,128)(2,1)S(1)}, u32[]{:S(2)}) copy-start(bf16[12,64,128]{2,1,0:T(8,128)(2,1)S(1)} %collective-permute-done.10.refs_1_) | copy-start | bytes 589828
  178.4 33.7 %collective-permute-start.17 = (bf16[128,1024]{1,0:T(8,128)(2,1)}, bf16[128,1024]{1,0:T(8,128)(2,1)S(1)}, u32[]{:S(2)}, u32[]{:S(2)}) collective-permute-start(bf16[128,1024]{1,0:T(8,128)(2,1)} %get-tuple-element.67), channel_id=1, source_target_pairs={{0,1},{1,2},{2,3},{3,0},{4,5},{5,6},{6,7},{7,4},{8,9},{9,10},{10,1... | collective-permute-start | bytes 786440 | tf_op jit(solution)/shard_map/ppermute | solution.py:938
  178.4 27.4 %copy-start.17 = (bf16[12,64,128]{2,1,0:T(8,128)(2,1)}, bf16[12,64,128]{2,1,0:T(8,128)(2,1)S(1)}, u32[]{:S(2)}) copy-start(bf16[12,64,128]{2,1,0:T(8,128)(2,1)S(1)} %collective-permute-done.11.refs_2_) | copy-start | bytes 589828
  178.5 33.6 %collective-permute-start.18 = (bf16[128,1024]{1,0:T(8,128)(2,1)}, bf16[128,1024]{1,0:T(8,128)(2,1)S(1)}, u32[]{:S(2)}, u32[]{:S(2)}) collective-permute-start(bf16[128,1024]{1,0:T(8,128)(2,1)} %get-tuple-element.68), channel_id=1, source_target_pairs={{0,2},{1,3},{2,0},{3,1},{4,6},{5,7},{6,4},{7,5},{8,10},{9,11},{10,... | collective-permute-start | bytes 786440 | tf_op jit(solution)/shard_map/ppermute | solution.py:938
  190.0 15.9 %copy-start.18 = (bf16[12,64,128]{2,1,0:T(8,128)(2,1)}, bf16[12,64,128]{2,1,0:T(8,128)(2,1)S(1)}, u32[]{:S(2)}) copy-start(bf16[12,64,128]{2,1,0:T(8,128)(2,1)S(1)} %collective-permute-done.12.refs_3_) | copy-start | bytes 589828
  190.0 22.1 %collective-permute-start.19 = (bf16[128,1024]{1,0:T(8,128)(2,1)}, bf16[128,1024]{1,0:T(8,128)(2,1)S(1)}, u32[]{:S(2)}, u32[]{:S(2)}) collective-permute-start(bf16[128,1024]{1,0:T(8,128)(2,1)} %get-tuple-element.69), channel_id=1, source_target_pairs={{0,3},{1,0},{2,1},{3,2},{4,7},{5,4},{6,5},{7,6},{8,11},{9,8},{10,9... | collective-permute-start | bytes 786440 | tf_op jit(solution)/shard_map/ppermute | solution.py:938
  191.2 11.4 %collective-permute-start.15 = (bf16[12,64,128]{2,1,0:T(8,128)(2,1)}, bf16[12,64,128]{2,1,0:T(8,128)(2,1)}, u32[]{:S(2)}, u32[]{:S(2)}) collective-permute-start(bf16[12,64,128]{2,1,0:T(8,128)(2,1)} %get-tuple-element.57), channel_id=1, source_target_pairs={{0,24},{4,28},{8,0},{12,4},{16,8},{20,12},{24,16},{28,20},{1,25},{... | collective-permute-start | bytes 589832 | tf_op jit(solution)/shard_map/ppermute | solution.py:938
  196.9 9.0 %collective-permute-start.16 = (bf16[12,64,128]{2,1,0:T(8,128)(2,1)}, bf16[12,64,128]{2,1,0:T(8,128)(2,1)}, u32[]{:S(2)}, u32[]{:S(2)}) collective-permute-start(bf16[12,64,128]{2,1,0:T(8,128)(2,1)} %get-tuple-element.58), channel_id=1, source_target_pairs={{0,28},{4,0},{8,4},{12,8},{16,12},{20,16},{24,20},{28,24},{1,29},{... | collective-permute-start | bytes 589832 | tf_op jit(solution)/shard_map/ppermute | solution.py:938
  (17 other events, 89.4 us)

commit v8 on v7

--- a/solution.py
+++ b/solution.py
@@ -19,7 +19,6 @@
 PAIR_DIM = 2 * HEAD_DIM
 LANES = 128
 TILE = 128
-SLOT_TILE = 4
 SLOT_PAD = 16
 PEER_TILE = 2
 PACK_TILE = 2
@@ -34,7 +33,8 @@
 
 
 def silu(v):
-    return v / (1.0 + jnp.exp(-v))
+    half = 0.5 * v
+    return half + half * jnp.tanh(half)
 
 
 def conv_silu(tail, rows, weight, bias_row):
@@ -456,25 +456,24 @@
 
 
 def pack_lead_kernel(own_ref, mask_ref, state_ref, out_ref):
-    first_slot = pl.program_id(0) * SLOT_TILE
-    for j in range(SLOT_TILE):
-        keep = mask_ref[jnp.minimum(first_slot + j, mask_ref.shape[0] - 1)].astype(F32)
-        out_ref[j] = (state_ref[j, 0] * keep).astype(BF16)
+    for slot in range(out_ref.shape[0]):
+        keep = mask_ref[slot].astype(F32)
+        out_ref[slot] = (state_ref[slot, 0] * keep).astype(BF16)
 
 
 def pack_lead(own, mask, states, hop):
     slots, peers, piece, width = states.shape
 
     def from_peer(t, own, mask):
-        return t, lax.rem(own[0] + hop, peers), 0, 0
+        return 0, lax.rem(own[0] + hop, peers), 0, 0
 
     return pl.pallas_call(
         pack_lead_kernel,
         grid_spec=pltpu.PrefetchScalarGridSpec(
             num_scalar_prefetch=2,
-            grid=(pl.cdiv(slots, SLOT_TILE),),
-            in_specs=[pl.BlockSpec((SLOT_TILE, 1, piece, width), from_peer)],
-            out_specs=pl.BlockSpec((SLOT_TILE, piece, width), lambda t, own, mask: (t, 0, 0)),
+            grid=(1,),
+            in_specs=[pl.BlockSpec((slots, 1, piece, width), from_peer)],
+            out_specs=pl.BlockSpec((slots, piece, width), lambda t, own, mask: (0, 0, 0)),
         ),
         out_shape=jax.ShapeDtypeStruct((slots, piece, width), BF16),
         compiler_params=pltpu.CompilerParams(dimension_semantics=("arbitrary",)),
@@ -939,9 +938,9 @@
 
 
 def rotate(values, axis):
-    got = list(values)
+    got = [values[hop] for hop in range(lax.axis_size(axis))]
     for hop in hop_order(len(got)):
-        got[hop] = send(values[hop], axis, hop)
+        got[hop] = send(got[hop], axis, hop)
     return got
 
 
@@ -984,6 +983,7 @@
     inner_taps = inner_window.transpose(1, 0, 2)
     outer_taps = state_window.transpose(1, 0, 2)
     packed = mark(plan, active_mask, inner_taps, outer_taps, peers)
+    packets = window_packets(plan, active_mask, inner_taps, outer_taps, peers)
     every = exchange(packed, "req")
     others = [0] + others
     for hop, pieces in zip(others, pack(own, active_mask, pool_pieces, others)):
@@ -1015,7 +1015,6 @@
     tail, kept_inner, kept_outer, own_decay = tails(
         chain, shared, channels, inner_local, outer_local, columns
     )
-    packets = window_packets(plan, active_mask, inner_taps, outer_taps, peers)
 
     part, local_end, read_rows, decay = block_parts(
         chain,

time: 231 us -> 230 us (level)
  no operation moved by 1% of the time
where the time goes in v8:
time: 230 us; the launch traced here: 229 us
  Pallas kernels  87.7 us (38%)
  waiting for transfers between devices  63.3 us (28%)
  starting transfers between devices  60.5 us (26%)
  local copies, waits for them, and re-layouts  8.12 us (4%)
  blocking collectives  6.54 us (3%)
    ppermute x20, waiting for transfers between devices, send(): return lax.ppermute(value, axis, pairs)  51.8 us
    ppermute x20, starting transfers between devices, send(): return lax.ppermute(value, axis, pairs)  37.5 us
    pallas_call x1, Pallas kernels, block_parts(): pl.pallas_call(block_kernel, grid_spec=pltpu.PrefetchScalarGridSpec(num_s...  32.4 us
    all_to_all x3, starting transfers between devices, exchange(): return lax.all_to_all(value, axis, split_axis=0, concat_axis=0, tiled=True)  22.9 us
    pallas_call x1, Pallas kernels, finish(): pl.pallas_call(finish_kernel, grid=(length // TILE,), in_specs=[pl.BlockS...  11.5 us
    all_to_all x3, waiting for transfers between devices, exchange(): return lax.all_to_all(value, axis, split_axis=0, concat_axis=0, tiled=True)  11.5 us
    pallas_call x2, Pallas kernels, reorder(): pl.pallas_call(reorder_kernel if part == 0 else reorder_rest_kernel, grid...  7.82 us
    pallas_call x1, Pallas kernels, pack(): pl.pallas_call(functools.partial(pack_kernel, hops), grid=(pl.cdiv(slots,...  6.59 us
  transfers between devices with their start and end apart: 23, of which 9 were waited for; matrix products, arithmetic and copies ran while one was open for 3% of the time, Pallas kernels for 34%

profile of v8, /device:TPU:0, one launch (start us, length us, event | category | flops | bytes accessed | tf_op | source)
XLA Modules:
  0.0 228.9 jit_solution(17430799506189147606)
XLA Ops:
  0.6 2.6 %pack_lead.1 = bf16[13,128,128]{2,1,0:T(8,128)(2,1)} custom-call(s32[1]{0:T(128)} %bitcast.18.own_ref, s32[13]{0:T(128)} %mask_ref.7, f32[13,8,128,128]{3,2,1,0:T(8,128)} %bitcast.36), custom_call_target="tpu_custom_call" | custom-call | tf_op jit(solution)/shard_map/pack_lead/pallas_call | solution.py:470
  3.3 4.1 %collective-permute-start.6 = (bf16[13,128,128]{2,1,0:T(8,128)(2,1)}, bf16[13,128,128]{2,1,0:T(8,128)(2,1)S(1)}, u32[]{:S(2)}, u32[]{:S(2)}) collective-permute-start(bf16[13,128,128]{2,1,0:T(8,128)(2,1)} %pack_lead.1), channel_id=1, source_target_pairs={{0,16},{4,20},{8,24},{12,28},{16,0},{20,4},{24,8},{28,12},{1,17},{... | collective-permute-start | bytes 1277960 | tf_op jit(solution)/shard_map/ppermute | solution.py:937
  7.4 6.6 %pack.1 = (bf16[13,128,128]{2,1,0:T(8,128)(2,1)}, bf16[13,128,128]{2,1,0:T(8,128)(2,1)}, bf16[13,128,128]{2,1,0:T(8,128)(2,1)}, bf16[13,128,128]{2,1,0:T(8,128)(...) custom-call(s32[1]{0:T(128)} %bitcast.18.own_ref, s32[13]{0:T(128)} %mask_ref.7, ...), custom_call_target="tpu_custom_call" | custom-call | tf_op jit(solution)/shard_map/pack/pallas_call | solution.py:496
  17.2 4.5 %all-to-all-start = ((bf16[8,32,128]{2,1,0:T(8,128)(2,1)}), bf16[8,32,128]{2,1,0:T(8,128)(2,1)S(1)}, u32[]{:S(2)}, u32[]{:S(2)}) async-start(bf16[8,32,128]{2,1,0:T(8,128)(2,1)} %mark.1), calls=%async_computation | async-start | bytes 131072 | tf_op jit(solution)/shard_map/all_to_all | solution.py:927
  21.7 2.0 collective-permute-start.4
  23.8 2.4 %collective-permute-start.5 = (bf16[13,128,128]{2,1,0:T(8,128)(2,1)}, bf16[13,128,128]{2,1,0:T(8,128)(2,1)S(1)}, u32[]{:S(2)}, u32[]{:S(2)}) collective-permute-start(bf16[13,128,128]{2,1,0:T(8,128)(2,1)} %get-tuple-element.46), channel_id=1, source_target_pairs={{0,12},{4,16},{8,20},{12,24},{16,28},{20,0},{24,4},{28,8},{1,13},{... | collective-permute-start | bytes 1277960 | tf_op jit(solution)/shard_map/ppermute | solution.py:937
  27.6 27.6 %collective-permute-done.6.refs_4_ = bf16[13,128,128]{2,1,0:T(8,128)(2,1)S(1)} collective-permute-done((bf16[13,128,128]{2,1,0:T(8,128)(2,1)}, bf16[13,128,128]{2,1,0:T(8,128)(2,1)S(1)}, u32[]{:S(2)}, u32[]{:S(2)}) %collective-permute-start.6) | collective-permute-done | bytes 426016 | tf_op jit(solution)/shard_map/ppermute | solution.py:937
  55.2 2.6 %collective-permute-start.9 = (bf16[13,128,128]{2,1,0:T(8,128)(2,1)}, bf16[13,128,128]{2,1,0:T(8,128)(2,1)S(1)}, u32[]{:S(2)}, u32[]{:S(2)}) collective-permute-start(bf16[13,128,128]{2,1,0:T(8,128)(2,1)} %get-tuple-element.49), channel_id=1, source_target_pairs={{0,28},{4,0},{8,4},{12,8},{16,12},{20,16},{24,20},{28,24},{1,29},{... | collective-permute-start | bytes 1277960 | tf_op jit(solution)/shard_map/ppermute | solution.py:937
  63.0 3.1 %share.1 = (bf16[3,10112]{1,0:T(4,128)(2,1)}, f32[512,128]{1,0:T(8,128)}, s32[8,128]{1,0:T(8,128)}) custom-call(s32[4]{0:T(128)} %pad_add_fusion.place_ref, bf16[8,32,128]{2,1,0:T(8,128)(2,1)} %copy-done.12, bf16[512,4096]{1,0:T(8,128)(2,1)} %bitcast.31, bf16[512,4096]{1,0:T(8,128)(2,1)} %bitcast.32, bf16[512,4096]{1,0:T(8,128)(2,1)} %bitcast.33, ...), custom_call_target="tpu_custom_call" | custom-call | tf_op jit(solution)/shard_map/share/pallas_call | solution.py:820
  66.6 7.1 %collective-permute-done.8.refs_6_ = bf16[13,128,128]{2,1,0:T(8,128)(2,1)S(1)} collective-permute-done((bf16[13,128,128]{2,1,0:T(8,128)(2,1)}, bf16[13,128,128]{2,1,0:T(8,128)(2,1)S(1)}, u32[]{:S(2)}, u32[]{:S(2)}) %collective-permute-start.8) | collective-permute-done | bytes 426016 | tf_op jit(solution)/shard_map/ppermute | solution.py:937
  74.9 2.7 %pick_first.1 = bf16[8,272,128]{2,1,0:T(8,128)(2,1)} custom-call(s32[1]{0:T(128)} %bitcast.18.own_ref, s32[8,128]{1,0:T(8,128)} %get-tuple-element.42.table_ref, bf16[8,144,128]{2,1,0:T(8,128)(2,1)} %window_packets.1.packet_ref, bf16[13,128,128]{2,1,0:T(8,128)(2,1)} %get-tuple-element.43.refs_0_, bf16[13,128,128]{2,1,0:T(8,128)(2,1)} %copy-done.3, ...), custom_call_target="tpu_custom_call" | custom-call | tf_op jit(solution)/shard_map/pick_first/pallas_call | solution.py:545
  77.6 14.8 %all-to-all-start.1 = ((bf16[8,272,128]{2,1,0:T(8,128)(2,1)}), bf16[8,272,128]{2,1,0:T(8,128)(2,1)S(1)}, u32[]{:S(2)}, u32[]{:S(2)}) async-start(bf16[8,272,128]{2,1,0:T(8,128)(2,1)} %pick_first.1), calls=%async_computation.1 | async-start | bytes 1114112 | tf_op jit(solution)/shard_map/all_to_all | solution.py:927
  92.5 3.9 %reorder_rest.1 = bf16[8,12,64,128]{3,2,1,0:T(8,128)(2,1)} custom-call(s32[1]{0:T(128)} %bitcast.18.own_ref, s32[8,128]{1,0:T(8,128)} %get-tuple-element.42.table_ref, bf16[13,128,128]{2,1,0:T(8,128)(2,1)} %get-tuple-element.43.refs_0_, bf16[13,128,128]{2,1,0:T(8,128)(2,1)} %copy-done.3, bf16[13,128,128]{2,1,0:T(8,128)(2,1)} %copy-done.4, ...), custom_call_target="tpu_custom_call" | custom-call | tf_op jit(solution)/shard_map/reorder_rest/pallas_call | solution.py:605
  96.4 11.5 %all-to-all-done.1.refs_4_.got_ref = bf16[8,272,128]{2,1,0:T(8,128)(2,1)S(1)} async-done(((bf16[8,272,128]{2,1,0:T(8,128)(2,1)}), bf16[8,272,128]{2,1,0:T(8,128)(2,1)S(1)}, u32[]{:S(2)}, u32[]{:S(2)}) %all-to-all-start.1) | async-done | bytes 557088 | tf_op jit(solution)/shard_map/all_to_all | solution.py:927
  107.8 3.6 %all-to-all-start.2 = ((bf16[8,12,64,128]{3,2,1,0:T(8,128)(2,1)}), bf16[8,12,64,128]{3,2,1,0:T(8,128)(2,1)S(1)}, u32[]{:S(2)}, u32[]{:S(2)}) async-start(bf16[8,12,64,128]{3,2,1,0:T(8,128)(2,1)} %reorder_rest.1), calls=%async_computation.2 | async-start | bytes 3145728 | tf_op jit(solution)/shard_map/all_to_all | solution.py:927
  112.8 6.5 %all-gather.1.shared_ref = bf16[4,3,10112]{2,1,0:T(4,128)(2,1)} all-gather(bf16[1,3,10112]{2,1,0:T(4,128)(2,1)S(1)} %bitcast.49), channel_id=2, replica_groups=mesh['req'=8,'seq'=4] {'seq'}, dimensions={0}, use_global_device_ids=true | all-gather | bytes 303360 | tf_op jit(solution)/shard_map/all_gather | solution.py:1013
  119.4 2.0 tails.1
  121.4 32.4 %block_parts.1 = (f32[512,4096]{1,0:T(8,128)}, bf16[4,128,1024]{2,1,0:T(8,128)(2,1)}, bf16[512,128]{1,0:T(8,128)(2,1)}, f32[512,128]{1,0:T(8,128)}) custom-call(s32[1]{0:T(128)} %bitcast.chain_ref.place_ref, f32[8,4352]{1,0:T(8,128)} %get-tuple-element.39.tail_ref.state_tail_ref, bf16[512,4096]{1,0:T(8,128)(2,1)} %bitcast.34, bf16[512,4096]{1,0:T(8,128)(2,1)} %bitcast.35, ...), custom_call_target="tpu_custom_call" | custom-call | flops 6000000000 | bytes 20000000 | tf_op jit(solution)/shard_map/block_parts/pallas_call | solution.py:178
  157.7 3.9 %reorder.1 = (bf16[12,64,128]{2,1,0:T(8,128)(2,1)}, bf16[12,64,128]{2,1,0:T(8,128)(2,1)}, bf16[12,64,128]{2,1,0:T(8,128)(2,1)}, bf16[12,64,128]{2,1,0:T(8,128)(2...) custom-call(s32[1]{0:T(128)} %bitcast.18.own_ref, ...), custom_call_target="tpu_custom_call" | custom-call | tf_op jit(solution)/shard_map/reorder/pallas_call | solution.py:605
  161.6 2.0 collective-permute-start.10
  165.1 2.4 %collective-permute-start.12 = (bf16[12,64,128]{2,1,0:T(8,128)(2,1)}, bf16[12,64,128]{2,1,0:T(8,128)(2,1)S(1)}, u32[]{:S(2)}, u32[]{:S(2)}) collective-permute-start(bf16[12,64,128]{2,1,0:T(8,128)(2,1)} %get-tuple-element.54), channel_id=1, source_target_pairs={{0,12},{4,16},{8,20},{12,24},{16,28},{20,0},{24,4},{28,8},{1,13},{... | collective-permute-start | bytes 589832 | tf_op jit(solution)/shard_map/ppermute | solution.py:937
  167.5 2.6 %collective-permute-done.1.refs_2_ = bf16[128,1024]{1,0:T(8,128)(2,1)S(1)} collective-permute-done((bf16[128,1024]{1,0:T(8,128)(2,1)S(1)}, bf16[128,1024]{1,0:T(8,128)(2,1)S(1)}, u32[]{:S(2)}, u32[]{:S(2)}) %collective-permute-start.1) | collective-permute-done | bytes 262176 | tf_op jit(solution)/shard_map/ppermute | solution.py:937
  170.1 2.9 %collective-permute-start.13 = (bf16[12,64,128]{2,1,0:T(8,128)(2,1)}, bf16[12,64,128]{2,1,0:T(8,128)(2,1)S(1)}, u32[]{:S(2)}, u32[]{:S(2)}) collective-permute-start(bf16[12,64,128]{2,1,0:T(8,128)(2,1)} %get-tuple-element.55), channel_id=1, source_target_pairs={{0,16},{4,20},{8,24},{12,28},{16,0},{20,4},{24,8},{28,12},{1,17},{... | collective-permute-start | bytes 589832 | tf_op jit(solution)/shard_map/ppermute | solution.py:937
  174.5 3.1 %combine.1 = (bf16[128,1024]{1,0:T(8,128)(2,1)}, bf16[128,1024]{1,0:T(8,128)(2,1)}, bf16[128,1024]{1,0:T(8,128)(2,1)}, bf16[128,1024]{1,0:T(8,128)(2,1)}, f32[1024,128]{1,0:T(8,128)}) custom-call(s32[1]{0:T(128)} %bitcast.chain_ref.place_ref, f32[4,1024]{1,0:T(4,128)} %get-tuple-element.38.decay_ref, bf16[128,1024]{1,0:T(8,128)(2,1)} %get-tuple-element.73.refs_0_, ...), custom_call_target="tpu_custom_call" | custom-call | tf_op jit(solution)/shard_map/combine/pallas_call | solution.py:704
  179.1 10.1 %collective-permute-done.12.refs_3_ = bf16[12,64,128]{2,1,0:T(8,128)(2,1)S(1)} collective-permute-done((bf16[12,64,128]{2,1,0:T(8,128)(2,1)}, bf16[12,64,128]{2,1,0:T(8,128)(2,1)S(1)}, u32[]{:S(2)}, u32[]{:S(2)}) %collective-permute-start.12) | collective-permute-done | bytes 196640 | tf_op jit(solution)/shard_map/ppermute | solution.py:937
  190.4 5.7 %collective-permute-start.15 = (bf16[12,64,128]{2,1,0:T(8,128)(2,1)}, bf16[12,64,128]{2,1,0:T(8,128)(2,1)}, u32[]{:S(2)}, u32[]{:S(2)}) collective-permute-start(bf16[12,64,128]{2,1,0:T(8,128)(2,1)} %get-tuple-element.57), channel_id=1, source_target_pairs={{0,24},{4,28},{8,0},{12,4},{16,8},{20,12},{24,16},{28,20},{1,25},{... | collective-permute-start | bytes 589832 | tf_op jit(solution)/shard_map/ppermute | solution.py:937
  196.1 3.1 %collective-permute-start.16 = (bf16[12,64,128]{2,1,0:T(8,128)(2,1)}, bf16[12,64,128]{2,1,0:T(8,128)(2,1)}, u32[]{:S(2)}, u32[]{:S(2)}) collective-permute-start(bf16[12,64,128]{2,1,0:T(8,128)(2,1)} %get-tuple-element.58), channel_id=1, source_target_pairs={{0,28},{4,0},{8,4},{12,8},{16,12},{20,16},{24,20},{28,24},{1,29},{... | collective-permute-start | bytes 589832 | tf_op jit(solution)/shard_map/ppermute | solution.py:937
  199.8 2.0 settle.1
  201.8 3.3 %collective-permute-done.16.refs_7_ = bf16[12,64,128]{2,1,0:T(8,128)(2,1)} collective-permute-done((bf16[12,64,128]{2,1,0:T(8,128)(2,1)}, bf16[12,64,128]{2,1,0:T(8,128)(2,1)}, u32[]{:S(2)}, u32[]{:S(2)}) %collective-permute-start.16) | collective-permute-done | bytes 196640 | tf_op jit(solution)/shard_map/ppermute | solution.py:937
  205.1 6.1 %unpack.1.states_ref = f32[13,8,128,128]{3,2,1,0:T(8,128)} custom-call(s32[1]{0:T(128)} %bitcast.18.own_ref, f32[1024,128]{1,0:T(8,128)} %get-tuple-element.50.final_ref, bf16[12,64,128]{2,1,0:T(8,128)(2,1)} %get-tuple-element.51.refs_0_, bf16[12,64,128]{2,1,0:T(8,128)(2,1)} %copy-done.16, bf16[12,64,128]{2,1,0:T(8,128)(2,1)} %copy-done.17, ...), custom_call_target="tpu_custom_call" | custom-call | tf_op jit(solution)/shard_map/unpack/pallas_call | solution.py:637
  212.1 11.5 %finish.1 = bf16[512,4096]{1,0:T(8,128)(2,1)} custom-call(s32[3]{0:T(128)} %pad_add_fusion.1.place_ref, f32[512,4096]{1,0:T(8,128)} %get-tuple-element.63.part_ref, bf16[512,4096]{1,0:T(8,128)(2,1)} %bitcast.39, bf16[512,128]{1,0:T(8,128)(2,1)} %get-tuple-element.64.read_ref, f32[512,128]{1,0:T(8,128)} %get-tuple-element.65.decay_ref, f32[1,4096]{1,0:T(1,128)} %bitcast.52, ...), custom_call_target="tpu_custom_call" | custom-call | flops 3000000000 | bytes 16000000 | tf_op jit(solution)/shard_map/finish/pallas_call | solution.py:284
  224.8 4.1 %unpack_rest.1 = f32[13,8,128,128]{3,2,1,0:T(8,128)} custom-call(f32[1024,128]{1,0:T(8,128)} %get-tuple-element.50.final_ref, bf16[8,12,64,128]{3,2,1,0:T(8,128)(2,1)} %copy-done, f32[13,8,128,128]{3,2,1,0:T(8,128)} %unpack.1.states_ref), custom_call_target="tpu_custom_call", output_to_operand_aliasing={{}: (2, {})} | custom-call | tf_op jit(solution)/shard_map/unpack_rest/pallas_call | solution.py:664
  (91 shorter events, 24.5 us)
Async XLA Ops:
  3.3 54.6 %copy-start.25 = (f32[64]{0:T(128)S(1)}, f32[64]{0:T(128)}, u32[]{:S(2)}) copy-start(f32[64]{0:T(128)} %param.29) | copy-start | bytes 772
  3.3 57.6 %copy-start.22 = (bf16[1,512,64]{1,2,0:T(8,128)(2,1)S(1)}, bf16[1,512,64]{1,2,0:T(8,128)(2,1)}, u32[]{:S(2)}) copy-start(bf16[1,512,64]{1,2,0:T(8,128)(2,1)} %param.24) | copy-start | bytes 196612
  3.3 51.9 %collective-permute-start.6 = (bf16[13,128,128]{2,1,0:T(8,128)(2,1)}, bf16[13,128,128]{2,1,0:T(8,128)(2,1)S(1)}, u32[]{:S(2)}, u32[]{:S(2)}) collective-permute-start(bf16[13,128,128]{2,1,0:T(8,128)(2,1)} %pack_lead.1), channel_id=1, source_target_pairs={{0,16},{4,20},{8,24},{12,28},{16,0},{20,4},{24,8},{28,12},{1,17},{... | collective-permute-start | bytes 1277960 | tf_op jit(solution)/shard_map/ppermute | solution.py:937
  13.9 41.3 %collective-permute-start.3 = (bf16[13,128,128]{2,1,0:T(8,128)(2,1)}, bf16[13,128,128]{2,1,0:T(8,128)(2,1)S(1)}, u32[]{:S(2)}, u32[]{:S(2)}) collective-permute-start(bf16[13,128,128]{2,1,0:T(8,128)(2,1)} %get-tuple-element.44), channel_id=1, source_target_pairs={{0,4},{4,8},{8,12},{12,16},{16,20},{20,24},{24,28},{28,0},{1,5},{5... | collective-permute-start | bytes 1277960 | tf_op jit(solution)/shard_map/ppermute | solution.py:937
  17.2 45.1 %all-to-all-start = ((bf16[8,32,128]{2,1,0:T(8,128)(2,1)}), bf16[8,32,128]{2,1,0:T(8,128)(2,1)S(1)}, u32[]{:S(2)}, u32[]{:S(2)}) async-start(bf16[8,32,128]{2,1,0:T(8,128)(2,1)} %mark.1), calls=%async_computation | async-start | bytes 131072 | tf_op jit(solution)/shard_map/all_to_all | solution.py:927
  21.7 44.3 %collective-permute-start.4 = (bf16[13,128,128]{2,1,0:T(8,128)(2,1)}, bf16[13,128,128]{2,1,0:T(8,128)(2,1)S(1)}, u32[]{:S(2)}, u32[]{:S(2)}) collective-permute-start(bf16[13,128,128]{2,1,0:T(8,128)(2,1)} %get-tuple-element.45), channel_id=1, source_target_pairs={{0,8},{4,12},{8,16},{12,20},{16,24},{20,28},{24,0},{28,4},{1,9},{5... | collective-permute-start | bytes 1277960 | tf_op jit(solution)/shard_map/ppermute | solution.py:937
  23.8 42.8 %collective-permute-start.5 = (bf16[13,128,128]{2,1,0:T(8,128)(2,1)}, bf16[13,128,128]{2,1,0:T(8,128)(2,1)S(1)}, u32[]{:S(2)}, u32[]{:S(2)}) collective-permute-start(bf16[13,128,128]{2,1,0:T(8,128)(2,1)} %get-tuple-element.46), channel_id=1, source_target_pairs={{0,12},{4,16},{8,20},{12,24},{16,28},{20,0},{24,4},{28,8},{1,13},{... | collective-permute-start | bytes 1277960 | tf_op jit(solution)/shard_map/ppermute | solution.py:937
  26.1 40.5 %collective-permute-start.7 = (bf16[13,128,128]{2,1,0:T(8,128)(2,1)}, bf16[13,128,128]{2,1,0:T(8,128)(2,1)S(1)}, u32[]{:S(2)}, u32[]{:S(2)}) collective-permute-start(bf16[13,128,128]{2,1,0:T(8,128)(2,1)} %get-tuple-element.47), channel_id=1, source_target_pairs={{0,20},{4,24},{8,28},{12,0},{16,4},{20,8},{24,12},{28,16},{1,21},{... | collective-permute-start | bytes 1277960 | tf_op jit(solution)/shard_map/ppermute | solution.py:937
  55.2 18.5 %collective-permute-start.8 = (bf16[13,128,128]{2,1,0:T(8,128)(2,1)}, bf16[13,128,128]{2,1,0:T(8,128)(2,1)S(1)}, u32[]{:S(2)}, u32[]{:S(2)}) collective-permute-start(bf16[13,128,128]{2,1,0:T(8,128)(2,1)} %get-tuple-element.48), channel_id=1, source_target_pairs={{0,24},{4,28},{8,0},{12,4},{16,8},{20,12},{24,16},{28,20},{1,25},{... | collective-permute-start | bytes 1277960 | tf_op jit(solution)/shard_map/ppermute | solution.py:937
  55.2 18.9 %collective-permute-start.9 = (bf16[13,128,128]{2,1,0:T(8,128)(2,1)}, bf16[13,128,128]{2,1,0:T(8,128)(2,1)S(1)}, u32[]{:S(2)}, u32[]{:S(2)}) collective-permute-start(bf16[13,128,128]{2,1,0:T(8,128)(2,1)} %get-tuple-element.49), channel_id=1, source_target_pairs={{0,28},{4,0},{8,4},{12,8},{16,12},{20,16},{24,20},{28,24},{1,29},{... | collective-permute-start | bytes 1277960 | tf_op jit(solution)/shard_map/ppermute | solution.py:937
  77.6 30.2 %all-to-all-start.1 = ((bf16[8,272,128]{2,1,0:T(8,128)(2,1)}), bf16[8,272,128]{2,1,0:T(8,128)(2,1)S(1)}, u32[]{:S(2)}, u32[]{:S(2)}) async-start(bf16[8,272,128]{2,1,0:T(8,128)(2,1)} %pick_first.1), calls=%async_computation.1 | async-start | bytes 1114112 | tf_op jit(solution)/shard_map/all_to_all | solution.py:927
  92.4 19.0 %copy-start.23 = (f32[4352]{0:T(1024)S(1)}, f32[4352]{0:T(1024)}, u32[]{:S(2)}) copy-start(f32[4352]{0:T(1024)} %param.27) | copy-start | bytes 52228
  92.4 19.6 %copy-start.24 = (f32[64]{0:T(128)S(1)}, f32[64]{0:T(128)}, u32[]{:S(2)}) copy-start(f32[64]{0:T(128)} %param.30) | copy-start | bytes 772
  92.5 20.4 %copy-start.21 = (bf16[3,10112]{1,0:T(4,128)(2,1)S(1)}, bf16[3,10112]{1,0:T(4,128)(2,1)}, u32[]{:S(2)}) copy-start(bf16[3,10112]{1,0:T(4,128)(2,1)} %get-tuple-element.37) | copy-start | bytes 182020
  107.8 45.9 %copy-start.1 = (bf16[8,272,128]{2,1,0:T(8,128)(2,1)}, bf16[8,272,128]{2,1,0:T(8,128)(2,1)S(1)}, u32[]{:S(2)}) copy-start(bf16[8,272,128]{2,1,0:T(8,128)(2,1)S(1)} %all-to-all-done.1.refs_4_.got_ref) | copy-start | bytes 1671172
  107.8 115.8 %all-to-all-start.2 = ((bf16[8,12,64,128]{3,2,1,0:T(8,128)(2,1)}), bf16[8,12,64,128]{3,2,1,0:T(8,128)(2,1)S(1)}, u32[]{:S(2)}, u32[]{:S(2)}) async-start(bf16[8,12,64,128]{3,2,1,0:T(8,128)(2,1)} %reorder_rest.1), calls=%async_computation.2 | async-start | bytes 3145728 | tf_op jit(solution)/shard_map/all_to_all | solution.py:927
  155.7 9.4 %collective-permute-start.2 = (bf16[128,1024]{1,0:T(8,128)(2,1)S(1)}, bf16[128,1024]{1,0:T(8,128)(2,1)S(1)}, u32[]{:S(2)}, u32[]{:S(2)}) collective-permute-start(bf16[128,1024]{1,0:T(8,128)(2,1)S(1)} %get-tuple-element.70), channel_id=1, source_target_pairs={{0,3},{1,0},{2,1},{3,2},{4,7},{5,4},{6,5},{7,6},{8,11},{9,8},{10,9... | collective-permute-start | bytes 786440 | tf_op jit(solution)/shard_map/ppermute | solution.py:937
  157.0 13.0 %collective-permute-start.1 = (bf16[128,1024]{1,0:T(8,128)(2,1)S(1)}, bf16[128,1024]{1,0:T(8,128)(2,1)S(1)}, u32[]{:S(2)}, u32[]{:S(2)}) collective-permute-start(bf16[128,1024]{1,0:T(8,128)(2,1)S(1)} %get-tuple-element.71), channel_id=1, source_target_pairs={{0,2},{1,3},{2,0},{3,1},{4,6},{5,7},{6,4},{7,5},{8,10},{9,11},{10,... | collective-permute-start | bytes 786440 | tf_op jit(solution)/shard_map/ppermute | solution.py:937
  157.7 15.3 %collective-permute-start = (bf16[128,1024]{1,0:T(8,128)(2,1)S(1)}, bf16[128,1024]{1,0:T(8,128)(2,1)S(1)}, u32[]{:S(2)}, u32[]{:S(2)}) collective-permute-start(bf16[128,1024]{1,0:T(8,128)(2,1)S(1)} %get-tuple-element.72), channel_id=1, source_target_pairs={{0,1},{1,2},{2,3},{3,0},{4,5},{5,6},{6,7},{7,4},{8,9},{9,10},{10,1... | collective-permute-start | bytes 786440 | tf_op jit(solution)/shard_map/ppermute | solution.py:937
  161.6 15.9 %collective-permute-start.10 = (bf16[12,64,128]{2,1,0:T(8,128)(2,1)}, bf16[12,64,128]{2,1,0:T(8,128)(2,1)S(1)}, u32[]{:S(2)}, u32[]{:S(2)}) collective-permute-start(bf16[12,64,128]{2,1,0:T(8,128)(2,1)} %get-tuple-element.52), channel_id=1, source_target_pairs={{0,4},{4,8},{8,12},{12,16},{16,20},{20,24},{24,28},{28,0},{1,5},{5... | collective-permute-start | bytes 589832 | tf_op jit(solution)/shard_map/ppermute | solution.py:937
  163.6 14.0 %collective-permute-start.11 = (bf16[12,64,128]{2,1,0:T(8,128)(2,1)}, bf16[12,64,128]{2,1,0:T(8,128)(2,1)S(1)}, u32[]{:S(2)}, u32[]{:S(2)}) collective-permute-start(bf16[12,64,128]{2,1,0:T(8,128)(2,1)} %get-tuple-element.53), channel_id=1, source_target_pairs={{0,8},{4,12},{8,16},{12,20},{16,24},{20,28},{24,0},{28,4},{1,9},{5... | collective-permute-start | bytes 589832 | tf_op jit(solution)/shard_map/ppermute | solution.py:937
  165.1 24.1 %collective-permute-start.12 = (bf16[12,64,128]{2,1,0:T(8,128)(2,1)}, bf16[12,64,128]{2,1,0:T(8,128)(2,1)S(1)}, u32[]{:S(2)}, u32[]{:S(2)}) collective-permute-start(bf16[12,64,128]{2,1,0:T(8,128)(2,1)} %get-tuple-element.54), channel_id=1, source_target_pairs={{0,12},{4,16},{8,20},{12,24},{16,28},{20,0},{24,4},{28,8},{1,13},{... | collective-permute-start | bytes 589832 | tf_op jit(solution)/shard_map/ppermute | solution.py:937
  170.1 20.3 %collective-permute-start.13 = (bf16[12,64,128]{2,1,0:T(8,128)(2,1)}, bf16[12,64,128]{2,1,0:T(8,128)(2,1)S(1)}, u32[]{:S(2)}, u32[]{:S(2)}) collective-permute-start(bf16[12,64,128]{2,1,0:T(8,128)(2,1)} %get-tuple-element.55), channel_id=1, source_target_pairs={{0,16},{4,20},{8,24},{12,28},{16,0},{20,4},{24,8},{28,12},{1,17},{... | collective-permute-start | bytes 589832 | tf_op jit(solution)/shard_map/ppermute | solution.py:937
  173.0 23.1 %collective-permute-start.14 = (bf16[12,64,128]{2,1,0:T(8,128)(2,1)}, bf16[12,64,128]{2,1,0:T(8,128)(2,1)S(1)}, u32[]{:S(2)}, u32[]{:S(2)}) collective-permute-start(bf16[12,64,128]{2,1,0:T(8,128)(2,1)} %get-tuple-element.56), channel_id=1, source_target_pairs={{0,20},{4,24},{8,28},{12,0},{16,4},{20,8},{24,12},{28,16},{1,21},{... | collective-permute-start | bytes 589832 | tf_op jit(solution)/shard_map/ppermute | solution.py:937
  177.6 27.5 %copy-start.16 = (bf16[12,64,128]{2,1,0:T(8,128)(2,1)}, bf16[12,64,128]{2,1,0:T(8,128)(2,1)S(1)}, u32[]{:S(2)}) copy-start(bf16[12,64,128]{2,1,0:T(8,128)(2,1)S(1)} %collective-permute-done.10.refs_1_) | copy-start | bytes 589828
  177.6 33.7 %collective-permute-start.17 = (bf16[128,1024]{1,0:T(8,128)(2,1)}, bf16[128,1024]{1,0:T(8,128)(2,1)S(1)}, u32[]{:S(2)}, u32[]{:S(2)}) collective-permute-start(bf16[128,1024]{1,0:T(8,128)(2,1)} %get-tuple-element.67), channel_id=1, source_target_pairs={{0,1},{1,2},{2,3},{3,0},{4,5},{5,6},{6,7},{7,4},{8,9},{9,10},{10,1... | collective-permute-start | bytes 786440 | tf_op jit(solution)/shard_map/ppermute | solution.py:937
  177.6 27.5 %copy-start.17 = (bf16[12,64,128]{2,1,0:T(8,128)(2,1)}, bf16[12,64,128]{2,1,0:T(8,128)(2,1)S(1)}, u32[]{:S(2)}) copy-start(bf16[12,64,128]{2,1,0:T(8,128)(2,1)S(1)} %collective-permute-done.11.refs_2_) | copy-start | bytes 589828
  177.7 33.6 %collective-permute-start.18 = (bf16[128,1024]{1,0:T(8,128)(2,1)}, bf16[128,1024]{1,0:T(8,128)(2,1)S(1)}, u32[]{:S(2)}, u32[]{:S(2)}) collective-permute-start(bf16[128,1024]{1,0:T(8,128)(2,1)} %get-tuple-element.68), channel_id=1, source_target_pairs={{0,2},{1,3},{2,0},{3,1},{4,6},{5,7},{6,4},{7,5},{8,10},{9,11},{10,... | collective-permute-start | bytes 786440 | tf_op jit(solution)/shard_map/ppermute | solution.py:937
  189.2 15.9 %copy-start.18 = (bf16[12,64,128]{2,1,0:T(8,128)(2,1)}, bf16[12,64,128]{2,1,0:T(8,128)(2,1)S(1)}, u32[]{:S(2)}) copy-start(bf16[12,64,128]{2,1,0:T(8,128)(2,1)S(1)} %collective-permute-done.12.refs_3_) | copy-start | bytes 589828
  189.2 22.1 %collective-permute-start.19 = (bf16[128,1024]{1,0:T(8,128)(2,1)}, bf16[128,1024]{1,0:T(8,128)(2,1)S(1)}, u32[]{:S(2)}, u32[]{:S(2)}) collective-permute-start(bf16[128,1024]{1,0:T(8,128)(2,1)} %get-tuple-element.69), channel_id=1, source_target_pairs={{0,3},{1,0},{2,1},{3,2},{4,7},{5,4},{6,5},{7,6},{8,11},{9,8},{10,9... | collective-permute-start | bytes 786440 | tf_op jit(solution)/shard_map/ppermute | solution.py:937
  190.4 11.4 %collective-permute-start.15 = (bf16[12,64,128]{2,1,0:T(8,128)(2,1)}, bf16[12,64,128]{2,1,0:T(8,128)(2,1)}, u32[]{:S(2)}, u32[]{:S(2)}) collective-permute-start(bf16[12,64,128]{2,1,0:T(8,128)(2,1)} %get-tuple-element.57), channel_id=1, source_target_pairs={{0,24},{4,28},{8,0},{12,4},{16,8},{20,12},{24,16},{28,20},{1,25},{... | collective-permute-start | bytes 589832 | tf_op jit(solution)/shard_map/ppermute | solution.py:937
  196.1 9.0 %collective-permute-start.16 = (bf16[12,64,128]{2,1,0:T(8,128)(2,1)}, bf16[12,64,128]{2,1,0:T(8,128)(2,1)}, u32[]{:S(2)}, u32[]{:S(2)}) collective-permute-start(bf16[12,64,128]{2,1,0:T(8,128)(2,1)} %get-tuple-element.58), channel_id=1, source_target_pairs={{0,28},{4,0},{8,4},{12,8},{16,12},{20,16},{24,20},{28,24},{1,29},{... | collective-permute-start | bytes 589832 | tf_op jit(solution)/shard_map/ppermute | solution.py:937
  (17 other events, 89.4 us)

commit v9 on v8

--- a/solution.py
+++ b/solution.py
@@ -415,8 +415,9 @@
     )(plan, mask, inner, outer)
 
 
-def settle_kernel(got_ref, inner_own_ref, outer_own_ref, inner_ref, outer_ref):
-    peers, lines, _ = got_ref.shape
+def settle_kernel(inner_own_ref, outer_own_ref, *refs):
+    got_refs, inner_ref, outer_ref = refs[:-2], refs[-2], refs[-1]
+    peers, lines = len(got_refs), got_refs[0].shape[0]
     taps, slots, inner_local = inner_ref.shape
     width = inner_local + outer_ref.shape[2]
     chunks = width // LANES + 1
@@ -426,8 +427,8 @@
     parts = []
     for chunk in range(chunks):
         at = start + chunk * padded
-        part = got_ref[:, at : at + padded, :].astype(F32)
-        parts.append(part.reshape(rows, LANES))
+        part = [got_ref[at : at + padded, :] for got_ref in got_refs]
+        parts.append(jnp.concatenate(part, axis=0).astype(F32))
     tags = parts[-1][:, LANES - 1 :]
     lane = lax.broadcasted_iota(jnp.int32, (rows, LANES), 1).astype(F32)
     pick = (tags == lane).astype(BF16)
@@ -446,13 +447,13 @@
     whole = pl.BlockSpec(memory_space=pltpu.VMEM)
     return pl.pallas_call(
         settle_kernel,
-        in_specs=[whole, whole, whole],
+        in_specs=[whole] * (2 + len(got)),
         out_shape=[
             jax.ShapeDtypeStruct((taps, slots, inner_local), BF16),
             jax.ShapeDtypeStruct((taps, slots, outer_own.shape[1]), BF16),
         ],
         name="settle",
-    )(got, inner_own, outer_own)
+    )(inner_own, outer_own, *got)
 
 
 def pack_lead_kernel(own_ref, mask_ref, state_ref, out_ref):
@@ -515,11 +516,12 @@
 
 
 def pick_first_kernel(own_ref, table_ref, packet_ref, *refs):
-    in_refs, out_ref, sem = refs[:-2], refs[-2], refs[-1]
-    peers = len(in_refs)
+    peers = (len(refs) - 1) // 2
+    in_refs, out_refs, sem = refs[:peers], refs[peers:-1], refs[-1]
     slots, piece, _ = in_refs[0].shape
     own_piece = pl.ds(0, piece)
-    for target in range(peers):
+    for to in range(peers):
+        target = lax.rem(own_ref[0] + to, peers)
         peer, index = source_of(table_ref, target * slots)
         source = lax.rem(own_ref[0] - peer + peers, peers)
         for hop in range(peers):
@@ -527,14 +529,14 @@
             @pl.when(source == hop)
             def _():
                 pltpu.make_async_copy(
-                    in_refs[hop].at[index], out_ref.at[target, own_piece], sem.at[target]
+                    in_refs[hop].at[index], out_refs[to].at[own_piece], sem.at[to]
                 ).start()
 
-    for target in range(peers):
-        out_ref[target, piece:, :] = packet_ref[target]
-    for target in range(peers):
+    for to in range(peers):
+        out_refs[to][piece:, :] = packet_ref[lax.rem(own_ref[0] + to, peers)]
+    for to in range(peers):
         pltpu.make_async_copy(
-            in_refs[0].at[0], out_ref.at[target, own_piece], sem.at[target]
+            in_refs[0].at[0], out_refs[to].at[own_piece], sem.at[to]
         ).wait()
 
 
@@ -546,8 +548,8 @@
         pick_first_kernel,
         in_specs=[scalar, scalar, pl.BlockSpec(memory_space=pltpu.VMEM)]
         + [pl.BlockSpec(memory_space=pl.ANY)] * peers,
-        out_specs=pl.BlockSpec(memory_space=pltpu.VMEM),
-        out_shape=jax.ShapeDtypeStruct((peers, piece + packets.shape[1], width), BF16),
+        out_specs=[pl.BlockSpec(memory_space=pltpu.VMEM)] * peers,
+        out_shape=[jax.ShapeDtypeStruct((piece + packets.shape[1], width), BF16)] * peers,
         scratch_shapes=[pltpu.SemaphoreType.DMA((peers,))],
         name="pick_first",
     )(own, table, packets, *pieces)
@@ -679,15 +681,22 @@
 
 def combine_kernel(place_ref, decay_ref, *refs):
     count = decay_ref.shape[0]
-    end_scr, enter_scr = refs[-2:]
+    end_scr, enter_scr, first_scr = refs[-3:]
+    refs = refs[:-1]
     final_ref = refs[-3]
     entering_refs = refs[-3 - count : -3]
-    end_refs, first_ref = refs[:count], refs[count]
+    inputs = refs[: -3 - count]
+    end_refs, first_refs = inputs[:count], inputs[count:]
     chain = place_ref[0]
+    peers = len(first_refs)
+    piece = first_refs[0].shape[0]
+    for hop in range(peers):
+        peer = lax.rem(place_ref[1] - hop + peers, peers)
+        at = pl.multiple_of(peer * piece, 16)
+        first_scr[pl.ds(at, piece), :] = first_refs[hop][...]
     for hop in range(count):
         end_scr[lax.rem(chain - hop + count, count)] = end_refs[hop][...]
-    peers, piece, width = first_ref.shape
-    state = first_ref[...].astype(F32).reshape(peers * piece, width).T
+    state = first_scr[...].astype(F32).T
     for k in range(count):
         enter_scr[k] = state.astype(BF16)
         state = state * decay_ref[k : k + 1, :] + end_scr[k].astype(F32)
@@ -700,7 +709,7 @@
     count = len(ends)
     whole = pl.BlockSpec(memory_space=pltpu.VMEM)
     rows, columns = ends[0].shape
-    peers = first.shape[0]
+    peers = len(first)
     outs = pl.pallas_call(
         combine_kernel,
         grid=(1,),
@@ -709,7 +718,7 @@
             pl.BlockSpec(decay.shape, lambda t: (0, 0)),
         ]
         + [pl.BlockSpec((rows, columns), lambda t: (0, 0))] * count
-        + [pl.BlockSpec((peers, columns // peers, rows), lambda t: (0, 0, 0))],
+        + [pl.BlockSpec((columns // peers, rows), lambda t: (0, 0))] * peers,
         out_specs=[pl.BlockSpec((rows, columns), lambda t: (0, 0))] * count
         + [pl.BlockSpec((columns, rows), lambda t: (0, 0))],
         out_shape=[jax.ShapeDtypeStruct((rows, columns), BF16)] * count
@@ -717,9 +726,10 @@
         scratch_shapes=[
             pltpu.VMEM((count, rows, columns), BF16),
             pltpu.VMEM((count, rows, columns), BF16),
+            pltpu.VMEM((columns, rows), BF16),
         ],
         name="combine",
-    )(place, decay, *ends, first)
+    )(place, decay, *ends, *first)
     return outs[:count], outs[count]
 
 
@@ -1030,10 +1040,12 @@
     )
     own_ends = rotate(local_end, "seq")
 
-    first = exchange(pick_first(own, table, packets, spread), "req")
+    first = rotate(pick_first(own, table, packets, spread), "req")
     moved_a = rotate(reorder(own, table, spread, 0), "req")
     moved_b = exchange(reorder(own, table, spread, 1), "req")
-    entering, final = combine(chain, own_decay, own_ends, first)
+    entering, final = combine(
+        jnp.concatenate([chain, own]), own_decay, own_ends, first
+    )
     new_inner, new_outer = settle(first, kept_inner, kept_outer, slots)
     incoming = rotate(entering, "seq")
     mixer_out = finish(

time: 230 us -> 229 us (level)
  waiting for transfers between devices: 63.3 us -> 55.1 us
  starting transfers between devices: 60.5 us -> 66.2 us
    all_to_all x3 -> x2, waiting for transfers between devices: 11.5 us -> 0.01 us  [exchange(): return lax.all_to_all(value, axis, split_axis=0, concat_axis=0, tiled=True)]
    ppermute x20 -> x27, starting transfers between devices: 37.5 us -> 46.8 us  [send(): return lax.ppermute(value, axis, pairs)]
    all_to_all x3 -> x2, starting transfers between devices: 22.9 us -> 19.4 us  [exchange(): return lax.all_to_all(value, axis, split_axis=0, concat_axis=0, tiled=True)]
    ppermute x20 -> x27, waiting for transfers between devices: 51.8 us -> 55.1 us  [send(): return lax.ppermute(value, axis, pairs)]
    unnamed x53 -> x65, local copies, waits for them, and re-layouts: 4.24 us -> 4.91 us
  transfers between devices with their start and end apart: 23 -> 29, of which waited for: 9 -> 10; matrix products, arithmetic and copies ran while one was open for 3% -> 3% of each run, Pallas kernels for 34% -> 34%
where the time goes in v9:
time: 229 us; the launch traced here: 228 us
  Pallas kernels  87.8 us (38%)
  starting transfers between devices  66.2 us (29%)
  waiting for transfers between devices  55.1 us (24%)
  local copies, waits for them, and re-layouts  8.79 us (4%)
  blocking collectives  6.54 us (3%)
    ppermute x27, waiting for transfers between devices, send(): return lax.ppermute(value, axis, pairs)  55.1 us
    ppermute x27, starting transfers between devices, send(): return lax.ppermute(value, axis, pairs)  46.8 us
    pallas_call x1, Pallas kernels, block_parts(): pl.pallas_call(block_kernel, grid_spec=pltpu.PrefetchScalarGridSpec(num_s...  32.4 us
    all_to_all x2, starting transfers between devices, exchange(): return lax.all_to_all(value, axis, split_axis=0, concat_axis=0, tiled=True)  19.4 us
    pallas_call x1, Pallas kernels, finish(): pl.pallas_call(finish_kernel, grid=(length // TILE,), in_specs=[pl.BlockS...  11.5 us
    pallas_call x2, Pallas kernels, reorder(): pl.pallas_call(reorder_kernel if part == 0 else reorder_rest_kernel, grid...  7.77 us
    pallas_call x1, Pallas kernels, pack(): pl.pallas_call(functools.partial(pack_kernel, hops), grid=(pl.cdiv(slots,...  6.64 us
    all_gather x1, blocking collectives, device_body(): shared = lax.all_gather(payload, 'seq', axis=0)  6.54 us
  transfers between devices with their start and end apart: 29, of which 10 were waited for; matrix products, arithmetic and copies ran while one was open for 3% of the time, Pallas kernels for 34%

profile of v9, /device:TPU:0, one launch (start us, length us, event | category | flops | bytes accessed | tf_op | source)
XLA Modules:
  0.0 227.9 jit_solution(18365078545272925994)
XLA Ops:
  0.6 2.6 %pack_lead.1 = bf16[13,128,128]{2,1,0:T(8,128)(2,1)} custom-call(s32[1]{0:T(128)} %bitcast.1.own_ref, s32[13]{0:T(128)} %mask_ref.7, f32[13,8,128,128]{3,2,1,0:T(8,128)} %bitcast.36), custom_call_target="tpu_custom_call" | custom-call | tf_op jit(solution)/shard_map/pack_lead/pallas_call | solution.py:471
  3.3 4.1 %collective-permute-start.6 = (bf16[13,128,128]{2,1,0:T(8,128)(2,1)}, bf16[13,128,128]{2,1,0:T(8,128)(2,1)S(1)}, u32[]{:S(2)}, u32[]{:S(2)}) collective-permute-start(bf16[13,128,128]{2,1,0:T(8,128)(2,1)} %pack_lead.1), channel_id=1, source_target_pairs={{0,16},{4,20},{8,24},{12,28},{16,0},{20,4},{24,8},{28,12},{1,17},{... | collective-permute-start | bytes 1277960 | tf_op jit(solution)/shard_map/ppermute | solution.py:947
  7.3 6.6 %pack.1 = (bf16[13,128,128]{2,1,0:T(8,128)(2,1)}, bf16[13,128,128]{2,1,0:T(8,128)(2,1)}, bf16[13,128,128]{2,1,0:T(8,128)(2,1)}, bf16[13,128,128]{2,1,0:T(8,128)(...) custom-call(s32[1]{0:T(128)} %bitcast.1.own_ref, s32[13]{0:T(128)} %mask_ref.7, ...), custom_call_target="tpu_custom_call" | custom-call | tf_op jit(solution)/shard_map/pack/pallas_call | solution.py:497
  17.3 4.5 %all-to-all-start = ((bf16[8,32,128]{2,1,0:T(8,128)(2,1)}), bf16[8,32,128]{2,1,0:T(8,128)(2,1)S(1)}, u32[]{:S(2)}, u32[]{:S(2)}) async-start(bf16[8,32,128]{2,1,0:T(8,128)(2,1)} %mark.1), calls=%async_computation | async-start | bytes 131072 | tf_op jit(solution)/shard_map/all_to_all | solution.py:937
  21.8 2.0 collective-permute-start.4
  23.8 2.4 %collective-permute-start.5 = (bf16[13,128,128]{2,1,0:T(8,128)(2,1)}, bf16[13,128,128]{2,1,0:T(8,128)(2,1)S(1)}, u32[]{:S(2)}, u32[]{:S(2)}) collective-permute-start(bf16[13,128,128]{2,1,0:T(8,128)(2,1)} %get-tuple-element.54), channel_id=1, source_target_pairs={{0,12},{4,16},{8,20},{12,24},{16,28},{20,0},{24,4},{28,8},{1,13},{... | collective-permute-start | bytes 1277960 | tf_op jit(solution)/shard_map/ppermute | solution.py:947
  27.6 27.6 %collective-permute-done.6.refs_4_ = bf16[13,128,128]{2,1,0:T(8,128)(2,1)S(1)} collective-permute-done((bf16[13,128,128]{2,1,0:T(8,128)(2,1)}, bf16[13,128,128]{2,1,0:T(8,128)(2,1)S(1)}, u32[]{:S(2)}, u32[]{:S(2)}) %collective-permute-start.6) | collective-permute-done | bytes 426016 | tf_op jit(solution)/shard_map/ppermute | solution.py:947
  55.2 2.6 %collective-permute-start.9 = (bf16[13,128,128]{2,1,0:T(8,128)(2,1)}, bf16[13,128,128]{2,1,0:T(8,128)(2,1)S(1)}, u32[]{:S(2)}, u32[]{:S(2)}) collective-permute-start(bf16[13,128,128]{2,1,0:T(8,128)(2,1)} %get-tuple-element.57), channel_id=1, source_target_pairs={{0,28},{4,0},{8,4},{12,8},{16,12},{20,16},{24,20},{28,24},{1,29},{... | collective-permute-start | bytes 1277960 | tf_op jit(solution)/shard_map/ppermute | solution.py:947
  61.1 3.1 %share.1 = (bf16[3,10112]{1,0:T(4,128)(2,1)}, f32[512,128]{1,0:T(8,128)}, s32[8,128]{1,0:T(8,128)}) custom-call(s32[4]{0:T(128)} %pad_add_fusion.1.place_ref, bf16[8,32,128]{2,1,0:T(8,128)(2,1)} %copy-done.18, bf16[512,4096]{1,0:T(8,128)(2,1)} %bitcast.31, bf16[512,4096]{1,0:T(8,128)(2,1)} %bitcast.32, bf16[512,4096]{1,0:T(8,128)(2,1)} %bitcast.33, ...), custom_call_target="tpu_custom_call" | custom-call | tf_op jit(solution)/shard_map/share/pallas_call | solution.py:830
  64.2 2.3 %collective-permute-done.5.refs_3_ = bf16[13,128,128]{2,1,0:T(8,128)(2,1)S(1)} collective-permute-done((bf16[13,128,128]{2,1,0:T(8,128)(2,1)}, bf16[13,128,128]{2,1,0:T(8,128)(2,1)S(1)}, u32[]{:S(2)}, u32[]{:S(2)}) %collective-permute-start.5) | collective-permute-done | bytes 426016 | tf_op jit(solution)/shard_map/ppermute | solution.py:947
  66.6 7.0 %collective-permute-done.8.refs_6_ = bf16[13,128,128]{2,1,0:T(8,128)(2,1)S(1)} collective-permute-done((bf16[13,128,128]{2,1,0:T(8,128)(2,1)}, bf16[13,128,128]{2,1,0:T(8,128)(2,1)S(1)}, u32[]{:S(2)}, u32[]{:S(2)}) %collective-permute-start.8) | collective-permute-done | bytes 426016 | tf_op jit(solution)/shard_map/ppermute | solution.py:947
  74.9 3.9 %reorder_rest.1 = bf16[8,12,64,128]{3,2,1,0:T(8,128)(2,1)} custom-call(s32[1]{0:T(128)} %bitcast.1.own_ref, s32[8,128]{1,0:T(8,128)} %get-tuple-element.50.table_ref, bf16[13,128,128]{2,1,0:T(8,128)(2,1)} %get-tuple-element.51.refs_0_, bf16[13,128,128]{2,1,0:T(8,128)(2,1)} %copy-done.2, bf16[13,128,128]{2,1,0:T(8,128)(2,1)} %copy-done.3, ...), custom_call_target="tpu_custom_call" | custom-call | tf_op jit(solution)/shard_map/reorder_rest/pallas_call | solution.py:607
  78.7 14.9 %all-to-all-start.1 = ((bf16[8,12,64,128]{3,2,1,0:T(8,128)(2,1)}), bf16[8,12,64,128]{3,2,1,0:T(8,128)(2,1)S(1)}, u32[]{:S(2)}, u32[]{:S(2)}) async-start(bf16[8,12,64,128]{3,2,1,0:T(8,128)(2,1)} %reorder_rest.1), calls=%async_computation.1 | async-start | bytes 3145728 | tf_op jit(solution)/shard_map/all_to_all | solution.py:937
  95.0 6.5 %all-gather.1.shared_ref = bf16[4,3,10112]{2,1,0:T(4,128)(2,1)} all-gather(bf16[1,3,10112]{2,1,0:T(4,128)(2,1)S(1)} %bitcast.49), channel_id=2, replica_groups=mesh['req'=8,'seq'=4] {'seq'}, dimensions={0}, use_global_device_ids=true | all-gather | bytes 303360 | tf_op jit(solution)/shard_map/all_gather | solution.py:1023
  103.5 32.4 %block_parts.1 = (f32[512,4096]{1,0:T(8,128)}, bf16[4,128,1024]{2,1,0:T(8,128)(2,1)}, bf16[512,128]{1,0:T(8,128)(2,1)}, f32[512,128]{1,0:T(8,128)}) custom-call(s32[1]{0:T(128)} %bitcast.chain_ref, f32[8,4352]{1,0:T(8,128)} %get-tuple-element.47.tail_ref.state_tail_ref, bf16[512,4096]{1,0:T(8,128)(2,1)} %bitcast.34, bf16[512,4096]{1,0:T(8,128)(2,1)} %bitcast.35, ...), custom_call_target="tpu_custom_call" | custom-call | flops 6000000000 | bytes 20000000 | tf_op jit(solution)/shard_map/block_parts/pallas_call | solution.py:178
  135.9 2.0 slice_bitcast_fusion
  141.7 2.7 %pick_first.1 = (bf16[272,128]{1,0:T(8,128)(2,1)}, bf16[272,128]{1,0:T(8,128)(2,1)}, bf16[272,128]{1,0:T(8,128)(2,1)}, bf16[272,128]{1,0:T(8,128)(2,1)}, bf16[27...) custom-call(s32[1]{0:T(128)} %bitcast.1.own_ref, ...), custom_call_target="tpu_custom_call" | custom-call | tf_op jit(solution)/shard_map/pick_first/pallas_call | solution.py:547
  144.5 2.1 collective-permute-start.10
  148.0 2.4 %collective-permute-start.12 = (bf16[272,128]{1,0:T(8,128)(2,1)}, bf16[272,128]{1,0:T(8,128)(2,1)S(1)}, u32[]{:S(2)}, u32[]{:S(2)}) collective-permute-start(bf16[272,128]{1,0:T(8,128)(2,1)} %get-tuple-element.61), channel_id=1, source_target_pairs={{0,12},{4,16},{8,20},{12,24},{16,28},{20,0},{24,4},{28,8},{1,13},{... | collective-permute-start | bytes 208904 | tf_op jit(solution)/shard_map/ppermute | solution.py:947
  152.2 2.9 %collective-permute-start.13 = (bf16[272,128]{1,0:T(8,128)(2,1)}, bf16[272,128]{1,0:T(8,128)(2,1)S(1)}, u32[]{:S(2)}, u32[]{:S(2)}) collective-permute-start(bf16[272,128]{1,0:T(8,128)(2,1)} %get-tuple-element.62), channel_id=1, source_target_pairs={{0,16},{4,20},{8,24},{12,28},{16,0},{20,4},{24,8},{28,12},{1,17},{... | collective-permute-start | bytes 208904 | tf_op jit(solution)/shard_map/ppermute | solution.py:947
  156.6 3.3 %collective-permute-start.15 = (bf16[272,128]{1,0:T(8,128)(2,1)}, bf16[272,128]{1,0:T(8,128)(2,1)S(1)}, u32[]{:S(2)}, u32[]{:S(2)}) collective-permute-start(bf16[272,128]{1,0:T(8,128)(2,1)} %get-tuple-element.64), channel_id=1, source_target_pairs={{0,24},{4,28},{8,0},{12,4},{16,8},{20,12},{24,16},{28,20},{1,25},{... | collective-permute-start | bytes 208904 | tf_op jit(solution)/shard_map/ppermute | solution.py:947
  160.5 3.9 %reorder.1 = (bf16[12,64,128]{2,1,0:T(8,128)(2,1)}, bf16[12,64,128]{2,1,0:T(8,128)(2,1)}, bf16[12,64,128]{2,1,0:T(8,128)(2,1)}, bf16[12,64,128]{2,1,0:T(8,128)(2...) custom-call(s32[1]{0:T(128)} %bitcast.1.own_ref, ...), custom_call_target="tpu_custom_call" | custom-call | tf_op jit(solution)/shard_map/reorder/pallas_call | solution.py:607
  167.0 2.8 %collective-permute-start.20 = (bf16[12,64,128]{2,1,0:T(8,128)(2,1)}, bf16[12,64,128]{2,1,0:T(8,128)(2,1)}, u32[]{:S(2)}, u32[]{:S(2)}) collective-permute-start(bf16[12,64,128]{2,1,0:T(8,128)(2,1)} %get-tuple-element.71), channel_id=1, source_target_pairs={{0,16},{4,20},{8,24},{12,28},{16,0},{20,4},{24,8},{28,12},{1,17},{... | collective-permute-start | bytes 589832 | tf_op jit(solution)/shard_map/ppermute | solution.py:947
  171.5 3.2 %combine.1 = (bf16[128,1024]{1,0:T(8,128)(2,1)}, bf16[128,1024]{1,0:T(8,128)(2,1)}, bf16[128,1024]{1,0:T(8,128)(2,1)}, bf16[128,1024]{1,0:T(8,128)(2,1)}, f32[1024,128]{1,0:T(8,128)}) custom-call(s32[2]{0:T(128)} %pad_add_fusion.place_ref, f32[4,1024]{1,0:T(4,128)} %get-tuple-element.46.decay_ref, bf16[128,1024]{1,0:T(8,128)(2,1)} %get-tuple-element.89.refs_0_, ...), custom_call_target="tpu_custom_call" | custom-call | tf_op jit(solution)/shard_map/combine/pallas_call | solution.py:713
  176.9 10.4 %collective-permute-done.19.refs_3_ = bf16[12,64,128]{2,1,0:T(8,128)(2,1)S(1)} collective-permute-done((bf16[12,64,128]{2,1,0:T(8,128)(2,1)}, bf16[12,64,128]{2,1,0:T(8,128)(2,1)S(1)}, u32[]{:S(2)}, u32[]{:S(2)}) %collective-permute-start.19) | collective-permute-done | bytes 196640 | tf_op jit(solution)/shard_map/ppermute | solution.py:947
  187.5 6.7 %collective-permute-start.22 = (bf16[12,64,128]{2,1,0:T(8,128)(2,1)}, bf16[12,64,128]{2,1,0:T(8,128)(2,1)S(1)}, u32[]{:S(2)}, u32[]{:S(2)}) collective-permute-start(bf16[12,64,128]{2,1,0:T(8,128)(2,1)} %get-tuple-element.73), channel_id=1, source_target_pairs={{0,24},{4,28},{8,0},{12,4},{16,8},{20,12},{24,16},{28,20},{1,25},{... | collective-permute-start | bytes 589832 | tf_op jit(solution)/shard_map/ppermute | solution.py:947
  194.2 2.2 collective-permute-start.23
  197.0 2.1 settle.1
  199.8 3.7 %collective-permute-done.23.refs_7_ = bf16[12,64,128]{2,1,0:T(8,128)(2,1)S(1)} collective-permute-done((bf16[12,64,128]{2,1,0:T(8,128)(2,1)}, bf16[12,64,128]{2,1,0:T(8,128)(2,1)S(1)}, u32[]{:S(2)}, u32[]{:S(2)}) %collective-permute-start.23) | collective-permute-done | bytes 196640 | tf_op jit(solution)/shard_map/ppermute | solution.py:947
  204.2 6.1 %unpack.1.states_ref = f32[13,8,128,128]{3,2,1,0:T(8,128)} custom-call(s32[1]{0:T(128)} %bitcast.1.own_ref, f32[1024,128]{1,0:T(8,128)} %get-tuple-element.66.final_ref, bf16[12,64,128]{2,1,0:T(8,128)(2,1)} %get-tuple-element.67.refs_0_, bf16[12,64,128]{2,1,0:T(8,128)(2,1)} %copy-done.22, bf16[12,64,128]{2,1,0:T(8,128)(2,1)} %copy-done.23, ...), custom_call_target="tpu_custom_call" | custom-call | tf_op jit(solution)/shard_map/unpack/pallas_call | solution.py:639
  211.2 11.5 %finish.1 = bf16[512,4096]{1,0:T(8,128)(2,1)} custom-call(s32[3]{0:T(128)} %pad_add_fusion.2.place_ref, f32[512,4096]{1,0:T(8,128)} %get-tuple-element.79.part_ref, bf16[512,4096]{1,0:T(8,128)(2,1)} %bitcast.39, bf16[512,128]{1,0:T(8,128)(2,1)} %get-tuple-element.80.read_ref, f32[512,128]{1,0:T(8,128)} %get-tuple-element.81.decay_ref, f32[1,4096]{1,0:T(1,128)} %bitcast.52, ...), custom_call_target="tpu_custom_call" | custom-call | flops 3000000000 | bytes 16000000 | tf_op jit(solution)/shard_map/finish/pallas_call | solution.py:284
  223.9 4.1 %unpack_rest.1 = f32[13,8,128,128]{3,2,1,0:T(8,128)} custom-call(f32[1024,128]{1,0:T(8,128)} %get-tuple-element.66.final_ref, bf16[8,12,64,128]{3,2,1,0:T(8,128)(2,1)} %copy-done, f32[13,8,128,128]{3,2,1,0:T(8,128)} %unpack.1.states_ref), custom_call_target="tpu_custom_call", output_to_operand_aliasing={{}: (2, {})} | custom-call | tf_op jit(solution)/shard_map/unpack_rest/pallas_call | solution.py:666
  (116 shorter events, 31.9 us)
Async XLA Ops:
  3.3 54.6 %copy-start.31 = (f32[64]{0:T(128)S(1)}, f32[64]{0:T(128)}, u32[]{:S(2)}) copy-start(f32[64]{0:T(128)} %param.29) | copy-start | bytes 772
  3.3 55.8 %copy-start.28 = (bf16[1,512,64]{1,2,0:T(8,128)(2,1)S(1)}, bf16[1,512,64]{1,2,0:T(8,128)(2,1)}, u32[]{:S(2)}) copy-start(bf16[1,512,64]{1,2,0:T(8,128)(2,1)} %param.24) | copy-start | bytes 196612
  3.3 51.9 %collective-permute-start.6 = (bf16[13,128,128]{2,1,0:T(8,128)(2,1)}, bf16[13,128,128]{2,1,0:T(8,128)(2,1)S(1)}, u32[]{:S(2)}, u32[]{:S(2)}) collective-permute-start(bf16[13,128,128]{2,1,0:T(8,128)(2,1)} %pack_lead.1), channel_id=1, source_target_pairs={{0,16},{4,20},{8,24},{12,28},{16,0},{20,4},{24,8},{28,12},{1,17},{... | collective-permute-start | bytes 1277960 | tf_op jit(solution)/shard_map/ppermute | solution.py:947
  14.0 41.2 %collective-permute-start.3 = (bf16[13,128,128]{2,1,0:T(8,128)(2,1)}, bf16[13,128,128]{2,1,0:T(8,128)(2,1)S(1)}, u32[]{:S(2)}, u32[]{:S(2)}) collective-permute-start(bf16[13,128,128]{2,1,0:T(8,128)(2,1)} %get-tuple-element.52), channel_id=1, source_target_pairs={{0,4},{4,8},{8,12},{12,16},{16,20},{20,24},{24,28},{28,0},{1,5},{5... | collective-permute-start | bytes 1277960 | tf_op jit(solution)/shard_map/ppermute | solution.py:947
  17.3 43.2 %all-to-all-start = ((bf16[8,32,128]{2,1,0:T(8,128)(2,1)}), bf16[8,32,128]{2,1,0:T(8,128)(2,1)S(1)}, u32[]{:S(2)}, u32[]{:S(2)}) async-start(bf16[8,32,128]{2,1,0:T(8,128)(2,1)} %mark.1), calls=%async_computation | async-start | bytes 131072 | tf_op jit(solution)/shard_map/all_to_all | solution.py:937
  21.8 42.5 %collective-permute-start.4 = (bf16[13,128,128]{2,1,0:T(8,128)(2,1)}, bf16[13,128,128]{2,1,0:T(8,128)(2,1)S(1)}, u32[]{:S(2)}, u32[]{:S(2)}) collective-permute-start(bf16[13,128,128]{2,1,0:T(8,128)(2,1)} %get-tuple-element.53), channel_id=1, source_target_pairs={{0,8},{4,12},{8,16},{12,20},{16,24},{20,28},{24,0},{28,4},{1,9},{5... | collective-permute-start | bytes 1277960 | tf_op jit(solution)/shard_map/ppermute | solution.py:947
  23.8 42.8 %collective-permute-start.5 = (bf16[13,128,128]{2,1,0:T(8,128)(2,1)}, bf16[13,128,128]{2,1,0:T(8,128)(2,1)S(1)}, u32[]{:S(2)}, u32[]{:S(2)}) collective-permute-start(bf16[13,128,128]{2,1,0:T(8,128)(2,1)} %get-tuple-element.54), channel_id=1, source_target_pairs={{0,12},{4,16},{8,20},{12,24},{16,28},{20,0},{24,4},{28,8},{1,13},{... | collective-permute-start | bytes 1277960 | tf_op jit(solution)/shard_map/ppermute | solution.py:947
  26.2 40.4 %collective-permute-start.7 = (bf16[13,128,128]{2,1,0:T(8,128)(2,1)}, bf16[13,128,128]{2,1,0:T(8,128)(2,1)S(1)}, u32[]{:S(2)}, u32[]{:S(2)}) collective-permute-start(bf16[13,128,128]{2,1,0:T(8,128)(2,1)} %get-tuple-element.55), channel_id=1, source_target_pairs={{0,20},{4,24},{8,28},{12,0},{16,4},{20,8},{24,12},{28,16},{1,21},{... | collective-permute-start | bytes 1277960 | tf_op jit(solution)/shard_map/ppermute | solution.py:947
  55.2 18.4 %collective-permute-start.8 = (bf16[13,128,128]{2,1,0:T(8,128)(2,1)}, bf16[13,128,128]{2,1,0:T(8,128)(2,1)S(1)}, u32[]{:S(2)}, u32[]{:S(2)}) collective-permute-start(bf16[13,128,128]{2,1,0:T(8,128)(2,1)} %get-tuple-element.56), channel_id=1, source_target_pairs={{0,24},{4,28},{8,0},{12,4},{16,8},{20,12},{24,16},{28,20},{1,25},{... | collective-permute-start | bytes 1277960 | tf_op jit(solution)/shard_map/ppermute | solution.py:947
  55.2 18.9 %collective-permute-start.9 = (bf16[13,128,128]{2,1,0:T(8,128)(2,1)}, bf16[13,128,128]{2,1,0:T(8,128)(2,1)S(1)}, u32[]{:S(2)}, u32[]{:S(2)}) collective-permute-start(bf16[13,128,128]{2,1,0:T(8,128)(2,1)} %get-tuple-element.57), channel_id=1, source_target_pairs={{0,28},{4,0},{8,4},{12,8},{16,12},{20,16},{24,20},{28,24},{1,29},{... | collective-permute-start | bytes 1277960 | tf_op jit(solution)/shard_map/ppermute | solution.py:947
  64.2 30.8 %copy-start.27 = (bf16[3,10112]{1,0:T(4,128)(2,1)S(1)}, bf16[3,10112]{1,0:T(4,128)(2,1)}, u32[]{:S(2)}) copy-start(bf16[3,10112]{1,0:T(4,128)(2,1)} %get-tuple-element.45) | copy-start | bytes 182020
  78.7 144.0 %all-to-all-start.1 = ((bf16[8,12,64,128]{3,2,1,0:T(8,128)(2,1)}), bf16[8,12,64,128]{3,2,1,0:T(8,128)(2,1)S(1)}, u32[]{:S(2)}, u32[]{:S(2)}) async-start(bf16[8,12,64,128]{3,2,1,0:T(8,128)(2,1)} %reorder_rest.1), calls=%async_computation.1 | async-start | bytes 3145728 | tf_op jit(solution)/shard_map/all_to_all | solution.py:937
  137.9 10.1 %collective-permute-start.2 = (bf16[128,1024]{1,0:T(8,128)(2,1)S(1)}, bf16[128,1024]{1,0:T(8,128)(2,1)S(1)}, u32[]{:S(2)}, u32[]{:S(2)}) collective-permute-start(bf16[128,1024]{1,0:T(8,128)(2,1)S(1)} %get-tuple-element.86), channel_id=1, source_target_pairs={{0,3},{1,0},{2,1},{3,2},{4,7},{5,4},{6,5},{7,6},{8,11},{9,8},{10,9... | collective-permute-start | bytes 786440 | tf_op jit(solution)/shard_map/ppermute | solution.py:947
  139.2 13.0 %collective-permute-start.1 = (bf16[128,1024]{1,0:T(8,128)(2,1)S(1)}, bf16[128,1024]{1,0:T(8,128)(2,1)S(1)}, u32[]{:S(2)}, u32[]{:S(2)}) collective-permute-start(bf16[128,1024]{1,0:T(8,128)(2,1)S(1)} %get-tuple-element.87), channel_id=1, source_target_pairs={{0,2},{1,3},{2,0},{3,1},{4,6},{5,7},{6,4},{7,5},{8,10},{9,11},{10,... | collective-permute-start | bytes 786440 | tf_op jit(solution)/shard_map/ppermute | solution.py:947
  139.9 15.3 %collective-permute-start = (bf16[128,1024]{1,0:T(8,128)(2,1)S(1)}, bf16[128,1024]{1,0:T(8,128)(2,1)S(1)}, u32[]{:S(2)}, u32[]{:S(2)}) collective-permute-start(bf16[128,1024]{1,0:T(8,128)(2,1)S(1)} %get-tuple-element.88), channel_id=1, source_target_pairs={{0,1},{1,2},{2,3},{3,0},{4,5},{5,6},{6,7},{7,4},{8,9},{9,10},{10,1... | collective-permute-start | bytes 786440 | tf_op jit(solution)/shard_map/ppermute | solution.py:947
  144.5 12.1 %collective-permute-start.10 = (bf16[272,128]{1,0:T(8,128)(2,1)}, bf16[272,128]{1,0:T(8,128)(2,1)S(1)}, u32[]{:S(2)}, u32[]{:S(2)}) collective-permute-start(bf16[272,128]{1,0:T(8,128)(2,1)} %get-tuple-element.59), channel_id=1, source_target_pairs={{0,4},{4,8},{8,12},{12,16},{16,20},{20,24},{24,28},{28,0},{1,5},{5... | collective-permute-start | bytes 208904 | tf_op jit(solution)/shard_map/ppermute | solution.py:947
  146.6 13.3 %collective-permute-start.11 = (bf16[272,128]{1,0:T(8,128)(2,1)}, bf16[272,128]{1,0:T(8,128)(2,1)S(1)}, u32[]{:S(2)}, u32[]{:S(2)}) collective-permute-start(bf16[272,128]{1,0:T(8,128)(2,1)} %get-tuple-element.60), channel_id=1, source_target_pairs={{0,8},{4,12},{8,16},{12,20},{16,24},{20,28},{24,0},{28,4},{1,9},{5... | collective-permute-start | bytes 208904 | tf_op jit(solution)/shard_map/ppermute | solution.py:947
  148.0 16.3 %collective-permute-start.12 = (bf16[272,128]{1,0:T(8,128)(2,1)}, bf16[272,128]{1,0:T(8,128)(2,1)S(1)}, u32[]{:S(2)}, u32[]{:S(2)}) collective-permute-start(bf16[272,128]{1,0:T(8,128)(2,1)} %get-tuple-element.61), channel_id=1, source_target_pairs={{0,12},{4,16},{8,20},{12,24},{16,28},{20,0},{24,4},{28,8},{1,13},{... | collective-permute-start | bytes 208904 | tf_op jit(solution)/shard_map/ppermute | solution.py:947
  152.2 13.7 %collective-permute-start.13 = (bf16[272,128]{1,0:T(8,128)(2,1)}, bf16[272,128]{1,0:T(8,128)(2,1)S(1)}, u32[]{:S(2)}, u32[]{:S(2)}) collective-permute-start(bf16[272,128]{1,0:T(8,128)(2,1)} %get-tuple-element.62), channel_id=1, source_target_pairs={{0,16},{4,20},{8,24},{12,28},{16,0},{20,4},{24,8},{28,12},{1,17},{... | collective-permute-start | bytes 208904 | tf_op jit(solution)/shard_map/ppermute | solution.py:947
  155.2 10.8 %collective-permute-start.14 = (bf16[272,128]{1,0:T(8,128)(2,1)}, bf16[272,128]{1,0:T(8,128)(2,1)S(1)}, u32[]{:S(2)}, u32[]{:S(2)}) collective-permute-start(bf16[272,128]{1,0:T(8,128)(2,1)} %get-tuple-element.63), channel_id=1, source_target_pairs={{0,20},{4,24},{8,28},{12,0},{16,4},{20,8},{24,12},{28,16},{1,21},{... | collective-permute-start | bytes 208904 | tf_op jit(solution)/shard_map/ppermute | solution.py:947
  156.6 10.4 %collective-permute-start.15 = (bf16[272,128]{1,0:T(8,128)(2,1)}, bf16[272,128]{1,0:T(8,128)(2,1)S(1)}, u32[]{:S(2)}, u32[]{:S(2)}) collective-permute-start(bf16[272,128]{1,0:T(8,128)(2,1)} %get-tuple-element.64), channel_id=1, source_target_pairs={{0,24},{4,28},{8,0},{12,4},{16,8},{20,12},{24,16},{28,20},{1,25},{... | collective-permute-start | bytes 208904 | tf_op jit(solution)/shard_map/ppermute | solution.py:947
  159.9 9.9 %collective-permute-start.16 = (bf16[272,128]{1,0:T(8,128)(2,1)}, bf16[272,128]{1,0:T(8,128)(2,1)S(1)}, u32[]{:S(2)}, u32[]{:S(2)}) collective-permute-start(bf16[272,128]{1,0:T(8,128)(2,1)} %get-tuple-element.65), channel_id=1, source_target_pairs={{0,28},{4,0},{8,4},{12,8},{16,12},{20,16},{24,20},{28,24},{1,29},{... | collective-permute-start | bytes 208904 | tf_op jit(solution)/shard_map/ppermute | solution.py:947
  164.4 10.8 %collective-permute-start.17 = (bf16[12,64,128]{2,1,0:T(8,128)(2,1)}, bf16[12,64,128]{2,1,0:T(8,128)(2,1)S(1)}, u32[]{:S(2)}, u32[]{:S(2)}) collective-permute-start(bf16[12,64,128]{2,1,0:T(8,128)(2,1)} %get-tuple-element.68), channel_id=1, source_target_pairs={{0,4},{4,8},{8,12},{12,16},{16,20},{20,24},{24,28},{28,0},{1,5},{5... | collective-permute-start | bytes 589832 | tf_op jit(solution)/shard_map/ppermute | solution.py:947
  165.9 9.8 %collective-permute-start.18 = (bf16[12,64,128]{2,1,0:T(8,128)(2,1)}, bf16[12,64,128]{2,1,0:T(8,128)(2,1)S(1)}, u32[]{:S(2)}, u32[]{:S(2)}) collective-permute-start(bf16[12,64,128]{2,1,0:T(8,128)(2,1)} %get-tuple-element.69), channel_id=1, source_target_pairs={{0,8},{4,12},{8,16},{12,20},{16,24},{20,28},{24,0},{28,4},{1,9},{5... | collective-permute-start | bytes 589832 | tf_op jit(solution)/shard_map/ppermute | solution.py:947
  165.9 21.4 %collective-permute-start.19 = (bf16[12,64,128]{2,1,0:T(8,128)(2,1)}, bf16[12,64,128]{2,1,0:T(8,128)(2,1)S(1)}, u32[]{:S(2)}, u32[]{:S(2)}) collective-permute-start(bf16[12,64,128]{2,1,0:T(8,128)(2,1)} %get-tuple-element.70), channel_id=1, source_target_pairs={{0,12},{4,16},{8,20},{12,24},{16,28},{20,0},{24,4},{28,8},{1,13},{... | collective-permute-start | bytes 589832 | tf_op jit(solution)/shard_map/ppermute | solution.py:947
  167.0 20.5 %collective-permute-start.20 = (bf16[12,64,128]{2,1,0:T(8,128)(2,1)}, bf16[12,64,128]{2,1,0:T(8,128)(2,1)}, u32[]{:S(2)}, u32[]{:S(2)}) collective-permute-start(bf16[12,64,128]{2,1,0:T(8,128)(2,1)} %get-tuple-element.71), channel_id=1, source_target_pairs={{0,16},{4,20},{8,24},{12,28},{16,0},{20,4},{24,8},{28,12},{1,17},{... | collective-permute-start | bytes 589832 | tf_op jit(solution)/shard_map/ppermute | solution.py:947
  169.8 24.4 %collective-permute-start.21 = (bf16[12,64,128]{2,1,0:T(8,128)(2,1)}, bf16[12,64,128]{2,1,0:T(8,128)(2,1)}, u32[]{:S(2)}, u32[]{:S(2)}) collective-permute-start(bf16[12,64,128]{2,1,0:T(8,128)(2,1)} %get-tuple-element.72), channel_id=1, source_target_pairs={{0,20},{4,24},{8,28},{12,0},{16,4},{20,8},{24,12},{28,16},{1,21},{... | collective-permute-start | bytes 589832 | tf_op jit(solution)/shard_map/ppermute | solution.py:947
  175.2 35.1 %collective-permute-start.24 = (bf16[128,1024]{1,0:T(8,128)(2,1)}, bf16[128,1024]{1,0:T(8,128)(2,1)S(1)}, u32[]{:S(2)}, u32[]{:S(2)}) collective-permute-start(bf16[128,1024]{1,0:T(8,128)(2,1)} %get-tuple-element.83), channel_id=1, source_target_pairs={{0,1},{1,2},{2,3},{3,0},{4,5},{5,6},{6,7},{7,4},{8,9},{9,10},{10,1... | collective-permute-start | bytes 786440 | tf_op jit(solution)/shard_map/ppermute | solution.py:947
  175.7 34.5 %collective-permute-start.25 = (bf16[128,1024]{1,0:T(8,128)(2,1)}, bf16[128,1024]{1,0:T(8,128)(2,1)S(1)}, u32[]{:S(2)}, u32[]{:S(2)}) collective-permute-start(bf16[128,1024]{1,0:T(8,128)(2,1)} %get-tuple-element.84), channel_id=1, source_target_pairs={{0,2},{1,3},{2,0},{3,1},{4,6},{5,7},{6,4},{7,5},{8,10},{9,11},{10,... | collective-permute-start | bytes 786440 | tf_op jit(solution)/shard_map/ppermute | solution.py:947
  187.3 23.0 %collective-permute-start.26 = (bf16[128,1024]{1,0:T(8,128)(2,1)}, bf16[128,1024]{1,0:T(8,128)(2,1)S(1)}, u32[]{:S(2)}, u32[]{:S(2)}) collective-permute-start(bf16[128,1024]{1,0:T(8,128)(2,1)} %get-tuple-element.85), channel_id=1, source_target_pairs={{0,3},{1,0},{2,1},{3,2},{4,7},{5,4},{6,5},{7,6},{8,11},{9,8},{10,9... | collective-permute-start | bytes 786440 | tf_op jit(solution)/shard_map/ppermute | solution.py:947
  187.5 12.3 %collective-permute-start.22 = (bf16[12,64,128]{2,1,0:T(8,128)(2,1)}, bf16[12,64,128]{2,1,0:T(8,128)(2,1)S(1)}, u32[]{:S(2)}, u32[]{:S(2)}) collective-permute-start(bf16[12,64,128]{2,1,0:T(8,128)(2,1)} %get-tuple-element.73), channel_id=1, source_target_pairs={{0,24},{4,28},{8,0},{12,4},{16,8},{20,12},{24,16},{28,20},{1,25},{... | collective-permute-start | bytes 589832 | tf_op jit(solution)/shard_map/ppermute | solution.py:947
  194.2 9.3 %collective-permute-start.23 = (bf16[12,64,128]{2,1,0:T(8,128)(2,1)}, bf16[12,64,128]{2,1,0:T(8,128)(2,1)S(1)}, u32[]{:S(2)}, u32[]{:S(2)}) collective-permute-start(bf16[12,64,128]{2,1,0:T(8,128)(2,1)} %get-tuple-element.74), channel_id=1, source_target_pairs={{0,28},{4,0},{8,4},{12,8},{16,12},{20,16},{24,20},{28,24},{1,29},{... | collective-permute-start | bytes 589832 | tf_op jit(solution)/shard_map/ppermute | solution.py:947
  (29 other events, 294.6 us)
